TPU v7x, 256 devices: a whole 4x4x8 slice. The times are simulated.
256 devices in a mesh: img: 8 (over y, x_lo), cls: 8 (over z), emb: 4 (over x_hi, core).
Axes of the slice: x: 4 (x_hi: 2, x_lo: 2; x = x_hi * 2 + x_lo), y: 4, z: 8, core: 2. Of those that a mesh axis runs over, the one named last changes fastest.
Arguments:
- regions: bfloat16 [8192, 1024], P('img', 'emb'), may hold values from -8 to 8
- table: bfloat16 [21504, 1024], P('cls', 'emb'), may hold values from -1 to 1
- shift: float32 [8192], P('img'), may hold values from -0.5 to 0.1
- scale: float32 [8192], P('img'), may hold values from 2 to 20
- labels: int32 [8192], P('img'), may hold values from -1 to 21503, as said below
- valid: int32 [16, 21504], P('img', 'cls'), may hold values 0 or 1
Outputs:
- loss: float32 [], replicated
- region_grad: bfloat16 [8192, 1024], P('img', 'emb')
- table_grad: bfloat16 [21504, 1024], P('cls', 'emb')
Inputs may be any that keep to these rules, and one draw needn't show every extreme that they name: `labels`: -1 marks background; the first region of every image is foreground.
All inputs are finite; a program needn't handle non-finite values. No bound on the sum of `valid` on one device may be relied on, other than what follows from the above.
Results may differ from a plain program's by a relative error of at most 0.0034.
Values may be sent and summed in bfloat16 or wider, within the bound.
No kernel may reach another device: no remote copies, remote signals or barrier semaphores. Data moves between devices by JAX's collectives and lax.ppermute only.
A program may use at most 64 MiB of HBM per device.

v0:
```python
import jax
import jax.numpy as jnp
from jax import lax
from jax.experimental import pallas as pl
from jax.experimental.pallas import tpu as pltpu
from jax.sharding import Mesh
from jax.sharding import PartitionSpec as P

CLASSES = 21504
REGIONS = 8192
EMB = ("emb_0", "emb_1")
IMG = ("img_0", "img_1")
CLS = ("cls",)
CLS_EMB = CLS + EMB[:1]
F32 = jnp.float32
BF16 = jnp.bfloat16
NT = (((1,), (1,)), ((), ()))
TN = (((0,), (0,)), ((), ()))

K, BASE, E, Y, XL, Z = range(6)


PART = 336


def vmem(n):
    return [pl.BlockSpec(memory_space=pltpu.VMEM)] * n


def in_hbm(shape, dtype):
    return pltpu.HBM(shape, dtype)


def smem():
    return pl.BlockSpec(memory_space=pltpu.SMEM)


def params(mebibytes=16):
    return pltpu.CompilerParams(vmem_limit_bytes=mebibytes * 1024 * 1024)


def cost(flops):
    return pl.CostEstimate(flops=int(flops), bytes_accessed=1 << 20, transcendentals=0)


def swap(x, axis):
    return lax.ppermute(x, axis, [(0, 1), (1, 0)])


def split3(value, width):
    hi = value.astype(BF16).astype(F32)
    mid = (value - hi).astype(BF16).astype(F32)
    lo = value - hi - mid
    lane = lax.broadcasted_iota(jnp.int32, (8, width), 1)
    row = lax.broadcasted_iota(jnp.int32, (8, width), 0)
    packed = jnp.where(lane == 0, hi, jnp.where(lane == 1, mid, jnp.where(lane == 2, lo, 0.0)))
    return jnp.where(row == 0, packed, 0.0)


def unit_kernel(a, b, c, d, out, scale):
    blocks = [r[...].astype(F32) for r in (a, b, c, d)]
    squares = sum(jnp.sum(v * v, axis=1, keepdims=True) for v in blocks)
    inv = lax.rsqrt(squares + 1e-06)
    scale[...] = jnp.broadcast_to(inv, scale.shape)
    for q, v in enumerate(blocks):
        out[:, 256 * q : 256 * q + 256] = (v * inv).astype(BF16)


def make_unit(blocks):
    rows = blocks[0].shape[0]
    tile = 256
    return pl.pallas_call(
        unit_kernel,
        grid=(rows // tile,),
        in_specs=[pl.BlockSpec((tile, 256), lambda i: (i, 0))] * 4,
        out_specs=[
            pl.BlockSpec((tile, 1024), lambda i: (i, 0)),
            pl.BlockSpec((tile, 128), lambda i: (i, 0)),
        ],
        out_shape=[
            jax.ShapeDtypeStruct((rows, 1024), BF16),
            jax.ShapeDtypeStruct((rows, 128), F32),
        ],
        compiler_params=params(),
        cost_estimate=cost(2e7),
        name="unit",
    )(*blocks)


def rows_kernel(s, x, out):
    out[...] = x[...]


def take_rows(x, at, rows):
    return pl.pallas_call(
        rows_kernel,
        grid_spec=pltpu.PrefetchScalarGridSpec(
            num_scalar_prefetch=1,
            grid=(1,),
            in_specs=[pl.BlockSpec((rows, 256), lambda i, s: (s[0], 0))],
            out_specs=pl.BlockSpec((rows, 256), lambda i, s: (0, 0)),
        ),
        out_shape=jax.ShapeDtypeStruct((rows, 256), BF16),
        compiler_params=params(),
        name="rows",
    )(at.reshape(1), x)


def message_kernel(part, mine, theirs, out):
    count = mine[...] + theirs[...]
    high = jnp.floor(count / 32.0)
    lane = lax.broadcasted_iota(jnp.int32, (8, 128), 1)
    extra = jnp.where(lane == 0, high, jnp.where(lane == 1, count - 32.0 * high, 0.0))
    extra = jnp.concatenate([extra, jnp.zeros((8, 128), F32)], axis=1).astype(BF16)
    for y in range(4):
        out[y, 0:PART, :] = part[...]
        out[y, PART : PART + 8, :] = extra


def make_message(part, mine, theirs):
    return pl.pallas_call(
        message_kernel,
        in_specs=vmem(3),
        out_specs=vmem(1)[0],
        out_shape=in_hbm((4, PART + 8, 256), BF16),
        compiler_params=params(),
        name="message",
    )(part, mine, theirs)


def read_count(far):
    lane = lax.broadcasted_iota(jnp.int32, (1, 256), 1)
    row = sum(far[y, PART : PART + 8, :].astype(F32)[0:1, :] for y in range(4))
    return jnp.sum(jnp.where(lane == 0, 32.0 * row, jnp.where(lane == 1, row, 0.0)))


def focal_kernel(s, t0, t1, t2, t3, unit, lane_f, labels, mask, keep, send, loss, count_out, acc):
    rows = unit.shape[0]
    half = keep.shape[0]
    count = read_count(t2)
    count_out[0, 0] = count
    u = [unit[:, 256 * q : 256 * q + 256] for q in range(4)]

    def dot(t, q):
        return lax.dot_general(t, u[q], NT, preferred_element_type=F32)

    for c in range(4):
        at = slice(PART * c, PART * c + PART)
        acc[at, :] = (
            dot(t0[at, :], 0) + dot(t1[at, :], 1) + dot(t2[c, 0:PART, :], 2) + dot(t3[c, 0:PART, :], 3)
        )
    shift = lane_f[0:1, :]
    scale = lane_f[1:2, :]
    factor = scale * (REGIONS / count)
    step = 32

    def part(out, start, total):
        wanted = labels[...] - (s[BASE] + start)

        def body(g, total):
            to = pl.multiple_of(g * step, step)
            at = pl.multiple_of(start + to, step)
            logit = (acc[pl.ds(at, step), :] + shift) * scale
            ids = lax.broadcasted_iota(jnp.int32, (step, rows), 0)
            target = (wanted - to) == ids
            m = jnp.where(target, -logit, logit)
            e = jnp.exp(-jnp.abs(m))
            r = 1.0 / (1.0 + e)
            er = e * r
            positive = m >= 0.0
            prob = jnp.where(positive, r, er)
            rest = jnp.where(positive, er, r)
            series = e * (1.0 - e * (0.5 - e * (1.0 / 3.0 - e * 0.25)))
            soft = jnp.maximum(m, 0.0) + jnp.where(e < 2e-3, series, jnp.log(1.0 + e))
            weight = jnp.where(target, 0.25, 0.75) * mask[pl.ds(at, step), :] * (prob * prob)
            slope = weight * (2.0 * rest * soft + prob)
            slope = jnp.where(target, -slope, slope)
            out[pl.ds(to, step), :] = (slope * factor).astype(BF16)
            term = weight * soft
            return total + sum(term[8 * i : 8 * i + 8, :] for i in range(step // 8))

        return lax.fori_loop(0, half // step, body, total)

    total = part(send, (1 - s[K]) * half, jnp.zeros((8, rows), F32))
    total = part(keep, s[K] * half, total)
    loss[...] = sum(total[:, 128 * i : 128 * i + 128] for i in range(4))


def make_focal(scalars, tables, unit, lane_f, labels, mask):
    rows = unit.shape[0] // 2
    classes = mask.shape[0]
    whole = lambda i, s: (0, 0)
    cube = lambda i, s: (0, 0, 0)
    return pl.pallas_call(
        focal_kernel,
        grid_spec=pltpu.PrefetchScalarGridSpec(
            num_scalar_prefetch=1,
            grid=(1,),
            in_specs=[pl.BlockSpec((classes, 256), whole)] * 2
            + [pl.BlockSpec((4, PART + 8, 256), cube)] * 2
            + [
                pl.BlockSpec((rows, 1024), lambda i, s: (s[K], 0)),
                pl.BlockSpec((8, rows), lambda i, s: (0, s[K])),
                pl.BlockSpec((1, rows), lambda i, s: (0, s[K])),
                pl.BlockSpec((classes, 1), whole),
            ],
            out_specs=[
                pl.BlockSpec((classes // 2, rows), whole),
                pl.BlockSpec((classes // 2, rows), whole),
                pl.BlockSpec((8, 128), whole),
                smem(),
            ],
            scratch_shapes=[pltpu.VMEM((classes, rows), F32)],
        ),
        out_shape=[
            jax.ShapeDtypeStruct((classes // 2, rows), BF16),
            jax.ShapeDtypeStruct((classes // 2, rows), BF16),
            jax.ShapeDtypeStruct((8, 128), F32),
            jax.ShapeDtypeStruct((1, 1), F32),
        ],
        compiler_params=params(24),
        cost_estimate=cost(1.4e9),
        name="focal",
    )(scalars, *tables, unit, lane_f, labels, mask)


def region_kernel(s, keep, send, k0, k1, k2, k3, o0, o1, o2, o3, a, b, c, d, inv_ref, out, acc):
    inv = inv_ref[:, 0:1]
    mine = keep[...]
    theirs = send[...]

    def dot(g, t):
        return lax.dot_general(g, t, TN, preferred_element_type=F32)

    along = 0.0
    rows = (a, b, c, d)
    for q, (t, o) in enumerate(zip((k0, k1, k2, k3), (o0, o1, o2, o3))):
        if q < 2:
            part = dot(mine, t[...]) + dot(theirs, o[...])
        else:
            part = sum(
                dot(g[PART * i : PART * i + PART, :], x[i, 0:PART, :])
                for g, x in ((mine, t), (theirs, o))
                for i in range(2)
            )
        acc[:, 256 * q : 256 * q + 256] = part
        along += jnp.sum(part * rows[q][...].astype(F32), axis=1, keepdims=True)
    back = inv * inv * along
    for q, r in enumerate(rows):
        grad = inv * (acc[:, 256 * q : 256 * q + 256] - r[...].astype(F32) * back)
        to = s[E] ^ q
        for i in range(out.shape[0]):
            out[i, to] = grad[64 * i : 64 * i + 64, :].astype(BF16)


def make_region(scalars, keep, send, tables, blocks, inv):
    half, rows = keep.shape
    tile = 256
    steps = rows // tile
    flat = lambda f: pl.BlockSpec((half, 256), lambda i, s: (f(s), 0))
    cube = lambda f: pl.BlockSpec((2, PART + 8, 256), lambda i, s: (f(s), 0, 0))
    own = lambda s: s[K]
    other = lambda s: 1 - s[K]
    return pl.pallas_call(
        region_kernel,
        grid_spec=pltpu.PrefetchScalarGridSpec(
            num_scalar_prefetch=1,
            grid=(steps,),
            in_specs=[pl.BlockSpec((half, tile), lambda i, s: (0, i))] * 2
            + [flat(own)] * 2
            + [cube(own)] * 2
            + [flat(other)] * 2
            + [cube(other)] * 2
            + [pl.BlockSpec((tile, 256), lambda i, s: (s[K] * steps + i, 0))] * 4
            + [pl.BlockSpec((tile, 128), lambda i, s: (s[K] * steps + i, 0))],
            out_specs=pl.BlockSpec((tile // 64, 4, 64, 256), lambda i, s: (i, 0, 0, 0)),
            scratch_shapes=[pltpu.VMEM((tile, 1024), F32)],
        ),
        out_shape=in_hbm((8, 4, 64, 256), BF16),
        compiler_params=params(),
        cost_estimate=cost(1.4e9),
        name="region",
    )(scalars, keep, send, *tables, *tables, *blocks, inv)


def table_kernel(s, keep, other, unit, l0, l1, l2, l3, *refs):
    outs, acc = refs[:8], refs[8]
    half, rows = other.shape
    mine = keep[...]
    theirs = other[...]
    mine_at = pl.multiple_of(s[K] * rows, rows)
    theirs_at = pl.multiple_of((1 - s[K]) * rows, rows)
    loss = jnp.sum(l0[...] + l1[...] + l2[...] + l3[...])
    extra = split3(loss, 128).astype(BF16)
    for dy in range(4):
        cols = pl.ds(pl.multiple_of(256 * ((s[Y] + dy) % 4), 256), 256)
        acc[...] = jnp.dot(
            mine, unit[pl.ds(mine_at, rows), cols], preferred_element_type=F32
        ) + jnp.dot(theirs, unit[pl.ds(theirs_at, rows), cols], preferred_element_type=F32)
        for dx in range(2):
            at = pl.multiple_of(128 * (s[XL] ^ dx), 128)
            out = outs[2 * dy + dx]
            out[0:half, :] = acc[:, pl.ds(at, 128)].astype(BF16)
            out[half : half + 8, :] = extra


def make_table(scalars, keep, other, unit, losses):
    half = other.shape[0]
    return pl.pallas_call(
        table_kernel,
        in_specs=[smem()] + vmem(7),
        out_specs=vmem(8),
        out_shape=[jax.ShapeDtypeStruct((half + 8, 128), BF16)] * 8,
        scratch_shapes=[pltpu.VMEM((half, 256), F32)],
        compiler_params=params(),
        cost_estimate=cost(1.4e9),
        name="table",
    )(scalars, keep, other, unit, *losses)


def table_sum_kernel(*refs):
    terms, (out, loss) = refs[:8], refs[8:]
    half = out.shape[1]
    total = sum(t[0:half, :].astype(F32) for t in terms).astype(BF16)
    for j in range(8):
        out[j] = total
    loss[...] = sum(t[half : half + 8, :].astype(F32) for t in terms)


def make_table_sum(terms):
    half = terms[0].shape[0] - 8
    return pl.pallas_call(
        table_sum_kernel,
        in_specs=vmem(8),
        out_specs=vmem(2),
        out_shape=[in_hbm((8, half, 128), BF16), jax.ShapeDtypeStruct((8, 128), F32)],
        compiler_params=params(),
        cost_estimate=cost(1e7),
        name="table_sum",
    )(*terms)


def region_sum_kernel(s, pieces, mine, theirs):
    totals = [
        sum(pieces[z, x, k].astype(F32) for z in range(8) for x in range(2)) for k in range(2)
    ]
    first = s[K] == 0
    mine[...] = jnp.where(first, totals[0], totals[1]).astype(BF16)
    theirs[...] = jnp.where(first, totals[1], totals[0]).astype(BF16)


def make_region_sum(scalars, pieces):
    return pl.pallas_call(
        region_sum_kernel,
        in_specs=[smem()] + vmem(1),
        out_specs=vmem(2),
        out_shape=[jax.ShapeDtypeStruct((64, 256), BF16)] * 2,
        compiler_params=params(),
        cost_estimate=cost(1e7),
        name="region_sum",
    )(scalars, pieces)


def share_kernel(s, mine, other, loss, out):
    out[pl.ds(pl.multiple_of(64 * s[K], 64), 64), :] = mine[...]
    out[pl.ds(pl.multiple_of(64 * (1 - s[K]), 64), 64), :] = other[...]
    out[128:136, :] = split3(jnp.sum(loss[...]), 256).astype(BF16)


def make_share(scalars, mine, other, loss):
    return pl.pallas_call(
        share_kernel,
        in_specs=[smem()] + vmem(3),
        out_specs=vmem(1)[0],
        out_shape=jax.ShapeDtypeStruct((136, 256), BF16),
        compiler_params=params(),
        cost_estimate=cost(1e7),
        name="share",
    )(scalars, mine, other, loss)


def final_kernel(s, count, tables, *refs):
    regions, (region_out, table_out, loss_out) = refs[:8], refs[8:]
    total = 0.0
    for d in range(8):
        source = (s[Z] + 8 - d) % 8
        for k in range(2):
            region_out[k, source] = regions[d][64 * k : 64 * k + 64, :]
        total += jnp.sum(regions[d][128:136, :].astype(F32))
    loss_out[0, 0] = total / count[0, 0] / CLASSES
    for y in range(4):
        at = pl.multiple_of(672 * (s[E] ^ y), 32)
        for x in range(2):
            table_out[pl.ds(at, 672), 128 * x : 128 * x + 128] = tables[2 * y + x]


def make_final(scalars, count, tables, regions):
    return pl.pallas_call(
        final_kernel,
        in_specs=[smem(), smem()] + vmem(9),
        out_specs=vmem(2) + [smem()],
        out_shape=[
            jax.ShapeDtypeStruct((2, 8, 64, 256), BF16),
            jax.ShapeDtypeStruct((2688, 256), BF16),
            jax.ShapeDtypeStruct((1, 1), F32),
        ],
        compiler_params=params(),
        cost_estimate=cost(1e7),
        name="final",
    )(scalars, count, tables, *regions)


def to_owner(x, dy, dx):
    pairs = []
    for y in range(4):
        for xl in range(2):
            for e in range(4):
                to = (y + dy) % 4
                pairs.append((8 * y + 4 * xl + e, 8 * to + 4 * (xl ^ dx) + (e ^ to)))
    return lax.ppermute(x, IMG + EMB, pairs)


def along_cls(x, d):
    return lax.ppermute(x, CLS, [(i, (i + d) % 8) for i in range(8)])


def exchange(x, axes):
    return lax.all_to_all(x, axes, split_axis=0, concat_axis=0, tiled=True)


def shards(regions, table, shift, scale, labels, valid):
    rows = regions.shape[0]
    y = lax.axis_index("img_0")
    xl = lax.axis_index("img_1")
    xh = lax.axis_index("emb_0")
    k = lax.axis_index("emb_1")
    z = lax.axis_index(CLS)
    scalars = jnp.stack([k, z * 2688 + xh * 1344, 2 * xh + k, y, xl, z]).astype(jnp.int32)

    t_send = take_rows(pltpu.with_memory_space_constraint(table, pltpu.HBM), 4 * (1 - xh) + y, PART)
    t_send, regions_in = lax.optimization_barrier((t_send, regions))
    t_got = swap(t_send, "emb_0")
    r_far = swap(regions_in, "emb_0")
    r_near = swap(regions_in, "emb_1")
    local = jnp.broadcast_to(jnp.sum((labels >= 0).astype(F32)), (8, 128))
    t_far = exchange(make_message(t_got, local, swap(local, "img_1")), "img_0")
    t_own = lax.dynamic_slice_in_dim(table, xh * 1344, 1344, 0)
    t_near = swap(t_own, "emb_1")
    r_both = swap(r_far, "emb_1")
    t_both = swap(t_far, "emb_1")
    blocks = (regions, r_near, r_far, r_both)
    tables = (t_own, t_near, t_far, t_both)
    unit, inv = make_unit(blocks)

    lane_f = jnp.concatenate([shift[None], scale[None], jnp.zeros((6, rows), F32)], axis=0)
    mask = lax.dynamic_slice(valid, (k, xh * 1344), (1, 1344)).astype(F32).T
    keep, send, loss, count = make_focal(scalars, tables, unit, lane_f, labels[None], mask)

    theirs = swap(send, "emb_1")
    loss_0 = swap(loss, "emb_0")
    loss_1 = swap(loss, "emb_1")
    loss_2 = lax.ppermute(loss, EMB, [(i, i ^ 3) for i in range(4)])
    terms = make_region(scalars, keep, send, tables, blocks, inv)
    pieces = exchange(terms.reshape(16, 128, 256), CLS_EMB).reshape(8, 2, 2, 64, 256)
    chunks = make_table(scalars, keep, theirs, unit, [loss, loss_0, loss_1, loss_2])
    chunks = [to_owner(chunks[o], o // 2, o % 2) for o in range(8)]
    table_part, loss_part = make_table_sum(chunks)
    mine, other = make_region_sum(scalars, pieces)
    share = make_share(scalars, mine, swap(other, "emb_1"), loss_part)
    table_part, share = lax.optimization_barrier((table_part, share))
    table_all = exchange(table_part, IMG)
    shares = [share] + [along_cls(share, d) for d in range(1, 8)]
    region_grad, table_grad, total = make_final(scalars, count, table_all, shares)
    return (total[0, 0], region_grad.reshape(rows, 256), table_grad)


def solution(mesh):
    torus = Mesh(
        mesh.devices.reshape(4, 2, mesh.shape["cls"], 2, 2),
        ("img_0", "img_1", "cls", "emb_0", "emb_1"),
    )
    return jax.shard_map(
        shards,
        mesh=torus,
        in_specs=(P(IMG, EMB), P(CLS, EMB), P(IMG), P(IMG), P(IMG), P(IMG, CLS)),
        out_specs=(P(), P(IMG, EMB), P(CLS, EMB)),
        check_vma=False,
    )
```

profile of v0, /device:TPU:1, one launch (start us, length us, event | category | flops | bytes accessed | tf_op | source)
XLA Modules:
  0.0 141.9 jit_solution(11555879004345295578)
XLA Ops:
  1.6 3.6 %collective-permute-start.1 = (bf16[336,256]{1,0:T(8,128)(2,1)S(1)}, bf16[336,256]{1,0:T(8,128)(2,1)S(1)}, u32[]{:S(2)}, u32[]{:S(2)}) collective-permute-start(bf16[336,256]{1,0:T(8,128)(2,1)S(1)} %rows.1), channel_id=1, source_target_pairs={{0,2},{2,0},{1,3},{3,1},{4,6},{6,4},{5,7},{7,5},{8,10},{10,8},{9,1... | collective-permute-start | bytes 516104 | tf_op jit(solution)/shard_map/ppermute | solution.py:47
  6.9 2.2 %collective-permute-done.2.theirs = f32[8,128]{1,0:T(8,128)S(1)} collective-permute-done((f32[8,128]{1,0:T(8,128)S(1)}, f32[8,128]{1,0:T(8,128)S(1)}, u32[]{:S(2)}, u32[]{:S(2)}) %collective-permute-start.2) | collective-permute-done | bytes 4128 | tf_op jit(solution)/shard_map/ppermute | solution.py:47
  10.1 4.5 %all-to-all-start = ((bf16[4,344,256]{2,1,0:T(8,128)(2,1)}), bf16[4,344,256]{2,1,0:T(8,128)(2,1)S(1)}, u32[]{:S(2)}, u32[]{:S(2)}) async-start(bf16[4,344,256]{2,1,0:T(8,128)(2,1)} %message.1), calls=%async_computation | async-start | bytes 1409024 | tf_op jit(solution)/shard_map/all_to_all | solution.py:428
  14.5 2.6 %collective-permute-start.5 = (bf16[1024,256]{1,0:T(8,128)(2,1)}, bf16[1024,256]{1,0:T(8,128)(2,1)}, u32[]{:S(2)}, u32[]{:S(2)}) collective-permute-start(bf16[1024,256]{1,0:T(8,128)(2,1)} %a.3), channel_id=1, source_target_pairs={{0,2},{2,0},{1,3},{3,1},{4,6},{6,4},{5,7},{7,5},{8,10},{10,8},{9,1... | collective-permute-start | bytes 1572872 | tf_op jit(solution)/shard_map/ppermute | solution.py:47
  17.1 7.1 %all-to-all-done.t2.k2.o2 = bf16[4,344,256]{2,1,0:T(8,128)(2,1)S(1)} async-done(((bf16[4,344,256]{2,1,0:T(8,128)(2,1)}), bf16[4,344,256]{2,1,0:T(8,128)(2,1)S(1)}, u32[]{:S(2)}, u32[]{:S(2)}) %all-to-all-start) | async-done | bytes 704544 | tf_op jit(solution)/shard_map/all_to_all | solution.py:428
  24.2 2.7 %collective-permute-start.3 = (bf16[4,344,256]{2,1,0:T(8,128)(2,1)S(1)}, bf16[4,344,256]{2,1,0:T(8,128)(2,1)S(1)}, u32[]{:S(2)}, u32[]{:S(2)}) collective-permute-start(bf16[4,344,256]{2,1,0:T(8,128)(2,1)S(1)} %all-to-all-done.t2.k2.o2), channel_id=1, source_target_pairs={{0,1},{1,0},{2,3},{3,2},{4,5},{5,4},{6,7},{7,6},{8,9},{9,8},{10,11... | collective-permute-start | bytes 2113544 | tf_op jit(solution)/shard_map/ppermute | solution.py:47
  27.9 2.8 %collective-permute-start.6 = (bf16[1024,256]{1,0:T(8,128)(2,1)}, bf16[1024,256]{1,0:T(8,128)(2,1)}, u32[]{:S(2)}, u32[]{:S(2)}) collective-permute-start(bf16[1024,256]{1,0:T(8,128)(2,1)} %collective-permute-done.5.c), channel_id=1, source_target_pairs={{0,1},{1,0},{2,3},{3,2},{4,5},{5,4},{6,7},{7,6},{8,9},{9,8},{10,11... | collective-permute-start | bytes 1572872 | tf_op jit(solution)/shard_map/ppermute | solution.py:47
  32.6 3.0 %unit.1 = (bf16[1024,1024]{1,0:T(8,128)(2,1)S(1)}, f32[1024,128]{1,0:T(8,128)S(1)}) custom-call(bf16[1024,256]{1,0:T(8,128)(2,1)} %a.3, bf16[1024,256]{1,0:T(8,128)(2,1)} %collective-permute-done.4.b, bf16[1024,256]{1,0:T(8,128)(2,1)} %collective-permute-done.5.c, bf16[1024,256]{1,0:T(8,128)(2,1)} %collective-permute-done.6.d), custom_call_target="tpu_custom_call" | custom-call | flops 20000000 | bytes 1048576 | tf_op jit(solution)/shard_map/unit/pallas_call | solution.py:72
  35.6 7.1 %focal.1 = (bf16[672,512]{1,0:T(8,128)(2,1)S(1)}, bf16[672,512]{1,0:T(8,128)(2,1)S(1)}, f32[8,128]{1,0:T(8,128)S(1)}, f32[1,1]{1,0:T(1,128)}) custom-call(s32[6]{0:T(128)S(1)} %stack.27.s, bf16[1344,256]{1,0:T(8,128)(2,1)S(1)} %constant_dynamic-slice_fusion.t0.k0.o0, bf16[1344,256]{1,0:T(8,128)(2,1)S(1)} %collective-permute-done.t1.k1.o1, ...), custom_call_target="tpu_custom_call" | custom-call | flops 1400000000 | bytes 1048576 | tf_op jit(solution)/shard_map/focal/pallas_call | solution.py:194
  42.7 5.5 %region.1 = bf16[8,4,64,256]{3,2,1,0:T(8,128)(2,1)} custom-call(s32[6]{0:T(128)S(1)} %stack.27.s, bf16[672,512]{1,0:T(8,128)(2,1)S(1)} %get-tuple-element.32.keep, bf16[672,512]{1,0:T(8,128)(2,1)S(1)} %get-tuple-element.33.send, bf16[1344,256]{1,0:T(8,128)(2,1)S(1)} %constant_dynamic-slice_fusion.t0.k0.o0, ...), custom_call_target="tpu_custom_call" | custom-call | flops 1400000000 | bytes 1048576 | tf_op jit(solution)/shard_map/region/pallas_call | solution.py:264
  48.2 10.7 %all-to-all-start.1 = ((bf16[16,128,256]{2,1,0:T(8,128)(2,1)}), bf16[16,128,256]{2,1,0:T(8,128)(2,1)S(1)}, u32[]{:S(2)}, u32[]{:S(2)}) async-start(bf16[16,128,256]{2,1,0:T(8,128)(2,1)} %bitcast.18), calls=%async_computation.1 | async-start | bytes 2097152 | tf_op jit(solution)/shard_map/all_to_all | solution.py:428
  59.6 3.0 %collective-permute-start.10 = (f32[8,128]{1,0:T(8,128)S(1)}, f32[8,128]{1,0:T(8,128)S(1)}, u32[]{:S(2)}, u32[]{:S(2)}) collective-permute-start(f32[8,128]{1,0:T(8,128)S(1)} %get-tuple-element.34.l0), channel_id=1, source_target_pairs={{0,3},{1,2},{2,1},{3,0},{4,7},{5,6},{6,5},{7,4},{8,11},{9,10},{10,... | collective-permute-start | bytes 12296 | tf_op jit(solution)/shard_map/ppermute | solution.py:462
  63.1 1.9 %collective-permute-done.10.l3 = f32[8,128]{1,0:T(8,128)S(1)} collective-permute-done((f32[8,128]{1,0:T(8,128)S(1)}, f32[8,128]{1,0:T(8,128)S(1)}, u32[]{:S(2)}, u32[]{:S(2)}) %collective-permute-start.10) | collective-permute-done | bytes 4128 | tf_op jit(solution)/shard_map/ppermute | solution.py:462
  65.0 2.3 %collective-permute-done.8.l1 = f32[8,128]{1,0:T(8,128)S(1)} collective-permute-done((f32[8,128]{1,0:T(8,128)S(1)}, f32[8,128]{1,0:T(8,128)S(1)}, u32[]{:S(2)}, u32[]{:S(2)}) %collective-permute-start.8) | collective-permute-done | bytes 4128 | tf_op jit(solution)/shard_map/ppermute | solution.py:47
  68.5 3.1 %table.1 = (bf16[680,128]{1,0:T(8,128)(2,1)S(1)}, bf16[680,128]{1,0:T(8,128)(2,1)S(1)}, bf16[680,128]{1,0:T(8,128)(2,1)S(1)}, bf16[680,128]{1,0:T(8,128)(2,1)}, ...) custom-call(s32[6]{0:T(128)S(1)} %stack.27.s, ...), custom_call_target="tpu_custom_call" | custom-call | flops 1400000000 | bytes 1048576 | tf_op jit(solution)/shard_map/table/pallas_call | solution.py:309
  72.7 4.0 %collective-permute-start.13 = (bf16[680,128]{1,0:T(8,128)(2,1)S(1)}, bf16[680,128]{1,0:T(8,128)(2,1)S(1)}, u32[]{:S(2)}, u32[]{:S(2)}) collective-permute-start(bf16[680,128]{1,0:T(8,128)(2,1)S(1)} %get-tuple-element.37), channel_id=1, source_target_pairs={{0,65},{1,64},{2,67},{3,66},{32,97},{33,96},{34,99},{35,98},{64,13... | collective-permute-start | bytes 522248 | tf_op jit(solution)/shard_map/ppermute | solution.py:420
  76.6 4.0 %collective-permute-start.14 = (bf16[680,128]{1,0:T(8,128)(2,1)}, bf16[680,128]{1,0:T(8,128)(2,1)S(1)}, u32[]{:S(2)}, u32[]{:S(2)}) collective-permute-start(bf16[680,128]{1,0:T(8,128)(2,1)} %get-tuple-element.38), channel_id=1, source_target_pairs={{0,97},{1,96},{2,99},{3,98},{32,65},{33,64},{34,67},{35,66},{64,16... | collective-permute-start | bytes 522248 | tf_op jit(solution)/shard_map/ppermute | solution.py:420
  80.6 3.1 %collective-permute-start.15 = (bf16[680,128]{1,0:T(8,128)(2,1)}, bf16[680,128]{1,0:T(8,128)(2,1)S(1)}, u32[]{:S(2)}, u32[]{:S(2)}) collective-permute-start(bf16[680,128]{1,0:T(8,128)(2,1)} %get-tuple-element.39), channel_id=1, source_target_pairs={{0,130},{1,131},{2,128},{3,129},{32,162},{33,163},{34,160},{35,161... | collective-permute-start | bytes 522248 | tf_op jit(solution)/shard_map/ppermute | solution.py:420
  83.7 8.1 %collective-permute-start.16 = (bf16[680,128]{1,0:T(8,128)(2,1)}, bf16[680,128]{1,0:T(8,128)(2,1)S(1)}, u32[]{:S(2)}, u32[]{:S(2)}) collective-permute-start(bf16[680,128]{1,0:T(8,128)(2,1)} %get-tuple-element.40), channel_id=1, source_target_pairs={{0,162},{1,163},{2,160},{3,161},{32,130},{33,131},{34,128},{35,129... | collective-permute-start | bytes 522248 | tf_op jit(solution)/shard_map/ppermute | solution.py:420
  91.8 4.1 %collective-permute-start.17 = (bf16[680,128]{1,0:T(8,128)(2,1)}, bf16[680,128]{1,0:T(8,128)(2,1)S(1)}, u32[]{:S(2)}, u32[]{:S(2)}) collective-permute-start(bf16[680,128]{1,0:T(8,128)(2,1)} %get-tuple-element.41), channel_id=1, source_target_pairs={{0,195},{1,194},{2,193},{3,192},{32,227},{33,226},{34,225},{35,224... | collective-permute-start | bytes 522248 | tf_op jit(solution)/shard_map/ppermute | solution.py:420
  96.0 6.7 %collective-permute-start.18 = (bf16[680,128]{1,0:T(8,128)(2,1)S(1)}, bf16[680,128]{1,0:T(8,128)(2,1)S(1)}, u32[]{:S(2)}, u32[]{:S(2)}) collective-permute-start(bf16[680,128]{1,0:T(8,128)(2,1)S(1)} %get-tuple-element.42), channel_id=1, source_target_pairs={{0,227},{1,226},{2,225},{3,224},{32,195},{33,194},{34,193},{35,192... | collective-permute-start | bytes 522248 | tf_op jit(solution)/shard_map/ppermute | solution.py:420
  103.5 5.1 %collective-permute-done.17.refs_6_ = bf16[680,128]{1,0:T(8,128)(2,1)S(1)} collective-permute-done((bf16[680,128]{1,0:T(8,128)(2,1)}, bf16[680,128]{1,0:T(8,128)(2,1)S(1)}, u32[]{:S(2)}, u32[]{:S(2)}) %collective-permute-start.17) | collective-permute-done | bytes 174112 | tf_op jit(solution)/shard_map/ppermute | solution.py:420
  108.6 1.3 table_sum.1
  110.6 6.3 %all-to-all-start.2 = ((bf16[8,672,128]{2,1,0:T(8,128)(2,1)}), bf16[8,672,128]{2,1,0:T(8,128)(2,1)S(1)}, u32[]{:S(2)}, u32[]{:S(2)}) async-start(bf16[8,672,128]{2,1,0:T(8,128)(2,1)} %get-tuple-element.48), calls=%async_computation.2 | async-start | bytes 2752512 | tf_op jit(solution)/shard_map/all_to_all | solution.py:428
  117.9 1.7 %collective-permute-start.25 = (bf16[136,256]{1,0:T(8,128)(2,1)S(1)}, bf16[136,256]{1,0:T(8,128)(2,1)S(1)}, u32[]{:S(2)}, u32[]{:S(2)}) collective-permute-start(bf16[136,256]{1,0:T(8,128)(2,1)S(1)} %share.1.refs_0_), channel_id=1, source_target_pairs={{0,24},{4,28},{8,0},{12,4},{16,8},{20,12},{24,16},{28,20},{1,25},{... | collective-permute-start | bytes 208904 | tf_op jit(solution)/shard_map/ppermute | solution.py:424
  119.6 2.4 %collective-permute-start.24 = (bf16[136,256]{1,0:T(8,128)(2,1)S(1)}, bf16[136,256]{1,0:T(8,128)(2,1)S(1)}, u32[]{:S(2)}, u32[]{:S(2)}) collective-permute-start(bf16[136,256]{1,0:T(8,128)(2,1)S(1)} %share.1.refs_0_), channel_id=1, source_target_pairs={{0,20},{4,24},{8,28},{12,0},{16,4},{20,8},{24,12},{28,16},{1,21},{... | collective-permute-start | bytes 208904 | tf_op jit(solution)/shard_map/ppermute | solution.py:424
  122.0 3.2 %collective-permute-start.23 = (bf16[136,256]{1,0:T(8,128)(2,1)S(1)}, bf16[136,256]{1,0:T(8,128)(2,1)S(1)}, u32[]{:S(2)}, u32[]{:S(2)}) collective-permute-start(bf16[136,256]{1,0:T(8,128)(2,1)S(1)} %share.1.refs_0_), channel_id=1, source_target_pairs={{0,16},{4,20},{8,24},{12,28},{16,0},{20,4},{24,8},{28,12},{1,17},{... | collective-permute-start | bytes 208904 | tf_op jit(solution)/shard_map/ppermute | solution.py:424
  125.8 1.4 collective-permute-start.21
  128.5 1.5 %collective-permute-done.23.refs_4_ = bf16[136,256]{1,0:T(8,128)(2,1)S(1)} collective-permute-done((bf16[136,256]{1,0:T(8,128)(2,1)S(1)}, bf16[136,256]{1,0:T(8,128)(2,1)S(1)}, u32[]{:S(2)}, u32[]{:S(2)}) %collective-permute-start.23) | collective-permute-done | bytes 69664 | tf_op jit(solution)/shard_map/ppermute | solution.py:424
  130.0 5.6 %collective-permute-done.22.refs_3_ = bf16[136,256]{1,0:T(8,128)(2,1)S(1)} collective-permute-done((bf16[136,256]{1,0:T(8,128)(2,1)S(1)}, bf16[136,256]{1,0:T(8,128)(2,1)S(1)}, u32[]{:S(2)}, u32[]{:S(2)}) %collective-permute-start.22) | collective-permute-done | bytes 69664 | tf_op jit(solution)/shard_map/ppermute | solution.py:424
  135.5 3.6 %collective-permute-done.20.refs_1_ = bf16[136,256]{1,0:T(8,128)(2,1)S(1)} collective-permute-done((bf16[136,256]{1,0:T(8,128)(2,1)S(1)}, bf16[136,256]{1,0:T(8,128)(2,1)S(1)}, u32[]{:S(2)}, u32[]{:S(2)}) %collective-permute-start.20) | collective-permute-done | bytes 69664 | tf_op jit(solution)/shard_map/ppermute | solution.py:424
  139.1 2.6 %final.1 = (bf16[2,8,64,256]{3,2,1,0:T(8,128)(2,1)}, bf16[2688,256]{1,0:T(8,128)(2,1)}, f32[1,1]{1,0:T(1,128)}) custom-call(s32[6]{0:T(128)S(1)} %stack.27.s, f32[1,1]{1,0:T(1,128)} %get-tuple-element.31.count, bf16[8,672,128]{2,1,0:T(8,128)(2,1)S(1)} %all-to-all-done.2.tables, bf16[136,256]{1,0:T(8,128)(2,1)S(1)} %share.1.refs_0_, ...), custom_call_target="tpu_custom_call" | custom-call | flops 10000000 | bytes 1048576 | tf_op jit(solution)/shard_map/final/pallas_call | solution.py:398
  (65 shorter events, 14.1 us)
Async XLA Ops:
  1.6 25.3 %copy-start.6 = (bf16[2688,256]{1,0:T(8,128)(2,1)S(1)}, bf16[2688,256]{1,0:T(8,128)(2,1)}, u32[]{:S(2)}) copy-start(bf16[2688,256]{1,0:T(8,128)(2,1)} %x.1) | copy-start | bytes 4128772
  1.6 7.6 %collective-permute-start.1 = (bf16[336,256]{1,0:T(8,128)(2,1)S(1)}, bf16[336,256]{1,0:T(8,128)(2,1)S(1)}, u32[]{:S(2)}, u32[]{:S(2)}) collective-permute-start(bf16[336,256]{1,0:T(8,128)(2,1)S(1)} %rows.1), channel_id=1, source_target_pairs={{0,2},{2,0},{1,3},{3,1},{4,6},{6,4},{5,7},{7,5},{8,10},{10,8},{9,1... | collective-permute-start | bytes 516104 | tf_op jit(solution)/shard_map/ppermute | solution.py:47
  6.5 2.6 %collective-permute-start.2 = (f32[8,128]{1,0:T(8,128)S(1)}, f32[8,128]{1,0:T(8,128)S(1)}, u32[]{:S(2)}, u32[]{:S(2)}) collective-permute-start(f32[8,128]{1,0:T(8,128)S(1)} %broadcast_in_dim.15.mine), channel_id=1, source_target_pairs={{0,32},{32,0},{1,33},{33,1},{2,34},{34,2},{3,35},{35,3},{4,36},{36... | collective-permute-start | bytes 12296 | tf_op jit(solution)/shard_map/ppermute | solution.py:47
  10.1 14.1 %all-to-all-start = ((bf16[4,344,256]{2,1,0:T(8,128)(2,1)}), bf16[4,344,256]{2,1,0:T(8,128)(2,1)S(1)}, u32[]{:S(2)}, u32[]{:S(2)}) async-start(bf16[4,344,256]{2,1,0:T(8,128)(2,1)} %message.1), calls=%async_computation | async-start | bytes 1409024 | tf_op jit(solution)/shard_map/all_to_all | solution.py:428
  14.5 13.3 %collective-permute-start.5 = (bf16[1024,256]{1,0:T(8,128)(2,1)}, bf16[1024,256]{1,0:T(8,128)(2,1)}, u32[]{:S(2)}, u32[]{:S(2)}) collective-permute-start(bf16[1024,256]{1,0:T(8,128)(2,1)} %a.3), channel_id=1, source_target_pairs={{0,2},{2,0},{1,3},{3,1},{4,6},{6,4},{5,7},{7,5},{8,10},{10,8},{9,1... | collective-permute-start | bytes 1572872 | tf_op jit(solution)/shard_map/ppermute | solution.py:47
  24.2 11.5 %collective-permute-start.3 = (bf16[4,344,256]{2,1,0:T(8,128)(2,1)S(1)}, bf16[4,344,256]{2,1,0:T(8,128)(2,1)S(1)}, u32[]{:S(2)}, u32[]{:S(2)}) collective-permute-start(bf16[4,344,256]{2,1,0:T(8,128)(2,1)S(1)} %all-to-all-done.t2.k2.o2), channel_id=1, source_target_pairs={{0,1},{1,0},{2,3},{3,2},{4,5},{5,4},{6,7},{7,6},{8,9},{9,8},{10,11... | collective-permute-start | bytes 2113544 | tf_op jit(solution)/shard_map/ppermute | solution.py:47
  27.0 8.6 %collective-permute-start = (bf16[1344,256]{1,0:T(8,128)(2,1)S(1)}, bf16[1344,256]{1,0:T(8,128)(2,1)S(1)}, u32[]{:S(2)}, u32[]{:S(2)}) collective-permute-start(bf16[1344,256]{1,0:T(8,128)(2,1)S(1)} %constant_dynamic-slice_fusion.t0.k0.o0), channel_id=1, source_target_pairs={{0,1},{1,0},{2,3},{3,2},{4,5},{5,4},{6,7},{7,6},{8,9},{9,8},{10,11... | collective-permute-start | bytes 2064392 | tf_op jit(solution)/shard_map/ppermute | solution.py:47
  27.1 5.0 %collective-permute-start.4 = (bf16[1024,256]{1,0:T(8,128)(2,1)}, bf16[1024,256]{1,0:T(8,128)(2,1)}, u32[]{:S(2)}, u32[]{:S(2)}) collective-permute-start(bf16[1024,256]{1,0:T(8,128)(2,1)} %a.3), channel_id=1, source_target_pairs={{0,1},{1,0},{2,3},{3,2},{4,5},{5,4},{6,7},{7,6},{8,9},{9,8},{10,11... | collective-permute-start | bytes 1572872 | tf_op jit(solution)/shard_map/ppermute | solution.py:47
  27.9 4.7 %collective-permute-start.6 = (bf16[1024,256]{1,0:T(8,128)(2,1)}, bf16[1024,256]{1,0:T(8,128)(2,1)}, u32[]{:S(2)}, u32[]{:S(2)}) collective-permute-start(bf16[1024,256]{1,0:T(8,128)(2,1)} %collective-permute-done.5.c), channel_id=1, source_target_pairs={{0,1},{1,0},{2,3},{3,2},{4,5},{5,4},{6,7},{7,6},{8,9},{9,8},{10,11... | collective-permute-start | bytes 1572872 | tf_op jit(solution)/shard_map/ppermute | solution.py:47
  48.2 19.2 %copy-start.1 = (bf16[1024,1024]{1,0:T(8,128)(2,1)S(1)}, bf16[1024,1024]{1,0:T(8,128)(2,1)}, u32[]{:S(2)}) copy-start(bf16[1024,1024]{1,0:T(8,128)(2,1)} %copy-done) | copy-start | bytes 6291460
  48.2 54.5 %all-to-all-start.1 = ((bf16[16,128,256]{2,1,0:T(8,128)(2,1)}), bf16[16,128,256]{2,1,0:T(8,128)(2,1)S(1)}, u32[]{:S(2)}, u32[]{:S(2)}) async-start(bf16[16,128,256]{2,1,0:T(8,128)(2,1)} %bitcast.18), calls=%async_computation.1 | async-start | bytes 2097152 | tf_op jit(solution)/shard_map/all_to_all | solution.py:428
  58.9 8.5 %collective-permute-start.7 = (bf16[672,512]{1,0:T(8,128)(2,1)}, bf16[672,512]{1,0:T(8,128)(2,1)S(1)}, u32[]{:S(2)}, u32[]{:S(2)}) collective-permute-start(bf16[672,512]{1,0:T(8,128)(2,1)} %copy-done.4), channel_id=1, source_target_pairs={{0,1},{1,0},{2,3},{3,2},{4,5},{5,4},{6,7},{7,6},{8,9},{9,8},{10,11... | collective-permute-start | bytes 2064392 | tf_op jit(solution)/shard_map/ppermute | solution.py:47
  59.6 5.4 %collective-permute-start.10 = (f32[8,128]{1,0:T(8,128)S(1)}, f32[8,128]{1,0:T(8,128)S(1)}, u32[]{:S(2)}, u32[]{:S(2)}) collective-permute-start(f32[8,128]{1,0:T(8,128)S(1)} %get-tuple-element.34.l0), channel_id=1, source_target_pairs={{0,3},{1,2},{2,1},{3,0},{4,7},{5,6},{6,5},{7,4},{8,11},{9,10},{10,... | collective-permute-start | bytes 12296 | tf_op jit(solution)/shard_map/ppermute | solution.py:462
  62.7 2.4 %collective-permute-start.9 = (f32[8,128]{1,0:T(8,128)S(1)}, f32[8,128]{1,0:T(8,128)S(1)}, u32[]{:S(2)}, u32[]{:S(2)}) collective-permute-start(f32[8,128]{1,0:T(8,128)S(1)} %get-tuple-element.34.l0), channel_id=1, source_target_pairs={{0,1},{1,0},{2,3},{3,2},{4,5},{5,4},{6,7},{7,6},{8,9},{9,8},{10,11... | collective-permute-start | bytes 12296 | tf_op jit(solution)/shard_map/ppermute | solution.py:47
  63.1 4.3 %collective-permute-start.8 = (f32[8,128]{1,0:T(8,128)S(1)}, f32[8,128]{1,0:T(8,128)S(1)}, u32[]{:S(2)}, u32[]{:S(2)}) collective-permute-start(f32[8,128]{1,0:T(8,128)S(1)} %get-tuple-element.34.l0), channel_id=1, source_target_pairs={{0,2},{2,0},{1,3},{3,1},{4,6},{6,4},{5,7},{7,5},{8,10},{10,8},{9,1... | collective-permute-start | bytes 12296 | tf_op jit(solution)/shard_map/ppermute | solution.py:47
  71.6 12.1 %collective-permute-start.11 = (bf16[680,128]{1,0:T(8,128)(2,1)S(1)}, bf16[680,128]{1,0:T(8,128)(2,1)S(1)}, u32[]{:S(2)}, u32[]{:S(2)}) collective-permute-start(bf16[680,128]{1,0:T(8,128)(2,1)S(1)} %get-tuple-element.35), channel_id=1, source_target_pairs={{0,0},{1,1},{2,2},{3,3},{32,32},{33,33},{34,34},{35,35},{64,65},{6... | collective-permute-start | bytes 522248 | tf_op jit(solution)/shard_map/ppermute | solution.py:420
  72.2 19.6 %collective-permute-start.12 = (bf16[680,128]{1,0:T(8,128)(2,1)S(1)}, bf16[680,128]{1,0:T(8,128)(2,1)S(1)}, u32[]{:S(2)}, u32[]{:S(2)}) collective-permute-start(bf16[680,128]{1,0:T(8,128)(2,1)S(1)} %get-tuple-element.36), channel_id=1, source_target_pairs={{0,32},{1,33},{2,34},{3,35},{32,0},{33,1},{34,2},{35,3},{64,97},{6... | collective-permute-start | bytes 522248 | tf_op jit(solution)/shard_map/ppermute | solution.py:420
  72.7 23.3 %collective-permute-start.13 = (bf16[680,128]{1,0:T(8,128)(2,1)S(1)}, bf16[680,128]{1,0:T(8,128)(2,1)S(1)}, u32[]{:S(2)}, u32[]{:S(2)}) collective-permute-start(bf16[680,128]{1,0:T(8,128)(2,1)S(1)} %get-tuple-element.37), channel_id=1, source_target_pairs={{0,65},{1,64},{2,67},{3,66},{32,97},{33,96},{34,99},{35,98},{64,13... | collective-permute-start | bytes 522248 | tf_op jit(solution)/shard_map/ppermute | solution.py:420
  76.6 26.8 %collective-permute-start.14 = (bf16[680,128]{1,0:T(8,128)(2,1)}, bf16[680,128]{1,0:T(8,128)(2,1)S(1)}, u32[]{:S(2)}, u32[]{:S(2)}) collective-permute-start(bf16[680,128]{1,0:T(8,128)(2,1)} %get-tuple-element.38), channel_id=1, source_target_pairs={{0,97},{1,96},{2,99},{3,98},{32,65},{33,64},{34,67},{35,66},{64,16... | collective-permute-start | bytes 522248 | tf_op jit(solution)/shard_map/ppermute | solution.py:420
  80.6 22.9 %collective-permute-start.15 = (bf16[680,128]{1,0:T(8,128)(2,1)}, bf16[680,128]{1,0:T(8,128)(2,1)S(1)}, u32[]{:S(2)}, u32[]{:S(2)}) collective-permute-start(bf16[680,128]{1,0:T(8,128)(2,1)} %get-tuple-element.39), channel_id=1, source_target_pairs={{0,130},{1,131},{2,128},{3,129},{32,162},{33,163},{34,160},{35,161... | collective-permute-start | bytes 522248 | tf_op jit(solution)/shard_map/ppermute | solution.py:420
  83.7 19.8 %collective-permute-start.16 = (bf16[680,128]{1,0:T(8,128)(2,1)}, bf16[680,128]{1,0:T(8,128)(2,1)S(1)}, u32[]{:S(2)}, u32[]{:S(2)}) collective-permute-start(bf16[680,128]{1,0:T(8,128)(2,1)} %get-tuple-element.40), channel_id=1, source_target_pairs={{0,162},{1,163},{2,160},{3,161},{32,130},{33,131},{34,128},{35,129... | collective-permute-start | bytes 522248 | tf_op jit(solution)/shard_map/ppermute | solution.py:420
  91.8 16.8 %collective-permute-start.17 = (bf16[680,128]{1,0:T(8,128)(2,1)}, bf16[680,128]{1,0:T(8,128)(2,1)S(1)}, u32[]{:S(2)}, u32[]{:S(2)}) collective-permute-start(bf16[680,128]{1,0:T(8,128)(2,1)} %get-tuple-element.41), channel_id=1, source_target_pairs={{0,195},{1,194},{2,193},{3,192},{32,227},{33,226},{34,225},{35,224... | collective-permute-start | bytes 522248 | tf_op jit(solution)/shard_map/ppermute | solution.py:420
  96.0 12.7 %collective-permute-start.18 = (bf16[680,128]{1,0:T(8,128)(2,1)S(1)}, bf16[680,128]{1,0:T(8,128)(2,1)S(1)}, u32[]{:S(2)}, u32[]{:S(2)}) collective-permute-start(bf16[680,128]{1,0:T(8,128)(2,1)S(1)} %get-tuple-element.42), channel_id=1, source_target_pairs={{0,227},{1,226},{2,225},{3,224},{32,195},{33,194},{34,193},{35,192... | collective-permute-start | bytes 522248 | tf_op jit(solution)/shard_map/ppermute | solution.py:420
  103.4 6.5 %collective-permute-start.19 = (bf16[64,256]{1,0:T(8,128)(2,1)S(1)}, bf16[64,256]{1,0:T(8,128)(2,1)S(1)}, u32[]{:S(2)}, u32[]{:S(2)}) collective-permute-start(bf16[64,256]{1,0:T(8,128)(2,1)S(1)} %get-tuple-element.46), channel_id=1, source_target_pairs={{0,1},{1,0},{2,3},{3,2},{4,5},{5,4},{6,7},{7,6},{8,9},{9,8},{10,11... | collective-permute-start | bytes 98312 | tf_op jit(solution)/shard_map/ppermute | solution.py:47
  110.6 28.5 %all-to-all-start.2 = ((bf16[8,672,128]{2,1,0:T(8,128)(2,1)}), bf16[8,672,128]{2,1,0:T(8,128)(2,1)S(1)}, u32[]{:S(2)}, u32[]{:S(2)}) async-start(bf16[8,672,128]{2,1,0:T(8,128)(2,1)} %get-tuple-element.48), calls=%async_computation.2 | async-start | bytes 2752512 | tf_op jit(solution)/shard_map/all_to_all | solution.py:428
  116.9 9.0 %collective-permute-start.26 = (bf16[136,256]{1,0:T(8,128)(2,1)S(1)}, bf16[136,256]{1,0:T(8,128)(2,1)S(1)}, u32[]{:S(2)}, u32[]{:S(2)}) collective-permute-start(bf16[136,256]{1,0:T(8,128)(2,1)S(1)} %share.1.refs_0_), channel_id=1, source_target_pairs={{0,28},{4,0},{8,4},{12,8},{16,12},{20,16},{24,20},{28,24},{1,29},{... | collective-permute-start | bytes 208904 | tf_op jit(solution)/shard_map/ppermute | solution.py:424
  117.9 9.3 %collective-permute-start.25 = (bf16[136,256]{1,0:T(8,128)(2,1)S(1)}, bf16[136,256]{1,0:T(8,128)(2,1)S(1)}, u32[]{:S(2)}, u32[]{:S(2)}) collective-permute-start(bf16[136,256]{1,0:T(8,128)(2,1)S(1)} %share.1.refs_0_), channel_id=1, source_target_pairs={{0,24},{4,28},{8,0},{12,4},{16,8},{20,12},{24,16},{28,20},{1,25},{... | collective-permute-start | bytes 208904 | tf_op jit(solution)/shard_map/ppermute | solution.py:424
  119.6 8.9 %collective-permute-start.24 = (bf16[136,256]{1,0:T(8,128)(2,1)S(1)}, bf16[136,256]{1,0:T(8,128)(2,1)S(1)}, u32[]{:S(2)}, u32[]{:S(2)}) collective-permute-start(bf16[136,256]{1,0:T(8,128)(2,1)S(1)} %share.1.refs_0_), channel_id=1, source_target_pairs={{0,20},{4,24},{8,28},{12,0},{16,4},{20,8},{24,12},{28,16},{1,21},{... | collective-permute-start | bytes 208904 | tf_op jit(solution)/shard_map/ppermute | solution.py:424
  122.0 8.0 %collective-permute-start.23 = (bf16[136,256]{1,0:T(8,128)(2,1)S(1)}, bf16[136,256]{1,0:T(8,128)(2,1)S(1)}, u32[]{:S(2)}, u32[]{:S(2)}) collective-permute-start(bf16[136,256]{1,0:T(8,128)(2,1)S(1)} %share.1.refs_0_), channel_id=1, source_target_pairs={{0,16},{4,20},{8,24},{12,28},{16,0},{20,4},{24,8},{28,12},{1,17},{... | collective-permute-start | bytes 208904 | tf_op jit(solution)/shard_map/ppermute | solution.py:424
  125.2 10.3 %collective-permute-start.22 = (bf16[136,256]{1,0:T(8,128)(2,1)S(1)}, bf16[136,256]{1,0:T(8,128)(2,1)S(1)}, u32[]{:S(2)}, u32[]{:S(2)}) collective-permute-start(bf16[136,256]{1,0:T(8,128)(2,1)S(1)} %share.1.refs_0_), channel_id=1, source_target_pairs={{0,12},{4,16},{8,20},{12,24},{16,28},{20,0},{24,4},{28,8},{1,13},{... | collective-permute-start | bytes 208904 | tf_op jit(solution)/shard_map/ppermute | solution.py:424
  125.8 9.7 %collective-permute-start.21 = (bf16[136,256]{1,0:T(8,128)(2,1)S(1)}, bf16[136,256]{1,0:T(8,128)(2,1)S(1)}, u32[]{:S(2)}, u32[]{:S(2)}) collective-permute-start(bf16[136,256]{1,0:T(8,128)(2,1)S(1)} %share.1.refs_0_), channel_id=1, source_target_pairs={{0,8},{4,12},{8,16},{12,20},{16,24},{20,28},{24,0},{28,4},{1,9},{5... | collective-permute-start | bytes 208904 | tf_op jit(solution)/shard_map/ppermute | solution.py:424
  127.3 11.9 %collective-permute-start.20 = (bf16[136,256]{1,0:T(8,128)(2,1)S(1)}, bf16[136,256]{1,0:T(8,128)(2,1)S(1)}, u32[]{:S(2)}, u32[]{:S(2)}) collective-permute-start(bf16[136,256]{1,0:T(8,128)(2,1)S(1)} %share.1.refs_0_), channel_id=1, source_target_pairs={{0,4},{4,8},{8,12},{12,16},{16,20},{20,24},{24,28},{28,0},{1,5},{5... | collective-permute-start | bytes 208904 | tf_op jit(solution)/shard_map/ppermute | solution.py:424
  (7 other events, 58.6 us)
where the time goes:
time: 142 us
  starting transfers between devices  81.3 us (57%)
  waiting for transfers between devices  30.2 us (21%)
  Pallas kernels  25.7 us (18%)
  local copies, waits for them, and re-layouts  2.25 us (2%)
  other arithmetic  1.46 us (1%)
    ppermute x8, starting transfers between devices, to_owner(): return lax.ppermute(x, IMG + EMB, pairs)  31.1 us
    all_to_all x3, starting transfers between devices, exchange(): return lax.all_to_all(x, axes, split_axis=0, concat_axis=0, tiled=True)  21.5 us
    ppermute x11, starting transfers between devices, swap(): return lax.ppermute(x, axis, [(0, 1), (1, 0)])  14 us
    ppermute x7, starting transfers between devices, along_cls(): return lax.ppermute(x, CLS, [(i, (i + d) % 8) for i in range(8)])  11.6 us
    ppermute x7, waiting for transfers between devices, along_cls(): return lax.ppermute(x, CLS, [(i, (i + d) % 8) for i in range(8)])  10.6 us
    all_to_all x3, waiting for transfers between devices, exchange(): return lax.all_to_all(x, axes, split_axis=0, concat_axis=0, tiled=True)  7.06 us
    pallas_call x1, Pallas kernels, make_focal(): pl.pallas_call(focal_kernel, grid_spec=pltpu.PrefetchScalarGridSpec(num_s...  7.05 us
    pallas_call x1, Pallas kernels, make_region(): pl.pallas_call(region_kernel, grid_spec=pltpu.PrefetchScalarGridSpec(num_...  5.46 us
  transfers between devices with their start and end apart: 30, of which 10 were waited for; matrix products, arithmetic and copies ran while one was open for 2% of the time, Pallas kernels for 6%

commit v1 on v0

--- a/solution.py
+++ b/solution.py
@@ -10,14 +10,14 @@
 REGIONS = 8192
 EMB = ("emb_0", "emb_1")
 IMG = ("img_0", "img_1")
-CLS = ("cls",)
-CLS_EMB = CLS + EMB[:1]
+CLS = ("cls_0", "cls_1")
+NEAR = ("cls_1", "emb_0", "emb_1")
 F32 = jnp.float32
 BF16 = jnp.bfloat16
 NT = (((1,), (1,)), ((), ()))
 TN = (((0,), (0,)), ((), ()))
 
-K, BASE, E, Y, XL, Z = range(6)
+K, BASE, E, Y, XL, ZH = range(6)
 
 
 PART = 336
@@ -224,74 +224,77 @@
     )(scalars, *tables, unit, lane_f, labels, mask)
 
 
-def region_kernel(s, keep, send, k0, k1, k2, k3, o0, o1, o2, o3, a, b, c, d, inv_ref, out, acc):
-    inv = inv_ref[:, 0:1]
-    mine = keep[...]
-    theirs = send[...]
+def region_kernel(s, keep, send, t0, t1, t2, t3, loss, a, b, c, d, inv_ref, out, acc):
+    half = keep.shape[0]
+    k = s[K]
+    tile = acc.shape[0]
+    blocks = (a, b, c, d)
+    extra = split3(jnp.sum(loss[...]), 256).astype(BF16)
+    mine_at = pl.multiple_of(k * half, 32)
+    theirs_at = pl.multiple_of((1 - k) * half, 32)
 
     def dot(g, t):
         return lax.dot_general(g, t, TN, preferred_element_type=F32)
 
-    along = 0.0
-    rows = (a, b, c, d)
-    for q, (t, o) in enumerate(zip((k0, k1, k2, k3), (o0, o1, o2, o3))):
-        if q < 2:
-            part = dot(mine, t[...]) + dot(theirs, o[...])
-        else:
-            part = sum(
-                dot(g[PART * i : PART * i + PART, :], x[i, 0:PART, :])
-                for g, x in ((mine, t), (theirs, o))
-                for i in range(2)
-            )
-        acc[:, 256 * q : 256 * q + 256] = part
-        along += jnp.sum(part * rows[q][...].astype(F32), axis=1, keepdims=True)
-    back = inv * inv * along
-    for q, r in enumerate(rows):
-        grad = inv * (acc[:, 256 * q : 256 * q + 256] - r[...].astype(F32) * back)
-        to = s[E] ^ q
-        for i in range(out.shape[0]):
-            out[i, to] = grad[64 * i : 64 * i + 64, :].astype(BF16)
-
-
-def make_region(scalars, keep, send, tables, blocks, inv):
+    for i in range(keep.shape[1] // tile):
+        rows = slice(tile * i, tile * i + tile)
+        mine = keep[:, rows]
+        theirs = send[:, rows]
+        inv = inv_ref[rows, 0:1]
+        along = 0.0
+        for q, t in enumerate((t0, t1, t2, t3)):
+            if q < 2:
+                part = dot(mine, t[pl.ds(mine_at, half), :]) + dot(theirs, t[pl.ds(theirs_at, half), :])
+            else:
+                part = sum(
+                    dot(g[PART * p : PART * p + PART, :], t[2 * at + p, 0:PART, :])
+                    for g, at in ((mine, k), (theirs, 1 - k))
+                    for p in range(2)
+                )
+            acc[:, 256 * q : 256 * q + 256] = part
+            along += jnp.sum(part * blocks[q][rows, :].astype(F32), axis=1, keepdims=True)
+        back = inv * inv * along
+        for q, r in enumerate(blocks):
+            cols = slice(256 * q, 256 * q + 256)
+            grad = inv * (acc[:, cols] - r[rows, :].astype(F32) * back)
+            for p in range(tile // 64):
+                z = tile // 64 * i + p
+                out[z, 0:64, cols] = grad[64 * p : 64 * p + 64, :].astype(BF16)
+                out[z, 64:72, cols] = extra
+
+
+def make_region(scalars, keep, send, tables, loss, blocks, inv):
     half, rows = keep.shape
-    tile = 256
-    steps = rows // tile
-    flat = lambda f: pl.BlockSpec((half, 256), lambda i, s: (f(s), 0))
-    cube = lambda f: pl.BlockSpec((2, PART + 8, 256), lambda i, s: (f(s), 0, 0))
-    own = lambda s: s[K]
-    other = lambda s: 1 - s[K]
+    flat = pl.BlockSpec((2 * half, 256), lambda i, s: (0, 0))
+    cube = pl.BlockSpec((4, PART + 8, 256), lambda i, s: (0, 0, 0))
     return pl.pallas_call(
         region_kernel,
         grid_spec=pltpu.PrefetchScalarGridSpec(
             num_scalar_prefetch=1,
-            grid=(steps,),
-            in_specs=[pl.BlockSpec((half, tile), lambda i, s: (0, i))] * 2
-            + [flat(own)] * 2
-            + [cube(own)] * 2
-            + [flat(other)] * 2
-            + [cube(other)] * 2
-            + [pl.BlockSpec((tile, 256), lambda i, s: (s[K] * steps + i, 0))] * 4
-            + [pl.BlockSpec((tile, 128), lambda i, s: (s[K] * steps + i, 0))],
-            out_specs=pl.BlockSpec((tile // 64, 4, 64, 256), lambda i, s: (i, 0, 0, 0)),
-            scratch_shapes=[pltpu.VMEM((tile, 1024), F32)],
+            grid=(1,),
+            in_specs=[pl.BlockSpec((half, rows), lambda i, s: (0, 0))] * 2
+            + [flat] * 2
+            + [cube] * 2
+            + [pl.BlockSpec((8, 128), lambda i, s: (0, 0))]
+            + [pl.BlockSpec((rows, 256), lambda i, s: (s[K], 0))] * 4
+            + [pl.BlockSpec((rows, 128), lambda i, s: (s[K], 0))],
+            out_specs=pl.BlockSpec((8, 72, 1024), lambda i, s: (0, 0, 0)),
+            scratch_shapes=[pltpu.VMEM((256, 1024), F32)],
         ),
-        out_shape=in_hbm((8, 4, 64, 256), BF16),
-        compiler_params=params(),
+        out_shape=in_hbm((8, 72, 1024), BF16),
+        compiler_params=params(24),
         cost_estimate=cost(1.4e9),
         name="region",
-    )(scalars, keep, send, *tables, *tables, *blocks, inv)
-
-
-def table_kernel(s, keep, other, unit, l0, l1, l2, l3, *refs):
+    )(scalars, keep, send, *tables, loss, *blocks, inv)
+
+
+def table_kernel(s, keep, other, unit, *refs):
     outs, acc = refs[:8], refs[8]
-    half, rows = other.shape
+    _, rows = other.shape
     mine = keep[...]
     theirs = other[...]
     mine_at = pl.multiple_of(s[K] * rows, rows)
     theirs_at = pl.multiple_of((1 - s[K]) * rows, rows)
-    loss = jnp.sum(l0[...] + l1[...] + l2[...] + l3[...])
-    extra = split3(loss, 128).astype(BF16)
     for dy in range(4):
         cols = pl.ds(pl.multiple_of(256 * ((s[Y] + dy) % 4), 256), 256)
         acc[...] = jnp.dot(
@@ -299,108 +302,115 @@
         ) + jnp.dot(theirs, unit[pl.ds(theirs_at, rows), cols], preferred_element_type=F32)
         for dx in range(2):
             at = pl.multiple_of(128 * (s[XL] ^ dx), 128)
-            out = outs[2 * dy + dx]
-            out[0:half, :] = acc[:, pl.ds(at, 128)].astype(BF16)
-            out[half : half + 8, :] = extra
-
-
-def make_table(scalars, keep, other, unit, losses):
+            outs[2 * dy + dx][...] = acc[:, pl.ds(at, 128)].astype(BF16)
+
+
+def make_table(scalars, keep, other, unit):
     half = other.shape[0]
     return pl.pallas_call(
         table_kernel,
-        in_specs=[smem()] + vmem(7),
+        in_specs=[smem()] + vmem(3),
         out_specs=vmem(8),
-        out_shape=[jax.ShapeDtypeStruct((half + 8, 128), BF16)] * 8,
+        out_shape=[jax.ShapeDtypeStruct((half, 128), BF16)] * 8,
         scratch_shapes=[pltpu.VMEM((half, 256), F32)],
         compiler_params=params(),
         cost_estimate=cost(1.4e9),
         name="table",
-    )(scalars, keep, other, unit, *losses)
+    )(scalars, keep, other, unit)
 
 
 def table_sum_kernel(*refs):
-    terms, (out, loss) = refs[:8], refs[8:]
-    half = out.shape[1]
-    total = sum(t[0:half, :].astype(F32) for t in terms).astype(BF16)
-    for j in range(8):
-        out[j] = total
-    loss[...] = sum(t[half : half + 8, :].astype(F32) for t in terms)
+    terms, out = refs[:8], refs[8]
+    out[...] = sum(t[...].astype(F32) for t in terms).astype(BF16)
 
 
 def make_table_sum(terms):
-    half = terms[0].shape[0] - 8
     return pl.pallas_call(
         table_sum_kernel,
         in_specs=vmem(8),
-        out_specs=vmem(2),
-        out_shape=[in_hbm((8, half, 128), BF16), jax.ShapeDtypeStruct((8, 128), F32)],
+        out_specs=vmem(1)[0],
+        out_shape=jax.ShapeDtypeStruct(terms[0].shape, BF16),
         compiler_params=params(),
         cost_estimate=cost(1e7),
         name="table_sum",
     )(*terms)
 
 
-def region_sum_kernel(s, pieces, mine, theirs):
-    totals = [
-        sum(pieces[z, x, k].astype(F32) for z in range(8) for x in range(2)) for k in range(2)
-    ]
-    first = s[K] == 0
-    mine[...] = jnp.where(first, totals[0], totals[1]).astype(BF16)
-    theirs[...] = jnp.where(first, totals[1], totals[0]).astype(BF16)
-
-
-def make_region_sum(scalars, pieces):
-    return pl.pallas_call(
-        region_sum_kernel,
+def merge_kernel(s, terms, out):
+    total = sum(terms[z].astype(F32) for z in range(8))
+    loss = jnp.sum(total[64:72, 0:256])
+    extra = split3(loss, 256).astype(BF16)
+    total = total[0:64, :].astype(BF16)
+    for q in range(4):
+        to = s[E] ^ q
+        for near in range(2):
+            out[near, to, 0:64, :] = total[:, 256 * q : 256 * q + 256]
+            out[near, to, 64:72, :] = extra
+
+
+def make_merge(scalars, terms):
+    return pl.pallas_call(
+        merge_kernel,
         in_specs=[smem()] + vmem(1),
+        out_specs=vmem(1)[0],
+        out_shape=in_hbm((2, 4, 72, 256), BF16),
+        compiler_params=params(),
+        cost_estimate=cost(1e7),
+        name="merge",
+    )(scalars, terms)
+
+
+def share_kernel(pieces, chunk, out, message):
+    half = chunk.shape[0]
+    for near in range(2):
+        for k in range(2):
+            both = pieces[near, 0, k, 0:64, :].astype(F32) + pieces[near, 1, k, 0:64, :].astype(F32)
+            at = 128 * near + 64 * k
+            out[at : at + 64, :] = both.astype(BF16)
+    loss = sum(jnp.sum(pieces[0, x, k, 64:72, :].astype(F32)) for x in range(2) for k in range(2))
+    extra = split3(loss, 128).astype(BF16)
+    rows = chunk[...]
+    for j in range(8):
+        message[j, 0:half, :] = rows
+        message[j, half : half + 8, :] = extra
+
+
+def make_share(pieces, chunk):
+    half = chunk.shape[0]
+    return pl.pallas_call(
+        share_kernel,
+        in_specs=vmem(2),
         out_specs=vmem(2),
-        out_shape=[jax.ShapeDtypeStruct((64, 256), BF16)] * 2,
-        compiler_params=params(),
-        cost_estimate=cost(1e7),
-        name="region_sum",
-    )(scalars, pieces)
-
-
-def share_kernel(s, mine, other, loss, out):
-    out[pl.ds(pl.multiple_of(64 * s[K], 64), 64), :] = mine[...]
-    out[pl.ds(pl.multiple_of(64 * (1 - s[K]), 64), 64), :] = other[...]
-    out[128:136, :] = split3(jnp.sum(loss[...]), 256).astype(BF16)
-
-
-def make_share(scalars, mine, other, loss):
-    return pl.pallas_call(
-        share_kernel,
-        in_specs=[smem()] + vmem(3),
-        out_specs=vmem(1)[0],
-        out_shape=jax.ShapeDtypeStruct((136, 256), BF16),
+        out_shape=[jax.ShapeDtypeStruct((256, 256), BF16), in_hbm((8, half + 8, 128), BF16)],
         compiler_params=params(),
         cost_estimate=cost(1e7),
         name="share",
-    )(scalars, mine, other, loss)
+    )(pieces, chunk)
 
 
 def final_kernel(s, count, tables, *refs):
-    regions, (region_out, table_out, loss_out) = refs[:8], refs[8:]
-    total = 0.0
-    for d in range(8):
-        source = (s[Z] + 8 - d) % 8
-        for k in range(2):
-            region_out[k, source] = regions[d][64 * k : 64 * k + 64, :]
-        total += jnp.sum(regions[d][128:136, :].astype(F32))
+    regions, (region_out, table_out, loss_out) = refs[:4], refs[4:]
+    total = sum(jnp.sum(tables[j, 672:680, :].astype(F32)) for j in range(8))
+    for d in range(4):
+        source = (s[ZH] + 4 - d) % 4
+        for near in range(2):
+            for k in range(2):
+                at = 128 * near + 64 * k
+                region_out[k, source, near] = regions[d][at : at + 64, :]
     loss_out[0, 0] = total / count[0, 0] / CLASSES
     for y in range(4):
         at = pl.multiple_of(672 * (s[E] ^ y), 32)
         for x in range(2):
-            table_out[pl.ds(at, 672), 128 * x : 128 * x + 128] = tables[2 * y + x]
+            table_out[pl.ds(at, 672), 128 * x : 128 * x + 128] = tables[2 * y + x, 0:672, :]
 
 
 def make_final(scalars, count, tables, regions):
     return pl.pallas_call(
         final_kernel,
-        in_specs=[smem(), smem()] + vmem(9),
+        in_specs=[smem(), smem()] + vmem(5),
         out_specs=vmem(2) + [smem()],
         out_shape=[
-            jax.ShapeDtypeStruct((2, 8, 64, 256), BF16),
+            jax.ShapeDtypeStruct((2, 4, 2, 64, 256), BF16),
             jax.ShapeDtypeStruct((2688, 256), BF16),
             jax.ShapeDtypeStruct((1, 1), F32),
         ],
@@ -410,18 +420,16 @@
     )(scalars, count, tables, *regions)
 
 
-def to_owner(x, dy, dx):
-    pairs = []
-    for y in range(4):
-        for xl in range(2):
-            for e in range(4):
-                to = (y + dy) % 4
-                pairs.append((8 * y + 4 * xl + e, 8 * to + 4 * (xl ^ dx) + (e ^ to)))
-    return lax.ppermute(x, IMG + EMB, pairs)
-
-
-def along_cls(x, d):
-    return lax.ppermute(x, CLS, [(i, (i + d) % 8) for i in range(8)])
+def over_img(x, dy, dx):
+    pairs = [
+        (2 * y + xl, 2 * ((y + dy) % 4) + (xl ^ dx)) for y in range(4) for xl in range(2)
+    ]
+    return lax.ppermute(x, IMG, pairs)
+
+
+def to_owner(x):
+    axes = ("img_0",) + EMB
+    return lax.ppermute(x, axes, [(4 * y + e, 4 * y + (e ^ y)) for y in range(4) for e in range(4)])
 
 
 def exchange(x, axes):
@@ -434,8 +442,9 @@
     xl = lax.axis_index("img_1")
     xh = lax.axis_index("emb_0")
     k = lax.axis_index("emb_1")
+    zh = lax.axis_index("cls_0")
     z = lax.axis_index(CLS)
-    scalars = jnp.stack([k, z * 2688 + xh * 1344, 2 * xh + k, y, xl, z]).astype(jnp.int32)
+    scalars = jnp.stack([k, z * 2688 + xh * 1344, 2 * xh + k, y, xl, zh]).astype(jnp.int32)
 
     t_send = take_rows(pltpu.with_memory_space_constraint(table, pltpu.HBM), 4 * (1 - xh) + y, PART)
     t_send, regions_in = lax.optimization_barrier((t_send, regions))
@@ -457,27 +466,26 @@
     keep, send, loss, count = make_focal(scalars, tables, unit, lane_f, labels[None], mask)
 
     theirs = swap(send, "emb_1")
-    loss_0 = swap(loss, "emb_0")
-    loss_1 = swap(loss, "emb_1")
-    loss_2 = lax.ppermute(loss, EMB, [(i, i ^ 3) for i in range(4)])
-    terms = make_region(scalars, keep, send, tables, blocks, inv)
-    pieces = exchange(terms.reshape(16, 128, 256), CLS_EMB).reshape(8, 2, 2, 64, 256)
-    chunks = make_table(scalars, keep, theirs, unit, [loss, loss_0, loss_1, loss_2])
-    chunks = [to_owner(chunks[o], o // 2, o % 2) for o in range(8)]
-    table_part, loss_part = make_table_sum(chunks)
-    mine, other = make_region_sum(scalars, pieces)
-    share = make_share(scalars, mine, swap(other, "emb_1"), loss_part)
-    table_part, share = lax.optimization_barrier((table_part, share))
-    table_all = exchange(table_part, IMG)
-    shares = [share] + [along_cls(share, d) for d in range(1, 8)]
+    terms = exchange(make_region(scalars, keep, send, tables, loss, blocks, inv), CLS)
+    chunks = list(make_table(scalars, keep, theirs, unit))
+    for o in range(1, 8):
+        chunks[o] = over_img(chunks[o], o // 2, o % 2)
+    table_part = to_owner(make_table_sum(chunks))
+    merged = make_merge(scalars, terms)
+    pieces = exchange(merged.reshape(8, 72, 256), NEAR).reshape(2, 2, 2, 72, 256)
+    share, message = make_share(pieces, table_part)
+    table_all = exchange(message, IMG)
+    shares = [share] + [
+        lax.ppermute(share, "cls_0", [(i, (i + d) % 4) for i in range(4)]) for d in range(1, 4)
+    ]
     region_grad, table_grad, total = make_final(scalars, count, table_all, shares)
     return (total[0, 0], region_grad.reshape(rows, 256), table_grad)
 
 
 def solution(mesh):
     torus = Mesh(
-        mesh.devices.reshape(4, 2, mesh.shape["cls"], 2, 2),
-        ("img_0", "img_1", "cls", "emb_0", "emb_1"),
+        mesh.devices.reshape(4, 2, 4, 2, 2, 2),
+        ("img_0", "img_1", "cls_0", "cls_1", "emb_0", "emb_1"),
     )
     return jax.shard_map(
         shards,

time: 142 us -> 153 us (1.077)
  waiting for transfers between devices: 30.2 us -> 56.9 us
  starting transfers between devices: 81.3 us -> 60.1 us
  local copies, waits for them, and re-layouts: 2.25 us -> 7.32 us
    ppermute x16 -> x11, starting transfers between devices: 45.8 us -> 15.1 us  [the longest x7 10.8 us: over_img(): return lax.ppermute(x, IMG, pairs)]
    all_to_all x3 -> x4, waiting for transfers between devices: 7.06 us -> 30.9 us  [exchange(): return lax.all_to_all(x, axes, split_axis=0, concat_axis=0, tiled=True)]
    all_to_all x3 -> x4, starting transfers between devices: 21.5 us -> 31.6 us  [exchange(): return lax.all_to_all(x, axes, split_axis=0, concat_axis=0, tiled=True)]
    unnamed x18 -> x38, local copies, waits for them, and re-layouts: 1.13 us -> 6.2 us
    ppermute x16 -> x11, waiting for transfers between devices: 17.7 us -> 21 us  [the longest x3 10.9 us: shards(): lax.ppermute(share, 'cls_0', [(i, (i + d) % 4) for i in range(4)])]
    ppermute x11 -> x8, starting transfers between devices: 14 us -> 13.4 us  [swap(): return lax.ppermute(x, axis, [(0, 1), (1, 0)])]
    ppermute x11 -> x8, waiting for transfers between devices: 5.44 us -> 5.1 us  [swap(): return lax.ppermute(x, axis, [(0, 1), (1, 0)])]
  transfers between devices with their start and end apart: 30 -> 23, of which waited for: 10 -> 13; matrix products, arithmetic and copies ran while one was open for 2% -> 2% of each run, Pallas kernels for 6% -> 5%
where the time goes in v1:
time: 153 us; the launch traced here: 152 us
  starting transfers between devices  60.1 us (39%)
  waiting for transfers between devices  56.9 us (37%)
  Pallas kernels  25.1 us (16%)
  local copies, waits for them, and re-layouts  7.32 us (5%)
    all_to_all x4, starting transfers between devices, exchange(): return lax.all_to_all(x, axes, split_axis=0, concat_axis=0, tiled=True)  31.6 us
    all_to_all x4, waiting for transfers between devices, exchange(): return lax.all_to_all(x, axes, split_axis=0, concat_axis=0, tiled=True)  30.9 us
    ppermute x8, starting transfers between devices, swap(): return lax.ppermute(x, axis, [(0, 1), (1, 0)])  13.4 us
    ppermute x3, waiting for transfers between devices, shards(): lax.ppermute(share, 'cls_0', [(i, (i + d) % 4) for i in range(4)])  10.9 us
    ppermute x7, starting transfers between devices, over_img(): return lax.ppermute(x, IMG, pairs)  10.8 us
    ppermute x7, waiting for transfers between devices, over_img(): return lax.ppermute(x, IMG, pairs)  10.1 us
    pallas_call x1, Pallas kernels, make_focal(): pl.pallas_call(focal_kernel, grid_spec=pltpu.PrefetchScalarGridSpec(num_s...  7.05 us
    unnamed x38, local copies, waits for them, and re-layouts  6.2 us
  transfers between devices with their start and end apart: 23, of which 13 were waited for; matrix products, arithmetic and copies ran while one was open for 2% of the time, Pallas kernels for 5%

profile of v1, /device:TPU:1, one launch (start us, length us, event | category | flops | bytes accessed | tf_op | source)
XLA Modules:
  0.0 151.9 jit_solution(1958170785304306029)
XLA Ops:
  1.6 3.6 %collective-permute-start.1 = (bf16[336,256]{1,0:T(8,128)(2,1)S(1)}, bf16[336,256]{1,0:T(8,128)(2,1)S(1)}, u32[]{:S(2)}, u32[]{:S(2)}) collective-permute-start(bf16[336,256]{1,0:T(8,128)(2,1)S(1)} %rows.1), channel_id=1, source_target_pairs={{0,2},{2,0},{1,3},{3,1},{4,6},{6,4},{5,7},{7,5},{8,10},{10,8},{9,1... | collective-permute-start | bytes 516104 | tf_op jit(solution)/shard_map/ppermute | solution.py:47
  6.9 2.2 %collective-permute-done.2.theirs = f32[8,128]{1,0:T(8,128)S(1)} collective-permute-done((f32[8,128]{1,0:T(8,128)S(1)}, f32[8,128]{1,0:T(8,128)S(1)}, u32[]{:S(2)}, u32[]{:S(2)}) %collective-permute-start.2) | collective-permute-done | bytes 4128 | tf_op jit(solution)/shard_map/ppermute | solution.py:47
  10.1 4.5 %all-to-all-start = ((bf16[4,344,256]{2,1,0:T(8,128)(2,1)}), bf16[4,344,256]{2,1,0:T(8,128)(2,1)S(1)}, u32[]{:S(2)}, u32[]{:S(2)}) async-start(bf16[4,344,256]{2,1,0:T(8,128)(2,1)} %message.1), calls=%async_computation | async-start | bytes 1409024 | tf_op jit(solution)/shard_map/all_to_all | solution.py:436
  14.5 2.6 %collective-permute-start.5 = (bf16[1024,256]{1,0:T(8,128)(2,1)}, bf16[1024,256]{1,0:T(8,128)(2,1)}, u32[]{:S(2)}, u32[]{:S(2)}) collective-permute-start(bf16[1024,256]{1,0:T(8,128)(2,1)} %a.3), channel_id=1, source_target_pairs={{0,2},{2,0},{1,3},{3,1},{4,6},{6,4},{5,7},{7,5},{8,10},{10,8},{9,1... | collective-permute-start | bytes 1572872 | tf_op jit(solution)/shard_map/ppermute | solution.py:47
  17.1 7.1 %all-to-all-done.t2 = bf16[4,344,256]{2,1,0:T(8,128)(2,1)S(1)} async-done(((bf16[4,344,256]{2,1,0:T(8,128)(2,1)}), bf16[4,344,256]{2,1,0:T(8,128)(2,1)S(1)}, u32[]{:S(2)}, u32[]{:S(2)}) %all-to-all-start) | async-done | bytes 704544 | tf_op jit(solution)/shard_map/all_to_all | solution.py:436
  24.2 2.7 %collective-permute-start.3 = (bf16[4,344,256]{2,1,0:T(8,128)(2,1)S(1)}, bf16[4,344,256]{2,1,0:T(8,128)(2,1)S(1)}, u32[]{:S(2)}, u32[]{:S(2)}) collective-permute-start(bf16[4,344,256]{2,1,0:T(8,128)(2,1)S(1)} %all-to-all-done.t2), channel_id=1, source_target_pairs={{0,1},{1,0},{2,3},{3,2},{4,5},{5,4},{6,7},{7,6},{8,9},{9,8},{10,11... | collective-permute-start | bytes 2113544 | tf_op jit(solution)/shard_map/ppermute | solution.py:47
  27.9 2.8 %collective-permute-start.6 = (bf16[1024,256]{1,0:T(8,128)(2,1)}, bf16[1024,256]{1,0:T(8,128)(2,1)}, u32[]{:S(2)}, u32[]{:S(2)}) collective-permute-start(bf16[1024,256]{1,0:T(8,128)(2,1)} %collective-permute-done.5.c), channel_id=1, source_target_pairs={{0,1},{1,0},{2,3},{3,2},{4,5},{5,4},{6,7},{7,6},{8,9},{9,8},{10,11... | collective-permute-start | bytes 1572872 | tf_op jit(solution)/shard_map/ppermute | solution.py:47
  32.6 3.0 %unit.1 = (bf16[1024,1024]{1,0:T(8,128)(2,1)S(1)}, f32[1024,128]{1,0:T(8,128)S(1)}) custom-call(bf16[1024,256]{1,0:T(8,128)(2,1)} %a.3, bf16[1024,256]{1,0:T(8,128)(2,1)} %collective-permute-done.4.b, bf16[1024,256]{1,0:T(8,128)(2,1)} %collective-permute-done.5.c, bf16[1024,256]{1,0:T(8,128)(2,1)} %collective-permute-done.6.d), custom_call_target="tpu_custom_call" | custom-call | flops 20000000 | bytes 1048576 | tf_op jit(solution)/shard_map/unit/pallas_call | solution.py:72
  35.6 7.1 %focal.1 = (bf16[672,512]{1,0:T(8,128)(2,1)S(1)}, bf16[672,512]{1,0:T(8,128)(2,1)S(1)}, f32[8,128]{1,0:T(8,128)S(1)}, f32[1,1]{1,0:T(1,128)}) custom-call(s32[6]{0:T(128)S(1)} %stack.27.s, bf16[1344,256]{1,0:T(8,128)(2,1)S(1)} %constant_dynamic-slice_fusion.t0, bf16[1344,256]{1,0:T(8,128)(2,1)S(1)} %collective-permute-done.t1, ...), custom_call_target="tpu_custom_call" | custom-call | flops 1400000000 | bytes 1048576 | tf_op jit(solution)/shard_map/focal/pallas_call | solution.py:194
  42.7 5.2 %region.1 = bf16[8,72,1024]{2,1,0:T(8,128)(2,1)} custom-call(s32[6]{0:T(128)S(1)} %stack.27.s, bf16[672,512]{1,0:T(8,128)(2,1)S(1)} %get-tuple-element.28.keep, bf16[672,512]{1,0:T(8,128)(2,1)S(1)} %get-tuple-element.29.send, bf16[1344,256]{1,0:T(8,128)(2,1)S(1)} %constant_dynamic-slice_fusion.t0, bf16[1344,256]{1,0:T(8,128)(2,1)S(1)} %collective-permute-done.t1, ...), custom_call_target="tpu_custom_call" | custom-call | flops 1400000000 | bytes 1048576 | tf_op jit(solution)/shard_map/region/pallas_call | solution.py:270
  49.6 8.3 %all-to-all-start.1 = ((bf16[8,72,1024]{2,1,0:T(8,128)(2,1)}), bf16[8,72,1024]{2,1,0:T(8,128)(2,1)S(1)}, u32[]{:S(2)}, u32[]{:S(2)}) async-start(bf16[8,72,1024]{2,1,0:T(8,128)(2,1)} %region.1), calls=%async_computation.1 | async-start | bytes 2359296 | tf_op jit(solution)/shard_map/all_to_all | solution.py:436
  58.5 2.0 %collective-permute-done.7.other = bf16[672,512]{1,0:T(8,128)(2,1)S(1)} collective-permute-done((bf16[672,512]{1,0:T(8,128)(2,1)}, bf16[672,512]{1,0:T(8,128)(2,1)S(1)}, u32[]{:S(2)}, u32[]{:S(2)}) %collective-permute-start.7) | collective-permute-done | bytes 688160 | tf_op jit(solution)/shard_map/ppermute | solution.py:47
  61.6 2.4 %table.1 = (bf16[672,128]{1,0:T(8,128)(2,1)S(1)}, bf16[672,128]{1,0:T(8,128)(2,1)}, bf16[672,128]{1,0:T(8,128)(2,1)}, bf16[672,128]{1,0:T(8,128)(2,1)S(1)}, bf16...) custom-call(s32[6]{0:T(128)S(1)} %stack.27.s, ...), custom_call_target="tpu_custom_call" | custom-call | flops 1400000000 | bytes 1048576 | tf_op jit(solution)/shard_map/table/pallas_call | solution.py:310
  68.7 1.5 collective-permute-start.9
  70.1 19.9 %all-to-all-done.1.terms = bf16[8,72,1024]{2,1,0:T(8,128)(2,1)S(1)} async-done(((bf16[8,72,1024]{2,1,0:T(8,128)(2,1)}), bf16[8,72,1024]{2,1,0:T(8,128)(2,1)S(1)}, u32[]{:S(2)}, u32[]{:S(2)}) %all-to-all-start.1) | async-done | bytes 1179680 | tf_op jit(solution)/shard_map/all_to_all | solution.py:436
  90.0 1.4 merge.1
  91.4 4.6 %all-to-all-start.2 = ((bf16[8,72,256]{2,1,0:T(8,128)(2,1)}), bf16[8,72,256]{2,1,0:T(8,128)(2,1)S(1)}, u32[]{:S(2)}, u32[]{:S(2)}) async-start(bf16[8,72,256]{2,1,0:T(8,128)(2,1)} %bitcast.18), calls=%async_computation.2 | async-start | bytes 589824 | tf_op jit(solution)/shard_map/all_to_all | solution.py:436
  96.1 1.5 %collective-permute-start.10 = (bf16[672,128]{1,0:T(8,128)(2,1)S(1)}, bf16[672,128]{1,0:T(8,128)(2,1)S(1)}, u32[]{:S(2)}, u32[]{:S(2)}) collective-permute-start(bf16[672,128]{1,0:T(8,128)(2,1)S(1)} %copy-done.15), channel_id=1, source_target_pairs={{0,96},{32,64},{64,160},{96,128},{128,224},{160,192},{192,32},{224... | collective-permute-start | bytes 516104 | tf_op jit(solution)/shard_map/ppermute | solution.py:427
  97.6 2.4 %collective-permute-start.11 = (bf16[672,128]{1,0:T(8,128)(2,1)S(1)}, bf16[672,128]{1,0:T(8,128)(2,1)S(1)}, u32[]{:S(2)}, u32[]{:S(2)}) collective-permute-start(bf16[672,128]{1,0:T(8,128)(2,1)S(1)} %copy-done.13), channel_id=1, source_target_pairs={{0,128},{32,160},{64,192},{96,224},{128,0},{160,32},{192,64},{224,... | collective-permute-start | bytes 516104 | tf_op jit(solution)/shard_map/ppermute | solution.py:427
  100.0 1.4 collective-permute-start.12
  102.6 1.5 %collective-permute-start.14 = (bf16[672,128]{1,0:T(8,128)(2,1)S(1)}, bf16[672,128]{1,0:T(8,128)(2,1)S(1)}, u32[]{:S(2)}, u32[]{:S(2)}) collective-permute-start(bf16[672,128]{1,0:T(8,128)(2,1)S(1)} %copy-done.7), channel_id=1, source_target_pairs={{0,224},{32,192},{64,32},{96,0},{128,96},{160,64},{192,160},{224,1... | collective-permute-start | bytes 516104 | tf_op jit(solution)/shard_map/ppermute | solution.py:427
  104.2 2.9 %collective-permute-done.10.refs_3_ = bf16[672,128]{1,0:T(8,128)(2,1)S(1)} collective-permute-done((bf16[672,128]{1,0:T(8,128)(2,1)S(1)}, bf16[672,128]{1,0:T(8,128)(2,1)S(1)}, u32[]{:S(2)}, u32[]{:S(2)}) %collective-permute-start.10) | collective-permute-done | bytes 172064 | tf_op jit(solution)/shard_map/ppermute | solution.py:427
  107.1 4.9 %collective-permute-done.11.refs_4_ = bf16[672,128]{1,0:T(8,128)(2,1)S(1)} collective-permute-done((bf16[672,128]{1,0:T(8,128)(2,1)S(1)}, bf16[672,128]{1,0:T(8,128)(2,1)S(1)}, u32[]{:S(2)}, u32[]{:S(2)}) %collective-permute-start.11) | collective-permute-done | bytes 172064 | tf_op jit(solution)/shard_map/ppermute | solution.py:427
  112.0 2.2 %collective-permute-done.13.refs_6_ = bf16[672,128]{1,0:T(8,128)(2,1)S(1)} collective-permute-done((bf16[672,128]{1,0:T(8,128)(2,1)S(1)}, bf16[672,128]{1,0:T(8,128)(2,1)S(1)}, u32[]{:S(2)}, u32[]{:S(2)}) %collective-permute-start.13) | collective-permute-done | bytes 172064 | tf_op jit(solution)/shard_map/ppermute | solution.py:427
  115.1 1.4 share.1
  116.5 14.2 %all-to-all-start.3 = ((bf16[8,680,128]{2,1,0:T(8,128)(2,1)}), bf16[8,680,128]{2,1,0:T(8,128)(2,1)S(1)}, u32[]{:S(2)}, u32[]{:S(2)}) async-start(bf16[8,680,128]{2,1,0:T(8,128)(2,1)} %get-tuple-element.40), calls=%async_computation.3 | async-start | bytes 2785280 | tf_op jit(solution)/shard_map/all_to_all | solution.py:436
  130.7 3.2 %collective-permute-start.17 = (bf16[256,256]{1,0:T(8,128)(2,1)S(1)}, bf16[256,256]{1,0:T(8,128)(2,1)S(1)}, u32[]{:S(2)}, u32[]{:S(2)}) collective-permute-start(bf16[256,256]{1,0:T(8,128)(2,1)S(1)} %get-tuple-element.41.refs_0_), channel_id=1, source_target_pairs={{0,16},{8,24},{16,0},{24,8},{1,17},{9,25},{17,1},{25,9},{2,18},{10... | collective-permute-start | bytes 393224 | tf_op jit(solution)/shard_map/ppermute | solution.py:479
  134.3 1.6 %collective-permute-done.18.refs_3_ = bf16[256,256]{1,0:T(8,128)(2,1)S(1)} collective-permute-done((bf16[256,256]{1,0:T(8,128)(2,1)S(1)}, bf16[256,256]{1,0:T(8,128)(2,1)S(1)}, u32[]{:S(2)}, u32[]{:S(2)}) %collective-permute-start.18) | collective-permute-done | bytes 131104 | tf_op jit(solution)/shard_map/ppermute | solution.py:479
  135.9 4.5 %collective-permute-done.17.refs_2_ = bf16[256,256]{1,0:T(8,128)(2,1)S(1)} collective-permute-done((bf16[256,256]{1,0:T(8,128)(2,1)S(1)}, bf16[256,256]{1,0:T(8,128)(2,1)S(1)}, u32[]{:S(2)}, u32[]{:S(2)}) %collective-permute-start.17) | collective-permute-done | bytes 131104 | tf_op jit(solution)/shard_map/ppermute | solution.py:479
  140.4 4.8 %collective-permute-done.16.refs_1_ = bf16[256,256]{1,0:T(8,128)(2,1)S(1)} collective-permute-done((bf16[256,256]{1,0:T(8,128)(2,1)S(1)}, bf16[256,256]{1,0:T(8,128)(2,1)S(1)}, u32[]{:S(2)}, u32[]{:S(2)}) %collective-permute-start.16) | collective-permute-done | bytes 131104 | tf_op jit(solution)/shard_map/ppermute | solution.py:479
  145.2 3.9 %all-to-all-done.3.tables = bf16[8,680,128]{2,1,0:T(8,128)(2,1)S(1)} async-done(((bf16[8,680,128]{2,1,0:T(8,128)(2,1)}), bf16[8,680,128]{2,1,0:T(8,128)(2,1)S(1)}, u32[]{:S(2)}, u32[]{:S(2)}) %all-to-all-start.3) | async-done | bytes 1392672 | tf_op jit(solution)/shard_map/all_to_all | solution.py:436
  149.2 2.6 %final.1 = (bf16[2,4,2,64,256]{4,3,2,1,0:T(8,128)(2,1)}, bf16[2688,256]{1,0:T(8,128)(2,1)}, f32[1,1]{1,0:T(1,128)}) custom-call(s32[6]{0:T(128)S(1)} %stack.27.s, f32[1,1]{1,0:T(1,128)} %get-tuple-element.27.count, bf16[8,680,128]{2,1,0:T(8,128)(2,1)S(1)} %all-to-all-done.3.tables, bf16[256,256]{1,0:T(8,128)(2,1)S(1)} %get-tuple-element.41.refs_0_, ...), custom_call_target="tpu_custom_call" | custom-call | flops 10000000 | bytes 1048576 | tf_op jit(solution)/shard_map/final/pallas_call | solution.py:408
  (71 shorter events, 16.8 us)
Async XLA Ops:
  1.6 25.3 %copy-start.16 = (bf16[2688,256]{1,0:T(8,128)(2,1)S(1)}, bf16[2688,256]{1,0:T(8,128)(2,1)}, u32[]{:S(2)}) copy-start(bf16[2688,256]{1,0:T(8,128)(2,1)} %x.1) | copy-start | bytes 4128772
  1.6 7.6 %collective-permute-start.1 = (bf16[336,256]{1,0:T(8,128)(2,1)S(1)}, bf16[336,256]{1,0:T(8,128)(2,1)S(1)}, u32[]{:S(2)}, u32[]{:S(2)}) collective-permute-start(bf16[336,256]{1,0:T(8,128)(2,1)S(1)} %rows.1), channel_id=1, source_target_pairs={{0,2},{2,0},{1,3},{3,1},{4,6},{6,4},{5,7},{7,5},{8,10},{10,8},{9,1... | collective-permute-start | bytes 516104 | tf_op jit(solution)/shard_map/ppermute | solution.py:47
  6.5 2.6 %collective-permute-start.2 = (f32[8,128]{1,0:T(8,128)S(1)}, f32[8,128]{1,0:T(8,128)S(1)}, u32[]{:S(2)}, u32[]{:S(2)}) collective-permute-start(f32[8,128]{1,0:T(8,128)S(1)} %broadcast_in_dim.15.mine), channel_id=1, source_target_pairs={{0,32},{32,0},{1,33},{33,1},{2,34},{34,2},{3,35},{35,3},{4,36},{36... | collective-permute-start | bytes 12296 | tf_op jit(solution)/shard_map/ppermute | solution.py:47
  10.1 14.1 %all-to-all-start = ((bf16[4,344,256]{2,1,0:T(8,128)(2,1)}), bf16[4,344,256]{2,1,0:T(8,128)(2,1)S(1)}, u32[]{:S(2)}, u32[]{:S(2)}) async-start(bf16[4,344,256]{2,1,0:T(8,128)(2,1)} %message.1), calls=%async_computation | async-start | bytes 1409024 | tf_op jit(solution)/shard_map/all_to_all | solution.py:436
  14.5 17.4 %copy-start.17 = (f32[1024]{0:T(1024)S(1)}, f32[1024]{0:T(1024)}, u32[]{:S(2)}) copy-start(f32[1024]{0:T(1024)} %param.9) | copy-start | bytes 12292
  14.5 17.4 %copy-start.18 = (f32[1024]{0:T(1024)S(1)}, f32[1024]{0:T(1024)}, u32[]{:S(2)}) copy-start(f32[1024]{0:T(1024)} %param.8) | copy-start | bytes 12292
  14.5 13.3 %collective-permute-start.5 = (bf16[1024,256]{1,0:T(8,128)(2,1)}, bf16[1024,256]{1,0:T(8,128)(2,1)}, u32[]{:S(2)}, u32[]{:S(2)}) collective-permute-start(bf16[1024,256]{1,0:T(8,128)(2,1)} %a.3), channel_id=1, source_target_pairs={{0,2},{2,0},{1,3},{3,1},{4,6},{6,4},{5,7},{7,5},{8,10},{10,8},{9,1... | collective-permute-start | bytes 1572872 | tf_op jit(solution)/shard_map/ppermute | solution.py:47
  24.2 11.5 %collective-permute-start.3 = (bf16[4,344,256]{2,1,0:T(8,128)(2,1)S(1)}, bf16[4,344,256]{2,1,0:T(8,128)(2,1)S(1)}, u32[]{:S(2)}, u32[]{:S(2)}) collective-permute-start(bf16[4,344,256]{2,1,0:T(8,128)(2,1)S(1)} %all-to-all-done.t2), channel_id=1, source_target_pairs={{0,1},{1,0},{2,3},{3,2},{4,5},{5,4},{6,7},{7,6},{8,9},{9,8},{10,11... | collective-permute-start | bytes 2113544 | tf_op jit(solution)/shard_map/ppermute | solution.py:47
  27.0 8.6 %collective-permute-start = (bf16[1344,256]{1,0:T(8,128)(2,1)S(1)}, bf16[1344,256]{1,0:T(8,128)(2,1)S(1)}, u32[]{:S(2)}, u32[]{:S(2)}) collective-permute-start(bf16[1344,256]{1,0:T(8,128)(2,1)S(1)} %constant_dynamic-slice_fusion.t0), channel_id=1, source_target_pairs={{0,1},{1,0},{2,3},{3,2},{4,5},{5,4},{6,7},{7,6},{8,9},{9,8},{10,11... | collective-permute-start | bytes 2064392 | tf_op jit(solution)/shard_map/ppermute | solution.py:47
  27.1 5.0 %collective-permute-start.4 = (bf16[1024,256]{1,0:T(8,128)(2,1)}, bf16[1024,256]{1,0:T(8,128)(2,1)}, u32[]{:S(2)}, u32[]{:S(2)}) collective-permute-start(bf16[1024,256]{1,0:T(8,128)(2,1)} %a.3), channel_id=1, source_target_pairs={{0,1},{1,0},{2,3},{3,2},{4,5},{5,4},{6,7},{7,6},{8,9},{9,8},{10,11... | collective-permute-start | bytes 1572872 | tf_op jit(solution)/shard_map/ppermute | solution.py:47
  27.9 4.7 %collective-permute-start.6 = (bf16[1024,256]{1,0:T(8,128)(2,1)}, bf16[1024,256]{1,0:T(8,128)(2,1)}, u32[]{:S(2)}, u32[]{:S(2)}) collective-permute-start(bf16[1024,256]{1,0:T(8,128)(2,1)} %collective-permute-done.5.c), channel_id=1, source_target_pairs={{0,1},{1,0},{2,3},{3,2},{4,5},{5,4},{6,7},{7,6},{8,9},{9,8},{10,11... | collective-permute-start | bytes 1572872 | tf_op jit(solution)/shard_map/ppermute | solution.py:47
  49.6 10.9 %copy-start.1 = (bf16[1024,1024]{1,0:T(8,128)(2,1)S(1)}, bf16[1024,1024]{1,0:T(8,128)(2,1)}, u32[]{:S(2)}) copy-start(bf16[1024,1024]{1,0:T(8,128)(2,1)} %copy-done) | copy-start | bytes 6291460
  49.6 40.4 %all-to-all-start.1 = ((bf16[8,72,1024]{2,1,0:T(8,128)(2,1)}), bf16[8,72,1024]{2,1,0:T(8,128)(2,1)S(1)}, u32[]{:S(2)}, u32[]{:S(2)}) async-start(bf16[8,72,1024]{2,1,0:T(8,128)(2,1)} %region.1), calls=%async_computation.1 | async-start | bytes 2359296 | tf_op jit(solution)/shard_map/all_to_all | solution.py:436
  57.9 2.6 %collective-permute-start.7 = (bf16[672,512]{1,0:T(8,128)(2,1)}, bf16[672,512]{1,0:T(8,128)(2,1)S(1)}, u32[]{:S(2)}, u32[]{:S(2)}) collective-permute-start(bf16[672,512]{1,0:T(8,128)(2,1)} %copy-done.4), channel_id=1, source_target_pairs={{0,1},{1,0},{2,3},{3,2},{4,5},{5,4},{6,7},{7,6},{8,9},{9,8},{10,11... | collective-permute-start | bytes 2064392 | tf_op jit(solution)/shard_map/ppermute | solution.py:47
  67.4 28.6 %copy-start.15 = (bf16[672,128]{1,0:T(8,128)(2,1)S(1)}, bf16[672,128]{1,0:T(8,128)(2,1)}, u32[]{:S(2)}) copy-start(bf16[672,128]{1,0:T(8,128)(2,1)} %copy-done.14) | copy-start | bytes 516100
  67.4 30.2 %copy-start.13 = (bf16[672,128]{1,0:T(8,128)(2,1)S(1)}, bf16[672,128]{1,0:T(8,128)(2,1)}, u32[]{:S(2)}) copy-start(bf16[672,128]{1,0:T(8,128)(2,1)} %copy-done.12) | copy-start | bytes 516100
  67.4 32.6 %copy-start.11 = (bf16[672,128]{1,0:T(8,128)(2,1)S(1)}, bf16[672,128]{1,0:T(8,128)(2,1)}, u32[]{:S(2)}) copy-start(bf16[672,128]{1,0:T(8,128)(2,1)} %copy-done.10) | copy-start | bytes 516100
  67.4 34.0 %copy-start.9 = (bf16[672,128]{1,0:T(8,128)(2,1)S(1)}, bf16[672,128]{1,0:T(8,128)(2,1)}, u32[]{:S(2)}) copy-start(bf16[672,128]{1,0:T(8,128)(2,1)} %copy-done.8) | copy-start | bytes 516100
  67.4 35.2 %copy-start.7 = (bf16[672,128]{1,0:T(8,128)(2,1)S(1)}, bf16[672,128]{1,0:T(8,128)(2,1)}, u32[]{:S(2)}) copy-start(bf16[672,128]{1,0:T(8,128)(2,1)} %copy-done.6) | copy-start | bytes 516100
  67.4 34.0 %collective-permute-start.8 = (bf16[672,128]{1,0:T(8,128)(2,1)}, bf16[672,128]{1,0:T(8,128)(2,1)S(1)}, u32[]{:S(2)}, u32[]{:S(2)}) collective-permute-start(bf16[672,128]{1,0:T(8,128)(2,1)} %get-tuple-element.33), channel_id=1, source_target_pairs={{0,32},{32,0},{64,96},{96,64},{128,160},{160,128},{192,224},{224,1... | collective-permute-start | bytes 516104 | tf_op jit(solution)/shard_map/ppermute | solution.py:427
  68.7 34.0 %collective-permute-start.9 = (bf16[672,128]{1,0:T(8,128)(2,1)}, bf16[672,128]{1,0:T(8,128)(2,1)S(1)}, u32[]{:S(2)}, u32[]{:S(2)}) collective-permute-start(bf16[672,128]{1,0:T(8,128)(2,1)} %get-tuple-element.34), channel_id=1, source_target_pairs={{0,64},{32,96},{64,128},{96,160},{128,192},{160,224},{192,0},{224,... | collective-permute-start | bytes 516104 | tf_op jit(solution)/shard_map/ppermute | solution.py:427
  91.4 23.7 %all-to-all-start.2 = ((bf16[8,72,256]{2,1,0:T(8,128)(2,1)}), bf16[8,72,256]{2,1,0:T(8,128)(2,1)S(1)}, u32[]{:S(2)}, u32[]{:S(2)}) async-start(bf16[8,72,256]{2,1,0:T(8,128)(2,1)} %bitcast.18), calls=%async_computation.2 | async-start | bytes 589824 | tf_op jit(solution)/shard_map/all_to_all | solution.py:436
  96.1 11.1 %collective-permute-start.10 = (bf16[672,128]{1,0:T(8,128)(2,1)S(1)}, bf16[672,128]{1,0:T(8,128)(2,1)S(1)}, u32[]{:S(2)}, u32[]{:S(2)}) collective-permute-start(bf16[672,128]{1,0:T(8,128)(2,1)S(1)} %copy-done.15), channel_id=1, source_target_pairs={{0,96},{32,64},{64,160},{96,128},{128,224},{160,192},{192,32},{224... | collective-permute-start | bytes 516104 | tf_op jit(solution)/shard_map/ppermute | solution.py:427
  97.6 14.4 %collective-permute-start.11 = (bf16[672,128]{1,0:T(8,128)(2,1)S(1)}, bf16[672,128]{1,0:T(8,128)(2,1)S(1)}, u32[]{:S(2)}, u32[]{:S(2)}) collective-permute-start(bf16[672,128]{1,0:T(8,128)(2,1)S(1)} %copy-done.13), channel_id=1, source_target_pairs={{0,128},{32,160},{64,192},{96,224},{128,0},{160,32},{192,64},{224,... | collective-permute-start | bytes 516104 | tf_op jit(solution)/shard_map/ppermute | solution.py:427
  100.0 12.0 %collective-permute-start.12 = (bf16[672,128]{1,0:T(8,128)(2,1)S(1)}, bf16[672,128]{1,0:T(8,128)(2,1)S(1)}, u32[]{:S(2)}, u32[]{:S(2)}) collective-permute-start(bf16[672,128]{1,0:T(8,128)(2,1)S(1)} %copy-done.11), channel_id=1, source_target_pairs={{0,160},{32,128},{64,224},{96,192},{128,32},{160,0},{192,96},{224,... | collective-permute-start | bytes 516104 | tf_op jit(solution)/shard_map/ppermute | solution.py:427
  101.4 12.8 %collective-permute-start.13 = (bf16[672,128]{1,0:T(8,128)(2,1)S(1)}, bf16[672,128]{1,0:T(8,128)(2,1)S(1)}, u32[]{:S(2)}, u32[]{:S(2)}) collective-permute-start(bf16[672,128]{1,0:T(8,128)(2,1)S(1)} %copy-done.9), channel_id=1, source_target_pairs={{0,192},{32,224},{64,0},{96,32},{128,64},{160,96},{192,128},{224,1... | collective-permute-start | bytes 516104 | tf_op jit(solution)/shard_map/ppermute | solution.py:427
  102.6 11.6 %collective-permute-start.14 = (bf16[672,128]{1,0:T(8,128)(2,1)S(1)}, bf16[672,128]{1,0:T(8,128)(2,1)S(1)}, u32[]{:S(2)}, u32[]{:S(2)}) collective-permute-start(bf16[672,128]{1,0:T(8,128)(2,1)S(1)} %copy-done.7), channel_id=1, source_target_pairs={{0,224},{32,192},{64,32},{96,0},{128,96},{160,64},{192,160},{224,1... | collective-permute-start | bytes 516104 | tf_op jit(solution)/shard_map/ppermute | solution.py:427
  114.4 0.7 collective-permute-start.15
  116.5 32.7 %all-to-all-start.3 = ((bf16[8,680,128]{2,1,0:T(8,128)(2,1)}), bf16[8,680,128]{2,1,0:T(8,128)(2,1)S(1)}, u32[]{:S(2)}, u32[]{:S(2)}) async-start(bf16[8,680,128]{2,1,0:T(8,128)(2,1)} %get-tuple-element.40), calls=%async_computation.3 | async-start | bytes 2785280 | tf_op jit(solution)/shard_map/all_to_all | solution.py:436
  130.7 5.2 %collective-permute-start.18 = (bf16[256,256]{1,0:T(8,128)(2,1)S(1)}, bf16[256,256]{1,0:T(8,128)(2,1)S(1)}, u32[]{:S(2)}, u32[]{:S(2)}) collective-permute-start(bf16[256,256]{1,0:T(8,128)(2,1)S(1)} %get-tuple-element.41.refs_0_), channel_id=1, source_target_pairs={{0,24},{8,0},{16,8},{24,16},{1,25},{9,1},{17,9},{25,17},{2,26},{10... | collective-permute-start | bytes 393224 | tf_op jit(solution)/shard_map/ppermute | solution.py:479
  130.7 9.7 %collective-permute-start.17 = (bf16[256,256]{1,0:T(8,128)(2,1)S(1)}, bf16[256,256]{1,0:T(8,128)(2,1)S(1)}, u32[]{:S(2)}, u32[]{:S(2)}) collective-permute-start(bf16[256,256]{1,0:T(8,128)(2,1)S(1)} %get-tuple-element.41.refs_0_), channel_id=1, source_target_pairs={{0,16},{8,24},{16,0},{24,8},{1,17},{9,25},{17,1},{25,9},{2,18},{10... | collective-permute-start | bytes 393224 | tf_op jit(solution)/shard_map/ppermute | solution.py:479
  133.9 11.3 %collective-permute-start.16 = (bf16[256,256]{1,0:T(8,128)(2,1)S(1)}, bf16[256,256]{1,0:T(8,128)(2,1)S(1)}, u32[]{:S(2)}, u32[]{:S(2)}) collective-permute-start(bf16[256,256]{1,0:T(8,128)(2,1)S(1)} %get-tuple-element.41.refs_0_), channel_id=1, source_target_pairs={{0,8},{8,16},{16,24},{24,0},{1,9},{9,17},{17,25},{25,1},{2,10},{10... | collective-permute-start | bytes 393224 | tf_op jit(solution)/shard_map/ppermute | solution.py:479
  (10 other events, 17.9 us)

commit v2 on v1

--- a/solution.py
+++ b/solution.py
@@ -224,12 +224,11 @@
     )(scalars, *tables, unit, lane_f, labels, mask)
 
 
-def region_kernel(s, keep, send, t0, t1, t2, t3, loss, a, b, c, d, inv_ref, out, acc):
+def region_kernel(s, keep, send, t0, t1, t2, t3, a, b, c, d, inv_ref, out, acc):
     half = keep.shape[0]
     k = s[K]
     tile = acc.shape[0]
     blocks = (a, b, c, d)
-    extra = split3(jnp.sum(loss[...]), 256).astype(BF16)
     mine_at = pl.multiple_of(k * half, 32)
     theirs_at = pl.multiple_of((1 - k) * half, 32)
 
@@ -259,11 +258,10 @@
             grad = inv * (acc[:, cols] - r[rows, :].astype(F32) * back)
             for p in range(tile // 64):
                 z = tile // 64 * i + p
-                out[z, 0:64, cols] = grad[64 * p : 64 * p + 64, :].astype(BF16)
-                out[z, 64:72, cols] = extra
-
-
-def make_region(scalars, keep, send, tables, loss, blocks, inv):
+                out[z, :, cols] = grad[64 * p : 64 * p + 64, :].astype(BF16)
+
+
+def make_region(scalars, keep, send, tables, blocks, inv):
     half, rows = keep.shape
     flat = pl.BlockSpec((2 * half, 256), lambda i, s: (0, 0))
     cube = pl.BlockSpec((4, PART + 8, 256), lambda i, s: (0, 0, 0))
@@ -275,26 +273,26 @@
             in_specs=[pl.BlockSpec((half, rows), lambda i, s: (0, 0))] * 2
             + [flat] * 2
             + [cube] * 2
-            + [pl.BlockSpec((8, 128), lambda i, s: (0, 0))]
             + [pl.BlockSpec((rows, 256), lambda i, s: (s[K], 0))] * 4
             + [pl.BlockSpec((rows, 128), lambda i, s: (s[K], 0))],
-            out_specs=pl.BlockSpec((8, 72, 1024), lambda i, s: (0, 0, 0)),
+            out_specs=pl.BlockSpec((8, 64, 1024), lambda i, s: (0, 0, 0)),
             scratch_shapes=[pltpu.VMEM((256, 1024), F32)],
         ),
-        out_shape=in_hbm((8, 72, 1024), BF16),
+        out_shape=in_hbm((8, 64, 1024), BF16),
         compiler_params=params(24),
         cost_estimate=cost(1.4e9),
         name="region",
-    )(scalars, keep, send, *tables, loss, *blocks, inv)
-
-
-def table_kernel(s, keep, other, unit, *refs):
+    )(scalars, keep, send, *tables, *blocks, inv)
+
+
+def table_kernel(s, keep, other, unit, loss, *refs):
     outs, acc = refs[:8], refs[8]
-    _, rows = other.shape
+    half, rows = other.shape
     mine = keep[...]
     theirs = other[...]
     mine_at = pl.multiple_of(s[K] * rows, rows)
     theirs_at = pl.multiple_of((1 - s[K]) * rows, rows)
+    extra = split3(jnp.sum(loss[...]), 128).astype(BF16)
     for dy in range(4):
         cols = pl.ds(pl.multiple_of(256 * ((s[Y] + dy) % 4), 256), 256)
         acc[...] = jnp.dot(
@@ -302,45 +300,50 @@
         ) + jnp.dot(theirs, unit[pl.ds(theirs_at, rows), cols], preferred_element_type=F32)
         for dx in range(2):
             at = pl.multiple_of(128 * (s[XL] ^ dx), 128)
-            outs[2 * dy + dx][...] = acc[:, pl.ds(at, 128)].astype(BF16)
-
-
-def make_table(scalars, keep, other, unit):
+            out = outs[2 * dy + dx]
+            out[0:half, :] = acc[:, pl.ds(at, 128)].astype(BF16)
+            out[half : half + 8, :] = extra
+
+
+def make_table(scalars, keep, other, unit, loss):
     half = other.shape[0]
     return pl.pallas_call(
         table_kernel,
-        in_specs=[smem()] + vmem(3),
+        in_specs=[smem()] + vmem(4),
         out_specs=vmem(8),
-        out_shape=[jax.ShapeDtypeStruct((half, 128), BF16)] * 8,
+        out_shape=[jax.ShapeDtypeStruct((half + 8, 128), BF16)] * 8,
         scratch_shapes=[pltpu.VMEM((half, 256), F32)],
         compiler_params=params(),
         cost_estimate=cost(1.4e9),
         name="table",
-    )(scalars, keep, other, unit)
+    )(scalars, keep, other, unit, loss)
 
 
 def table_sum_kernel(*refs):
-    terms, out = refs[:8], refs[8]
-    out[...] = sum(t[...].astype(F32) for t in terms).astype(BF16)
+    terms, (out, loss) = refs[:8], refs[8:]
+    half = out.shape[0]
+    out[...] = sum(t[0:half, :].astype(F32) for t in terms).astype(BF16)
+    loss[...] = sum(t[half : half + 8, :].astype(F32) for t in terms)
 
 
 def make_table_sum(terms):
     return pl.pallas_call(
         table_sum_kernel,
         in_specs=vmem(8),
-        out_specs=vmem(1)[0],
-        out_shape=jax.ShapeDtypeStruct(terms[0].shape, BF16),
+        out_specs=vmem(2),
+        out_shape=[
+            jax.ShapeDtypeStruct((terms[0].shape[0] - 8, 128), BF16),
+            jax.ShapeDtypeStruct((8, 128), F32),
+        ],
         compiler_params=params(),
         cost_estimate=cost(1e7),
         name="table_sum",
     )(*terms)
 
 
-def merge_kernel(s, terms, out):
-    total = sum(terms[z].astype(F32) for z in range(8))
-    loss = jnp.sum(total[64:72, 0:256])
-    extra = split3(loss, 256).astype(BF16)
-    total = total[0:64, :].astype(BF16)
+def merge_kernel(s, terms, loss, out):
+    total = sum(terms[z].astype(F32) for z in range(8)).astype(BF16)
+    extra = split3(jnp.sum(loss[...]), 256).astype(BF16)
     for q in range(4):
         to = s[E] ^ q
         for near in range(2):
@@ -348,31 +351,34 @@
             out[near, to, 64:72, :] = extra
 
 
-def make_merge(scalars, terms):
+def make_merge(scalars, terms, loss):
     return pl.pallas_call(
         merge_kernel,
-        in_specs=[smem()] + vmem(1),
+        in_specs=[smem()] + vmem(2),
         out_specs=vmem(1)[0],
         out_shape=in_hbm((2, 4, 72, 256), BF16),
         compiler_params=params(),
         cost_estimate=cost(1e7),
         name="merge",
-    )(scalars, terms)
+    )(scalars, terms, loss)
 
 
 def share_kernel(pieces, chunk, out, message):
-    half = chunk.shape[0]
     for near in range(2):
         for k in range(2):
             both = pieces[near, 0, k, 0:64, :].astype(F32) + pieces[near, 1, k, 0:64, :].astype(F32)
             at = 128 * near + 64 * k
             out[at : at + 64, :] = both.astype(BF16)
-    loss = sum(jnp.sum(pieces[0, x, k, 64:72, :].astype(F32)) for x in range(2) for k in range(2))
-    extra = split3(loss, 128).astype(BF16)
+    loss = sum(
+        jnp.sum(pieces[near, x, k, 64:72, :].astype(F32))
+        for near in range(2)
+        for x in range(2)
+        for k in range(2)
+    )
+    out[256:264, :] = split3(loss, 256).astype(BF16)
     rows = chunk[...]
     for j in range(8):
-        message[j, 0:half, :] = rows
-        message[j, half : half + 8, :] = extra
+        message[j] = rows
 
 
 def make_share(pieces, chunk):
@@ -381,7 +387,7 @@
         share_kernel,
         in_specs=vmem(2),
         out_specs=vmem(2),
-        out_shape=[jax.ShapeDtypeStruct((256, 256), BF16), in_hbm((8, half + 8, 128), BF16)],
+        out_shape=[jax.ShapeDtypeStruct((264, 256), BF16), in_hbm((8, half, 128), BF16)],
         compiler_params=params(),
         cost_estimate=cost(1e7),
         name="share",
@@ -390,18 +396,19 @@
 
 def final_kernel(s, count, tables, *refs):
     regions, (region_out, table_out, loss_out) = refs[:4], refs[4:]
-    total = sum(jnp.sum(tables[j, 672:680, :].astype(F32)) for j in range(8))
+    total = 0.0
     for d in range(4):
         source = (s[ZH] + 4 - d) % 4
         for near in range(2):
             for k in range(2):
                 at = 128 * near + 64 * k
                 region_out[k, source, near] = regions[d][at : at + 64, :]
+        total += jnp.sum(regions[d][256:264, :].astype(F32))
     loss_out[0, 0] = total / count[0, 0] / CLASSES
     for y in range(4):
         at = pl.multiple_of(672 * (s[E] ^ y), 32)
         for x in range(2):
-            table_out[pl.ds(at, 672), 128 * x : 128 * x + 128] = tables[2 * y + x, 0:672, :]
+            table_out[pl.ds(at, 672), 128 * x : 128 * x + 128] = tables[2 * y + x]
 
 
 def make_final(scalars, count, tables, regions):
@@ -452,7 +459,8 @@
     r_far = swap(regions_in, "emb_0")
     r_near = swap(regions_in, "emb_1")
     local = jnp.broadcast_to(jnp.sum((labels >= 0).astype(F32)), (8, 128))
-    t_far = exchange(make_message(t_got, local, swap(local, "img_1")), "img_0")
+    local_other = swap(local, "img_1")
+    t_far = exchange(make_message(t_got, local, local_other), "img_0")
     t_own = lax.dynamic_slice_in_dim(table, xh * 1344, 1344, 0)
     t_near = swap(t_own, "emb_1")
     r_both = swap(r_far, "emb_1")
@@ -466,12 +474,13 @@
     keep, send, loss, count = make_focal(scalars, tables, unit, lane_f, labels[None], mask)
 
     theirs = swap(send, "emb_1")
-    terms = exchange(make_region(scalars, keep, send, tables, loss, blocks, inv), CLS)
-    chunks = list(make_table(scalars, keep, theirs, unit))
+    terms = exchange(make_region(scalars, keep, send, tables, blocks, inv), CLS)
+    chunks = list(make_table(scalars, keep, theirs, unit, loss))
     for o in range(1, 8):
         chunks[o] = over_img(chunks[o], o // 2, o % 2)
-    table_part = to_owner(make_table_sum(chunks))
-    merged = make_merge(scalars, terms)
+    table_part, loss_part = make_table_sum(chunks)
+    table_part = to_owner(table_part)
+    merged = make_merge(scalars, terms, loss_part)
     pieces = exchange(merged.reshape(8, 72, 256), NEAR).reshape(2, 2, 2, 72, 256)
     share, message = make_share(pieces, table_part)
     table_all = exchange(message, IMG)

time: 153 us -> 134 us (0.88)
  waiting for transfers between devices: 56.9 us -> 43.2 us
  local copies, waits for them, and re-layouts: 7.32 us -> 3.96 us
  starting transfers between devices: 60.1 us -> 58.3 us
    all_to_all x4, waiting for transfers between devices: 30.9 us -> 19.7 us  [exchange(): return lax.all_to_all(x, axes, split_axis=0, concat_axis=0, tiled=True)]
    all_to_all x4, starting transfers between devices: 31.6 us -> 27.8 us  [exchange(): return lax.all_to_all(x, axes, split_axis=0, concat_axis=0, tiled=True)]
    unnamed x38 -> x18, local copies, waits for them, and re-layouts: 6.2 us -> 2.84 us
    ppermute x3, starting transfers between devices: 3.6 us -> 6.56 us  [shards(): lax.ppermute(share, 'cls_0', [(i, (i + d) % 4) for i in range(4)])]
    ppermute x3, waiting for transfers between devices: 10.9 us -> 8.05 us  [shards(): lax.ppermute(share, 'cls_0', [(i, (i + d) % 4) for i in range(4)])]
  transfers between devices with their start and end apart: 23 -> 23, of which waited for: 13 -> 13; matrix products, arithmetic and copies ran while one was open for 2% -> 2% of each run, Pallas kernels for 5% -> 4%
where the time goes in v2:
time: 134 us; the launch traced here: 133 us
  starting transfers between devices  58.3 us (44%)
  waiting for transfers between devices  43.2 us (32%)
  Pallas kernels  25.1 us (19%)
  local copies, waits for them, and re-layouts  3.96 us (3%)
  other arithmetic  1.46 us (1%)
    all_to_all x4, starting transfers between devices, exchange(): return lax.all_to_all(x, axes, split_axis=0, concat_axis=0, tiled=True)  27.8 us
    all_to_all x4, waiting for transfers between devices, exchange(): return lax.all_to_all(x, axes, split_axis=0, concat_axis=0, tiled=True)  19.7 us
    ppermute x8, starting transfers between devices, swap(): return lax.ppermute(x, axis, [(0, 1), (1, 0)])  13.5 us
    ppermute x7, waiting for transfers between devices, over_img(): return lax.ppermute(x, IMG, pairs)  10.4 us
    ppermute x7, starting transfers between devices, over_img(): return lax.ppermute(x, IMG, pairs)  9.79 us
    ppermute x3, waiting for transfers between devices, shards(): lax.ppermute(share, 'cls_0', [(i, (i + d) % 4) for i in range(4)])  8.05 us
    pallas_call x1, Pallas kernels, make_focal(): pl.pallas_call(focal_kernel, grid_spec=pltpu.PrefetchScalarGridSpec(num_s...  7.08 us
    ppermute x3, starting transfers between devices, shards(): lax.ppermute(share, 'cls_0', [(i, (i + d) % 4) for i in range(4)])  6.56 us
  transfers between devices with their start and end apart: 23, of which 13 were waited for; matrix products, arithmetic and copies ran while one was open for 2% of the time, Pallas kernels for 4%

profile of v2, /device:TPU:1, one launch (start us, length us, event | category | flops | bytes accessed | tf_op | source)
XLA Modules:
  0.0 133.0 jit_solution(17433317250600328796)
XLA Ops:
  1.6 3.6 %collective-permute-start.1 = (bf16[336,256]{1,0:T(8,128)(2,1)S(1)}, bf16[336,256]{1,0:T(8,128)(2,1)S(1)}, u32[]{:S(2)}, u32[]{:S(2)}) collective-permute-start(bf16[336,256]{1,0:T(8,128)(2,1)S(1)} %rows.1), channel_id=1, source_target_pairs={{0,2},{2,0},{1,3},{3,1},{4,6},{6,4},{5,7},{7,5},{8,10},{10,8},{9,1... | collective-permute-start | bytes 516104 | tf_op jit(solution)/shard_map/ppermute | solution.py:47
  6.9 2.2 %collective-permute-done.2.theirs = f32[8,128]{1,0:T(8,128)S(1)} collective-permute-done((f32[8,128]{1,0:T(8,128)S(1)}, f32[8,128]{1,0:T(8,128)S(1)}, u32[]{:S(2)}, u32[]{:S(2)}) %collective-permute-start.2) | collective-permute-done | bytes 4128 | tf_op jit(solution)/shard_map/ppermute | solution.py:47
  10.1 4.5 %all-to-all-start = ((bf16[4,344,256]{2,1,0:T(8,128)(2,1)}), bf16[4,344,256]{2,1,0:T(8,128)(2,1)S(1)}, u32[]{:S(2)}, u32[]{:S(2)}) async-start(bf16[4,344,256]{2,1,0:T(8,128)(2,1)} %message.1), calls=%async_computation | async-start | bytes 1409024 | tf_op jit(solution)/shard_map/all_to_all | solution.py:443
  14.5 2.6 %collective-permute-start.5 = (bf16[1024,256]{1,0:T(8,128)(2,1)}, bf16[1024,256]{1,0:T(8,128)(2,1)}, u32[]{:S(2)}, u32[]{:S(2)}) collective-permute-start(bf16[1024,256]{1,0:T(8,128)(2,1)} %a.3), channel_id=1, source_target_pairs={{0,2},{2,0},{1,3},{3,1},{4,6},{6,4},{5,7},{7,5},{8,10},{10,8},{9,1... | collective-permute-start | bytes 1572872 | tf_op jit(solution)/shard_map/ppermute | solution.py:47
  17.1 7.1 %all-to-all-done.t2 = bf16[4,344,256]{2,1,0:T(8,128)(2,1)S(1)} async-done(((bf16[4,344,256]{2,1,0:T(8,128)(2,1)}), bf16[4,344,256]{2,1,0:T(8,128)(2,1)S(1)}, u32[]{:S(2)}, u32[]{:S(2)}) %all-to-all-start) | async-done | bytes 704544 | tf_op jit(solution)/shard_map/all_to_all | solution.py:443
  24.2 2.7 %collective-permute-start.3 = (bf16[4,344,256]{2,1,0:T(8,128)(2,1)S(1)}, bf16[4,344,256]{2,1,0:T(8,128)(2,1)S(1)}, u32[]{:S(2)}, u32[]{:S(2)}) collective-permute-start(bf16[4,344,256]{2,1,0:T(8,128)(2,1)S(1)} %all-to-all-done.t2), channel_id=1, source_target_pairs={{0,1},{1,0},{2,3},{3,2},{4,5},{5,4},{6,7},{7,6},{8,9},{9,8},{10,11... | collective-permute-start | bytes 2113544 | tf_op jit(solution)/shard_map/ppermute | solution.py:47
  27.9 2.8 %collective-permute-start.6 = (bf16[1024,256]{1,0:T(8,128)(2,1)}, bf16[1024,256]{1,0:T(8,128)(2,1)}, u32[]{:S(2)}, u32[]{:S(2)}) collective-permute-start(bf16[1024,256]{1,0:T(8,128)(2,1)} %collective-permute-done.5.c), channel_id=1, source_target_pairs={{0,1},{1,0},{2,3},{3,2},{4,5},{5,4},{6,7},{7,6},{8,9},{9,8},{10,11... | collective-permute-start | bytes 1572872 | tf_op jit(solution)/shard_map/ppermute | solution.py:47
  32.6 3.0 %unit.1 = (bf16[1024,1024]{1,0:T(8,128)(2,1)S(1)}, f32[1024,128]{1,0:T(8,128)S(1)}) custom-call(bf16[1024,256]{1,0:T(8,128)(2,1)} %a.3, bf16[1024,256]{1,0:T(8,128)(2,1)} %collective-permute-done.4.b, bf16[1024,256]{1,0:T(8,128)(2,1)} %collective-permute-done.5.c, bf16[1024,256]{1,0:T(8,128)(2,1)} %collective-permute-done.6.d), custom_call_target="tpu_custom_call" | custom-call | flops 20000000 | bytes 1048576 | tf_op jit(solution)/shard_map/unit/pallas_call | solution.py:72
  35.6 7.1 %focal.1 = (bf16[672,512]{1,0:T(8,128)(2,1)S(1)}, bf16[672,512]{1,0:T(8,128)(2,1)S(1)}, f32[8,128]{1,0:T(8,128)S(1)}, f32[1,1]{1,0:T(1,128)}) custom-call(s32[6]{0:T(128)S(1)} %stack.27.s, bf16[1344,256]{1,0:T(8,128)(2,1)S(1)} %constant_dynamic-slice_fusion.t0, bf16[1344,256]{1,0:T(8,128)(2,1)S(1)} %collective-permute-done.t1, ...), custom_call_target="tpu_custom_call" | custom-call | flops 1400000000 | bytes 1048576 | tf_op jit(solution)/shard_map/focal/pallas_call | solution.py:194
  42.7 5.2 %region.1 = bf16[8,64,1024]{2,1,0:T(8,128)(2,1)} custom-call(s32[6]{0:T(128)S(1)} %stack.27.s, bf16[672,512]{1,0:T(8,128)(2,1)S(1)} %get-tuple-element.30.keep, bf16[672,512]{1,0:T(8,128)(2,1)S(1)} %get-tuple-element.31.send, bf16[1344,256]{1,0:T(8,128)(2,1)S(1)} %constant_dynamic-slice_fusion.t0, bf16[1344,256]{1,0:T(8,128)(2,1)S(1)} %collective-permute-done.t1, ...), custom_call_target="tpu_custom_call" | custom-call | flops 1400000000 | bytes 1048576 | tf_op jit(solution)/shard_map/region/pallas_call | solution.py:268
  49.6 8.3 %all-to-all-start.1 = ((bf16[8,64,1024]{2,1,0:T(8,128)(2,1)}), bf16[8,64,1024]{2,1,0:T(8,128)(2,1)S(1)}, u32[]{:S(2)}, u32[]{:S(2)}) async-start(bf16[8,64,1024]{2,1,0:T(8,128)(2,1)} %region.1), calls=%async_computation.1 | async-start | bytes 2097152 | tf_op jit(solution)/shard_map/all_to_all | solution.py:443
  58.6 2.0 %collective-permute-done.7.other = bf16[672,512]{1,0:T(8,128)(2,1)S(1)} collective-permute-done((bf16[672,512]{1,0:T(8,128)(2,1)}, bf16[672,512]{1,0:T(8,128)(2,1)S(1)}, u32[]{:S(2)}, u32[]{:S(2)}) %collective-permute-start.7) | collective-permute-done | bytes 688160 | tf_op jit(solution)/shard_map/ppermute | solution.py:47
  61.7 2.4 %table.1 = (bf16[680,128]{1,0:T(8,128)(2,1)S(1)}, bf16[680,128]{1,0:T(8,128)(2,1)S(1)}, bf16[680,128]{1,0:T(8,128)(2,1)S(1)}, bf16[680,128]{1,0:T(8,128)(2,1)S(1...) custom-call(s32[6]{0:T(128)S(1)} %stack.27.s, ...), custom_call_target="tpu_custom_call" | custom-call | flops 1400000000 | bytes 1048576 | tf_op jit(solution)/shard_map/table/pallas_call | solution.py:310
  65.3 1.5 %collective-permute-start.9 = (bf16[680,128]{1,0:T(8,128)(2,1)S(1)}, bf16[680,128]{1,0:T(8,128)(2,1)S(1)}, u32[]{:S(2)}, u32[]{:S(2)}) collective-permute-start(bf16[680,128]{1,0:T(8,128)(2,1)S(1)} %get-tuple-element.36), channel_id=1, source_target_pairs={{0,64},{32,96},{64,128},{96,160},{128,192},{160,224},{192,0},{224,... | collective-permute-start | bytes 522248 | tf_op jit(solution)/shard_map/ppermute | solution.py:434
  68.0 1.3 collective-permute-start.11
  69.3 2.6 %collective-permute-start.12 = (bf16[680,128]{1,0:T(8,128)(2,1)S(1)}, bf16[680,128]{1,0:T(8,128)(2,1)S(1)}, u32[]{:S(2)}, u32[]{:S(2)}) collective-permute-start(bf16[680,128]{1,0:T(8,128)(2,1)S(1)} %get-tuple-element.39), channel_id=1, source_target_pairs={{0,160},{32,128},{64,224},{96,192},{128,32},{160,0},{192,96},{224,... | collective-permute-start | bytes 522248 | tf_op jit(solution)/shard_map/ppermute | solution.py:434
  71.8 1.5 %collective-permute-start.13 = (bf16[680,128]{1,0:T(8,128)(2,1)S(1)}, bf16[680,128]{1,0:T(8,128)(2,1)S(1)}, u32[]{:S(2)}, u32[]{:S(2)}) collective-permute-start(bf16[680,128]{1,0:T(8,128)(2,1)S(1)} %get-tuple-element.40), channel_id=1, source_target_pairs={{0,192},{32,224},{64,0},{96,32},{128,64},{160,96},{192,128},{224,1... | collective-permute-start | bytes 522248 | tf_op jit(solution)/shard_map/ppermute | solution.py:434
  73.9 2.1 %collective-permute-done.10.refs_3_ = bf16[680,128]{1,0:T(8,128)(2,1)S(1)} collective-permute-done((bf16[680,128]{1,0:T(8,128)(2,1)S(1)}, bf16[680,128]{1,0:T(8,128)(2,1)S(1)}, u32[]{:S(2)}, u32[]{:S(2)}) %collective-permute-start.10) | collective-permute-done | bytes 174112 | tf_op jit(solution)/shard_map/ppermute | solution.py:434
  76.0 8.2 %collective-permute-done.11.refs_4_ = bf16[680,128]{1,0:T(8,128)(2,1)S(1)} collective-permute-done((bf16[680,128]{1,0:T(8,128)(2,1)S(1)}, bf16[680,128]{1,0:T(8,128)(2,1)S(1)}, u32[]{:S(2)}, u32[]{:S(2)}) %collective-permute-start.11) | collective-permute-done | bytes 174112 | tf_op jit(solution)/shard_map/ppermute | solution.py:434
  84.5 2.7 %all-to-all-done.1.terms = bf16[8,64,1024]{2,1,0:T(8,128)(2,1)S(1)} async-done(((bf16[8,64,1024]{2,1,0:T(8,128)(2,1)}), bf16[8,64,1024]{2,1,0:T(8,128)(2,1)S(1)}, u32[]{:S(2)}, u32[]{:S(2)}) %all-to-all-start.1) | async-done | bytes 1048608 | tf_op jit(solution)/shard_map/all_to_all | solution.py:443
  87.2 1.4 %merge.1 = bf16[2,4,72,256]{3,2,1,0:T(8,128)(2,1)} custom-call(s32[6]{0:T(128)S(1)} %stack.27.s, bf16[8,64,1024]{2,1,0:T(8,128)(2,1)S(1)} %all-to-all-done.1.terms, f32[8,128]{1,0:T(8,128)S(1)} %get-tuple-element.42.loss), custom_call_target="tpu_custom_call" | custom-call | flops 10000000 | bytes 1048576 | tf_op jit(solution)/shard_map/merge/pallas_call | solution.py:355
  88.6 5.4 %all-to-all-start.2 = ((bf16[8,72,256]{2,1,0:T(8,128)(2,1)}), bf16[8,72,256]{2,1,0:T(8,128)(2,1)S(1)}, u32[]{:S(2)}, u32[]{:S(2)}) async-start(bf16[8,72,256]{2,1,0:T(8,128)(2,1)} %bitcast.18), calls=%async_computation.2 | async-start | bytes 589824 | tf_op jit(solution)/shard_map/all_to_all | solution.py:443
  94.7 5.9 %all-to-all-done.2 = bf16[8,72,256]{2,1,0:T(8,128)(2,1)S(1)} async-done(((bf16[8,72,256]{2,1,0:T(8,128)(2,1)}), bf16[8,72,256]{2,1,0:T(8,128)(2,1)S(1)}, u32[]{:S(2)}, u32[]{:S(2)}) %all-to-all-start.2) | async-done | bytes 294944 | tf_op jit(solution)/shard_map/all_to_all | solution.py:443
  100.6 1.3 share.1
  101.9 9.6 %all-to-all-start.3 = ((bf16[8,672,128]{2,1,0:T(8,128)(2,1)}), bf16[8,672,128]{2,1,0:T(8,128)(2,1)S(1)}, u32[]{:S(2)}, u32[]{:S(2)}) async-start(bf16[8,672,128]{2,1,0:T(8,128)(2,1)} %get-tuple-element.44), calls=%async_computation.3 | async-start | bytes 2752512 | tf_op jit(solution)/shard_map/all_to_all | solution.py:443
  111.5 2.4 %collective-permute-start.18 = (bf16[264,256]{1,0:T(8,128)(2,1)S(1)}, bf16[264,256]{1,0:T(8,128)(2,1)S(1)}, u32[]{:S(2)}, u32[]{:S(2)}) collective-permute-start(bf16[264,256]{1,0:T(8,128)(2,1)S(1)} %get-tuple-element.45.refs_0_), channel_id=1, source_target_pairs={{0,24},{8,0},{16,8},{24,16},{1,25},{9,1},{17,9},{25,17},{2,26},{10... | collective-permute-start | bytes 405512 | tf_op jit(solution)/shard_map/ppermute | solution.py:488
  113.9 3.0 %collective-permute-start.17 = (bf16[264,256]{1,0:T(8,128)(2,1)S(1)}, bf16[264,256]{1,0:T(8,128)(2,1)S(1)}, u32[]{:S(2)}, u32[]{:S(2)}) collective-permute-start(bf16[264,256]{1,0:T(8,128)(2,1)S(1)} %get-tuple-element.45.refs_0_), channel_id=1, source_target_pairs={{0,16},{8,24},{16,0},{24,8},{1,17},{9,25},{17,1},{25,9},{2,18},{10... | collective-permute-start | bytes 405512 | tf_op jit(solution)/shard_map/ppermute | solution.py:488
  118.1 1.4 %collective-permute-done.18.refs_3_ = bf16[264,256]{1,0:T(8,128)(2,1)S(1)} collective-permute-done((bf16[264,256]{1,0:T(8,128)(2,1)S(1)}, bf16[264,256]{1,0:T(8,128)(2,1)S(1)}, u32[]{:S(2)}, u32[]{:S(2)}) %collective-permute-start.18) | collective-permute-done | bytes 135200 | tf_op jit(solution)/shard_map/ppermute | solution.py:488
  119.5 3.4 %collective-permute-done.17.refs_2_ = bf16[264,256]{1,0:T(8,128)(2,1)S(1)} collective-permute-done((bf16[264,256]{1,0:T(8,128)(2,1)S(1)}, bf16[264,256]{1,0:T(8,128)(2,1)S(1)}, u32[]{:S(2)}, u32[]{:S(2)}) %collective-permute-start.17) | collective-permute-done | bytes 135200 | tf_op jit(solution)/shard_map/ppermute | solution.py:488
  122.9 3.2 %collective-permute-done.16.refs_1_ = bf16[264,256]{1,0:T(8,128)(2,1)S(1)} collective-permute-done((bf16[264,256]{1,0:T(8,128)(2,1)S(1)}, bf16[264,256]{1,0:T(8,128)(2,1)S(1)}, u32[]{:S(2)}, u32[]{:S(2)}) %collective-permute-start.16) | collective-permute-done | bytes 135200 | tf_op jit(solution)/shard_map/ppermute | solution.py:488
  126.1 4.1 %all-to-all-done.3.tables = bf16[8,672,128]{2,1,0:T(8,128)(2,1)S(1)} async-done(((bf16[8,672,128]{2,1,0:T(8,128)(2,1)}), bf16[8,672,128]{2,1,0:T(8,128)(2,1)S(1)}, u32[]{:S(2)}, u32[]{:S(2)}) %all-to-all-start.3) | async-done | bytes 1376288 | tf_op jit(solution)/shard_map/all_to_all | solution.py:443
  130.2 2.7 %final.1 = (bf16[2,4,2,64,256]{4,3,2,1,0:T(8,128)(2,1)}, bf16[2688,256]{1,0:T(8,128)(2,1)}, f32[1,1]{1,0:T(1,128)}) custom-call(s32[6]{0:T(128)S(1)} %stack.27.s, f32[1,1]{1,0:T(1,128)} %get-tuple-element.29.count, bf16[8,672,128]{2,1,0:T(8,128)(2,1)S(1)} %all-to-all-done.3.tables, bf16[264,256]{1,0:T(8,128)(2,1)S(1)} %get-tuple-element.45.refs_0_, ...), custom_call_target="tpu_custom_call" | custom-call | flops 10000000 | bytes 1048576 | tf_op jit(solution)/shard_map/final/pallas_call | solution.py:415
  (51 shorter events, 14.9 us)
Async XLA Ops:
  0.6 4.6 %copy-start.5 = (s32[1024]{0:T(1024)S(1)}, s32[1024]{0:T(1024)}, u32[]{:S(2)}) copy-start(s32[1024]{0:T(1024)} %param.10) | copy-start | bytes 12292
  1.6 25.3 %copy-start.6 = (bf16[2688,256]{1,0:T(8,128)(2,1)S(1)}, bf16[2688,256]{1,0:T(8,128)(2,1)}, u32[]{:S(2)}) copy-start(bf16[2688,256]{1,0:T(8,128)(2,1)} %x.1) | copy-start | bytes 4128772
  1.6 7.6 %collective-permute-start.1 = (bf16[336,256]{1,0:T(8,128)(2,1)S(1)}, bf16[336,256]{1,0:T(8,128)(2,1)S(1)}, u32[]{:S(2)}, u32[]{:S(2)}) collective-permute-start(bf16[336,256]{1,0:T(8,128)(2,1)S(1)} %rows.1), channel_id=1, source_target_pairs={{0,2},{2,0},{1,3},{3,1},{4,6},{6,4},{5,7},{7,5},{8,10},{10,8},{9,1... | collective-permute-start | bytes 516104 | tf_op jit(solution)/shard_map/ppermute | solution.py:47
  6.5 2.6 %collective-permute-start.2 = (f32[8,128]{1,0:T(8,128)S(1)}, f32[8,128]{1,0:T(8,128)S(1)}, u32[]{:S(2)}, u32[]{:S(2)}) collective-permute-start(f32[8,128]{1,0:T(8,128)S(1)} %broadcast_in_dim.15.mine), channel_id=1, source_target_pairs={{0,32},{32,0},{1,33},{33,1},{2,34},{34,2},{3,35},{35,3},{4,36},{36... | collective-permute-start | bytes 12296 | tf_op jit(solution)/shard_map/ppermute | solution.py:47
  10.1 14.1 %all-to-all-start = ((bf16[4,344,256]{2,1,0:T(8,128)(2,1)}), bf16[4,344,256]{2,1,0:T(8,128)(2,1)S(1)}, u32[]{:S(2)}, u32[]{:S(2)}) async-start(bf16[4,344,256]{2,1,0:T(8,128)(2,1)} %message.1), calls=%async_computation | async-start | bytes 1409024 | tf_op jit(solution)/shard_map/all_to_all | solution.py:443
  14.5 17.4 %copy-start.7 = (f32[1024]{0:T(1024)S(1)}, f32[1024]{0:T(1024)}, u32[]{:S(2)}) copy-start(f32[1024]{0:T(1024)} %param.9) | copy-start | bytes 12292
  14.5 17.4 %copy-start.8 = (f32[1024]{0:T(1024)S(1)}, f32[1024]{0:T(1024)}, u32[]{:S(2)}) copy-start(f32[1024]{0:T(1024)} %param.8) | copy-start | bytes 12292
  14.5 13.3 %collective-permute-start.5 = (bf16[1024,256]{1,0:T(8,128)(2,1)}, bf16[1024,256]{1,0:T(8,128)(2,1)}, u32[]{:S(2)}, u32[]{:S(2)}) collective-permute-start(bf16[1024,256]{1,0:T(8,128)(2,1)} %a.3), channel_id=1, source_target_pairs={{0,2},{2,0},{1,3},{3,1},{4,6},{6,4},{5,7},{7,5},{8,10},{10,8},{9,1... | collective-permute-start | bytes 1572872 | tf_op jit(solution)/shard_map/ppermute | solution.py:47
  24.2 11.5 %collective-permute-start.3 = (bf16[4,344,256]{2,1,0:T(8,128)(2,1)S(1)}, bf16[4,344,256]{2,1,0:T(8,128)(2,1)S(1)}, u32[]{:S(2)}, u32[]{:S(2)}) collective-permute-start(bf16[4,344,256]{2,1,0:T(8,128)(2,1)S(1)} %all-to-all-done.t2), channel_id=1, source_target_pairs={{0,1},{1,0},{2,3},{3,2},{4,5},{5,4},{6,7},{7,6},{8,9},{9,8},{10,11... | collective-permute-start | bytes 2113544 | tf_op jit(solution)/shard_map/ppermute | solution.py:47
  27.0 8.6 %collective-permute-start = (bf16[1344,256]{1,0:T(8,128)(2,1)S(1)}, bf16[1344,256]{1,0:T(8,128)(2,1)S(1)}, u32[]{:S(2)}, u32[]{:S(2)}) collective-permute-start(bf16[1344,256]{1,0:T(8,128)(2,1)S(1)} %constant_dynamic-slice_fusion.t0), channel_id=1, source_target_pairs={{0,1},{1,0},{2,3},{3,2},{4,5},{5,4},{6,7},{7,6},{8,9},{9,8},{10,11... | collective-permute-start | bytes 2064392 | tf_op jit(solution)/shard_map/ppermute | solution.py:47
  27.1 5.0 %collective-permute-start.4 = (bf16[1024,256]{1,0:T(8,128)(2,1)}, bf16[1024,256]{1,0:T(8,128)(2,1)}, u32[]{:S(2)}, u32[]{:S(2)}) collective-permute-start(bf16[1024,256]{1,0:T(8,128)(2,1)} %a.3), channel_id=1, source_target_pairs={{0,1},{1,0},{2,3},{3,2},{4,5},{5,4},{6,7},{7,6},{8,9},{9,8},{10,11... | collective-permute-start | bytes 1572872 | tf_op jit(solution)/shard_map/ppermute | solution.py:47
  27.9 4.7 %collective-permute-start.6 = (bf16[1024,256]{1,0:T(8,128)(2,1)}, bf16[1024,256]{1,0:T(8,128)(2,1)}, u32[]{:S(2)}, u32[]{:S(2)}) collective-permute-start(bf16[1024,256]{1,0:T(8,128)(2,1)} %collective-permute-done.5.c), channel_id=1, source_target_pairs={{0,1},{1,0},{2,3},{3,2},{4,5},{5,4},{6,7},{7,6},{8,9},{9,8},{10,11... | collective-permute-start | bytes 1572872 | tf_op jit(solution)/shard_map/ppermute | solution.py:47
  35.6 7.1 %copy-start = (bf16[1024,1024]{1,0:T(8,128)(2,1)}, bf16[1024,1024]{1,0:T(8,128)(2,1)S(1)}, u32[]{:S(2)}) copy-start(bf16[1024,1024]{1,0:T(8,128)(2,1)S(1)} %get-tuple-element.28.unit) | copy-start | bytes 6291460
  47.9 0.9 copy-start.2
  48.7 0.9 copy-start.4
  49.6 11.0 %copy-start.1 = (bf16[1024,1024]{1,0:T(8,128)(2,1)S(1)}, bf16[1024,1024]{1,0:T(8,128)(2,1)}, u32[]{:S(2)}) copy-start(bf16[1024,1024]{1,0:T(8,128)(2,1)} %copy-done) | copy-start | bytes 6291460
  49.6 37.6 %all-to-all-start.1 = ((bf16[8,64,1024]{2,1,0:T(8,128)(2,1)}), bf16[8,64,1024]{2,1,0:T(8,128)(2,1)S(1)}, u32[]{:S(2)}, u32[]{:S(2)}) async-start(bf16[8,64,1024]{2,1,0:T(8,128)(2,1)} %region.1), calls=%async_computation.1 | async-start | bytes 2097152 | tf_op jit(solution)/shard_map/all_to_all | solution.py:443
  57.9 2.7 %collective-permute-start.7 = (bf16[672,512]{1,0:T(8,128)(2,1)}, bf16[672,512]{1,0:T(8,128)(2,1)S(1)}, u32[]{:S(2)}, u32[]{:S(2)}) collective-permute-start(bf16[672,512]{1,0:T(8,128)(2,1)} %copy-done.4), channel_id=1, source_target_pairs={{0,1},{1,0},{2,3},{3,2},{4,5},{5,4},{6,7},{7,6},{8,9},{9,8},{10,11... | collective-permute-start | bytes 2064392 | tf_op jit(solution)/shard_map/ppermute | solution.py:47
  60.6 1.1 copy-start.3
  64.1 7.7 %collective-permute-start.8 = (bf16[680,128]{1,0:T(8,128)(2,1)S(1)}, bf16[680,128]{1,0:T(8,128)(2,1)S(1)}, u32[]{:S(2)}, u32[]{:S(2)}) collective-permute-start(bf16[680,128]{1,0:T(8,128)(2,1)S(1)} %get-tuple-element.35), channel_id=1, source_target_pairs={{0,32},{32,0},{64,96},{96,64},{128,160},{160,128},{192,224},{224,1... | collective-permute-start | bytes 522248 | tf_op jit(solution)/shard_map/ppermute | solution.py:434
  65.3 8.0 %collective-permute-start.9 = (bf16[680,128]{1,0:T(8,128)(2,1)S(1)}, bf16[680,128]{1,0:T(8,128)(2,1)S(1)}, u32[]{:S(2)}, u32[]{:S(2)}) collective-permute-start(bf16[680,128]{1,0:T(8,128)(2,1)S(1)} %get-tuple-element.36), channel_id=1, source_target_pairs={{0,64},{32,96},{64,128},{96,160},{128,192},{160,224},{192,0},{224,... | collective-permute-start | bytes 522248 | tf_op jit(solution)/shard_map/ppermute | solution.py:434
  66.8 9.2 %collective-permute-start.10 = (bf16[680,128]{1,0:T(8,128)(2,1)S(1)}, bf16[680,128]{1,0:T(8,128)(2,1)S(1)}, u32[]{:S(2)}, u32[]{:S(2)}) collective-permute-start(bf16[680,128]{1,0:T(8,128)(2,1)S(1)} %get-tuple-element.37), channel_id=1, source_target_pairs={{0,96},{32,64},{64,160},{96,128},{128,224},{160,192},{192,32},{224... | collective-permute-start | bytes 522248 | tf_op jit(solution)/shard_map/ppermute | solution.py:434
  68.0 16.2 %collective-permute-start.11 = (bf16[680,128]{1,0:T(8,128)(2,1)S(1)}, bf16[680,128]{1,0:T(8,128)(2,1)S(1)}, u32[]{:S(2)}, u32[]{:S(2)}) collective-permute-start(bf16[680,128]{1,0:T(8,128)(2,1)S(1)} %get-tuple-element.38), channel_id=1, source_target_pairs={{0,128},{32,160},{64,192},{96,224},{128,0},{160,32},{192,64},{224,... | collective-permute-start | bytes 522248 | tf_op jit(solution)/shard_map/ppermute | solution.py:434
  69.3 15.0 %collective-permute-start.12 = (bf16[680,128]{1,0:T(8,128)(2,1)S(1)}, bf16[680,128]{1,0:T(8,128)(2,1)S(1)}, u32[]{:S(2)}, u32[]{:S(2)}) collective-permute-start(bf16[680,128]{1,0:T(8,128)(2,1)S(1)} %get-tuple-element.39), channel_id=1, source_target_pairs={{0,160},{32,128},{64,224},{96,192},{128,32},{160,0},{192,96},{224,... | collective-permute-start | bytes 522248 | tf_op jit(solution)/shard_map/ppermute | solution.py:434
  71.8 12.4 %collective-permute-start.13 = (bf16[680,128]{1,0:T(8,128)(2,1)S(1)}, bf16[680,128]{1,0:T(8,128)(2,1)S(1)}, u32[]{:S(2)}, u32[]{:S(2)}) collective-permute-start(bf16[680,128]{1,0:T(8,128)(2,1)S(1)} %get-tuple-element.40), channel_id=1, source_target_pairs={{0,192},{32,224},{64,0},{96,32},{128,64},{160,96},{192,128},{224,1... | collective-permute-start | bytes 522248 | tf_op jit(solution)/shard_map/ppermute | solution.py:434
  73.3 10.9 %collective-permute-start.14 = (bf16[680,128]{1,0:T(8,128)(2,1)S(1)}, bf16[680,128]{1,0:T(8,128)(2,1)S(1)}, u32[]{:S(2)}, u32[]{:S(2)}) collective-permute-start(bf16[680,128]{1,0:T(8,128)(2,1)S(1)} %get-tuple-element.41), channel_id=1, source_target_pairs={{0,224},{32,192},{64,32},{96,0},{128,96},{160,64},{192,160},{224,1... | collective-permute-start | bytes 522248 | tf_op jit(solution)/shard_map/ppermute | solution.py:434
  88.6 11.9 %all-to-all-start.2 = ((bf16[8,72,256]{2,1,0:T(8,128)(2,1)}), bf16[8,72,256]{2,1,0:T(8,128)(2,1)S(1)}, u32[]{:S(2)}, u32[]{:S(2)}) async-start(bf16[8,72,256]{2,1,0:T(8,128)(2,1)} %bitcast.18), calls=%async_computation.2 | async-start | bytes 589824 | tf_op jit(solution)/shard_map/all_to_all | solution.py:443
  94.0 0.7 collective-permute-start.15
  101.9 28.3 %all-to-all-start.3 = ((bf16[8,672,128]{2,1,0:T(8,128)(2,1)}), bf16[8,672,128]{2,1,0:T(8,128)(2,1)S(1)}, u32[]{:S(2)}, u32[]{:S(2)}) async-start(bf16[8,672,128]{2,1,0:T(8,128)(2,1)} %get-tuple-element.44), calls=%async_computation.3 | async-start | bytes 2752512 | tf_op jit(solution)/shard_map/all_to_all | solution.py:443
  111.5 8.0 %collective-permute-start.18 = (bf16[264,256]{1,0:T(8,128)(2,1)S(1)}, bf16[264,256]{1,0:T(8,128)(2,1)S(1)}, u32[]{:S(2)}, u32[]{:S(2)}) collective-permute-start(bf16[264,256]{1,0:T(8,128)(2,1)S(1)} %get-tuple-element.45.refs_0_), channel_id=1, source_target_pairs={{0,24},{8,0},{16,8},{24,16},{1,25},{9,1},{17,9},{25,17},{2,26},{10... | collective-permute-start | bytes 405512 | tf_op jit(solution)/shard_map/ppermute | solution.py:488
  113.9 9.0 %collective-permute-start.17 = (bf16[264,256]{1,0:T(8,128)(2,1)S(1)}, bf16[264,256]{1,0:T(8,128)(2,1)S(1)}, u32[]{:S(2)}, u32[]{:S(2)}) collective-permute-start(bf16[264,256]{1,0:T(8,128)(2,1)S(1)} %get-tuple-element.45.refs_0_), channel_id=1, source_target_pairs={{0,16},{8,24},{16,0},{24,8},{1,17},{9,25},{17,1},{25,9},{2,18},{10... | collective-permute-start | bytes 405512 | tf_op jit(solution)/shard_map/ppermute | solution.py:488
  116.9 9.2 %collective-permute-start.16 = (bf16[264,256]{1,0:T(8,128)(2,1)S(1)}, bf16[264,256]{1,0:T(8,128)(2,1)S(1)}, u32[]{:S(2)}, u32[]{:S(2)}) collective-permute-start(bf16[264,256]{1,0:T(8,128)(2,1)S(1)} %get-tuple-element.45.refs_0_), channel_id=1, source_target_pairs={{0,8},{8,16},{16,24},{24,0},{1,9},{9,17},{17,25},{25,1},{2,10},{10... | collective-permute-start | bytes 405512 | tf_op jit(solution)/shard_map/ppermute | solution.py:488

commit v3 on v2

--- a/solution.py
+++ b/solution.py
@@ -10,14 +10,13 @@
 REGIONS = 8192
 EMB = ("emb_0", "emb_1")
 IMG = ("img_0", "img_1")
-CLS = ("cls_0", "cls_1")
-NEAR = ("cls_1", "emb_0", "emb_1")
+CLS = ("cls",)
 F32 = jnp.float32
 BF16 = jnp.bfloat16
 NT = (((1,), (1,)), ((), ()))
 TN = (((0,), (0,)), ((), ()))
 
-K, BASE, E, Y, XL, ZH = range(6)
+K, BASE, E, Y, XL, Z = range(6)
 
 
 PART = 336
@@ -239,7 +238,8 @@
         rows = slice(tile * i, tile * i + tile)
         mine = keep[:, rows]
         theirs = send[:, rows]
-        inv = inv_ref[rows, 0:1]
+        here = pl.ds(pl.multiple_of(keep.shape[1] * k + tile * i, tile), tile)
+        inv = inv_ref[here, 0:1]
         along = 0.0
         for q, t in enumerate((t0, t1, t2, t3)):
             if q < 2:
@@ -251,34 +251,23 @@
                     for p in range(2)
                 )
             acc[:, 256 * q : 256 * q + 256] = part
-            along += jnp.sum(part * blocks[q][rows, :].astype(F32), axis=1, keepdims=True)
+            along += jnp.sum(part * blocks[q][here, :].astype(F32), axis=1, keepdims=True)
         back = inv * inv * along
         for q, r in enumerate(blocks):
             cols = slice(256 * q, 256 * q + 256)
-            grad = inv * (acc[:, cols] - r[rows, :].astype(F32) * back)
+            grad = inv * (acc[:, cols] - r[here, :].astype(F32) * back)
             for p in range(tile // 64):
                 z = tile // 64 * i + p
                 out[z, :, cols] = grad[64 * p : 64 * p + 64, :].astype(BF16)
 
 
 def make_region(scalars, keep, send, tables, blocks, inv):
-    half, rows = keep.shape
-    flat = pl.BlockSpec((2 * half, 256), lambda i, s: (0, 0))
-    cube = pl.BlockSpec((4, PART + 8, 256), lambda i, s: (0, 0, 0))
     return pl.pallas_call(
         region_kernel,
-        grid_spec=pltpu.PrefetchScalarGridSpec(
-            num_scalar_prefetch=1,
-            grid=(1,),
-            in_specs=[pl.BlockSpec((half, rows), lambda i, s: (0, 0))] * 2
-            + [flat] * 2
-            + [cube] * 2
-            + [pl.BlockSpec((rows, 256), lambda i, s: (s[K], 0))] * 4
-            + [pl.BlockSpec((rows, 128), lambda i, s: (s[K], 0))],
-            out_specs=pl.BlockSpec((8, 64, 1024), lambda i, s: (0, 0, 0)),
-            scratch_shapes=[pltpu.VMEM((256, 1024), F32)],
-        ),
+        in_specs=[smem()] + vmem(11),
+        out_specs=vmem(1)[0],
         out_shape=in_hbm((8, 64, 1024), BF16),
+        scratch_shapes=[pltpu.VMEM((256, 1024), F32)],
         compiler_params=params(24),
         cost_estimate=cost(1.4e9),
         name="region",
@@ -341,69 +330,73 @@
     )(*terms)
 
 
-def merge_kernel(s, terms, loss, out):
+def merge_kernel(terms, loss, *outs):
     total = sum(terms[z].astype(F32) for z in range(8)).astype(BF16)
     extra = split3(jnp.sum(loss[...]), 256).astype(BF16)
-    for q in range(4):
-        to = s[E] ^ q
-        for near in range(2):
-            out[near, to, 0:64, :] = total[:, 256 * q : 256 * q + 256]
-            out[near, to, 64:72, :] = extra
-
-
-def make_merge(scalars, terms, loss):
+    for q, out in enumerate(outs):
+        out[0:64, :] = total[:, 256 * q : 256 * q + 256]
+        out[64:72, :] = extra
+
+
+def make_merge(terms, loss):
     return pl.pallas_call(
         merge_kernel,
-        in_specs=[smem()] + vmem(2),
-        out_specs=vmem(1)[0],
-        out_shape=in_hbm((2, 4, 72, 256), BF16),
+        in_specs=vmem(2),
+        out_specs=vmem(4),
+        out_shape=[jax.ShapeDtypeStruct((72, 256), BF16)] * 4,
         compiler_params=params(),
         cost_estimate=cost(1e7),
         name="merge",
-    )(scalars, terms, loss)
-
-
-def share_kernel(pieces, chunk, out, message):
-    for near in range(2):
-        for k in range(2):
-            both = pieces[near, 0, k, 0:64, :].astype(F32) + pieces[near, 1, k, 0:64, :].astype(F32)
-            at = 128 * near + 64 * k
-            out[at : at + 64, :] = both.astype(BF16)
-    loss = sum(
-        jnp.sum(pieces[near, x, k, 64:72, :].astype(F32))
-        for near in range(2)
-        for x in range(2)
-        for k in range(2)
-    )
-    out[256:264, :] = split3(loss, 256).astype(BF16)
+    )(terms, loss)
+
+
+def gather_kernel(chunk, out):
     rows = chunk[...]
     for j in range(8):
-        message[j] = rows
-
-
-def make_share(pieces, chunk):
-    half = chunk.shape[0]
+        out[j] = rows
+
+
+def make_gather(chunk):
+    return pl.pallas_call(
+        gather_kernel,
+        in_specs=vmem(1),
+        out_specs=vmem(1)[0],
+        out_shape=in_hbm((8,) + chunk.shape, BF16),
+        compiler_params=params(),
+        cost_estimate=cost(1e7),
+        name="gather",
+    )(chunk)
+
+
+def share_kernel(s, own, near, far, both, out):
+    k = s[K]
+    for at, a, b in ((k, own, far), (1 - k, near, both)):
+        total = a[0:64, :].astype(F32) + b[0:64, :].astype(F32)
+        out[pl.ds(pl.multiple_of(64 * at, 64), 64), :] = total.astype(BF16)
+    loss = sum(jnp.sum(r[64:72, :].astype(F32)) for r in (own, near, far, both))
+    out[128:136, :] = split3(loss, 256).astype(BF16)
+
+
+def make_share(scalars, parts):
     return pl.pallas_call(
         share_kernel,
-        in_specs=vmem(2),
-        out_specs=vmem(2),
-        out_shape=[jax.ShapeDtypeStruct((264, 256), BF16), in_hbm((8, half, 128), BF16)],
+        in_specs=[smem()] + vmem(4),
+        out_specs=vmem(1)[0],
+        out_shape=jax.ShapeDtypeStruct((136, 256), BF16),
         compiler_params=params(),
         cost_estimate=cost(1e7),
         name="share",
-    )(pieces, chunk)
+    )(scalars, *parts)
 
 
 def final_kernel(s, count, tables, *refs):
-    regions, (region_out, table_out, loss_out) = refs[:4], refs[4:]
+    regions, (region_out, table_out, loss_out) = refs[:8], refs[8:]
     total = 0.0
-    for d in range(4):
-        source = (s[ZH] + 4 - d) % 4
-        for near in range(2):
-            for k in range(2):
-                at = 128 * near + 64 * k
-                region_out[k, source, near] = regions[d][at : at + 64, :]
-        total += jnp.sum(regions[d][256:264, :].astype(F32))
+    for d in range(8):
+        source = (s[Z] + 8 - d) % 8
+        for k in range(2):
+            region_out[k, source] = regions[d][64 * k : 64 * k + 64, :]
+        total += jnp.sum(regions[d][128:136, :].astype(F32))
     loss_out[0, 0] = total / count[0, 0] / CLASSES
     for y in range(4):
         at = pl.multiple_of(672 * (s[E] ^ y), 32)
@@ -414,10 +407,10 @@
 def make_final(scalars, count, tables, regions):
     return pl.pallas_call(
         final_kernel,
-        in_specs=[smem(), smem()] + vmem(5),
+        in_specs=[smem(), smem()] + vmem(9),
         out_specs=vmem(2) + [smem()],
         out_shape=[
-            jax.ShapeDtypeStruct((2, 4, 2, 64, 256), BF16),
+            jax.ShapeDtypeStruct((2, 8, 64, 256), BF16),
             jax.ShapeDtypeStruct((2688, 256), BF16),
             jax.ShapeDtypeStruct((1, 1), F32),
         ],
@@ -437,6 +430,10 @@
 def to_owner(x):
     axes = ("img_0",) + EMB
     return lax.ppermute(x, axes, [(4 * y + e, 4 * y + (e ^ y)) for y in range(4) for e in range(4)])
+
+
+def along_cls(x, d):
+    return lax.ppermute(x, CLS, [(i, (i + d) % 8) for i in range(8)])
 
 
 def exchange(x, axes):
@@ -449,9 +446,8 @@
     xl = lax.axis_index("img_1")
     xh = lax.axis_index("emb_0")
     k = lax.axis_index("emb_1")
-    zh = lax.axis_index("cls_0")
     z = lax.axis_index(CLS)
-    scalars = jnp.stack([k, z * 2688 + xh * 1344, 2 * xh + k, y, xl, zh]).astype(jnp.int32)
+    scalars = jnp.stack([k, z * 2688 + xh * 1344, 2 * xh + k, y, xl, z]).astype(jnp.int32)
 
     t_send = take_rows(pltpu.with_memory_space_constraint(table, pltpu.HBM), 4 * (1 - xh) + y, PART)
     t_send, regions_in = lax.optimization_barrier((t_send, regions))
@@ -476,25 +472,25 @@
     theirs = swap(send, "emb_1")
     terms = exchange(make_region(scalars, keep, send, tables, blocks, inv), CLS)
     chunks = list(make_table(scalars, keep, theirs, unit, loss))
-    for o in range(1, 8):
+    for o in (3, 6, 5, 2, 7, 4, 1):
         chunks[o] = over_img(chunks[o], o // 2, o % 2)
     table_part, loss_part = make_table_sum(chunks)
     table_part = to_owner(table_part)
-    merged = make_merge(scalars, terms, loss_part)
-    pieces = exchange(merged.reshape(8, 72, 256), NEAR).reshape(2, 2, 2, 72, 256)
-    share, message = make_share(pieces, table_part)
+    parts = list(make_merge(terms, loss_part))
+    for q in range(1, 4):
+        parts[q] = lax.ppermute(parts[q], EMB, [(i, i ^ q) for i in range(4)])
+    message = make_gather(table_part)
     table_all = exchange(message, IMG)
-    shares = [share] + [
-        lax.ppermute(share, "cls_0", [(i, (i + d) % 4) for i in range(4)]) for d in range(1, 4)
-    ]
+    share = make_share(scalars, parts)
+    shares = [share] + [along_cls(share, d) for d in range(1, 8)]
     region_grad, table_grad, total = make_final(scalars, count, table_all, shares)
     return (total[0, 0], region_grad.reshape(rows, 256), table_grad)
 
 
 def solution(mesh):
     torus = Mesh(
-        mesh.devices.reshape(4, 2, 4, 2, 2, 2),
-        ("img_0", "img_1", "cls_0", "cls_1", "emb_0", "emb_1"),
+        mesh.devices.reshape(4, 2, mesh.shape["cls"], 2, 2),
+        ("img_0", "img_1", "cls", "emb_0", "emb_1"),
     )
     return jax.shard_map(
         shards,

time: 134 us -> 150 us (1.12)
  starting transfers between devices: 58.3 us -> 72.1 us
  local copies, waits for them, and re-layouts: 3.96 us -> 5.53 us
    ppermute x3 -> x10, waiting for transfers between devices: 8.05 us -> 21 us  [the longest x3 12 us: shards(): parts[q] = lax.ppermute(parts[q], EMB, [(i, i ^ q) for i in range(4)])]
    all_to_all x4 -> x3, waiting for transfers between devices: 19.7 us -> 7.06 us  [exchange(): return lax.all_to_all(x, axes, split_axis=0, concat_axis=0, tiled=True)]
    ppermute x3 -> x10, starting transfers between devices: 6.56 us -> 19.2 us  [the longest x7 14 us: along_cls(): return lax.ppermute(x, CLS, [(i, (i + d) % 8) for i in range(8)])]
    unnamed x18, local copies, waits for them, and re-layouts: 2.84 us -> 4.41 us
    all_to_all x4 -> x3, starting transfers between devices: 27.8 us -> 28.9 us  [exchange(): return lax.all_to_all(x, axes, split_axis=0, concat_axis=0, tiled=True)]
    pallas_call x4 -> x5, Pallas kernels: 10.6 us -> 9.81 us  [the longest x1 5.02 us: make_region(): pl.pallas_call(region_kernel, in_specs=[smem()] + vmem(11), out_specs=vme...]
  transfers between devices with their start and end apart: 23 -> 29, of which waited for: 13 -> 13; matrix products, arithmetic and copies ran while one was open for 2% -> 2% of each run, Pallas kernels for 4% -> 5%
where the time goes in v3:
time: 150 us; the launch traced here: 148 us
  starting transfers between devices  72.1 us (48%)
  waiting for transfers between devices  43.4 us (29%)
  Pallas kernels  24.3 us (16%)
  local copies, waits for them, and re-layouts  5.53 us (4%)
    all_to_all x3, starting transfers between devices, exchange(): return lax.all_to_all(x, axes, split_axis=0, concat_axis=0, tiled=True)  28.9 us
    ppermute x7, starting transfers between devices, along_cls(): return lax.ppermute(x, CLS, [(i, (i + d) % 8) for i in range(8)])  14 us
    ppermute x8, starting transfers between devices, swap(): return lax.ppermute(x, axis, [(0, 1), (1, 0)])  13.4 us
    ppermute x3, waiting for transfers between devices, shards(): parts[q] = lax.ppermute(parts[q], EMB, [(i, i ^ q) for i in range(4)])  12 us
    ppermute x7, waiting for transfers between devices, over_img(): return lax.ppermute(x, IMG, pairs)  10.3 us
    ppermute x7, starting transfers between devices, over_img(): return lax.ppermute(x, IMG, pairs)  9.83 us
    ppermute x7, waiting for transfers between devices, along_cls(): return lax.ppermute(x, CLS, [(i, (i + d) % 8) for i in range(8)])  8.98 us
    pallas_call x1, Pallas kernels, make_focal(): pl.pallas_call(focal_kernel, grid_spec=pltpu.PrefetchScalarGridSpec(num_s...  7.08 us
  transfers between devices with their start and end apart: 29, of which 13 were waited for; matrix products, arithmetic and copies ran while one was open for 2% of the time, Pallas kernels for 5%

profile of v3, /device:TPU:1, one launch (start us, length us, event | category | flops | bytes accessed | tf_op | source)
XLA Modules:
  0.0 147.8 jit_solution(7381989301103312114)
XLA Ops:
  1.6 3.6 %collective-permute-start.1 = (bf16[336,256]{1,0:T(8,128)(2,1)S(1)}, bf16[336,256]{1,0:T(8,128)(2,1)S(1)}, u32[]{:S(2)}, u32[]{:S(2)}) collective-permute-start(bf16[336,256]{1,0:T(8,128)(2,1)S(1)} %rows.1), channel_id=1, source_target_pairs={{0,2},{2,0},{1,3},{3,1},{4,6},{6,4},{5,7},{7,5},{8,10},{10,8},{9,1... | collective-permute-start | bytes 516104 | tf_op jit(solution)/shard_map/ppermute | solution.py:46
  6.9 2.2 %collective-permute-done.2.theirs = f32[8,128]{1,0:T(8,128)S(1)} collective-permute-done((f32[8,128]{1,0:T(8,128)S(1)}, f32[8,128]{1,0:T(8,128)S(1)}, u32[]{:S(2)}, u32[]{:S(2)}) %collective-permute-start.2) | collective-permute-done | bytes 4128 | tf_op jit(solution)/shard_map/ppermute | solution.py:46
  10.1 4.5 %all-to-all-start = ((bf16[4,344,256]{2,1,0:T(8,128)(2,1)}), bf16[4,344,256]{2,1,0:T(8,128)(2,1)S(1)}, u32[]{:S(2)}, u32[]{:S(2)}) async-start(bf16[4,344,256]{2,1,0:T(8,128)(2,1)} %message.1), calls=%async_computation | async-start | bytes 1409024 | tf_op jit(solution)/shard_map/all_to_all | solution.py:440
  14.5 2.6 %collective-permute-start.5 = (bf16[1024,256]{1,0:T(8,128)(2,1)}, bf16[1024,256]{1,0:T(8,128)(2,1)}, u32[]{:S(2)}, u32[]{:S(2)}) collective-permute-start(bf16[1024,256]{1,0:T(8,128)(2,1)} %a.3), channel_id=1, source_target_pairs={{0,2},{2,0},{1,3},{3,1},{4,6},{6,4},{5,7},{7,5},{8,10},{10,8},{9,1... | collective-permute-start | bytes 1572872 | tf_op jit(solution)/shard_map/ppermute | solution.py:46
  17.1 7.1 %all-to-all-done.t2 = bf16[4,344,256]{2,1,0:T(8,128)(2,1)S(1)} async-done(((bf16[4,344,256]{2,1,0:T(8,128)(2,1)}), bf16[4,344,256]{2,1,0:T(8,128)(2,1)S(1)}, u32[]{:S(2)}, u32[]{:S(2)}) %all-to-all-start) | async-done | bytes 704544 | tf_op jit(solution)/shard_map/all_to_all | solution.py:440
  24.2 2.7 %collective-permute-start.3 = (bf16[4,344,256]{2,1,0:T(8,128)(2,1)S(1)}, bf16[4,344,256]{2,1,0:T(8,128)(2,1)S(1)}, u32[]{:S(2)}, u32[]{:S(2)}) collective-permute-start(bf16[4,344,256]{2,1,0:T(8,128)(2,1)S(1)} %all-to-all-done.t2), channel_id=1, source_target_pairs={{0,1},{1,0},{2,3},{3,2},{4,5},{5,4},{6,7},{7,6},{8,9},{9,8},{10,11... | collective-permute-start | bytes 2113544 | tf_op jit(solution)/shard_map/ppermute | solution.py:46
  27.9 2.8 %collective-permute-start.6 = (bf16[1024,256]{1,0:T(8,128)(2,1)}, bf16[1024,256]{1,0:T(8,128)(2,1)}, u32[]{:S(2)}, u32[]{:S(2)}) collective-permute-start(bf16[1024,256]{1,0:T(8,128)(2,1)} %collective-permute-done.5.c), channel_id=1, source_target_pairs={{0,1},{1,0},{2,3},{3,2},{4,5},{5,4},{6,7},{7,6},{8,9},{9,8},{10,11... | collective-permute-start | bytes 1572872 | tf_op jit(solution)/shard_map/ppermute | solution.py:46
  32.6 3.0 %unit.1 = (bf16[1024,1024]{1,0:T(8,128)(2,1)S(1)}, f32[1024,128]{1,0:T(8,128)S(1)}) custom-call(bf16[1024,256]{1,0:T(8,128)(2,1)} %a.3, bf16[1024,256]{1,0:T(8,128)(2,1)} %collective-permute-done.4.b, bf16[1024,256]{1,0:T(8,128)(2,1)} %collective-permute-done.5.c, bf16[1024,256]{1,0:T(8,128)(2,1)} %collective-permute-done.6.d), custom_call_target="tpu_custom_call" | custom-call | flops 20000000 | bytes 1048576 | tf_op jit(solution)/shard_map/unit/pallas_call | solution.py:71
  35.6 7.1 %focal.1 = (bf16[672,512]{1,0:T(8,128)(2,1)S(1)}, bf16[672,512]{1,0:T(8,128)(2,1)S(1)}, f32[8,128]{1,0:T(8,128)S(1)}, f32[1,1]{1,0:T(1,128)}) custom-call(s32[6]{0:T(128)S(1)} %stack.27.s, bf16[1344,256]{1,0:T(8,128)(2,1)S(1)} %constant_dynamic-slice_fusion.t0, bf16[1344,256]{1,0:T(8,128)(2,1)S(1)} %collective-permute-done.t1, ...), custom_call_target="tpu_custom_call" | custom-call | flops 1400000000 | bytes 1048576 | tf_op jit(solution)/shard_map/focal/pallas_call | solution.py:193
  42.7 5.0 %region.1 = bf16[8,64,1024]{2,1,0:T(8,128)(2,1)} custom-call(s32[6]{0:T(128)S(1)} %stack.27.s, bf16[672,512]{1,0:T(8,128)(2,1)S(1)} %get-tuple-element.32.keep, bf16[672,512]{1,0:T(8,128)(2,1)S(1)} %get-tuple-element.33.send, bf16[1344,256]{1,0:T(8,128)(2,1)S(1)} %constant_dynamic-slice_fusion.t0, bf16[1344,256]{1,0:T(8,128)(2,1)S(1)} %collective-permute-done.t1, ...), custom_call_target="tpu_custom_call" | custom-call | flops 1400000000 | bytes 1048576 | tf_op jit(solution)/shard_map/region/pallas_call | solution.py:265
  49.4 8.2 %all-to-all-start.2 = ((bf16[8,64,1024]{2,1,0:T(8,128)(2,1)}), bf16[8,64,1024]{2,1,0:T(8,128)(2,1)S(1)}, u32[]{:S(2)}, u32[]{:S(2)}) async-start(bf16[8,64,1024]{2,1,0:T(8,128)(2,1)} %region.1), calls=%async_computation.2 | async-start | bytes 2097152 | tf_op jit(solution)/shard_map/all_to_all | solution.py:440
  58.3 2.0 %collective-permute-done.7.other = bf16[672,512]{1,0:T(8,128)(2,1)S(1)} collective-permute-done((bf16[672,512]{1,0:T(8,128)(2,1)}, bf16[672,512]{1,0:T(8,128)(2,1)S(1)}, u32[]{:S(2)}, u32[]{:S(2)}) %collective-permute-start.7) | collective-permute-done | bytes 688160 | tf_op jit(solution)/shard_map/ppermute | solution.py:46
  60.3 1.6 %copy-done.1 = bf16[1024,1024]{1,0:T(8,128)(2,1)S(1)} copy-done((bf16[1024,1024]{1,0:T(8,128)(2,1)S(1)}, bf16[1024,1024]{1,0:T(8,128)(2,1)}, u32[]{:S(2)}) %copy-start.1) | copy-done | bytes 2097176
  63.0 2.4 %table.1 = (bf16[680,128]{1,0:T(8,128)(2,1)S(1)}, bf16[680,128]{1,0:T(8,128)(2,1)S(1)}, bf16[680,128]{1,0:T(8,128)(2,1)S(1)}, bf16[680,128]{1,0:T(8,128)(2,1)S(1...) custom-call(s32[6]{0:T(128)S(1)} %stack.27.s, ...), custom_call_target="tpu_custom_call" | custom-call | flops 1400000000 | bytes 1048576 | tf_op jit(solution)/shard_map/table/pallas_call | solution.py:299
  66.6 1.5 collective-permute-start.9
  70.5 2.6 %collective-permute-start.12 = (bf16[680,128]{1,0:T(8,128)(2,1)S(1)}, bf16[680,128]{1,0:T(8,128)(2,1)S(1)}, u32[]{:S(2)}, u32[]{:S(2)}) collective-permute-start(bf16[680,128]{1,0:T(8,128)(2,1)S(1)} %get-tuple-element.40), channel_id=1, source_target_pairs={{0,160},{32,128},{64,224},{96,192},{128,32},{160,0},{192,96},{224,... | collective-permute-start | bytes 522248 | tf_op jit(solution)/shard_map/ppermute | solution.py:427
  73.1 1.5 collective-permute-start.13
  75.2 2.1 %collective-permute-done.10.refs_3_ = bf16[680,128]{1,0:T(8,128)(2,1)S(1)} collective-permute-done((bf16[680,128]{1,0:T(8,128)(2,1)S(1)}, bf16[680,128]{1,0:T(8,128)(2,1)S(1)}, u32[]{:S(2)}, u32[]{:S(2)}) %collective-permute-start.10) | collective-permute-done | bytes 174112 | tf_op jit(solution)/shard_map/ppermute | solution.py:427
  77.3 8.2 %collective-permute-done.11.refs_4_ = bf16[680,128]{1,0:T(8,128)(2,1)S(1)} collective-permute-done((bf16[680,128]{1,0:T(8,128)(2,1)S(1)}, bf16[680,128]{1,0:T(8,128)(2,1)S(1)}, u32[]{:S(2)}, u32[]{:S(2)}) %collective-permute-start.11) | collective-permute-done | bytes 174112 | tf_op jit(solution)/shard_map/ppermute | solution.py:427
  87.6 16.3 %all-to-all-start.1 = ((bf16[8,672,128]{2,1,0:T(8,128)(2,1)}), bf16[8,672,128]{2,1,0:T(8,128)(2,1)S(1)}, u32[]{:S(2)}, u32[]{:S(2)}) async-start(bf16[8,672,128]{2,1,0:T(8,128)(2,1)} %gather.1), calls=%async_computation.1 | async-start | bytes 2752512 | tf_op jit(solution)/shard_map/all_to_all | solution.py:440
  104.2 1.9 %collective-permute-start.16 = (bf16[72,256]{1,0:T(8,128)(2,1)S(1)}, bf16[72,256]{1,0:T(8,128)(2,1)S(1)}, u32[]{:S(2)}, u32[]{:S(2)}) collective-permute-start(bf16[72,256]{1,0:T(8,128)(2,1)S(1)} %get-tuple-element.47), channel_id=1, source_target_pairs={{0,1},{1,0},{2,3},{3,2},{4,5},{5,4},{6,7},{7,6},{8,9},{9,8},{10,11... | collective-permute-start | bytes 110600 | tf_op jit(solution)/shard_map/ppermute | solution.py:481
  106.5 2.8 %collective-permute-start.18 = (bf16[72,256]{1,0:T(8,128)(2,1)S(1)}, bf16[72,256]{1,0:T(8,128)(2,1)S(1)}, u32[]{:S(2)}, u32[]{:S(2)}) collective-permute-start(bf16[72,256]{1,0:T(8,128)(2,1)S(1)} %get-tuple-element.49), channel_id=1, source_target_pairs={{0,3},{1,2},{2,1},{3,0},{4,7},{5,6},{6,5},{7,4},{8,11},{9,10},{10,... | collective-permute-start | bytes 110600 | tf_op jit(solution)/shard_map/ppermute | solution.py:481
  109.3 9.0 %collective-permute-done.17.far = bf16[72,256]{1,0:T(8,128)(2,1)S(1)} collective-permute-done((bf16[72,256]{1,0:T(8,128)(2,1)S(1)}, bf16[72,256]{1,0:T(8,128)(2,1)S(1)}, u32[]{:S(2)}, u32[]{:S(2)}) %collective-permute-start.17) | collective-permute-done | bytes 36896 | tf_op jit(solution)/shard_map/ppermute | solution.py:481
  118.3 3.0 %collective-permute-done.18.both = bf16[72,256]{1,0:T(8,128)(2,1)S(1)} collective-permute-done((bf16[72,256]{1,0:T(8,128)(2,1)S(1)}, bf16[72,256]{1,0:T(8,128)(2,1)S(1)}, u32[]{:S(2)}, u32[]{:S(2)}) %collective-permute-start.18) | collective-permute-done | bytes 36896 | tf_op jit(solution)/shard_map/ppermute | solution.py:481
  122.0 3.0 %collective-permute-start.25 = (bf16[136,256]{1,0:T(8,128)(2,1)S(1)}, bf16[136,256]{1,0:T(8,128)(2,1)S(1)}, u32[]{:S(2)}, u32[]{:S(2)}) collective-permute-start(bf16[136,256]{1,0:T(8,128)(2,1)S(1)} %share.1.refs_0_), channel_id=1, source_target_pairs={{0,28},{4,0},{8,4},{12,8},{16,12},{20,16},{24,20},{28,24},{1,29},{... | collective-permute-start | bytes 208904 | tf_op jit(solution)/shard_map/ppermute | solution.py:436
  125.0 2.1 %collective-permute-start.24 = (bf16[136,256]{1,0:T(8,128)(2,1)S(1)}, bf16[136,256]{1,0:T(8,128)(2,1)S(1)}, u32[]{:S(2)}, u32[]{:S(2)}) collective-permute-start(bf16[136,256]{1,0:T(8,128)(2,1)S(1)} %share.1.refs_0_), channel_id=1, source_target_pairs={{0,24},{4,28},{8,0},{12,4},{16,8},{20,12},{24,16},{28,20},{1,25},{... | collective-permute-start | bytes 208904 | tf_op jit(solution)/shard_map/ppermute | solution.py:436
  128.3 3.3 %collective-permute-start.22 = (bf16[136,256]{1,0:T(8,128)(2,1)S(1)}, bf16[136,256]{1,0:T(8,128)(2,1)S(1)}, u32[]{:S(2)}, u32[]{:S(2)}) collective-permute-start(bf16[136,256]{1,0:T(8,128)(2,1)S(1)} %share.1.refs_0_), channel_id=1, source_target_pairs={{0,16},{4,20},{8,24},{12,28},{16,0},{20,4},{24,8},{28,12},{1,17},{... | collective-permute-start | bytes 208904 | tf_op jit(solution)/shard_map/ppermute | solution.py:436
  131.6 3.3 %collective-permute-start.20 = (bf16[136,256]{1,0:T(8,128)(2,1)S(1)}, bf16[136,256]{1,0:T(8,128)(2,1)S(1)}, u32[]{:S(2)}, u32[]{:S(2)}) collective-permute-start(bf16[136,256]{1,0:T(8,128)(2,1)S(1)} %share.1.refs_0_), channel_id=1, source_target_pairs={{0,8},{4,12},{8,16},{12,20},{16,24},{20,28},{24,0},{28,4},{1,9},{5... | collective-permute-start | bytes 208904 | tf_op jit(solution)/shard_map/ppermute | solution.py:436
  137.1 5.1 %collective-permute-done.21.refs_3_ = bf16[136,256]{1,0:T(8,128)(2,1)S(1)} collective-permute-done((bf16[136,256]{1,0:T(8,128)(2,1)S(1)}, bf16[136,256]{1,0:T(8,128)(2,1)S(1)}, u32[]{:S(2)}, u32[]{:S(2)}) %collective-permute-start.21) | collective-permute-done | bytes 69664 | tf_op jit(solution)/shard_map/ppermute | solution.py:436
  142.2 1.3 collective-permute-done.20.refs_2_
  143.5 1.5 %collective-permute-done.19.refs_1_ = bf16[136,256]{1,0:T(8,128)(2,1)S(1)} collective-permute-done((bf16[136,256]{1,0:T(8,128)(2,1)S(1)}, bf16[136,256]{1,0:T(8,128)(2,1)S(1)}, u32[]{:S(2)}, u32[]{:S(2)}) %collective-permute-start.19) | collective-permute-done | bytes 69664 | tf_op jit(solution)/shard_map/ppermute | solution.py:436
  145.0 2.6 %final.1 = (bf16[2,8,64,256]{3,2,1,0:T(8,128)(2,1)}, bf16[2688,256]{1,0:T(8,128)(2,1)}, f32[1,1]{1,0:T(1,128)}) custom-call(s32[6]{0:T(128)S(1)} %stack.27.s, f32[1,1]{1,0:T(1,128)} %get-tuple-element.31.count, bf16[8,672,128]{2,1,0:T(8,128)(2,1)S(1)} %all-to-all-done.1.tables, bf16[136,256]{1,0:T(8,128)(2,1)S(1)} %share.1.refs_0_, ...), custom_call_target="tpu_custom_call" | custom-call | flops 10000000 | bytes 1048576 | tf_op jit(solution)/shard_map/final/pallas_call | solution.py:408
  (64 shorter events, 20.9 us)
Async XLA Ops:
  1.6 25.3 %copy-start.6 = (bf16[2688,256]{1,0:T(8,128)(2,1)S(1)}, bf16[2688,256]{1,0:T(8,128)(2,1)}, u32[]{:S(2)}) copy-start(bf16[2688,256]{1,0:T(8,128)(2,1)} %x.1) | copy-start | bytes 4128772
  1.6 7.6 %collective-permute-start.1 = (bf16[336,256]{1,0:T(8,128)(2,1)S(1)}, bf16[336,256]{1,0:T(8,128)(2,1)S(1)}, u32[]{:S(2)}, u32[]{:S(2)}) collective-permute-start(bf16[336,256]{1,0:T(8,128)(2,1)S(1)} %rows.1), channel_id=1, source_target_pairs={{0,2},{2,0},{1,3},{3,1},{4,6},{6,4},{5,7},{7,5},{8,10},{10,8},{9,1... | collective-permute-start | bytes 516104 | tf_op jit(solution)/shard_map/ppermute | solution.py:46
  6.5 2.6 %collective-permute-start.2 = (f32[8,128]{1,0:T(8,128)S(1)}, f32[8,128]{1,0:T(8,128)S(1)}, u32[]{:S(2)}, u32[]{:S(2)}) collective-permute-start(f32[8,128]{1,0:T(8,128)S(1)} %broadcast_in_dim.15.mine), channel_id=1, source_target_pairs={{0,32},{32,0},{1,33},{33,1},{2,34},{34,2},{3,35},{35,3},{4,36},{36... | collective-permute-start | bytes 12296 | tf_op jit(solution)/shard_map/ppermute | solution.py:46
  10.1 14.1 %all-to-all-start = ((bf16[4,344,256]{2,1,0:T(8,128)(2,1)}), bf16[4,344,256]{2,1,0:T(8,128)(2,1)S(1)}, u32[]{:S(2)}, u32[]{:S(2)}) async-start(bf16[4,344,256]{2,1,0:T(8,128)(2,1)} %message.1), calls=%async_computation | async-start | bytes 1409024 | tf_op jit(solution)/shard_map/all_to_all | solution.py:440
  14.5 17.4 %copy-start.7 = (f32[1024]{0:T(1024)S(1)}, f32[1024]{0:T(1024)}, u32[]{:S(2)}) copy-start(f32[1024]{0:T(1024)} %param.9) | copy-start | bytes 12292
  14.5 17.4 %copy-start.8 = (f32[1024]{0:T(1024)S(1)}, f32[1024]{0:T(1024)}, u32[]{:S(2)}) copy-start(f32[1024]{0:T(1024)} %param.8) | copy-start | bytes 12292
  14.5 13.3 %collective-permute-start.5 = (bf16[1024,256]{1,0:T(8,128)(2,1)}, bf16[1024,256]{1,0:T(8,128)(2,1)}, u32[]{:S(2)}, u32[]{:S(2)}) collective-permute-start(bf16[1024,256]{1,0:T(8,128)(2,1)} %a.3), channel_id=1, source_target_pairs={{0,2},{2,0},{1,3},{3,1},{4,6},{6,4},{5,7},{7,5},{8,10},{10,8},{9,1... | collective-permute-start | bytes 1572872 | tf_op jit(solution)/shard_map/ppermute | solution.py:46
  24.2 11.5 %collective-permute-start.3 = (bf16[4,344,256]{2,1,0:T(8,128)(2,1)S(1)}, bf16[4,344,256]{2,1,0:T(8,128)(2,1)S(1)}, u32[]{:S(2)}, u32[]{:S(2)}) collective-permute-start(bf16[4,344,256]{2,1,0:T(8,128)(2,1)S(1)} %all-to-all-done.t2), channel_id=1, source_target_pairs={{0,1},{1,0},{2,3},{3,2},{4,5},{5,4},{6,7},{7,6},{8,9},{9,8},{10,11... | collective-permute-start | bytes 2113544 | tf_op jit(solution)/shard_map/ppermute | solution.py:46
  27.0 8.6 %collective-permute-start = (bf16[1344,256]{1,0:T(8,128)(2,1)S(1)}, bf16[1344,256]{1,0:T(8,128)(2,1)S(1)}, u32[]{:S(2)}, u32[]{:S(2)}) collective-permute-start(bf16[1344,256]{1,0:T(8,128)(2,1)S(1)} %constant_dynamic-slice_fusion.t0), channel_id=1, source_target_pairs={{0,1},{1,0},{2,3},{3,2},{4,5},{5,4},{6,7},{7,6},{8,9},{9,8},{10,11... | collective-permute-start | bytes 2064392 | tf_op jit(solution)/shard_map/ppermute | solution.py:46
  27.1 5.0 %collective-permute-start.4 = (bf16[1024,256]{1,0:T(8,128)(2,1)}, bf16[1024,256]{1,0:T(8,128)(2,1)}, u32[]{:S(2)}, u32[]{:S(2)}) collective-permute-start(bf16[1024,256]{1,0:T(8,128)(2,1)} %a.3), channel_id=1, source_target_pairs={{0,1},{1,0},{2,3},{3,2},{4,5},{5,4},{6,7},{7,6},{8,9},{9,8},{10,11... | collective-permute-start | bytes 1572872 | tf_op jit(solution)/shard_map/ppermute | solution.py:46
  27.9 4.7 %collective-permute-start.6 = (bf16[1024,256]{1,0:T(8,128)(2,1)}, bf16[1024,256]{1,0:T(8,128)(2,1)}, u32[]{:S(2)}, u32[]{:S(2)}) collective-permute-start(bf16[1024,256]{1,0:T(8,128)(2,1)} %collective-permute-done.5.c), channel_id=1, source_target_pairs={{0,1},{1,0},{2,3},{3,2},{4,5},{5,4},{6,7},{7,6},{8,9},{9,8},{10,11... | collective-permute-start | bytes 1572872 | tf_op jit(solution)/shard_map/ppermute | solution.py:46
  49.4 38.2 %all-to-all-start.2 = ((bf16[8,64,1024]{2,1,0:T(8,128)(2,1)}), bf16[8,64,1024]{2,1,0:T(8,128)(2,1)S(1)}, u32[]{:S(2)}, u32[]{:S(2)}) async-start(bf16[8,64,1024]{2,1,0:T(8,128)(2,1)} %region.1), calls=%async_computation.2 | async-start | bytes 2097152 | tf_op jit(solution)/shard_map/all_to_all | solution.py:440
  57.6 2.6 %collective-permute-start.7 = (bf16[672,512]{1,0:T(8,128)(2,1)}, bf16[672,512]{1,0:T(8,128)(2,1)S(1)}, u32[]{:S(2)}, u32[]{:S(2)}) collective-permute-start(bf16[672,512]{1,0:T(8,128)(2,1)} %copy-done.4), channel_id=1, source_target_pairs={{0,1},{1,0},{2,3},{3,2},{4,5},{5,4},{6,7},{7,6},{8,9},{9,8},{10,11... | collective-permute-start | bytes 2064392 | tf_op jit(solution)/shard_map/ppermute | solution.py:46
  65.4 7.8 %collective-permute-start.8 = (bf16[680,128]{1,0:T(8,128)(2,1)S(1)}, bf16[680,128]{1,0:T(8,128)(2,1)S(1)}, u32[]{:S(2)}, u32[]{:S(2)}) collective-permute-start(bf16[680,128]{1,0:T(8,128)(2,1)S(1)} %get-tuple-element.36), channel_id=1, source_target_pairs={{0,32},{32,0},{64,96},{96,64},{128,160},{160,128},{192,224},{224,1... | collective-permute-start | bytes 522248 | tf_op jit(solution)/shard_map/ppermute | solution.py:427
  66.6 8.0 %collective-permute-start.9 = (bf16[680,128]{1,0:T(8,128)(2,1)S(1)}, bf16[680,128]{1,0:T(8,128)(2,1)S(1)}, u32[]{:S(2)}, u32[]{:S(2)}) collective-permute-start(bf16[680,128]{1,0:T(8,128)(2,1)S(1)} %get-tuple-element.37), channel_id=1, source_target_pairs={{0,64},{32,96},{64,128},{96,160},{128,192},{160,224},{192,0},{224,... | collective-permute-start | bytes 522248 | tf_op jit(solution)/shard_map/ppermute | solution.py:427
  68.1 9.2 %collective-permute-start.10 = (bf16[680,128]{1,0:T(8,128)(2,1)S(1)}, bf16[680,128]{1,0:T(8,128)(2,1)S(1)}, u32[]{:S(2)}, u32[]{:S(2)}) collective-permute-start(bf16[680,128]{1,0:T(8,128)(2,1)S(1)} %get-tuple-element.38), channel_id=1, source_target_pairs={{0,96},{32,64},{64,160},{96,128},{128,224},{160,192},{192,32},{224... | collective-permute-start | bytes 522248 | tf_op jit(solution)/shard_map/ppermute | solution.py:427
  69.3 16.2 %collective-permute-start.11 = (bf16[680,128]{1,0:T(8,128)(2,1)S(1)}, bf16[680,128]{1,0:T(8,128)(2,1)S(1)}, u32[]{:S(2)}, u32[]{:S(2)}) collective-permute-start(bf16[680,128]{1,0:T(8,128)(2,1)S(1)} %get-tuple-element.39), channel_id=1, source_target_pairs={{0,128},{32,160},{64,192},{96,224},{128,0},{160,32},{192,64},{224,... | collective-permute-start | bytes 522248 | tf_op jit(solution)/shard_map/ppermute | solution.py:427
  70.5 15.0 %collective-permute-start.12 = (bf16[680,128]{1,0:T(8,128)(2,1)S(1)}, bf16[680,128]{1,0:T(8,128)(2,1)S(1)}, u32[]{:S(2)}, u32[]{:S(2)}) collective-permute-start(bf16[680,128]{1,0:T(8,128)(2,1)S(1)} %get-tuple-element.40), channel_id=1, source_target_pairs={{0,160},{32,128},{64,224},{96,192},{128,32},{160,0},{192,96},{224,... | collective-permute-start | bytes 522248 | tf_op jit(solution)/shard_map/ppermute | solution.py:427
  73.1 12.4 %collective-permute-start.13 = (bf16[680,128]{1,0:T(8,128)(2,1)S(1)}, bf16[680,128]{1,0:T(8,128)(2,1)S(1)}, u32[]{:S(2)}, u32[]{:S(2)}) collective-permute-start(bf16[680,128]{1,0:T(8,128)(2,1)S(1)} %get-tuple-element.41), channel_id=1, source_target_pairs={{0,192},{32,224},{64,0},{96,32},{128,64},{160,96},{192,128},{224,1... | collective-permute-start | bytes 522248 | tf_op jit(solution)/shard_map/ppermute | solution.py:427
  74.6 10.9 %collective-permute-start.14 = (bf16[680,128]{1,0:T(8,128)(2,1)S(1)}, bf16[680,128]{1,0:T(8,128)(2,1)S(1)}, u32[]{:S(2)}, u32[]{:S(2)}) collective-permute-start(bf16[680,128]{1,0:T(8,128)(2,1)S(1)} %get-tuple-element.42), channel_id=1, source_target_pairs={{0,224},{32,192},{64,32},{96,0},{128,96},{160,64},{192,160},{224,1... | collective-permute-start | bytes 522248 | tf_op jit(solution)/shard_map/ppermute | solution.py:427
  85.7 0.7 collective-permute-start.15
  87.6 57.4 %all-to-all-start.1 = ((bf16[8,672,128]{2,1,0:T(8,128)(2,1)}), bf16[8,672,128]{2,1,0:T(8,128)(2,1)S(1)}, u32[]{:S(2)}, u32[]{:S(2)}) async-start(bf16[8,672,128]{2,1,0:T(8,128)(2,1)} %gather.1), calls=%async_computation.1 | async-start | bytes 2752512 | tf_op jit(solution)/shard_map/all_to_all | solution.py:440
  104.2 5.1 %collective-permute-start.16 = (bf16[72,256]{1,0:T(8,128)(2,1)S(1)}, bf16[72,256]{1,0:T(8,128)(2,1)S(1)}, u32[]{:S(2)}, u32[]{:S(2)}) collective-permute-start(bf16[72,256]{1,0:T(8,128)(2,1)S(1)} %get-tuple-element.47), channel_id=1, source_target_pairs={{0,1},{1,0},{2,3},{3,2},{4,5},{5,4},{6,7},{7,6},{8,9},{9,8},{10,11... | collective-permute-start | bytes 110600 | tf_op jit(solution)/shard_map/ppermute | solution.py:481
  106.1 12.2 %collective-permute-start.17 = (bf16[72,256]{1,0:T(8,128)(2,1)S(1)}, bf16[72,256]{1,0:T(8,128)(2,1)S(1)}, u32[]{:S(2)}, u32[]{:S(2)}) collective-permute-start(bf16[72,256]{1,0:T(8,128)(2,1)S(1)} %get-tuple-element.48), channel_id=1, source_target_pairs={{0,2},{1,3},{2,0},{3,1},{4,6},{5,7},{6,4},{7,5},{8,10},{9,11},{10,... | collective-permute-start | bytes 110600 | tf_op jit(solution)/shard_map/ppermute | solution.py:481
  106.5 14.8 %collective-permute-start.18 = (bf16[72,256]{1,0:T(8,128)(2,1)S(1)}, bf16[72,256]{1,0:T(8,128)(2,1)S(1)}, u32[]{:S(2)}, u32[]{:S(2)}) collective-permute-start(bf16[72,256]{1,0:T(8,128)(2,1)S(1)} %get-tuple-element.49), channel_id=1, source_target_pairs={{0,3},{1,2},{2,1},{3,0},{4,7},{5,6},{6,5},{7,4},{8,11},{9,10},{10,... | collective-permute-start | bytes 110600 | tf_op jit(solution)/shard_map/ppermute | solution.py:481
  122.0 9.6 %collective-permute-start.25 = (bf16[136,256]{1,0:T(8,128)(2,1)S(1)}, bf16[136,256]{1,0:T(8,128)(2,1)S(1)}, u32[]{:S(2)}, u32[]{:S(2)}) collective-permute-start(bf16[136,256]{1,0:T(8,128)(2,1)S(1)} %share.1.refs_0_), channel_id=1, source_target_pairs={{0,28},{4,0},{8,4},{12,8},{16,12},{20,16},{24,20},{28,24},{1,29},{... | collective-permute-start | bytes 208904 | tf_op jit(solution)/shard_map/ppermute | solution.py:436
  125.0 9.9 %collective-permute-start.24 = (bf16[136,256]{1,0:T(8,128)(2,1)S(1)}, bf16[136,256]{1,0:T(8,128)(2,1)S(1)}, u32[]{:S(2)}, u32[]{:S(2)}) collective-permute-start(bf16[136,256]{1,0:T(8,128)(2,1)S(1)} %share.1.refs_0_), channel_id=1, source_target_pairs={{0,24},{4,28},{8,0},{12,4},{16,8},{20,12},{24,16},{28,20},{1,25},{... | collective-permute-start | bytes 208904 | tf_op jit(solution)/shard_map/ppermute | solution.py:436
  127.2 8.9 %collective-permute-start.23 = (bf16[136,256]{1,0:T(8,128)(2,1)S(1)}, bf16[136,256]{1,0:T(8,128)(2,1)S(1)}, u32[]{:S(2)}, u32[]{:S(2)}) collective-permute-start(bf16[136,256]{1,0:T(8,128)(2,1)S(1)} %share.1.refs_0_), channel_id=1, source_target_pairs={{0,20},{4,24},{8,28},{12,0},{16,4},{20,8},{24,12},{28,16},{1,21},{... | collective-permute-start | bytes 208904 | tf_op jit(solution)/shard_map/ppermute | solution.py:436
  128.3 8.8 %collective-permute-start.22 = (bf16[136,256]{1,0:T(8,128)(2,1)S(1)}, bf16[136,256]{1,0:T(8,128)(2,1)S(1)}, u32[]{:S(2)}, u32[]{:S(2)}) collective-permute-start(bf16[136,256]{1,0:T(8,128)(2,1)S(1)} %share.1.refs_0_), channel_id=1, source_target_pairs={{0,16},{4,20},{8,24},{12,28},{16,0},{20,4},{24,8},{28,12},{1,17},{... | collective-permute-start | bytes 208904 | tf_op jit(solution)/shard_map/ppermute | solution.py:436
  131.6 10.6 %collective-permute-start.21 = (bf16[136,256]{1,0:T(8,128)(2,1)S(1)}, bf16[136,256]{1,0:T(8,128)(2,1)S(1)}, u32[]{:S(2)}, u32[]{:S(2)}) collective-permute-start(bf16[136,256]{1,0:T(8,128)(2,1)S(1)} %share.1.refs_0_), channel_id=1, source_target_pairs={{0,12},{4,16},{8,20},{12,24},{16,28},{20,0},{24,4},{28,8},{1,13},{... | collective-permute-start | bytes 208904 | tf_op jit(solution)/shard_map/ppermute | solution.py:436
  131.6 11.9 %collective-permute-start.20 = (bf16[136,256]{1,0:T(8,128)(2,1)S(1)}, bf16[136,256]{1,0:T(8,128)(2,1)S(1)}, u32[]{:S(2)}, u32[]{:S(2)}) collective-permute-start(bf16[136,256]{1,0:T(8,128)(2,1)S(1)} %share.1.refs_0_), channel_id=1, source_target_pairs={{0,8},{4,12},{8,16},{12,20},{16,24},{20,28},{24,0},{28,4},{1,9},{5... | collective-permute-start | bytes 208904 | tf_op jit(solution)/shard_map/ppermute | solution.py:436
  134.9 10.1 %collective-permute-start.19 = (bf16[136,256]{1,0:T(8,128)(2,1)S(1)}, bf16[136,256]{1,0:T(8,128)(2,1)S(1)}, u32[]{:S(2)}, u32[]{:S(2)}) collective-permute-start(bf16[136,256]{1,0:T(8,128)(2,1)S(1)} %share.1.refs_0_), channel_id=1, source_target_pairs={{0,4},{4,8},{8,12},{12,16},{16,20},{20,24},{24,28},{28,0},{1,5},{5... | collective-permute-start | bytes 208904 | tf_op jit(solution)/shard_map/ppermute | solution.py:436
  (6 other events, 16.1 us)

commit v4 on v3

--- a/solution.py
+++ b/solution.py
@@ -56,13 +56,14 @@
     return jnp.where(row == 0, packed, 0.0)
 
 
-def unit_kernel(a, b, c, d, out, scale):
+def unit_kernel(a, b, c, d, out, raw, scale):
     blocks = [r[...].astype(F32) for r in (a, b, c, d)]
     squares = sum(jnp.sum(v * v, axis=1, keepdims=True) for v in blocks)
     inv = lax.rsqrt(squares + 1e-06)
     scale[...] = jnp.broadcast_to(inv, scale.shape)
-    for q, v in enumerate(blocks):
+    for q, (v, r) in enumerate(zip(blocks, (a, b, c, d))):
         out[:, 256 * q : 256 * q + 256] = (v * inv).astype(BF16)
+        raw[:, 256 * q : 256 * q + 256] = r[...]
 
 
 def make_unit(blocks):
@@ -74,9 +75,11 @@
         in_specs=[pl.BlockSpec((tile, 256), lambda i: (i, 0))] * 4,
         out_specs=[
             pl.BlockSpec((tile, 1024), lambda i: (i, 0)),
+            pl.BlockSpec((tile, 1024), lambda i: (i, 0)),
             pl.BlockSpec((tile, 128), lambda i: (i, 0)),
         ],
         out_shape=[
+            jax.ShapeDtypeStruct((rows, 1024), BF16),
             jax.ShapeDtypeStruct((rows, 1024), BF16),
             jax.ShapeDtypeStruct((rows, 128), F32),
         ],
@@ -223,11 +226,10 @@
     )(scalars, *tables, unit, lane_f, labels, mask)
 
 
-def region_kernel(s, keep, send, t0, t1, t2, t3, a, b, c, d, inv_ref, out, acc):
+def region_kernel(s, keep, send, t0, t1, t2, t3, raw, inv_ref, out, acc):
     half = keep.shape[0]
     k = s[K]
     tile = acc.shape[0]
-    blocks = (a, b, c, d)
     mine_at = pl.multiple_of(k * half, 32)
     theirs_at = pl.multiple_of((1 - k) * half, 32)
 
@@ -251,27 +253,28 @@
                     for p in range(2)
                 )
             acc[:, 256 * q : 256 * q + 256] = part
-            along += jnp.sum(part * blocks[q][here, :].astype(F32), axis=1, keepdims=True)
+            value = raw[here, 256 * q : 256 * q + 256].astype(F32)
+            along += jnp.sum(part * value, axis=1, keepdims=True)
         back = inv * inv * along
-        for q, r in enumerate(blocks):
+        for q in range(4):
             cols = slice(256 * q, 256 * q + 256)
-            grad = inv * (acc[:, cols] - r[here, :].astype(F32) * back)
+            grad = inv * (acc[:, cols] - raw[here, cols].astype(F32) * back)
             for p in range(tile // 64):
                 z = tile // 64 * i + p
                 out[z, :, cols] = grad[64 * p : 64 * p + 64, :].astype(BF16)
 
 
-def make_region(scalars, keep, send, tables, blocks, inv):
+def make_region(scalars, keep, send, tables, raw, inv):
     return pl.pallas_call(
         region_kernel,
-        in_specs=[smem()] + vmem(11),
+        in_specs=[smem()] + vmem(8),
         out_specs=vmem(1)[0],
         out_shape=in_hbm((8, 64, 1024), BF16),
         scratch_shapes=[pltpu.VMEM((256, 1024), F32)],
         compiler_params=params(24),
         cost_estimate=cost(1.4e9),
         name="region",
-    )(scalars, keep, send, *tables, *blocks, inv)
+    )(scalars, keep, send, *tables, raw, inv)
 
 
 def table_kernel(s, keep, other, unit, loss, *refs):
@@ -390,7 +393,14 @@
 
 
 def final_kernel(s, count, tables, *refs):
-    regions, (region_out, table_out, loss_out) = refs[:8], refs[8:]
+    regions, (region_out, table_out, loss_out, sems) = refs[:8], refs[8:]
+    copies = []
+    for y in range(4):
+        at = pl.multiple_of(672 * (s[E] ^ y), 32)
+        for x in range(2):
+            to = table_out.at[pl.ds(at, 672), pl.ds(128 * x, 128)]
+            copies.append(pltpu.make_async_copy(tables.at[2 * y + x], to, sems.at[2 * y + x]))
+            copies[-1].start()
     total = 0.0
     for d in range(8):
         source = (s[Z] + 8 - d) % 8
@@ -398,17 +408,16 @@
             region_out[k, source] = regions[d][64 * k : 64 * k + 64, :]
         total += jnp.sum(regions[d][128:136, :].astype(F32))
     loss_out[0, 0] = total / count[0, 0] / CLASSES
-    for y in range(4):
-        at = pl.multiple_of(672 * (s[E] ^ y), 32)
-        for x in range(2):
-            table_out[pl.ds(at, 672), 128 * x : 128 * x + 128] = tables[2 * y + x]
+    for copy in copies:
+        copy.wait()
 
 
 def make_final(scalars, count, tables, regions):
     return pl.pallas_call(
         final_kernel,
         in_specs=[smem(), smem()] + vmem(9),
-        out_specs=vmem(2) + [smem()],
+        out_specs=vmem(1) + [pl.BlockSpec(memory_space=pltpu.HBM), smem()],
+        scratch_shapes=[pltpu.SemaphoreType.DMA((8,))],
         out_shape=[
             jax.ShapeDtypeStruct((2, 8, 64, 256), BF16),
             jax.ShapeDtypeStruct((2688, 256), BF16),
@@ -463,16 +472,16 @@
     t_both = swap(t_far, "emb_1")
     blocks = (regions, r_near, r_far, r_both)
     tables = (t_own, t_near, t_far, t_both)
-    unit, inv = make_unit(blocks)
+    unit, raw, inv = make_unit(blocks)
 
     lane_f = jnp.concatenate([shift[None], scale[None], jnp.zeros((6, rows), F32)], axis=0)
     mask = lax.dynamic_slice(valid, (k, xh * 1344), (1, 1344)).astype(F32).T
     keep, send, loss, count = make_focal(scalars, tables, unit, lane_f, labels[None], mask)
 
     theirs = swap(send, "emb_1")
-    terms = exchange(make_region(scalars, keep, send, tables, blocks, inv), CLS)
+    terms = exchange(make_region(scalars, keep, send, tables, raw, inv), CLS)
     chunks = list(make_table(scalars, keep, theirs, unit, loss))
-    for o in (3, 6, 5, 2, 7, 4, 1):
+    for o in OVER_IMG:
         chunks[o] = over_img(chunks[o], o // 2, o % 2)
     table_part, loss_part = make_table_sum(chunks)
     table_part = to_owner(table_part)
@@ -482,9 +491,15 @@
     message = make_gather(table_part)
     table_all = exchange(message, IMG)
     share = make_share(scalars, parts)
-    shares = [share] + [along_cls(share, d) for d in range(1, 8)]
+    shares = [share] * 8
+    for d in ALONG_CLS:
+        shares[d] = along_cls(share, d)
     region_grad, table_grad, total = make_final(scalars, count, table_all, shares)
     return (total[0, 0], region_grad.reshape(rows, 256), table_grad)
+
+
+OVER_IMG = (3, 6, 5, 2, 7, 4, 1)
+ALONG_CLS = (4, 3, 5, 2, 6, 1, 7)
 
 
 def solution(mesh):

time: 150 us -> 150 us (level)
  transfers between devices with their start and end apart: 29 -> 29, of which waited for: 13 -> 12; matrix products, arithmetic and copies ran while one was open for 2% -> 2% of each run, Pallas kernels for 5% -> 5%
where the time goes in v4:
time: 150 us; the launch traced here: 148 us
  starting transfers between devices  71.2 us (47%)
  waiting for transfers between devices  44.5 us (30%)
  Pallas kernels  24 us (16%)
  local copies, waits for them, and re-layouts  5.53 us (4%)
    all_to_all x3, starting transfers between devices, exchange(): return lax.all_to_all(x, axes, split_axis=0, concat_axis=0, tiled=True)  28.9 us
    ppermute x7, starting transfers between devices, along_cls(): return lax.ppermute(x, CLS, [(i, (i + d) % 8) for i in range(8)])  14 us
    ppermute x8, starting transfers between devices, swap(): return lax.ppermute(x, axis, [(0, 1), (1, 0)])  13.5 us
    ppermute x3, waiting for transfers between devices, shards(): parts[q] = lax.ppermute(parts[q], EMB, [(i, i ^ q) for i in range(4)])  13.1 us
    ppermute x7, waiting for transfers between devices, over_img(): return lax.ppermute(x, IMG, pairs)  10.3 us
    ppermute x7, starting transfers between devices, over_img(): return lax.ppermute(x, IMG, pairs)  9.81 us
    ppermute x7, waiting for transfers between devices, along_cls(): return lax.ppermute(x, CLS, [(i, (i + d) % 8) for i in range(8)])  8.93 us
    pallas_call x1, Pallas kernels, make_focal(): pl.pallas_call(focal_kernel, grid_spec=pltpu.PrefetchScalarGridSpec(num_s...  7.08 us
  transfers between devices with their start and end apart: 29, of which 12 were waited for; matrix products, arithmetic and copies ran while one was open for 2% of the time, Pallas kernels for 5%

profile of v4, /device:TPU:1, one launch (start us, length us, event | category | flops | bytes accessed | tf_op | source)
XLA Modules:
  0.0 147.8 jit_solution(4437945442513100798)
XLA Ops:
  1.6 3.6 %collective-permute-start.1 = (bf16[336,256]{1,0:T(8,128)(2,1)S(1)}, bf16[336,256]{1,0:T(8,128)(2,1)S(1)}, u32[]{:S(2)}, u32[]{:S(2)}) collective-permute-start(bf16[336,256]{1,0:T(8,128)(2,1)S(1)} %rows.1), channel_id=1, source_target_pairs={{0,2},{2,0},{1,3},{3,1},{4,6},{6,4},{5,7},{7,5},{8,10},{10,8},{9,1... | collective-permute-start | bytes 516104 | tf_op jit(solution)/shard_map/ppermute | solution.py:46
  6.9 2.2 %collective-permute-done.2.theirs = f32[8,128]{1,0:T(8,128)S(1)} collective-permute-done((f32[8,128]{1,0:T(8,128)S(1)}, f32[8,128]{1,0:T(8,128)S(1)}, u32[]{:S(2)}, u32[]{:S(2)}) %collective-permute-start.2) | collective-permute-done | bytes 4128 | tf_op jit(solution)/shard_map/ppermute | solution.py:46
  10.1 4.5 %all-to-all-start = ((bf16[4,344,256]{2,1,0:T(8,128)(2,1)}), bf16[4,344,256]{2,1,0:T(8,128)(2,1)S(1)}, u32[]{:S(2)}, u32[]{:S(2)}) async-start(bf16[4,344,256]{2,1,0:T(8,128)(2,1)} %message.1), calls=%async_computation | async-start | bytes 1409024 | tf_op jit(solution)/shard_map/all_to_all | solution.py:449
  14.5 2.6 %collective-permute-start.5 = (bf16[1024,256]{1,0:T(8,128)(2,1)}, bf16[1024,256]{1,0:T(8,128)(2,1)}, u32[]{:S(2)}, u32[]{:S(2)}) collective-permute-start(bf16[1024,256]{1,0:T(8,128)(2,1)} %a.1), channel_id=1, source_target_pairs={{0,2},{2,0},{1,3},{3,1},{4,6},{6,4},{5,7},{7,5},{8,10},{10,8},{9,1... | collective-permute-start | bytes 1572872 | tf_op jit(solution)/shard_map/ppermute | solution.py:46
  17.1 7.1 %all-to-all-done.t2 = bf16[4,344,256]{2,1,0:T(8,128)(2,1)S(1)} async-done(((bf16[4,344,256]{2,1,0:T(8,128)(2,1)}), bf16[4,344,256]{2,1,0:T(8,128)(2,1)S(1)}, u32[]{:S(2)}, u32[]{:S(2)}) %all-to-all-start) | async-done | bytes 704544 | tf_op jit(solution)/shard_map/all_to_all | solution.py:449
  24.2 2.7 %collective-permute-start.3 = (bf16[4,344,256]{2,1,0:T(8,128)(2,1)S(1)}, bf16[4,344,256]{2,1,0:T(8,128)(2,1)S(1)}, u32[]{:S(2)}, u32[]{:S(2)}) collective-permute-start(bf16[4,344,256]{2,1,0:T(8,128)(2,1)S(1)} %all-to-all-done.t2), channel_id=1, source_target_pairs={{0,1},{1,0},{2,3},{3,2},{4,5},{5,4},{6,7},{7,6},{8,9},{9,8},{10,11... | collective-permute-start | bytes 2113544 | tf_op jit(solution)/shard_map/ppermute | solution.py:46
  27.9 2.8 %collective-permute-start.6 = (bf16[1024,256]{1,0:T(8,128)(2,1)}, bf16[1024,256]{1,0:T(8,128)(2,1)}, u32[]{:S(2)}, u32[]{:S(2)}) collective-permute-start(bf16[1024,256]{1,0:T(8,128)(2,1)} %collective-permute-done.5.c), channel_id=1, source_target_pairs={{0,1},{1,0},{2,3},{3,2},{4,5},{5,4},{6,7},{7,6},{8,9},{9,8},{10,11... | collective-permute-start | bytes 1572872 | tf_op jit(solution)/shard_map/ppermute | solution.py:46
  32.6 3.1 %unit.1 = (bf16[1024,1024]{1,0:T(8,128)(2,1)S(1)}, bf16[1024,1024]{1,0:T(8,128)(2,1)S(1)}, f32[1024,128]{1,0:T(8,128)S(1)}) custom-call(bf16[1024,256]{1,0:T(8,128)(2,1)} %a.1, bf16[1024,256]{1,0:T(8,128)(2,1)} %collective-permute-done.4.b, bf16[1024,256]{1,0:T(8,128)(2,1)} %collective-permute-done.5.c, bf16[1024,256]{1,0:T(8,128)(2,1)} %collective-permute-done.6.d), custom_call_target="tpu_custom_call" | custom-call | flops 20000000 | bytes 1048576 | tf_op jit(solution)/shard_map/unit/pallas_call | solution.py:72
  35.7 7.1 %focal.1 = (bf16[672,512]{1,0:T(8,128)(2,1)S(1)}, bf16[672,512]{1,0:T(8,128)(2,1)S(1)}, f32[8,128]{1,0:T(8,128)S(1)}, f32[1,1]{1,0:T(1,128)}) custom-call(s32[6]{0:T(128)S(1)} %stack.27.s, bf16[1344,256]{1,0:T(8,128)(2,1)S(1)} %constant_dynamic-slice_fusion.t0, bf16[1344,256]{1,0:T(8,128)(2,1)S(1)} %collective-permute-done.t1, ...), custom_call_target="tpu_custom_call" | custom-call | flops 1400000000 | bytes 1048576 | tf_op jit(solution)/shard_map/focal/pallas_call | solution.py:196
  42.8 4.0 %region.1 = bf16[8,64,1024]{2,1,0:T(8,128)(2,1)} custom-call(s32[6]{0:T(128)S(1)} %stack.27.s, bf16[672,512]{1,0:T(8,128)(2,1)S(1)} %get-tuple-element.33.keep, bf16[672,512]{1,0:T(8,128)(2,1)S(1)} %get-tuple-element.34.send, bf16[1344,256]{1,0:T(8,128)(2,1)S(1)} %constant_dynamic-slice_fusion.t0, bf16[1344,256]{1,0:T(8,128)(2,1)S(1)} %collective-permute-done.t1, ...), custom_call_target="tpu_custom_call" | custom-call | flops 1400000000 | bytes 1048576 | tf_op jit(solution)/shard_map/region/pallas_call | solution.py:268
  48.5 8.2 %all-to-all-start.2 = ((bf16[8,64,1024]{2,1,0:T(8,128)(2,1)}), bf16[8,64,1024]{2,1,0:T(8,128)(2,1)S(1)}, u32[]{:S(2)}, u32[]{:S(2)}) async-start(bf16[8,64,1024]{2,1,0:T(8,128)(2,1)} %region.1), calls=%async_computation.2 | async-start | bytes 2097152 | tf_op jit(solution)/shard_map/all_to_all | solution.py:449
  57.4 2.0 %collective-permute-done.7.other = bf16[672,512]{1,0:T(8,128)(2,1)S(1)} collective-permute-done((bf16[672,512]{1,0:T(8,128)(2,1)}, bf16[672,512]{1,0:T(8,128)(2,1)S(1)}, u32[]{:S(2)}, u32[]{:S(2)}) %collective-permute-start.7) | collective-permute-done | bytes 688160 | tf_op jit(solution)/shard_map/ppermute | solution.py:46
  59.4 1.6 %copy-done.1 = bf16[1024,1024]{1,0:T(8,128)(2,1)S(1)} copy-done((bf16[1024,1024]{1,0:T(8,128)(2,1)S(1)}, bf16[1024,1024]{1,0:T(8,128)(2,1)}, u32[]{:S(2)}) %copy-start.1) | copy-done | bytes 2097176
  62.1 2.4 %table.1 = (bf16[680,128]{1,0:T(8,128)(2,1)S(1)}, bf16[680,128]{1,0:T(8,128)(2,1)S(1)}, bf16[680,128]{1,0:T(8,128)(2,1)S(1)}, bf16[680,128]{1,0:T(8,128)(2,1)S(1...) custom-call(s32[6]{0:T(128)S(1)} %stack.27.s, ...), custom_call_target="tpu_custom_call" | custom-call | flops 1400000000 | bytes 1048576 | tf_op jit(solution)/shard_map/table/pallas_call | solution.py:302
  65.7 1.5 collective-permute-start.9
  68.4 1.3 collective-permute-start.11
  69.7 2.6 %collective-permute-start.12 = (bf16[680,128]{1,0:T(8,128)(2,1)S(1)}, bf16[680,128]{1,0:T(8,128)(2,1)S(1)}, u32[]{:S(2)}, u32[]{:S(2)}) collective-permute-start(bf16[680,128]{1,0:T(8,128)(2,1)S(1)} %get-tuple-element.41), channel_id=1, source_target_pairs={{0,160},{32,128},{64,224},{96,192},{128,32},{160,0},{192,96},{224,... | collective-permute-start | bytes 522248 | tf_op jit(solution)/shard_map/ppermute | solution.py:436
  72.2 1.5 %collective-permute-start.13 = (bf16[680,128]{1,0:T(8,128)(2,1)S(1)}, bf16[680,128]{1,0:T(8,128)(2,1)S(1)}, u32[]{:S(2)}, u32[]{:S(2)}) collective-permute-start(bf16[680,128]{1,0:T(8,128)(2,1)S(1)} %get-tuple-element.42), channel_id=1, source_target_pairs={{0,192},{32,224},{64,0},{96,32},{128,64},{160,96},{192,128},{224,1... | collective-permute-start | bytes 522248 | tf_op jit(solution)/shard_map/ppermute | solution.py:436
  74.3 2.1 %collective-permute-done.10.refs_3_ = bf16[680,128]{1,0:T(8,128)(2,1)S(1)} collective-permute-done((bf16[680,128]{1,0:T(8,128)(2,1)S(1)}, bf16[680,128]{1,0:T(8,128)(2,1)S(1)}, u32[]{:S(2)}, u32[]{:S(2)}) %collective-permute-start.10) | collective-permute-done | bytes 174112 | tf_op jit(solution)/shard_map/ppermute | solution.py:436
  76.4 8.2 %collective-permute-done.11.refs_4_ = bf16[680,128]{1,0:T(8,128)(2,1)S(1)} collective-permute-done((bf16[680,128]{1,0:T(8,128)(2,1)S(1)}, bf16[680,128]{1,0:T(8,128)(2,1)S(1)}, u32[]{:S(2)}, u32[]{:S(2)}) %collective-permute-start.11) | collective-permute-done | bytes 174112 | tf_op jit(solution)/shard_map/ppermute | solution.py:436
  86.8 16.3 %all-to-all-start.1 = ((bf16[8,672,128]{2,1,0:T(8,128)(2,1)}), bf16[8,672,128]{2,1,0:T(8,128)(2,1)S(1)}, u32[]{:S(2)}, u32[]{:S(2)}) async-start(bf16[8,672,128]{2,1,0:T(8,128)(2,1)} %gather.1), calls=%async_computation.1 | async-start | bytes 2752512 | tf_op jit(solution)/shard_map/all_to_all | solution.py:449
  105.7 2.0 %collective-permute-start.18 = (bf16[72,256]{1,0:T(8,128)(2,1)S(1)}, bf16[72,256]{1,0:T(8,128)(2,1)S(1)}, u32[]{:S(2)}, u32[]{:S(2)}) collective-permute-start(bf16[72,256]{1,0:T(8,128)(2,1)S(1)} %get-tuple-element.51), channel_id=1, source_target_pairs={{0,3},{1,2},{2,1},{3,0},{4,7},{5,6},{6,5},{7,4},{8,11},{9,10},{10,... | collective-permute-start | bytes 110600 | tf_op jit(solution)/shard_map/ppermute | solution.py:490
  107.6 10.5 %collective-permute-done.17.far = bf16[72,256]{1,0:T(8,128)(2,1)S(1)} collective-permute-done((bf16[72,256]{1,0:T(8,128)(2,1)S(1)}, bf16[72,256]{1,0:T(8,128)(2,1)S(1)}, u32[]{:S(2)}, u32[]{:S(2)}) %collective-permute-start.17) | collective-permute-done | bytes 36896 | tf_op jit(solution)/shard_map/ppermute | solution.py:490
  118.2 2.6 %collective-permute-done.18.both = bf16[72,256]{1,0:T(8,128)(2,1)S(1)} collective-permute-done((bf16[72,256]{1,0:T(8,128)(2,1)S(1)}, bf16[72,256]{1,0:T(8,128)(2,1)S(1)}, u32[]{:S(2)}, u32[]{:S(2)}) %collective-permute-start.18) | collective-permute-done | bytes 36896 | tf_op jit(solution)/shard_map/ppermute | solution.py:490
  121.4 3.0 %collective-permute-start.25 = (bf16[136,256]{1,0:T(8,128)(2,1)S(1)}, bf16[136,256]{1,0:T(8,128)(2,1)S(1)}, u32[]{:S(2)}, u32[]{:S(2)}) collective-permute-start(bf16[136,256]{1,0:T(8,128)(2,1)S(1)} %share.1.refs_0_), channel_id=1, source_target_pairs={{0,28},{4,0},{8,4},{12,8},{16,12},{20,16},{24,20},{28,24},{1,29},{... | collective-permute-start | bytes 208904 | tf_op jit(solution)/shard_map/ppermute | solution.py:445
  124.5 2.1 %collective-permute-start.24 = (bf16[136,256]{1,0:T(8,128)(2,1)S(1)}, bf16[136,256]{1,0:T(8,128)(2,1)S(1)}, u32[]{:S(2)}, u32[]{:S(2)}) collective-permute-start(bf16[136,256]{1,0:T(8,128)(2,1)S(1)} %share.1.refs_0_), channel_id=1, source_target_pairs={{0,24},{4,28},{8,0},{12,4},{16,8},{20,12},{24,16},{28,20},{1,25},{... | collective-permute-start | bytes 208904 | tf_op jit(solution)/shard_map/ppermute | solution.py:445
  127.7 3.3 %collective-permute-start.22 = (bf16[136,256]{1,0:T(8,128)(2,1)S(1)}, bf16[136,256]{1,0:T(8,128)(2,1)S(1)}, u32[]{:S(2)}, u32[]{:S(2)}) collective-permute-start(bf16[136,256]{1,0:T(8,128)(2,1)S(1)} %share.1.refs_0_), channel_id=1, source_target_pairs={{0,16},{4,20},{8,24},{12,28},{16,0},{20,4},{24,8},{28,12},{1,17},{... | collective-permute-start | bytes 208904 | tf_op jit(solution)/shard_map/ppermute | solution.py:445
  131.0 3.3 %collective-permute-start.20 = (bf16[136,256]{1,0:T(8,128)(2,1)S(1)}, bf16[136,256]{1,0:T(8,128)(2,1)S(1)}, u32[]{:S(2)}, u32[]{:S(2)}) collective-permute-start(bf16[136,256]{1,0:T(8,128)(2,1)S(1)} %share.1.refs_0_), channel_id=1, source_target_pairs={{0,8},{4,12},{8,16},{12,20},{16,24},{20,28},{24,0},{28,4},{1,9},{5... | collective-permute-start | bytes 208904 | tf_op jit(solution)/shard_map/ppermute | solution.py:445
  135.5 1.4 collective-permute-done.22.refs_4_
  136.8 4.8 %collective-permute-done.21.refs_3_ = bf16[136,256]{1,0:T(8,128)(2,1)S(1)} collective-permute-done((bf16[136,256]{1,0:T(8,128)(2,1)S(1)}, bf16[136,256]{1,0:T(8,128)(2,1)S(1)}, u32[]{:S(2)}, u32[]{:S(2)}) %collective-permute-start.21) | collective-permute-done | bytes 69664 | tf_op jit(solution)/shard_map/ppermute | solution.py:445
  141.7 2.7 %collective-permute-done.20.refs_2_ = bf16[136,256]{1,0:T(8,128)(2,1)S(1)} collective-permute-done((bf16[136,256]{1,0:T(8,128)(2,1)S(1)}, bf16[136,256]{1,0:T(8,128)(2,1)S(1)}, u32[]{:S(2)}, u32[]{:S(2)}) %collective-permute-start.20) | collective-permute-done | bytes 69664 | tf_op jit(solution)/shard_map/ppermute | solution.py:445
  144.4 3.2 %final.1 = (bf16[2,8,64,256]{3,2,1,0:T(8,128)(2,1)}, bf16[2688,256]{1,0:T(8,128)(2,1)}, f32[1,1]{1,0:T(1,128)}) custom-call(s32[6]{0:T(128)S(1)} %stack.27.s, f32[1,1]{1,0:T(1,128)} %get-tuple-element.32.count, bf16[8,672,128]{2,1,0:T(8,128)(2,1)S(1)} %all-to-all-done.1.tables, bf16[136,256]{1,0:T(8,128)(2,1)S(1)} %share.1.refs_0_, ...), custom_call_target="tpu_custom_call" | custom-call | flops 10000000 | bytes 1048576 | tf_op jit(solution)/shard_map/final/pallas_call | solution.py:416
  (64 shorter events, 20.6 us)
Async XLA Ops:
  1.6 25.3 %copy-start.6 = (bf16[2688,256]{1,0:T(8,128)(2,1)S(1)}, bf16[2688,256]{1,0:T(8,128)(2,1)}, u32[]{:S(2)}) copy-start(bf16[2688,256]{1,0:T(8,128)(2,1)} %x.1) | copy-start | bytes 4128772
  1.6 7.6 %collective-permute-start.1 = (bf16[336,256]{1,0:T(8,128)(2,1)S(1)}, bf16[336,256]{1,0:T(8,128)(2,1)S(1)}, u32[]{:S(2)}, u32[]{:S(2)}) collective-permute-start(bf16[336,256]{1,0:T(8,128)(2,1)S(1)} %rows.1), channel_id=1, source_target_pairs={{0,2},{2,0},{1,3},{3,1},{4,6},{6,4},{5,7},{7,5},{8,10},{10,8},{9,1... | collective-permute-start | bytes 516104 | tf_op jit(solution)/shard_map/ppermute | solution.py:46
  6.5 2.6 %collective-permute-start.2 = (f32[8,128]{1,0:T(8,128)S(1)}, f32[8,128]{1,0:T(8,128)S(1)}, u32[]{:S(2)}, u32[]{:S(2)}) collective-permute-start(f32[8,128]{1,0:T(8,128)S(1)} %broadcast_in_dim.15.mine), channel_id=1, source_target_pairs={{0,32},{32,0},{1,33},{33,1},{2,34},{34,2},{3,35},{35,3},{4,36},{36... | collective-permute-start | bytes 12296 | tf_op jit(solution)/shard_map/ppermute | solution.py:46
  10.1 14.1 %all-to-all-start = ((bf16[4,344,256]{2,1,0:T(8,128)(2,1)}), bf16[4,344,256]{2,1,0:T(8,128)(2,1)S(1)}, u32[]{:S(2)}, u32[]{:S(2)}) async-start(bf16[4,344,256]{2,1,0:T(8,128)(2,1)} %message.1), calls=%async_computation | async-start | bytes 1409024 | tf_op jit(solution)/shard_map/all_to_all | solution.py:449
  14.5 17.4 %copy-start.7 = (f32[1024]{0:T(1024)S(1)}, f32[1024]{0:T(1024)}, u32[]{:S(2)}) copy-start(f32[1024]{0:T(1024)} %param.9) | copy-start | bytes 12292
  14.5 17.4 %copy-start.8 = (f32[1024]{0:T(1024)S(1)}, f32[1024]{0:T(1024)}, u32[]{:S(2)}) copy-start(f32[1024]{0:T(1024)} %param.8) | copy-start | bytes 12292
  14.5 13.3 %collective-permute-start.5 = (bf16[1024,256]{1,0:T(8,128)(2,1)}, bf16[1024,256]{1,0:T(8,128)(2,1)}, u32[]{:S(2)}, u32[]{:S(2)}) collective-permute-start(bf16[1024,256]{1,0:T(8,128)(2,1)} %a.1), channel_id=1, source_target_pairs={{0,2},{2,0},{1,3},{3,1},{4,6},{6,4},{5,7},{7,5},{8,10},{10,8},{9,1... | collective-permute-start | bytes 1572872 | tf_op jit(solution)/shard_map/ppermute | solution.py:46
  24.2 11.5 %collective-permute-start.3 = (bf16[4,344,256]{2,1,0:T(8,128)(2,1)S(1)}, bf16[4,344,256]{2,1,0:T(8,128)(2,1)S(1)}, u32[]{:S(2)}, u32[]{:S(2)}) collective-permute-start(bf16[4,344,256]{2,1,0:T(8,128)(2,1)S(1)} %all-to-all-done.t2), channel_id=1, source_target_pairs={{0,1},{1,0},{2,3},{3,2},{4,5},{5,4},{6,7},{7,6},{8,9},{9,8},{10,11... | collective-permute-start | bytes 2113544 | tf_op jit(solution)/shard_map/ppermute | solution.py:46
  27.0 8.7 %collective-permute-start = (bf16[1344,256]{1,0:T(8,128)(2,1)S(1)}, bf16[1344,256]{1,0:T(8,128)(2,1)S(1)}, u32[]{:S(2)}, u32[]{:S(2)}) collective-permute-start(bf16[1344,256]{1,0:T(8,128)(2,1)S(1)} %constant_dynamic-slice_fusion.t0), channel_id=1, source_target_pairs={{0,1},{1,0},{2,3},{3,2},{4,5},{5,4},{6,7},{7,6},{8,9},{9,8},{10,11... | collective-permute-start | bytes 2064392 | tf_op jit(solution)/shard_map/ppermute | solution.py:46
  27.1 5.0 %collective-permute-start.4 = (bf16[1024,256]{1,0:T(8,128)(2,1)}, bf16[1024,256]{1,0:T(8,128)(2,1)}, u32[]{:S(2)}, u32[]{:S(2)}) collective-permute-start(bf16[1024,256]{1,0:T(8,128)(2,1)} %a.1), channel_id=1, source_target_pairs={{0,1},{1,0},{2,3},{3,2},{4,5},{5,4},{6,7},{7,6},{8,9},{9,8},{10,11... | collective-permute-start | bytes 1572872 | tf_op jit(solution)/shard_map/ppermute | solution.py:46
  27.9 4.7 %collective-permute-start.6 = (bf16[1024,256]{1,0:T(8,128)(2,1)}, bf16[1024,256]{1,0:T(8,128)(2,1)}, u32[]{:S(2)}, u32[]{:S(2)}) collective-permute-start(bf16[1024,256]{1,0:T(8,128)(2,1)} %collective-permute-done.5.c), channel_id=1, source_target_pairs={{0,1},{1,0},{2,3},{3,2},{4,5},{5,4},{6,7},{7,6},{8,9},{9,8},{10,11... | collective-permute-start | bytes 1572872 | tf_op jit(solution)/shard_map/ppermute | solution.py:46
  48.5 38.2 %all-to-all-start.2 = ((bf16[8,64,1024]{2,1,0:T(8,128)(2,1)}), bf16[8,64,1024]{2,1,0:T(8,128)(2,1)S(1)}, u32[]{:S(2)}, u32[]{:S(2)}) async-start(bf16[8,64,1024]{2,1,0:T(8,128)(2,1)} %region.1), calls=%async_computation.2 | async-start | bytes 2097152 | tf_op jit(solution)/shard_map/all_to_all | solution.py:449
  56.7 2.6 %collective-permute-start.7 = (bf16[672,512]{1,0:T(8,128)(2,1)}, bf16[672,512]{1,0:T(8,128)(2,1)S(1)}, u32[]{:S(2)}, u32[]{:S(2)}) collective-permute-start(bf16[672,512]{1,0:T(8,128)(2,1)} %copy-done.4), channel_id=1, source_target_pairs={{0,1},{1,0},{2,3},{3,2},{4,5},{5,4},{6,7},{7,6},{8,9},{9,8},{10,11... | collective-permute-start | bytes 2064392 | tf_op jit(solution)/shard_map/ppermute | solution.py:46
  64.5 7.8 %collective-permute-start.8 = (bf16[680,128]{1,0:T(8,128)(2,1)S(1)}, bf16[680,128]{1,0:T(8,128)(2,1)S(1)}, u32[]{:S(2)}, u32[]{:S(2)}) collective-permute-start(bf16[680,128]{1,0:T(8,128)(2,1)S(1)} %get-tuple-element.37), channel_id=1, source_target_pairs={{0,32},{32,0},{64,96},{96,64},{128,160},{160,128},{192,224},{224,1... | collective-permute-start | bytes 522248 | tf_op jit(solution)/shard_map/ppermute | solution.py:436
  65.7 8.0 %collective-permute-start.9 = (bf16[680,128]{1,0:T(8,128)(2,1)S(1)}, bf16[680,128]{1,0:T(8,128)(2,1)S(1)}, u32[]{:S(2)}, u32[]{:S(2)}) collective-permute-start(bf16[680,128]{1,0:T(8,128)(2,1)S(1)} %get-tuple-element.38), channel_id=1, source_target_pairs={{0,64},{32,96},{64,128},{96,160},{128,192},{160,224},{192,0},{224,... | collective-permute-start | bytes 522248 | tf_op jit(solution)/shard_map/ppermute | solution.py:436
  67.2 9.2 %collective-permute-start.10 = (bf16[680,128]{1,0:T(8,128)(2,1)S(1)}, bf16[680,128]{1,0:T(8,128)(2,1)S(1)}, u32[]{:S(2)}, u32[]{:S(2)}) collective-permute-start(bf16[680,128]{1,0:T(8,128)(2,1)S(1)} %get-tuple-element.39), channel_id=1, source_target_pairs={{0,96},{32,64},{64,160},{96,128},{128,224},{160,192},{192,32},{224... | collective-permute-start | bytes 522248 | tf_op jit(solution)/shard_map/ppermute | solution.py:436
  68.4 16.2 %collective-permute-start.11 = (bf16[680,128]{1,0:T(8,128)(2,1)S(1)}, bf16[680,128]{1,0:T(8,128)(2,1)S(1)}, u32[]{:S(2)}, u32[]{:S(2)}) collective-permute-start(bf16[680,128]{1,0:T(8,128)(2,1)S(1)} %get-tuple-element.40), channel_id=1, source_target_pairs={{0,128},{32,160},{64,192},{96,224},{128,0},{160,32},{192,64},{224,... | collective-permute-start | bytes 522248 | tf_op jit(solution)/shard_map/ppermute | solution.py:436
  69.7 15.0 %collective-permute-start.12 = (bf16[680,128]{1,0:T(8,128)(2,1)S(1)}, bf16[680,128]{1,0:T(8,128)(2,1)S(1)}, u32[]{:S(2)}, u32[]{:S(2)}) collective-permute-start(bf16[680,128]{1,0:T(8,128)(2,1)S(1)} %get-tuple-element.41), channel_id=1, source_target_pairs={{0,160},{32,128},{64,224},{96,192},{128,32},{160,0},{192,96},{224,... | collective-permute-start | bytes 522248 | tf_op jit(solution)/shard_map/ppermute | solution.py:436
  72.2 12.4 %collective-permute-start.13 = (bf16[680,128]{1,0:T(8,128)(2,1)S(1)}, bf16[680,128]{1,0:T(8,128)(2,1)S(1)}, u32[]{:S(2)}, u32[]{:S(2)}) collective-permute-start(bf16[680,128]{1,0:T(8,128)(2,1)S(1)} %get-tuple-element.42), channel_id=1, source_target_pairs={{0,192},{32,224},{64,0},{96,32},{128,64},{160,96},{192,128},{224,1... | collective-permute-start | bytes 522248 | tf_op jit(solution)/shard_map/ppermute | solution.py:436
  73.7 10.9 %collective-permute-start.14 = (bf16[680,128]{1,0:T(8,128)(2,1)S(1)}, bf16[680,128]{1,0:T(8,128)(2,1)S(1)}, u32[]{:S(2)}, u32[]{:S(2)}) collective-permute-start(bf16[680,128]{1,0:T(8,128)(2,1)S(1)} %get-tuple-element.43), channel_id=1, source_target_pairs={{0,224},{32,192},{64,32},{96,0},{128,96},{160,64},{192,160},{224,1... | collective-permute-start | bytes 522248 | tf_op jit(solution)/shard_map/ppermute | solution.py:436
  84.8 0.7 collective-permute-start.15
  86.8 57.6 %all-to-all-start.1 = ((bf16[8,672,128]{2,1,0:T(8,128)(2,1)}), bf16[8,672,128]{2,1,0:T(8,128)(2,1)S(1)}, u32[]{:S(2)}, u32[]{:S(2)}) async-start(bf16[8,672,128]{2,1,0:T(8,128)(2,1)} %gather.1), calls=%async_computation.1 | async-start | bytes 2752512 | tf_op jit(solution)/shard_map/all_to_all | solution.py:449
  103.3 4.3 %collective-permute-start.16 = (bf16[72,256]{1,0:T(8,128)(2,1)S(1)}, bf16[72,256]{1,0:T(8,128)(2,1)S(1)}, u32[]{:S(2)}, u32[]{:S(2)}) collective-permute-start(bf16[72,256]{1,0:T(8,128)(2,1)S(1)} %get-tuple-element.49), channel_id=1, source_target_pairs={{0,1},{1,0},{2,3},{3,2},{4,5},{5,4},{6,7},{7,6},{8,9},{9,8},{10,11... | collective-permute-start | bytes 110600 | tf_op jit(solution)/shard_map/ppermute | solution.py:490
  104.4 13.8 %collective-permute-start.17 = (bf16[72,256]{1,0:T(8,128)(2,1)S(1)}, bf16[72,256]{1,0:T(8,128)(2,1)S(1)}, u32[]{:S(2)}, u32[]{:S(2)}) collective-permute-start(bf16[72,256]{1,0:T(8,128)(2,1)S(1)} %get-tuple-element.50), channel_id=1, source_target_pairs={{0,2},{1,3},{2,0},{3,1},{4,6},{5,7},{6,4},{7,5},{8,10},{9,11},{10,... | collective-permute-start | bytes 110600 | tf_op jit(solution)/shard_map/ppermute | solution.py:490
  105.7 15.1 %collective-permute-start.18 = (bf16[72,256]{1,0:T(8,128)(2,1)S(1)}, bf16[72,256]{1,0:T(8,128)(2,1)S(1)}, u32[]{:S(2)}, u32[]{:S(2)}) collective-permute-start(bf16[72,256]{1,0:T(8,128)(2,1)S(1)} %get-tuple-element.51), channel_id=1, source_target_pairs={{0,3},{1,2},{2,1},{3,0},{4,7},{5,6},{6,5},{7,4},{8,11},{9,10},{10,... | collective-permute-start | bytes 110600 | tf_op jit(solution)/shard_map/ppermute | solution.py:490
  121.4 9.6 %collective-permute-start.25 = (bf16[136,256]{1,0:T(8,128)(2,1)S(1)}, bf16[136,256]{1,0:T(8,128)(2,1)S(1)}, u32[]{:S(2)}, u32[]{:S(2)}) collective-permute-start(bf16[136,256]{1,0:T(8,128)(2,1)S(1)} %share.1.refs_0_), channel_id=1, source_target_pairs={{0,28},{4,0},{8,4},{12,8},{16,12},{20,16},{24,20},{28,24},{1,29},{... | collective-permute-start | bytes 208904 | tf_op jit(solution)/shard_map/ppermute | solution.py:445
  124.5 9.9 %collective-permute-start.24 = (bf16[136,256]{1,0:T(8,128)(2,1)S(1)}, bf16[136,256]{1,0:T(8,128)(2,1)S(1)}, u32[]{:S(2)}, u32[]{:S(2)}) collective-permute-start(bf16[136,256]{1,0:T(8,128)(2,1)S(1)} %share.1.refs_0_), channel_id=1, source_target_pairs={{0,24},{4,28},{8,0},{12,4},{16,8},{20,12},{24,16},{28,20},{1,25},{... | collective-permute-start | bytes 208904 | tf_op jit(solution)/shard_map/ppermute | solution.py:445
  126.6 8.9 %collective-permute-start.23 = (bf16[136,256]{1,0:T(8,128)(2,1)S(1)}, bf16[136,256]{1,0:T(8,128)(2,1)S(1)}, u32[]{:S(2)}, u32[]{:S(2)}) collective-permute-start(bf16[136,256]{1,0:T(8,128)(2,1)S(1)} %share.1.refs_0_), channel_id=1, source_target_pairs={{0,20},{4,24},{8,28},{12,0},{16,4},{20,8},{24,12},{28,16},{1,21},{... | collective-permute-start | bytes 208904 | tf_op jit(solution)/shard_map/ppermute | solution.py:445
  127.7 9.1 %collective-permute-start.22 = (bf16[136,256]{1,0:T(8,128)(2,1)S(1)}, bf16[136,256]{1,0:T(8,128)(2,1)S(1)}, u32[]{:S(2)}, u32[]{:S(2)}) collective-permute-start(bf16[136,256]{1,0:T(8,128)(2,1)S(1)} %share.1.refs_0_), channel_id=1, source_target_pairs={{0,16},{4,20},{8,24},{12,28},{16,0},{20,4},{24,8},{28,12},{1,17},{... | collective-permute-start | bytes 208904 | tf_op jit(solution)/shard_map/ppermute | solution.py:445
  131.0 10.7 %collective-permute-start.21 = (bf16[136,256]{1,0:T(8,128)(2,1)S(1)}, bf16[136,256]{1,0:T(8,128)(2,1)S(1)}, u32[]{:S(2)}, u32[]{:S(2)}) collective-permute-start(bf16[136,256]{1,0:T(8,128)(2,1)S(1)} %share.1.refs_0_), channel_id=1, source_target_pairs={{0,12},{4,16},{8,20},{12,24},{16,28},{20,0},{24,4},{28,8},{1,13},{... | collective-permute-start | bytes 208904 | tf_op jit(solution)/shard_map/ppermute | solution.py:445
  131.0 13.3 %collective-permute-start.20 = (bf16[136,256]{1,0:T(8,128)(2,1)S(1)}, bf16[136,256]{1,0:T(8,128)(2,1)S(1)}, u32[]{:S(2)}, u32[]{:S(2)}) collective-permute-start(bf16[136,256]{1,0:T(8,128)(2,1)S(1)} %share.1.refs_0_), channel_id=1, source_target_pairs={{0,8},{4,12},{8,16},{12,20},{16,24},{20,28},{24,0},{28,4},{1,9},{5... | collective-permute-start | bytes 208904 | tf_op jit(solution)/shard_map/ppermute | solution.py:445
  134.3 10.1 %collective-permute-start.19 = (bf16[136,256]{1,0:T(8,128)(2,1)S(1)}, bf16[136,256]{1,0:T(8,128)(2,1)S(1)}, u32[]{:S(2)}, u32[]{:S(2)}) collective-permute-start(bf16[136,256]{1,0:T(8,128)(2,1)S(1)} %share.1.refs_0_), channel_id=1, source_target_pairs={{0,4},{4,8},{8,12},{12,16},{16,20},{20,24},{24,28},{28,0},{1,5},{5... | collective-permute-start | bytes 208904 | tf_op jit(solution)/shard_map/ppermute | solution.py:445
  (6 other events, 16.1 us)

commit v5 on v4

--- a/solution.py
+++ b/solution.py
@@ -68,7 +68,7 @@
 
 def make_unit(blocks):
     rows = blocks[0].shape[0]
-    tile = 256
+    tile = 128
     return pl.pallas_call(
         unit_kernel,
         grid=(rows // tile,),
@@ -392,41 +392,53 @@
     )(scalars, *parts)
 
 
-def final_kernel(s, count, tables, *refs):
-    regions, (region_out, table_out, loss_out, sems) = refs[:8], refs[8:]
-    copies = []
+def table_final_kernel(s, tables, out, token):
     for y in range(4):
         at = pl.multiple_of(672 * (s[E] ^ y), 32)
         for x in range(2):
-            to = table_out.at[pl.ds(at, 672), pl.ds(128 * x, 128)]
-            copies.append(pltpu.make_async_copy(tables.at[2 * y + x], to, sems.at[2 * y + x]))
-            copies[-1].start()
+            out[pl.ds(at, 672), 128 * x : 128 * x + 128] = tables[2 * y + x]
+    token[0, 0] = s[E]
+
+
+def make_table_final(scalars, tables):
+    return pl.pallas_call(
+        table_final_kernel,
+        in_specs=[smem()] + vmem(1),
+        out_specs=vmem(1) + [smem()],
+        out_shape=[
+            jax.ShapeDtypeStruct((2688, 256), BF16),
+            jax.ShapeDtypeStruct((1, 1), jnp.int32),
+        ],
+        compiler_params=params(),
+        cost_estimate=cost(1e7),
+        name="table_final",
+    )(scalars, tables)
+
+
+def region_final_kernel(s, token, count, *refs):
+    regions, (out, loss_out) = refs[:8], refs[8:]
     total = 0.0
     for d in range(8):
         source = (s[Z] + 8 - d) % 8
         for k in range(2):
-            region_out[k, source] = regions[d][64 * k : 64 * k + 64, :]
+            out[k, source] = regions[d][64 * k : 64 * k + 64, :]
         total += jnp.sum(regions[d][128:136, :].astype(F32))
     loss_out[0, 0] = total / count[0, 0] / CLASSES
-    for copy in copies:
-        copy.wait()
-
-
-def make_final(scalars, count, tables, regions):
-    return pl.pallas_call(
-        final_kernel,
-        in_specs=[smem(), smem()] + vmem(9),
-        out_specs=vmem(1) + [pl.BlockSpec(memory_space=pltpu.HBM), smem()],
-        scratch_shapes=[pltpu.SemaphoreType.DMA((8,))],
+
+
+def make_region_final(scalars, token, count, regions):
+    return pl.pallas_call(
+        region_final_kernel,
+        in_specs=[smem()] * 3 + vmem(8),
+        out_specs=vmem(1) + [smem()],
         out_shape=[
             jax.ShapeDtypeStruct((2, 8, 64, 256), BF16),
-            jax.ShapeDtypeStruct((2688, 256), BF16),
             jax.ShapeDtypeStruct((1, 1), F32),
         ],
         compiler_params=params(),
         cost_estimate=cost(1e7),
-        name="final",
-    )(scalars, count, tables, *regions)
+        name="region_final",
+    )(scalars, token, count, *regions)
 
 
 def over_img(x, dy, dx):
@@ -494,7 +506,8 @@
     shares = [share] * 8
     for d in ALONG_CLS:
         shares[d] = along_cls(share, d)
-    region_grad, table_grad, total = make_final(scalars, count, table_all, shares)
+    table_grad, token = make_table_final(scalars, table_all)
+    region_grad, total = make_region_final(scalars, token, count, shares)
     return (total[0, 0], region_grad.reshape(rows, 256), table_grad)
 
 

time: 150 us -> 151 us (level)
  Pallas kernels: 24 us -> 27 us
  waiting for transfers between devices: 44.5 us -> 42.7 us
    ppermute x7, waiting for transfers between devices: 8.93 us -> 7.07 us  [along_cls(): return lax.ppermute(x, CLS, [(i, (i + d) % 8) for i in range(8)])]
    pallas_call x1, Pallas kernels: 3.09 us -> 4.82 us  [make_unit(): pl.pallas_call(unit_kernel, grid=(rows // tile,), in_specs=[pl.BlockSpec(...]
    pallas_call x1 -> x2, Pallas kernels: 3.22 us -> 4.49 us  [the longest x1 2.62 us: make_region_final(): pl.pallas_call(region_final_kernel, in_specs=[smem()] * 3 + vmem(8), out_...]
  transfers between devices with their start and end apart: 29 -> 29, of which waited for: 12 -> 11; matrix products, arithmetic and copies ran while one was open for 2% -> 2% of each run, Pallas kernels for 5% -> 8%
where the time goes in v5:
time: 151 us; the launch traced here: 149 us
  starting transfers between devices  71.3 us (47%)
  waiting for transfers between devices  42.7 us (28%)
  Pallas kernels  27 us (18%)
  local copies, waits for them, and re-layouts  5.53 us (4%)
    all_to_all x3, starting transfers between devices, exchange(): return lax.all_to_all(x, axes, split_axis=0, concat_axis=0, tiled=True)  28.9 us
    ppermute x7, starting transfers between devices, along_cls(): return lax.ppermute(x, CLS, [(i, (i + d) % 8) for i in range(8)])  14 us
    ppermute x8, starting transfers between devices, swap(): return lax.ppermute(x, axis, [(0, 1), (1, 0)])  13.5 us
    ppermute x3, waiting for transfers between devices, shards(): parts[q] = lax.ppermute(parts[q], EMB, [(i, i ^ q) for i in range(4)])  13.1 us
    ppermute x7, waiting for transfers between devices, over_img(): return lax.ppermute(x, IMG, pairs)  10.4 us
    ppermute x7, starting transfers between devices, over_img(): return lax.ppermute(x, IMG, pairs)  9.8 us
    pallas_call x1, Pallas kernels, make_focal(): pl.pallas_call(focal_kernel, grid_spec=pltpu.PrefetchScalarGridSpec(num_s...  7.08 us
    ppermute x7, waiting for transfers between devices, along_cls(): return lax.ppermute(x, CLS, [(i, (i + d) % 8) for i in range(8)])  7.07 us
  transfers between devices with their start and end apart: 29, of which 11 were waited for; matrix products, arithmetic and copies ran while one was open for 2% of the time, Pallas kernels for 8%

profile of v5, /device:TPU:1, one launch (start us, length us, event | category | flops | bytes accessed | tf_op | source)
XLA Modules:
  0.0 149.0 jit_solution(7940930224785623359)
XLA Ops:
  1.6 3.6 %collective-permute-start.1 = (bf16[336,256]{1,0:T(8,128)(2,1)S(1)}, bf16[336,256]{1,0:T(8,128)(2,1)S(1)}, u32[]{:S(2)}, u32[]{:S(2)}) collective-permute-start(bf16[336,256]{1,0:T(8,128)(2,1)S(1)} %rows.1), channel_id=1, source_target_pairs={{0,2},{2,0},{1,3},{3,1},{4,6},{6,4},{5,7},{7,5},{8,10},{10,8},{9,1... | collective-permute-start | bytes 516104 | tf_op jit(solution)/shard_map/ppermute | solution.py:46
  6.9 2.2 %collective-permute-done.2.theirs = f32[8,128]{1,0:T(8,128)S(1)} collective-permute-done((f32[8,128]{1,0:T(8,128)S(1)}, f32[8,128]{1,0:T(8,128)S(1)}, u32[]{:S(2)}, u32[]{:S(2)}) %collective-permute-start.2) | collective-permute-done | bytes 4128 | tf_op jit(solution)/shard_map/ppermute | solution.py:46
  10.1 4.5 %all-to-all-start = ((bf16[4,344,256]{2,1,0:T(8,128)(2,1)}), bf16[4,344,256]{2,1,0:T(8,128)(2,1)S(1)}, u32[]{:S(2)}, u32[]{:S(2)}) async-start(bf16[4,344,256]{2,1,0:T(8,128)(2,1)} %message.1), calls=%async_computation | async-start | bytes 1409024 | tf_op jit(solution)/shard_map/all_to_all | solution.py:461
  14.5 2.6 %collective-permute-start.5 = (bf16[1024,256]{1,0:T(8,128)(2,1)}, bf16[1024,256]{1,0:T(8,128)(2,1)}, u32[]{:S(2)}, u32[]{:S(2)}) collective-permute-start(bf16[1024,256]{1,0:T(8,128)(2,1)} %a.1), channel_id=1, source_target_pairs={{0,2},{2,0},{1,3},{3,1},{4,6},{6,4},{5,7},{7,5},{8,10},{10,8},{9,1... | collective-permute-start | bytes 1572872 | tf_op jit(solution)/shard_map/ppermute | solution.py:46
  17.1 7.1 %all-to-all-done.t2 = bf16[4,344,256]{2,1,0:T(8,128)(2,1)S(1)} async-done(((bf16[4,344,256]{2,1,0:T(8,128)(2,1)}), bf16[4,344,256]{2,1,0:T(8,128)(2,1)S(1)}, u32[]{:S(2)}, u32[]{:S(2)}) %all-to-all-start) | async-done | bytes 704544 | tf_op jit(solution)/shard_map/all_to_all | solution.py:461
  24.2 2.7 %collective-permute-start.3 = (bf16[4,344,256]{2,1,0:T(8,128)(2,1)S(1)}, bf16[4,344,256]{2,1,0:T(8,128)(2,1)S(1)}, u32[]{:S(2)}, u32[]{:S(2)}) collective-permute-start(bf16[4,344,256]{2,1,0:T(8,128)(2,1)S(1)} %all-to-all-done.t2), channel_id=1, source_target_pairs={{0,1},{1,0},{2,3},{3,2},{4,5},{5,4},{6,7},{7,6},{8,9},{9,8},{10,11... | collective-permute-start | bytes 2113544 | tf_op jit(solution)/shard_map/ppermute | solution.py:46
  27.9 2.8 %collective-permute-start.6 = (bf16[1024,256]{1,0:T(8,128)(2,1)}, bf16[1024,256]{1,0:T(8,128)(2,1)}, u32[]{:S(2)}, u32[]{:S(2)}) collective-permute-start(bf16[1024,256]{1,0:T(8,128)(2,1)} %collective-permute-done.5.c), channel_id=1, source_target_pairs={{0,1},{1,0},{2,3},{3,2},{4,5},{5,4},{6,7},{7,6},{8,9},{9,8},{10,11... | collective-permute-start | bytes 1572872 | tf_op jit(solution)/shard_map/ppermute | solution.py:46
  32.6 4.8 %unit.1 = (bf16[1024,1024]{1,0:T(8,128)(2,1)S(1)}, bf16[1024,1024]{1,0:T(8,128)(2,1)S(1)}, f32[1024,128]{1,0:T(8,128)S(1)}) custom-call(bf16[1024,256]{1,0:T(8,128)(2,1)} %a.1, bf16[1024,256]{1,0:T(8,128)(2,1)} %collective-permute-done.4.b, bf16[1024,256]{1,0:T(8,128)(2,1)} %collective-permute-done.5.c, bf16[1024,256]{1,0:T(8,128)(2,1)} %collective-permute-done.6.d), custom_call_target="tpu_custom_call" | custom-call | flops 20000000 | bytes 1048576 | tf_op jit(solution)/shard_map/unit/pallas_call | solution.py:72
  37.4 7.1 %focal.1 = (bf16[672,512]{1,0:T(8,128)(2,1)S(1)}, bf16[672,512]{1,0:T(8,128)(2,1)S(1)}, f32[8,128]{1,0:T(8,128)S(1)}, f32[1,1]{1,0:T(1,128)}) custom-call(s32[6]{0:T(128)S(1)} %stack.27.s, bf16[1344,256]{1,0:T(8,128)(2,1)S(1)} %constant_dynamic-slice_fusion.t0, bf16[1344,256]{1,0:T(8,128)(2,1)S(1)} %collective-permute-done.t1, ...), custom_call_target="tpu_custom_call" | custom-call | flops 1400000000 | bytes 1048576 | tf_op jit(solution)/shard_map/focal/pallas_call | solution.py:196
  44.5 4.0 %region.1 = bf16[8,64,1024]{2,1,0:T(8,128)(2,1)} custom-call(s32[6]{0:T(128)S(1)} %stack.27.s, bf16[672,512]{1,0:T(8,128)(2,1)S(1)} %get-tuple-element.33.keep, bf16[672,512]{1,0:T(8,128)(2,1)S(1)} %get-tuple-element.34.send, bf16[1344,256]{1,0:T(8,128)(2,1)S(1)} %constant_dynamic-slice_fusion.t0, bf16[1344,256]{1,0:T(8,128)(2,1)S(1)} %collective-permute-done.t1, ...), custom_call_target="tpu_custom_call" | custom-call | flops 1400000000 | bytes 1048576 | tf_op jit(solution)/shard_map/region/pallas_call | solution.py:268
  50.3 8.2 %all-to-all-start.2 = ((bf16[8,64,1024]{2,1,0:T(8,128)(2,1)}), bf16[8,64,1024]{2,1,0:T(8,128)(2,1)S(1)}, u32[]{:S(2)}, u32[]{:S(2)}) async-start(bf16[8,64,1024]{2,1,0:T(8,128)(2,1)} %region.1), calls=%async_computation.2 | async-start | bytes 2097152 | tf_op jit(solution)/shard_map/all_to_all | solution.py:461
  59.1 2.0 %collective-permute-done.7.other = bf16[672,512]{1,0:T(8,128)(2,1)S(1)} collective-permute-done((bf16[672,512]{1,0:T(8,128)(2,1)}, bf16[672,512]{1,0:T(8,128)(2,1)S(1)}, u32[]{:S(2)}, u32[]{:S(2)}) %collective-permute-start.7) | collective-permute-done | bytes 688160 | tf_op jit(solution)/shard_map/ppermute | solution.py:46
  61.1 1.6 %copy-done.1 = bf16[1024,1024]{1,0:T(8,128)(2,1)S(1)} copy-done((bf16[1024,1024]{1,0:T(8,128)(2,1)S(1)}, bf16[1024,1024]{1,0:T(8,128)(2,1)}, u32[]{:S(2)}) %copy-start.1) | copy-done | bytes 2097176
  63.8 2.4 %table.1 = (bf16[680,128]{1,0:T(8,128)(2,1)S(1)}, bf16[680,128]{1,0:T(8,128)(2,1)S(1)}, bf16[680,128]{1,0:T(8,128)(2,1)S(1)}, bf16[680,128]{1,0:T(8,128)(2,1)S(1...) custom-call(s32[6]{0:T(128)S(1)} %stack.27.s, ...), custom_call_target="tpu_custom_call" | custom-call | flops 1400000000 | bytes 1048576 | tf_op jit(solution)/shard_map/table/pallas_call | solution.py:302
  67.4 1.5 collective-permute-start.9
  70.1 1.3 collective-permute-start.11
  71.4 2.6 %collective-permute-start.12 = (bf16[680,128]{1,0:T(8,128)(2,1)S(1)}, bf16[680,128]{1,0:T(8,128)(2,1)S(1)}, u32[]{:S(2)}, u32[]{:S(2)}) collective-permute-start(bf16[680,128]{1,0:T(8,128)(2,1)S(1)} %get-tuple-element.41), channel_id=1, source_target_pairs={{0,160},{32,128},{64,224},{96,192},{128,32},{160,0},{192,96},{224,... | collective-permute-start | bytes 522248 | tf_op jit(solution)/shard_map/ppermute | solution.py:448
  73.9 1.5 %collective-permute-start.13 = (bf16[680,128]{1,0:T(8,128)(2,1)S(1)}, bf16[680,128]{1,0:T(8,128)(2,1)S(1)}, u32[]{:S(2)}, u32[]{:S(2)}) collective-permute-start(bf16[680,128]{1,0:T(8,128)(2,1)S(1)} %get-tuple-element.42), channel_id=1, source_target_pairs={{0,192},{32,224},{64,0},{96,32},{128,64},{160,96},{192,128},{224,1... | collective-permute-start | bytes 522248 | tf_op jit(solution)/shard_map/ppermute | solution.py:448
  76.0 2.1 %collective-permute-done.10.refs_3_ = bf16[680,128]{1,0:T(8,128)(2,1)S(1)} collective-permute-done((bf16[680,128]{1,0:T(8,128)(2,1)S(1)}, bf16[680,128]{1,0:T(8,128)(2,1)S(1)}, u32[]{:S(2)}, u32[]{:S(2)}) %collective-permute-start.10) | collective-permute-done | bytes 174112 | tf_op jit(solution)/shard_map/ppermute | solution.py:448
  78.1 8.3 %collective-permute-done.11.refs_4_ = bf16[680,128]{1,0:T(8,128)(2,1)S(1)} collective-permute-done((bf16[680,128]{1,0:T(8,128)(2,1)S(1)}, bf16[680,128]{1,0:T(8,128)(2,1)S(1)}, u32[]{:S(2)}, u32[]{:S(2)}) %collective-permute-start.11) | collective-permute-done | bytes 174112 | tf_op jit(solution)/shard_map/ppermute | solution.py:448
  88.5 16.3 %all-to-all-start.1 = ((bf16[8,672,128]{2,1,0:T(8,128)(2,1)}), bf16[8,672,128]{2,1,0:T(8,128)(2,1)S(1)}, u32[]{:S(2)}, u32[]{:S(2)}) async-start(bf16[8,672,128]{2,1,0:T(8,128)(2,1)} %gather.1), calls=%async_computation.1 | async-start | bytes 2752512 | tf_op jit(solution)/shard_map/all_to_all | solution.py:461
  107.4 2.0 %collective-permute-start.18 = (bf16[72,256]{1,0:T(8,128)(2,1)S(1)}, bf16[72,256]{1,0:T(8,128)(2,1)S(1)}, u32[]{:S(2)}, u32[]{:S(2)}) collective-permute-start(bf16[72,256]{1,0:T(8,128)(2,1)S(1)} %get-tuple-element.53), channel_id=1, source_target_pairs={{0,3},{1,2},{2,1},{3,0},{4,7},{5,6},{6,5},{7,4},{8,11},{9,10},{10,... | collective-permute-start | bytes 110600 | tf_op jit(solution)/shard_map/ppermute | solution.py:502
  109.4 10.6 %collective-permute-done.17.far = bf16[72,256]{1,0:T(8,128)(2,1)S(1)} collective-permute-done((bf16[72,256]{1,0:T(8,128)(2,1)S(1)}, bf16[72,256]{1,0:T(8,128)(2,1)S(1)}, u32[]{:S(2)}, u32[]{:S(2)}) %collective-permute-start.17) | collective-permute-done | bytes 36896 | tf_op jit(solution)/shard_map/ppermute | solution.py:502
  119.9 2.5 %collective-permute-done.18.both = bf16[72,256]{1,0:T(8,128)(2,1)S(1)} collective-permute-done((bf16[72,256]{1,0:T(8,128)(2,1)S(1)}, bf16[72,256]{1,0:T(8,128)(2,1)S(1)}, u32[]{:S(2)}, u32[]{:S(2)}) %collective-permute-start.18) | collective-permute-done | bytes 36896 | tf_op jit(solution)/shard_map/ppermute | solution.py:502
  123.2 3.0 %collective-permute-start.25 = (bf16[136,256]{1,0:T(8,128)(2,1)S(1)}, bf16[136,256]{1,0:T(8,128)(2,1)S(1)}, u32[]{:S(2)}, u32[]{:S(2)}) collective-permute-start(bf16[136,256]{1,0:T(8,128)(2,1)S(1)} %share.1.refs_0_), channel_id=1, source_target_pairs={{0,28},{4,0},{8,4},{12,8},{16,12},{20,16},{24,20},{28,24},{1,29},{... | collective-permute-start | bytes 208904 | tf_op jit(solution)/shard_map/ppermute | solution.py:457
  126.2 2.1 %collective-permute-start.24 = (bf16[136,256]{1,0:T(8,128)(2,1)S(1)}, bf16[136,256]{1,0:T(8,128)(2,1)S(1)}, u32[]{:S(2)}, u32[]{:S(2)}) collective-permute-start(bf16[136,256]{1,0:T(8,128)(2,1)S(1)} %share.1.refs_0_), channel_id=1, source_target_pairs={{0,24},{4,28},{8,0},{12,4},{16,8},{20,12},{24,16},{28,20},{1,25},{... | collective-permute-start | bytes 208904 | tf_op jit(solution)/shard_map/ppermute | solution.py:457
  129.4 3.3 %collective-permute-start.22 = (bf16[136,256]{1,0:T(8,128)(2,1)S(1)}, bf16[136,256]{1,0:T(8,128)(2,1)S(1)}, u32[]{:S(2)}, u32[]{:S(2)}) collective-permute-start(bf16[136,256]{1,0:T(8,128)(2,1)S(1)} %share.1.refs_0_), channel_id=1, source_target_pairs={{0,16},{4,20},{8,24},{12,28},{16,0},{20,4},{24,8},{28,12},{1,17},{... | collective-permute-start | bytes 208904 | tf_op jit(solution)/shard_map/ppermute | solution.py:457
  132.8 3.3 %collective-permute-start.20 = (bf16[136,256]{1,0:T(8,128)(2,1)S(1)}, bf16[136,256]{1,0:T(8,128)(2,1)S(1)}, u32[]{:S(2)}, u32[]{:S(2)}) collective-permute-start(bf16[136,256]{1,0:T(8,128)(2,1)S(1)} %share.1.refs_0_), channel_id=1, source_target_pairs={{0,8},{4,12},{8,16},{12,20},{16,24},{20,28},{24,0},{28,4},{1,9},{5... | collective-permute-start | bytes 208904 | tf_op jit(solution)/shard_map/ppermute | solution.py:457
  137.2 1.9 %table_final.1 = (bf16[2688,256]{1,0:T(8,128)(2,1)}, s32[1,1]{1,0:T(1,128)}) custom-call(s32[6]{0:T(128)S(1)} %stack.27.s, bf16[8,672,128]{2,1,0:T(8,128)(2,1)S(1)} %all-to-all-done.1.tables), custom_call_target="tpu_custom_call" | custom-call | flops 10000000 | bytes 1048576 | tf_op jit(solution)/shard_map/table_final/pallas_call | solution.py:404
  139.1 4.3 %collective-permute-done.21.refs_3_ = bf16[136,256]{1,0:T(8,128)(2,1)S(1)} collective-permute-done((bf16[136,256]{1,0:T(8,128)(2,1)S(1)}, bf16[136,256]{1,0:T(8,128)(2,1)S(1)}, u32[]{:S(2)}, u32[]{:S(2)}) %collective-permute-start.21) | collective-permute-done | bytes 69664 | tf_op jit(solution)/shard_map/ppermute | solution.py:457
  143.4 2.7 %collective-permute-done.20.refs_2_ = bf16[136,256]{1,0:T(8,128)(2,1)S(1)} collective-permute-done((bf16[136,256]{1,0:T(8,128)(2,1)S(1)}, bf16[136,256]{1,0:T(8,128)(2,1)S(1)}, u32[]{:S(2)}, u32[]{:S(2)}) %collective-permute-start.20) | collective-permute-done | bytes 69664 | tf_op jit(solution)/shard_map/ppermute | solution.py:457
  146.2 2.6 %region_final.1 = (bf16[2,8,64,256]{3,2,1,0:T(8,128)(2,1)}, f32[1,1]{1,0:T(1,128)}) custom-call(s32[6]{0:T(128)S(1)} %stack.27.s, s32[1,1]{1,0:T(1,128)} %get-tuple-element.45.token, f32[1,1]{1,0:T(1,128)} %get-tuple-element.46.count, bf16[136,256]{1,0:T(8,128)(2,1)S(1)} %share.1.refs_0_, bf16[136,256]{1,0:T(8,128)(2,1)S(1)} %collective-permute-done.19.refs_1_, ...), custom_call_target="tpu_custom_call" | custom-call | flops 10000000 | bytes 1048576 | tf_op jit(solution)/shard_map/region_final/pallas_call | solution.py:430
  (65 shorter events, 20.5 us)
Async XLA Ops:
  1.6 25.3 %copy-start.6 = (bf16[2688,256]{1,0:T(8,128)(2,1)S(1)}, bf16[2688,256]{1,0:T(8,128)(2,1)}, u32[]{:S(2)}) copy-start(bf16[2688,256]{1,0:T(8,128)(2,1)} %x.1) | copy-start | bytes 4128772
  1.6 7.6 %collective-permute-start.1 = (bf16[336,256]{1,0:T(8,128)(2,1)S(1)}, bf16[336,256]{1,0:T(8,128)(2,1)S(1)}, u32[]{:S(2)}, u32[]{:S(2)}) collective-permute-start(bf16[336,256]{1,0:T(8,128)(2,1)S(1)} %rows.1), channel_id=1, source_target_pairs={{0,2},{2,0},{1,3},{3,1},{4,6},{6,4},{5,7},{7,5},{8,10},{10,8},{9,1... | collective-permute-start | bytes 516104 | tf_op jit(solution)/shard_map/ppermute | solution.py:46
  6.5 2.6 %collective-permute-start.2 = (f32[8,128]{1,0:T(8,128)S(1)}, f32[8,128]{1,0:T(8,128)S(1)}, u32[]{:S(2)}, u32[]{:S(2)}) collective-permute-start(f32[8,128]{1,0:T(8,128)S(1)} %broadcast_in_dim.15.mine), channel_id=1, source_target_pairs={{0,32},{32,0},{1,33},{33,1},{2,34},{34,2},{3,35},{35,3},{4,36},{36... | collective-permute-start | bytes 12296 | tf_op jit(solution)/shard_map/ppermute | solution.py:46
  10.1 14.1 %all-to-all-start = ((bf16[4,344,256]{2,1,0:T(8,128)(2,1)}), bf16[4,344,256]{2,1,0:T(8,128)(2,1)S(1)}, u32[]{:S(2)}, u32[]{:S(2)}) async-start(bf16[4,344,256]{2,1,0:T(8,128)(2,1)} %message.1), calls=%async_computation | async-start | bytes 1409024 | tf_op jit(solution)/shard_map/all_to_all | solution.py:461
  14.5 17.4 %copy-start.7 = (f32[1024]{0:T(1024)S(1)}, f32[1024]{0:T(1024)}, u32[]{:S(2)}) copy-start(f32[1024]{0:T(1024)} %param.9) | copy-start | bytes 12292
  14.5 17.4 %copy-start.8 = (f32[1024]{0:T(1024)S(1)}, f32[1024]{0:T(1024)}, u32[]{:S(2)}) copy-start(f32[1024]{0:T(1024)} %param.8) | copy-start | bytes 12292
  14.5 13.3 %collective-permute-start.5 = (bf16[1024,256]{1,0:T(8,128)(2,1)}, bf16[1024,256]{1,0:T(8,128)(2,1)}, u32[]{:S(2)}, u32[]{:S(2)}) collective-permute-start(bf16[1024,256]{1,0:T(8,128)(2,1)} %a.1), channel_id=1, source_target_pairs={{0,2},{2,0},{1,3},{3,1},{4,6},{6,4},{5,7},{7,5},{8,10},{10,8},{9,1... | collective-permute-start | bytes 1572872 | tf_op jit(solution)/shard_map/ppermute | solution.py:46
  24.2 13.3 %collective-permute-start.3 = (bf16[4,344,256]{2,1,0:T(8,128)(2,1)S(1)}, bf16[4,344,256]{2,1,0:T(8,128)(2,1)S(1)}, u32[]{:S(2)}, u32[]{:S(2)}) collective-permute-start(bf16[4,344,256]{2,1,0:T(8,128)(2,1)S(1)} %all-to-all-done.t2), channel_id=1, source_target_pairs={{0,1},{1,0},{2,3},{3,2},{4,5},{5,4},{6,7},{7,6},{8,9},{9,8},{10,11... | collective-permute-start | bytes 2113544 | tf_op jit(solution)/shard_map/ppermute | solution.py:46
  27.0 10.5 %collective-permute-start = (bf16[1344,256]{1,0:T(8,128)(2,1)S(1)}, bf16[1344,256]{1,0:T(8,128)(2,1)S(1)}, u32[]{:S(2)}, u32[]{:S(2)}) collective-permute-start(bf16[1344,256]{1,0:T(8,128)(2,1)S(1)} %constant_dynamic-slice_fusion.t0), channel_id=1, source_target_pairs={{0,1},{1,0},{2,3},{3,2},{4,5},{5,4},{6,7},{7,6},{8,9},{9,8},{10,11... | collective-permute-start | bytes 2064392 | tf_op jit(solution)/shard_map/ppermute | solution.py:46
  27.1 5.0 %collective-permute-start.4 = (bf16[1024,256]{1,0:T(8,128)(2,1)}, bf16[1024,256]{1,0:T(8,128)(2,1)}, u32[]{:S(2)}, u32[]{:S(2)}) collective-permute-start(bf16[1024,256]{1,0:T(8,128)(2,1)} %a.1), channel_id=1, source_target_pairs={{0,1},{1,0},{2,3},{3,2},{4,5},{5,4},{6,7},{7,6},{8,9},{9,8},{10,11... | collective-permute-start | bytes 1572872 | tf_op jit(solution)/shard_map/ppermute | solution.py:46
  27.9 4.7 %collective-permute-start.6 = (bf16[1024,256]{1,0:T(8,128)(2,1)}, bf16[1024,256]{1,0:T(8,128)(2,1)}, u32[]{:S(2)}, u32[]{:S(2)}) collective-permute-start(bf16[1024,256]{1,0:T(8,128)(2,1)} %collective-permute-done.5.c), channel_id=1, source_target_pairs={{0,1},{1,0},{2,3},{3,2},{4,5},{5,4},{6,7},{7,6},{8,9},{9,8},{10,11... | collective-permute-start | bytes 1572872 | tf_op jit(solution)/shard_map/ppermute | solution.py:46
  50.3 38.2 %all-to-all-start.2 = ((bf16[8,64,1024]{2,1,0:T(8,128)(2,1)}), bf16[8,64,1024]{2,1,0:T(8,128)(2,1)S(1)}, u32[]{:S(2)}, u32[]{:S(2)}) async-start(bf16[8,64,1024]{2,1,0:T(8,128)(2,1)} %region.1), calls=%async_computation.2 | async-start | bytes 2097152 | tf_op jit(solution)/shard_map/all_to_all | solution.py:461
  58.5 2.6 %collective-permute-start.7 = (bf16[672,512]{1,0:T(8,128)(2,1)}, bf16[672,512]{1,0:T(8,128)(2,1)S(1)}, u32[]{:S(2)}, u32[]{:S(2)}) collective-permute-start(bf16[672,512]{1,0:T(8,128)(2,1)} %copy-done.4), channel_id=1, source_target_pairs={{0,1},{1,0},{2,3},{3,2},{4,5},{5,4},{6,7},{7,6},{8,9},{9,8},{10,11... | collective-permute-start | bytes 2064392 | tf_op jit(solution)/shard_map/ppermute | solution.py:46
  66.2 7.8 %collective-permute-start.8 = (bf16[680,128]{1,0:T(8,128)(2,1)S(1)}, bf16[680,128]{1,0:T(8,128)(2,1)S(1)}, u32[]{:S(2)}, u32[]{:S(2)}) collective-permute-start(bf16[680,128]{1,0:T(8,128)(2,1)S(1)} %get-tuple-element.37), channel_id=1, source_target_pairs={{0,32},{32,0},{64,96},{96,64},{128,160},{160,128},{192,224},{224,1... | collective-permute-start | bytes 522248 | tf_op jit(solution)/shard_map/ppermute | solution.py:448
  67.4 8.0 %collective-permute-start.9 = (bf16[680,128]{1,0:T(8,128)(2,1)S(1)}, bf16[680,128]{1,0:T(8,128)(2,1)S(1)}, u32[]{:S(2)}, u32[]{:S(2)}) collective-permute-start(bf16[680,128]{1,0:T(8,128)(2,1)S(1)} %get-tuple-element.38), channel_id=1, source_target_pairs={{0,64},{32,96},{64,128},{96,160},{128,192},{160,224},{192,0},{224,... | collective-permute-start | bytes 522248 | tf_op jit(solution)/shard_map/ppermute | solution.py:448
  68.9 9.2 %collective-permute-start.10 = (bf16[680,128]{1,0:T(8,128)(2,1)S(1)}, bf16[680,128]{1,0:T(8,128)(2,1)S(1)}, u32[]{:S(2)}, u32[]{:S(2)}) collective-permute-start(bf16[680,128]{1,0:T(8,128)(2,1)S(1)} %get-tuple-element.39), channel_id=1, source_target_pairs={{0,96},{32,64},{64,160},{96,128},{128,224},{160,192},{192,32},{224... | collective-permute-start | bytes 522248 | tf_op jit(solution)/shard_map/ppermute | solution.py:448
  70.1 16.2 %collective-permute-start.11 = (bf16[680,128]{1,0:T(8,128)(2,1)S(1)}, bf16[680,128]{1,0:T(8,128)(2,1)S(1)}, u32[]{:S(2)}, u32[]{:S(2)}) collective-permute-start(bf16[680,128]{1,0:T(8,128)(2,1)S(1)} %get-tuple-element.40), channel_id=1, source_target_pairs={{0,128},{32,160},{64,192},{96,224},{128,0},{160,32},{192,64},{224,... | collective-permute-start | bytes 522248 | tf_op jit(solution)/shard_map/ppermute | solution.py:448
  71.4 15.0 %collective-permute-start.12 = (bf16[680,128]{1,0:T(8,128)(2,1)S(1)}, bf16[680,128]{1,0:T(8,128)(2,1)S(1)}, u32[]{:S(2)}, u32[]{:S(2)}) collective-permute-start(bf16[680,128]{1,0:T(8,128)(2,1)S(1)} %get-tuple-element.41), channel_id=1, source_target_pairs={{0,160},{32,128},{64,224},{96,192},{128,32},{160,0},{192,96},{224,... | collective-permute-start | bytes 522248 | tf_op jit(solution)/shard_map/ppermute | solution.py:448
  73.9 12.4 %collective-permute-start.13 = (bf16[680,128]{1,0:T(8,128)(2,1)S(1)}, bf16[680,128]{1,0:T(8,128)(2,1)S(1)}, u32[]{:S(2)}, u32[]{:S(2)}) collective-permute-start(bf16[680,128]{1,0:T(8,128)(2,1)S(1)} %get-tuple-element.42), channel_id=1, source_target_pairs={{0,192},{32,224},{64,0},{96,32},{128,64},{160,96},{192,128},{224,1... | collective-permute-start | bytes 522248 | tf_op jit(solution)/shard_map/ppermute | solution.py:448
  75.5 10.9 %collective-permute-start.14 = (bf16[680,128]{1,0:T(8,128)(2,1)S(1)}, bf16[680,128]{1,0:T(8,128)(2,1)S(1)}, u32[]{:S(2)}, u32[]{:S(2)}) collective-permute-start(bf16[680,128]{1,0:T(8,128)(2,1)S(1)} %get-tuple-element.43), channel_id=1, source_target_pairs={{0,224},{32,192},{64,32},{96,0},{128,96},{160,64},{192,160},{224,1... | collective-permute-start | bytes 522248 | tf_op jit(solution)/shard_map/ppermute | solution.py:448
  86.6 0.7 collective-permute-start.15
  88.5 48.7 %all-to-all-start.1 = ((bf16[8,672,128]{2,1,0:T(8,128)(2,1)}), bf16[8,672,128]{2,1,0:T(8,128)(2,1)S(1)}, u32[]{:S(2)}, u32[]{:S(2)}) async-start(bf16[8,672,128]{2,1,0:T(8,128)(2,1)} %gather.1), calls=%async_computation.1 | async-start | bytes 2752512 | tf_op jit(solution)/shard_map/all_to_all | solution.py:461
  105.0 4.3 %collective-permute-start.16 = (bf16[72,256]{1,0:T(8,128)(2,1)S(1)}, bf16[72,256]{1,0:T(8,128)(2,1)S(1)}, u32[]{:S(2)}, u32[]{:S(2)}) collective-permute-start(bf16[72,256]{1,0:T(8,128)(2,1)S(1)} %get-tuple-element.51), channel_id=1, source_target_pairs={{0,1},{1,0},{2,3},{3,2},{4,5},{5,4},{6,7},{7,6},{8,9},{9,8},{10,11... | collective-permute-start | bytes 110600 | tf_op jit(solution)/shard_map/ppermute | solution.py:502
  106.1 13.8 %collective-permute-start.17 = (bf16[72,256]{1,0:T(8,128)(2,1)S(1)}, bf16[72,256]{1,0:T(8,128)(2,1)S(1)}, u32[]{:S(2)}, u32[]{:S(2)}) collective-permute-start(bf16[72,256]{1,0:T(8,128)(2,1)S(1)} %get-tuple-element.52), channel_id=1, source_target_pairs={{0,2},{1,3},{2,0},{3,1},{4,6},{5,7},{6,4},{7,5},{8,10},{9,11},{10,... | collective-permute-start | bytes 110600 | tf_op jit(solution)/shard_map/ppermute | solution.py:502
  107.4 15.1 %collective-permute-start.18 = (bf16[72,256]{1,0:T(8,128)(2,1)S(1)}, bf16[72,256]{1,0:T(8,128)(2,1)S(1)}, u32[]{:S(2)}, u32[]{:S(2)}) collective-permute-start(bf16[72,256]{1,0:T(8,128)(2,1)S(1)} %get-tuple-element.53), channel_id=1, source_target_pairs={{0,3},{1,2},{2,1},{3,0},{4,7},{5,6},{6,5},{7,4},{8,11},{9,10},{10,... | collective-permute-start | bytes 110600 | tf_op jit(solution)/shard_map/ppermute | solution.py:502
  123.2 9.6 %collective-permute-start.25 = (bf16[136,256]{1,0:T(8,128)(2,1)S(1)}, bf16[136,256]{1,0:T(8,128)(2,1)S(1)}, u32[]{:S(2)}, u32[]{:S(2)}) collective-permute-start(bf16[136,256]{1,0:T(8,128)(2,1)S(1)} %share.1.refs_0_), channel_id=1, source_target_pairs={{0,28},{4,0},{8,4},{12,8},{16,12},{20,16},{24,20},{28,24},{1,29},{... | collective-permute-start | bytes 208904 | tf_op jit(solution)/shard_map/ppermute | solution.py:457
  126.2 9.8 %collective-permute-start.24 = (bf16[136,256]{1,0:T(8,128)(2,1)S(1)}, bf16[136,256]{1,0:T(8,128)(2,1)S(1)}, u32[]{:S(2)}, u32[]{:S(2)}) collective-permute-start(bf16[136,256]{1,0:T(8,128)(2,1)S(1)} %share.1.refs_0_), channel_id=1, source_target_pairs={{0,24},{4,28},{8,0},{12,4},{16,8},{20,12},{24,16},{28,20},{1,25},{... | collective-permute-start | bytes 208904 | tf_op jit(solution)/shard_map/ppermute | solution.py:457
  128.3 10.8 %collective-permute-start.23 = (bf16[136,256]{1,0:T(8,128)(2,1)S(1)}, bf16[136,256]{1,0:T(8,128)(2,1)S(1)}, u32[]{:S(2)}, u32[]{:S(2)}) collective-permute-start(bf16[136,256]{1,0:T(8,128)(2,1)S(1)} %share.1.refs_0_), channel_id=1, source_target_pairs={{0,20},{4,24},{8,28},{12,0},{16,4},{20,8},{24,12},{28,16},{1,21},{... | collective-permute-start | bytes 208904 | tf_op jit(solution)/shard_map/ppermute | solution.py:457
  129.4 9.7 %collective-permute-start.22 = (bf16[136,256]{1,0:T(8,128)(2,1)S(1)}, bf16[136,256]{1,0:T(8,128)(2,1)S(1)}, u32[]{:S(2)}, u32[]{:S(2)}) collective-permute-start(bf16[136,256]{1,0:T(8,128)(2,1)S(1)} %share.1.refs_0_), channel_id=1, source_target_pairs={{0,16},{4,20},{8,24},{12,28},{16,0},{20,4},{24,8},{28,12},{1,17},{... | collective-permute-start | bytes 208904 | tf_op jit(solution)/shard_map/ppermute | solution.py:457
  132.8 10.7 %collective-permute-start.21 = (bf16[136,256]{1,0:T(8,128)(2,1)S(1)}, bf16[136,256]{1,0:T(8,128)(2,1)S(1)}, u32[]{:S(2)}, u32[]{:S(2)}) collective-permute-start(bf16[136,256]{1,0:T(8,128)(2,1)S(1)} %share.1.refs_0_), channel_id=1, source_target_pairs={{0,12},{4,16},{8,20},{12,24},{16,28},{20,0},{24,4},{28,8},{1,13},{... | collective-permute-start | bytes 208904 | tf_op jit(solution)/shard_map/ppermute | solution.py:457
  132.8 13.4 %collective-permute-start.20 = (bf16[136,256]{1,0:T(8,128)(2,1)S(1)}, bf16[136,256]{1,0:T(8,128)(2,1)S(1)}, u32[]{:S(2)}, u32[]{:S(2)}) collective-permute-start(bf16[136,256]{1,0:T(8,128)(2,1)S(1)} %share.1.refs_0_), channel_id=1, source_target_pairs={{0,8},{4,12},{8,16},{12,20},{16,24},{20,28},{24,0},{28,4},{1,9},{5... | collective-permute-start | bytes 208904 | tf_op jit(solution)/shard_map/ppermute | solution.py:457
  136.0 10.1 %collective-permute-start.19 = (bf16[136,256]{1,0:T(8,128)(2,1)S(1)}, bf16[136,256]{1,0:T(8,128)(2,1)S(1)}, u32[]{:S(2)}, u32[]{:S(2)}) collective-permute-start(bf16[136,256]{1,0:T(8,128)(2,1)S(1)} %share.1.refs_0_), channel_id=1, source_target_pairs={{0,4},{4,8},{8,12},{12,16},{16,20},{20,24},{24,28},{28,0},{1,5},{5... | collective-permute-start | bytes 208904 | tf_op jit(solution)/shard_map/ppermute | solution.py:457
  (6 other events, 16.1 us)

commit v6 on v5

--- a/solution.py
+++ b/solution.py
@@ -68,7 +68,7 @@
 
 def make_unit(blocks):
     rows = blocks[0].shape[0]
-    tile = 128
+    tile = 512
     return pl.pallas_call(
         unit_kernel,
         grid=(rows // tile,),
@@ -376,7 +376,7 @@
     for at, a, b in ((k, own, far), (1 - k, near, both)):
         total = a[0:64, :].astype(F32) + b[0:64, :].astype(F32)
         out[pl.ds(pl.multiple_of(64 * at, 64), 64), :] = total.astype(BF16)
-    loss = sum(jnp.sum(r[64:72, :].astype(F32)) for r in (own, near, far, both))
+    loss = jnp.sum(sum(r[64:72, :].astype(F32) for r in (own, near, far, both)))
     out[128:136, :] = split3(loss, 256).astype(BF16)
 
 
@@ -417,12 +417,11 @@
 
 def region_final_kernel(s, token, count, *refs):
     regions, (out, loss_out) = refs[:8], refs[8:]
-    total = 0.0
+    total = jnp.sum(sum(r[128:136, :].astype(F32) for r in regions))
     for d in range(8):
         source = (s[Z] + 8 - d) % 8
         for k in range(2):
             out[k, source] = regions[d][64 * k : 64 * k + 64, :]
-        total += jnp.sum(regions[d][128:136, :].astype(F32))
     loss_out[0, 0] = total / count[0, 0] / CLASSES
 
 
@@ -511,7 +510,7 @@
     return (total[0, 0], region_grad.reshape(rows, 256), table_grad)
 
 
-OVER_IMG = (3, 6, 5, 2, 7, 4, 1)
+OVER_IMG = (5, 3, 7, 1, 4, 2, 6)
 ALONG_CLS = (4, 3, 5, 2, 6, 1, 7)
 
 

time: 151 us -> 148 us (0.980)
  Pallas kernels: 27 us -> 24.5 us
    pallas_call x1, Pallas kernels: 4.82 us -> 2.29 us  [make_unit(): pl.pallas_call(unit_kernel, grid=(rows // tile,), in_specs=[pl.BlockSpec(...]
  transfers between devices with their start and end apart: 29 -> 29, of which waited for: 11 -> 11; matrix products, arithmetic and copies ran while one was open for 2% -> 2% of each run, Pallas kernels for 8% -> 6%
where the time goes in v6:
time: 148 us; the launch traced here: 146 us
  starting transfers between devices  71.2 us (48%)
  waiting for transfers between devices  42.7 us (29%)
  Pallas kernels  24.5 us (17%)
  local copies, waits for them, and re-layouts  5.53 us (4%)
    all_to_all x3, starting transfers between devices, exchange(): return lax.all_to_all(x, axes, split_axis=0, concat_axis=0, tiled=True)  29 us
    ppermute x7, starting transfers between devices, along_cls(): return lax.ppermute(x, CLS, [(i, (i + d) % 8) for i in range(8)])  14 us
    ppermute x8, starting transfers between devices, swap(): return lax.ppermute(x, axis, [(0, 1), (1, 0)])  13.4 us
    ppermute x3, waiting for transfers between devices, shards(): parts[q] = lax.ppermute(parts[q], EMB, [(i, i ^ q) for i in range(4)])  13.2 us
    ppermute x7, waiting for transfers between devices, over_img(): return lax.ppermute(x, IMG, pairs)  10.3 us
    ppermute x7, starting transfers between devices, over_img(): return lax.ppermute(x, IMG, pairs)  9.81 us
    pallas_call x1, Pallas kernels, make_focal(): pl.pallas_call(focal_kernel, grid_spec=pltpu.PrefetchScalarGridSpec(num_s...  7.08 us
    ppermute x7, waiting for transfers between devices, along_cls(): return lax.ppermute(x, CLS, [(i, (i + d) % 8) for i in range(8)])  7.08 us
  transfers between devices with their start and end apart: 29, of which 11 were waited for; matrix products, arithmetic and copies ran while one was open for 2% of the time, Pallas kernels for 6%

profile of v6, /device:TPU:1, one launch (start us, length us, event | category | flops | bytes accessed | tf_op | source)
XLA Modules:
  0.0 146.5 jit_solution(15891410047175249719)
XLA Ops:
  1.6 3.6 %collective-permute-start.1 = (bf16[336,256]{1,0:T(8,128)(2,1)S(1)}, bf16[336,256]{1,0:T(8,128)(2,1)S(1)}, u32[]{:S(2)}, u32[]{:S(2)}) collective-permute-start(bf16[336,256]{1,0:T(8,128)(2,1)S(1)} %rows.1), channel_id=1, source_target_pairs={{0,2},{2,0},{1,3},{3,1},{4,6},{6,4},{5,7},{7,5},{8,10},{10,8},{9,1... | collective-permute-start | bytes 516104 | tf_op jit(solution)/shard_map/ppermute | solution.py:46
  6.9 2.2 %collective-permute-done.2.theirs = f32[8,128]{1,0:T(8,128)S(1)} collective-permute-done((f32[8,128]{1,0:T(8,128)S(1)}, f32[8,128]{1,0:T(8,128)S(1)}, u32[]{:S(2)}, u32[]{:S(2)}) %collective-permute-start.2) | collective-permute-done | bytes 4128 | tf_op jit(solution)/shard_map/ppermute | solution.py:46
  10.1 4.5 %all-to-all-start = ((bf16[4,344,256]{2,1,0:T(8,128)(2,1)}), bf16[4,344,256]{2,1,0:T(8,128)(2,1)S(1)}, u32[]{:S(2)}, u32[]{:S(2)}) async-start(bf16[4,344,256]{2,1,0:T(8,128)(2,1)} %message.1), calls=%async_computation | async-start | bytes 1409024 | tf_op jit(solution)/shard_map/all_to_all | solution.py:460
  14.5 2.6 %collective-permute-start.5 = (bf16[1024,256]{1,0:T(8,128)(2,1)}, bf16[1024,256]{1,0:T(8,128)(2,1)}, u32[]{:S(2)}, u32[]{:S(2)}) collective-permute-start(bf16[1024,256]{1,0:T(8,128)(2,1)} %a.1), channel_id=1, source_target_pairs={{0,2},{2,0},{1,3},{3,1},{4,6},{6,4},{5,7},{7,5},{8,10},{10,8},{9,1... | collective-permute-start | bytes 1572872 | tf_op jit(solution)/shard_map/ppermute | solution.py:46
  17.1 7.1 %all-to-all-done.t2 = bf16[4,344,256]{2,1,0:T(8,128)(2,1)S(1)} async-done(((bf16[4,344,256]{2,1,0:T(8,128)(2,1)}), bf16[4,344,256]{2,1,0:T(8,128)(2,1)S(1)}, u32[]{:S(2)}, u32[]{:S(2)}) %all-to-all-start) | async-done | bytes 704544 | tf_op jit(solution)/shard_map/all_to_all | solution.py:460
  24.2 2.7 %collective-permute-start.3 = (bf16[4,344,256]{2,1,0:T(8,128)(2,1)S(1)}, bf16[4,344,256]{2,1,0:T(8,128)(2,1)S(1)}, u32[]{:S(2)}, u32[]{:S(2)}) collective-permute-start(bf16[4,344,256]{2,1,0:T(8,128)(2,1)S(1)} %all-to-all-done.t2), channel_id=1, source_target_pairs={{0,1},{1,0},{2,3},{3,2},{4,5},{5,4},{6,7},{7,6},{8,9},{9,8},{10,11... | collective-permute-start | bytes 2113544 | tf_op jit(solution)/shard_map/ppermute | solution.py:46
  27.9 2.8 %collective-permute-start.6 = (bf16[1024,256]{1,0:T(8,128)(2,1)}, bf16[1024,256]{1,0:T(8,128)(2,1)}, u32[]{:S(2)}, u32[]{:S(2)}) collective-permute-start(bf16[1024,256]{1,0:T(8,128)(2,1)} %collective-permute-done.5.c), channel_id=1, source_target_pairs={{0,1},{1,0},{2,3},{3,2},{4,5},{5,4},{6,7},{7,6},{8,9},{9,8},{10,11... | collective-permute-start | bytes 1572872 | tf_op jit(solution)/shard_map/ppermute | solution.py:46
  32.6 2.3 %unit.1 = (bf16[1024,1024]{1,0:T(8,128)(2,1)S(1)}, bf16[1024,1024]{1,0:T(8,128)(2,1)S(1)}, f32[1024,128]{1,0:T(8,128)S(1)}) custom-call(bf16[1024,256]{1,0:T(8,128)(2,1)} %a.1, bf16[1024,256]{1,0:T(8,128)(2,1)} %collective-permute-done.4.b, bf16[1024,256]{1,0:T(8,128)(2,1)} %collective-permute-done.5.c, bf16[1024,256]{1,0:T(8,128)(2,1)} %collective-permute-done.6.d), custom_call_target="tpu_custom_call" | custom-call | flops 20000000 | bytes 1048576 | tf_op jit(solution)/shard_map/unit/pallas_call | solution.py:72
  34.9 7.1 %focal.1 = (bf16[672,512]{1,0:T(8,128)(2,1)S(1)}, bf16[672,512]{1,0:T(8,128)(2,1)S(1)}, f32[8,128]{1,0:T(8,128)S(1)}, f32[1,1]{1,0:T(1,128)}) custom-call(s32[6]{0:T(128)S(1)} %stack.27.s, bf16[1344,256]{1,0:T(8,128)(2,1)S(1)} %constant_dynamic-slice_fusion.t0, bf16[1344,256]{1,0:T(8,128)(2,1)S(1)} %collective-permute-done.t1, ...), custom_call_target="tpu_custom_call" | custom-call | flops 1400000000 | bytes 1048576 | tf_op jit(solution)/shard_map/focal/pallas_call | solution.py:196
  42.0 4.0 %region.1 = bf16[8,64,1024]{2,1,0:T(8,128)(2,1)} custom-call(s32[6]{0:T(128)S(1)} %stack.27.s, bf16[672,512]{1,0:T(8,128)(2,1)S(1)} %get-tuple-element.33.keep, bf16[672,512]{1,0:T(8,128)(2,1)S(1)} %get-tuple-element.34.send, bf16[1344,256]{1,0:T(8,128)(2,1)S(1)} %constant_dynamic-slice_fusion.t0, bf16[1344,256]{1,0:T(8,128)(2,1)S(1)} %collective-permute-done.t1, ...), custom_call_target="tpu_custom_call" | custom-call | flops 1400000000 | bytes 1048576 | tf_op jit(solution)/shard_map/region/pallas_call | solution.py:268
  47.7 8.2 %all-to-all-start.2 = ((bf16[8,64,1024]{2,1,0:T(8,128)(2,1)}), bf16[8,64,1024]{2,1,0:T(8,128)(2,1)S(1)}, u32[]{:S(2)}, u32[]{:S(2)}) async-start(bf16[8,64,1024]{2,1,0:T(8,128)(2,1)} %region.1), calls=%async_computation.2 | async-start | bytes 2097152 | tf_op jit(solution)/shard_map/all_to_all | solution.py:460
  56.6 2.0 %collective-permute-done.7.other = bf16[672,512]{1,0:T(8,128)(2,1)S(1)} collective-permute-done((bf16[672,512]{1,0:T(8,128)(2,1)}, bf16[672,512]{1,0:T(8,128)(2,1)S(1)}, u32[]{:S(2)}, u32[]{:S(2)}) %collective-permute-start.7) | collective-permute-done | bytes 688160 | tf_op jit(solution)/shard_map/ppermute | solution.py:46
  58.6 1.6 %copy-done.1 = bf16[1024,1024]{1,0:T(8,128)(2,1)S(1)} copy-done((bf16[1024,1024]{1,0:T(8,128)(2,1)S(1)}, bf16[1024,1024]{1,0:T(8,128)(2,1)}, u32[]{:S(2)}) %copy-start.1) | copy-done | bytes 2097176
  61.3 2.4 %table.1 = (bf16[680,128]{1,0:T(8,128)(2,1)S(1)}, bf16[680,128]{1,0:T(8,128)(2,1)S(1)}, bf16[680,128]{1,0:T(8,128)(2,1)S(1)}, bf16[680,128]{1,0:T(8,128)(2,1)S(1...) custom-call(s32[6]{0:T(128)S(1)} %stack.27.s, ...), custom_call_target="tpu_custom_call" | custom-call | flops 1400000000 | bytes 1048576 | tf_op jit(solution)/shard_map/table/pallas_call | solution.py:302
  64.9 1.5 %collective-permute-start.9 = (bf16[680,128]{1,0:T(8,128)(2,1)S(1)}, bf16[680,128]{1,0:T(8,128)(2,1)S(1)}, u32[]{:S(2)}, u32[]{:S(2)}) collective-permute-start(bf16[680,128]{1,0:T(8,128)(2,1)S(1)} %get-tuple-element.38), channel_id=1, source_target_pairs={{0,64},{32,96},{64,128},{96,160},{128,192},{160,224},{192,0},{224,... | collective-permute-start | bytes 522248 | tf_op jit(solution)/shard_map/ppermute | solution.py:447
  68.8 2.6 %collective-permute-start.12 = (bf16[680,128]{1,0:T(8,128)(2,1)S(1)}, bf16[680,128]{1,0:T(8,128)(2,1)S(1)}, u32[]{:S(2)}, u32[]{:S(2)}) collective-permute-start(bf16[680,128]{1,0:T(8,128)(2,1)S(1)} %get-tuple-element.41), channel_id=1, source_target_pairs={{0,160},{32,128},{64,224},{96,192},{128,32},{160,0},{192,96},{224,... | collective-permute-start | bytes 522248 | tf_op jit(solution)/shard_map/ppermute | solution.py:447
  71.4 1.5 %collective-permute-start.13 = (bf16[680,128]{1,0:T(8,128)(2,1)S(1)}, bf16[680,128]{1,0:T(8,128)(2,1)S(1)}, u32[]{:S(2)}, u32[]{:S(2)}) collective-permute-start(bf16[680,128]{1,0:T(8,128)(2,1)S(1)} %get-tuple-element.42), channel_id=1, source_target_pairs={{0,192},{32,224},{64,0},{96,32},{128,64},{160,96},{192,128},{224,1... | collective-permute-start | bytes 522248 | tf_op jit(solution)/shard_map/ppermute | solution.py:447
  73.5 2.1 %collective-permute-done.10.refs_3_ = bf16[680,128]{1,0:T(8,128)(2,1)S(1)} collective-permute-done((bf16[680,128]{1,0:T(8,128)(2,1)S(1)}, bf16[680,128]{1,0:T(8,128)(2,1)S(1)}, u32[]{:S(2)}, u32[]{:S(2)}) %collective-permute-start.10) | collective-permute-done | bytes 174112 | tf_op jit(solution)/shard_map/ppermute | solution.py:447
  75.6 8.2 %collective-permute-done.11.refs_4_ = bf16[680,128]{1,0:T(8,128)(2,1)S(1)} collective-permute-done((bf16[680,128]{1,0:T(8,128)(2,1)S(1)}, bf16[680,128]{1,0:T(8,128)(2,1)S(1)}, u32[]{:S(2)}, u32[]{:S(2)}) %collective-permute-start.11) | collective-permute-done | bytes 174112 | tf_op jit(solution)/shard_map/ppermute | solution.py:447
  86.0 16.3 %all-to-all-start.1 = ((bf16[8,672,128]{2,1,0:T(8,128)(2,1)}), bf16[8,672,128]{2,1,0:T(8,128)(2,1)S(1)}, u32[]{:S(2)}, u32[]{:S(2)}) async-start(bf16[8,672,128]{2,1,0:T(8,128)(2,1)} %gather.1), calls=%async_computation.1 | async-start | bytes 2752512 | tf_op jit(solution)/shard_map/all_to_all | solution.py:460
  103.6 1.3 collective-permute-start.17
  104.9 2.0 %collective-permute-start.18 = (bf16[72,256]{1,0:T(8,128)(2,1)S(1)}, bf16[72,256]{1,0:T(8,128)(2,1)S(1)}, u32[]{:S(2)}, u32[]{:S(2)}) collective-permute-start(bf16[72,256]{1,0:T(8,128)(2,1)S(1)} %get-tuple-element.53), channel_id=1, source_target_pairs={{0,3},{1,2},{2,1},{3,0},{4,7},{5,6},{6,5},{7,4},{8,11},{9,10},{10,... | collective-permute-start | bytes 110600 | tf_op jit(solution)/shard_map/ppermute | solution.py:501
  106.8 10.6 %collective-permute-done.17.far = bf16[72,256]{1,0:T(8,128)(2,1)S(1)} collective-permute-done((bf16[72,256]{1,0:T(8,128)(2,1)S(1)}, bf16[72,256]{1,0:T(8,128)(2,1)S(1)}, u32[]{:S(2)}, u32[]{:S(2)}) %collective-permute-start.17) | collective-permute-done | bytes 36896 | tf_op jit(solution)/shard_map/ppermute | solution.py:501
  117.4 2.6 %collective-permute-done.18.both = bf16[72,256]{1,0:T(8,128)(2,1)S(1)} collective-permute-done((bf16[72,256]{1,0:T(8,128)(2,1)S(1)}, bf16[72,256]{1,0:T(8,128)(2,1)S(1)}, u32[]{:S(2)}, u32[]{:S(2)}) %collective-permute-start.18) | collective-permute-done | bytes 36896 | tf_op jit(solution)/shard_map/ppermute | solution.py:501
  120.7 3.0 %collective-permute-start.25 = (bf16[136,256]{1,0:T(8,128)(2,1)S(1)}, bf16[136,256]{1,0:T(8,128)(2,1)S(1)}, u32[]{:S(2)}, u32[]{:S(2)}) collective-permute-start(bf16[136,256]{1,0:T(8,128)(2,1)S(1)} %share.1.refs_0_), channel_id=1, source_target_pairs={{0,28},{4,0},{8,4},{12,8},{16,12},{20,16},{24,20},{28,24},{1,29},{... | collective-permute-start | bytes 208904 | tf_op jit(solution)/shard_map/ppermute | solution.py:456
  123.7 2.1 %collective-permute-start.24 = (bf16[136,256]{1,0:T(8,128)(2,1)S(1)}, bf16[136,256]{1,0:T(8,128)(2,1)S(1)}, u32[]{:S(2)}, u32[]{:S(2)}) collective-permute-start(bf16[136,256]{1,0:T(8,128)(2,1)S(1)} %share.1.refs_0_), channel_id=1, source_target_pairs={{0,24},{4,28},{8,0},{12,4},{16,8},{20,12},{24,16},{28,20},{1,25},{... | collective-permute-start | bytes 208904 | tf_op jit(solution)/shard_map/ppermute | solution.py:456
  127.0 3.3 %collective-permute-start.22 = (bf16[136,256]{1,0:T(8,128)(2,1)S(1)}, bf16[136,256]{1,0:T(8,128)(2,1)S(1)}, u32[]{:S(2)}, u32[]{:S(2)}) collective-permute-start(bf16[136,256]{1,0:T(8,128)(2,1)S(1)} %share.1.refs_0_), channel_id=1, source_target_pairs={{0,16},{4,20},{8,24},{12,28},{16,0},{20,4},{24,8},{28,12},{1,17},{... | collective-permute-start | bytes 208904 | tf_op jit(solution)/shard_map/ppermute | solution.py:456
  130.3 3.3 %collective-permute-start.20 = (bf16[136,256]{1,0:T(8,128)(2,1)S(1)}, bf16[136,256]{1,0:T(8,128)(2,1)S(1)}, u32[]{:S(2)}, u32[]{:S(2)}) collective-permute-start(bf16[136,256]{1,0:T(8,128)(2,1)S(1)} %share.1.refs_0_), channel_id=1, source_target_pairs={{0,8},{4,12},{8,16},{12,20},{16,24},{20,28},{24,0},{28,4},{1,9},{5... | collective-permute-start | bytes 208904 | tf_op jit(solution)/shard_map/ppermute | solution.py:456
  134.7 1.9 %table_final.1 = (bf16[2688,256]{1,0:T(8,128)(2,1)}, s32[1,1]{1,0:T(1,128)}) custom-call(s32[6]{0:T(128)S(1)} %stack.27.s, bf16[8,672,128]{2,1,0:T(8,128)(2,1)S(1)} %all-to-all-done.1.tables), custom_call_target="tpu_custom_call" | custom-call | flops 10000000 | bytes 1048576 | tf_op jit(solution)/shard_map/table_final/pallas_call | solution.py:404
  136.6 4.4 %collective-permute-done.21.refs_3_ = bf16[136,256]{1,0:T(8,128)(2,1)S(1)} collective-permute-done((bf16[136,256]{1,0:T(8,128)(2,1)S(1)}, bf16[136,256]{1,0:T(8,128)(2,1)S(1)}, u32[]{:S(2)}, u32[]{:S(2)}) %collective-permute-start.21) | collective-permute-done | bytes 69664 | tf_op jit(solution)/shard_map/ppermute | solution.py:456
  141.0 2.7 %collective-permute-done.20.refs_2_ = bf16[136,256]{1,0:T(8,128)(2,1)S(1)} collective-permute-done((bf16[136,256]{1,0:T(8,128)(2,1)S(1)}, bf16[136,256]{1,0:T(8,128)(2,1)S(1)}, u32[]{:S(2)}, u32[]{:S(2)}) %collective-permute-start.20) | collective-permute-done | bytes 69664 | tf_op jit(solution)/shard_map/ppermute | solution.py:456
  143.7 2.6 %region_final.1 = (bf16[2,8,64,256]{3,2,1,0:T(8,128)(2,1)}, f32[1,1]{1,0:T(1,128)}) custom-call(s32[6]{0:T(128)S(1)} %stack.27.s, s32[1,1]{1,0:T(1,128)} %get-tuple-element.45.token, f32[1,1]{1,0:T(1,128)} %get-tuple-element.46.count, bf16[136,256]{1,0:T(8,128)(2,1)S(1)} %share.1.refs_0_, bf16[136,256]{1,0:T(8,128)(2,1)S(1)} %collective-permute-done.19.refs_1_, ...), custom_call_target="tpu_custom_call" | custom-call | flops 10000000 | bytes 1048576 | tf_op jit(solution)/shard_map/region_final/pallas_call | solution.py:429
  (65 shorter events, 20.6 us)
Async XLA Ops:
  1.6 25.3 %copy-start.6 = (bf16[2688,256]{1,0:T(8,128)(2,1)S(1)}, bf16[2688,256]{1,0:T(8,128)(2,1)}, u32[]{:S(2)}) copy-start(bf16[2688,256]{1,0:T(8,128)(2,1)} %x.1) | copy-start | bytes 4128772
  1.6 7.6 %collective-permute-start.1 = (bf16[336,256]{1,0:T(8,128)(2,1)S(1)}, bf16[336,256]{1,0:T(8,128)(2,1)S(1)}, u32[]{:S(2)}, u32[]{:S(2)}) collective-permute-start(bf16[336,256]{1,0:T(8,128)(2,1)S(1)} %rows.1), channel_id=1, source_target_pairs={{0,2},{2,0},{1,3},{3,1},{4,6},{6,4},{5,7},{7,5},{8,10},{10,8},{9,1... | collective-permute-start | bytes 516104 | tf_op jit(solution)/shard_map/ppermute | solution.py:46
  6.5 2.6 %collective-permute-start.2 = (f32[8,128]{1,0:T(8,128)S(1)}, f32[8,128]{1,0:T(8,128)S(1)}, u32[]{:S(2)}, u32[]{:S(2)}) collective-permute-start(f32[8,128]{1,0:T(8,128)S(1)} %broadcast_in_dim.15.mine), channel_id=1, source_target_pairs={{0,32},{32,0},{1,33},{33,1},{2,34},{34,2},{3,35},{35,3},{4,36},{36... | collective-permute-start | bytes 12296 | tf_op jit(solution)/shard_map/ppermute | solution.py:46
  10.1 14.1 %all-to-all-start = ((bf16[4,344,256]{2,1,0:T(8,128)(2,1)}), bf16[4,344,256]{2,1,0:T(8,128)(2,1)S(1)}, u32[]{:S(2)}, u32[]{:S(2)}) async-start(bf16[4,344,256]{2,1,0:T(8,128)(2,1)} %message.1), calls=%async_computation | async-start | bytes 1409024 | tf_op jit(solution)/shard_map/all_to_all | solution.py:460
  14.5 17.4 %copy-start.7 = (f32[1024]{0:T(1024)S(1)}, f32[1024]{0:T(1024)}, u32[]{:S(2)}) copy-start(f32[1024]{0:T(1024)} %param.9) | copy-start | bytes 12292
  14.5 17.4 %copy-start.8 = (f32[1024]{0:T(1024)S(1)}, f32[1024]{0:T(1024)}, u32[]{:S(2)}) copy-start(f32[1024]{0:T(1024)} %param.8) | copy-start | bytes 12292
  14.5 13.3 %collective-permute-start.5 = (bf16[1024,256]{1,0:T(8,128)(2,1)}, bf16[1024,256]{1,0:T(8,128)(2,1)}, u32[]{:S(2)}, u32[]{:S(2)}) collective-permute-start(bf16[1024,256]{1,0:T(8,128)(2,1)} %a.1), channel_id=1, source_target_pairs={{0,2},{2,0},{1,3},{3,1},{4,6},{6,4},{5,7},{7,5},{8,10},{10,8},{9,1... | collective-permute-start | bytes 1572872 | tf_op jit(solution)/shard_map/ppermute | solution.py:46
  24.2 10.7 %collective-permute-start.3 = (bf16[4,344,256]{2,1,0:T(8,128)(2,1)S(1)}, bf16[4,344,256]{2,1,0:T(8,128)(2,1)S(1)}, u32[]{:S(2)}, u32[]{:S(2)}) collective-permute-start(bf16[4,344,256]{2,1,0:T(8,128)(2,1)S(1)} %all-to-all-done.t2), channel_id=1, source_target_pairs={{0,1},{1,0},{2,3},{3,2},{4,5},{5,4},{6,7},{7,6},{8,9},{9,8},{10,11... | collective-permute-start | bytes 2113544 | tf_op jit(solution)/shard_map/ppermute | solution.py:46
  27.0 7.9 %collective-permute-start = (bf16[1344,256]{1,0:T(8,128)(2,1)S(1)}, bf16[1344,256]{1,0:T(8,128)(2,1)S(1)}, u32[]{:S(2)}, u32[]{:S(2)}) collective-permute-start(bf16[1344,256]{1,0:T(8,128)(2,1)S(1)} %constant_dynamic-slice_fusion.t0), channel_id=1, source_target_pairs={{0,1},{1,0},{2,3},{3,2},{4,5},{5,4},{6,7},{7,6},{8,9},{9,8},{10,11... | collective-permute-start | bytes 2064392 | tf_op jit(solution)/shard_map/ppermute | solution.py:46
  27.1 5.0 %collective-permute-start.4 = (bf16[1024,256]{1,0:T(8,128)(2,1)}, bf16[1024,256]{1,0:T(8,128)(2,1)}, u32[]{:S(2)}, u32[]{:S(2)}) collective-permute-start(bf16[1024,256]{1,0:T(8,128)(2,1)} %a.1), channel_id=1, source_target_pairs={{0,1},{1,0},{2,3},{3,2},{4,5},{5,4},{6,7},{7,6},{8,9},{9,8},{10,11... | collective-permute-start | bytes 1572872 | tf_op jit(solution)/shard_map/ppermute | solution.py:46
  27.9 4.7 %collective-permute-start.6 = (bf16[1024,256]{1,0:T(8,128)(2,1)}, bf16[1024,256]{1,0:T(8,128)(2,1)}, u32[]{:S(2)}, u32[]{:S(2)}) collective-permute-start(bf16[1024,256]{1,0:T(8,128)(2,1)} %collective-permute-done.5.c), channel_id=1, source_target_pairs={{0,1},{1,0},{2,3},{3,2},{4,5},{5,4},{6,7},{7,6},{8,9},{9,8},{10,11... | collective-permute-start | bytes 1572872 | tf_op jit(solution)/shard_map/ppermute | solution.py:46
  47.7 38.2 %all-to-all-start.2 = ((bf16[8,64,1024]{2,1,0:T(8,128)(2,1)}), bf16[8,64,1024]{2,1,0:T(8,128)(2,1)S(1)}, u32[]{:S(2)}, u32[]{:S(2)}) async-start(bf16[8,64,1024]{2,1,0:T(8,128)(2,1)} %region.1), calls=%async_computation.2 | async-start | bytes 2097152 | tf_op jit(solution)/shard_map/all_to_all | solution.py:460
  55.9 2.6 %collective-permute-start.7 = (bf16[672,512]{1,0:T(8,128)(2,1)}, bf16[672,512]{1,0:T(8,128)(2,1)S(1)}, u32[]{:S(2)}, u32[]{:S(2)}) collective-permute-start(bf16[672,512]{1,0:T(8,128)(2,1)} %copy-done.4), channel_id=1, source_target_pairs={{0,1},{1,0},{2,3},{3,2},{4,5},{5,4},{6,7},{7,6},{8,9},{9,8},{10,11... | collective-permute-start | bytes 2064392 | tf_op jit(solution)/shard_map/ppermute | solution.py:46
  63.7 7.8 %collective-permute-start.8 = (bf16[680,128]{1,0:T(8,128)(2,1)S(1)}, bf16[680,128]{1,0:T(8,128)(2,1)S(1)}, u32[]{:S(2)}, u32[]{:S(2)}) collective-permute-start(bf16[680,128]{1,0:T(8,128)(2,1)S(1)} %get-tuple-element.37), channel_id=1, source_target_pairs={{0,32},{32,0},{64,96},{96,64},{128,160},{160,128},{192,224},{224,1... | collective-permute-start | bytes 522248 | tf_op jit(solution)/shard_map/ppermute | solution.py:447
  64.9 8.0 %collective-permute-start.9 = (bf16[680,128]{1,0:T(8,128)(2,1)S(1)}, bf16[680,128]{1,0:T(8,128)(2,1)S(1)}, u32[]{:S(2)}, u32[]{:S(2)}) collective-permute-start(bf16[680,128]{1,0:T(8,128)(2,1)S(1)} %get-tuple-element.38), channel_id=1, source_target_pairs={{0,64},{32,96},{64,128},{96,160},{128,192},{160,224},{192,0},{224,... | collective-permute-start | bytes 522248 | tf_op jit(solution)/shard_map/ppermute | solution.py:447
  66.4 9.2 %collective-permute-start.10 = (bf16[680,128]{1,0:T(8,128)(2,1)S(1)}, bf16[680,128]{1,0:T(8,128)(2,1)S(1)}, u32[]{:S(2)}, u32[]{:S(2)}) collective-permute-start(bf16[680,128]{1,0:T(8,128)(2,1)S(1)} %get-tuple-element.39), channel_id=1, source_target_pairs={{0,96},{32,64},{64,160},{96,128},{128,224},{160,192},{192,32},{224... | collective-permute-start | bytes 522248 | tf_op jit(solution)/shard_map/ppermute | solution.py:447
  67.6 16.2 %collective-permute-start.11 = (bf16[680,128]{1,0:T(8,128)(2,1)S(1)}, bf16[680,128]{1,0:T(8,128)(2,1)S(1)}, u32[]{:S(2)}, u32[]{:S(2)}) collective-permute-start(bf16[680,128]{1,0:T(8,128)(2,1)S(1)} %get-tuple-element.40), channel_id=1, source_target_pairs={{0,128},{32,160},{64,192},{96,224},{128,0},{160,32},{192,64},{224,... | collective-permute-start | bytes 522248 | tf_op jit(solution)/shard_map/ppermute | solution.py:447
  68.8 15.0 %collective-permute-start.12 = (bf16[680,128]{1,0:T(8,128)(2,1)S(1)}, bf16[680,128]{1,0:T(8,128)(2,1)S(1)}, u32[]{:S(2)}, u32[]{:S(2)}) collective-permute-start(bf16[680,128]{1,0:T(8,128)(2,1)S(1)} %get-tuple-element.41), channel_id=1, source_target_pairs={{0,160},{32,128},{64,224},{96,192},{128,32},{160,0},{192,96},{224,... | collective-permute-start | bytes 522248 | tf_op jit(solution)/shard_map/ppermute | solution.py:447
  71.4 12.4 %collective-permute-start.13 = (bf16[680,128]{1,0:T(8,128)(2,1)S(1)}, bf16[680,128]{1,0:T(8,128)(2,1)S(1)}, u32[]{:S(2)}, u32[]{:S(2)}) collective-permute-start(bf16[680,128]{1,0:T(8,128)(2,1)S(1)} %get-tuple-element.42), channel_id=1, source_target_pairs={{0,192},{32,224},{64,0},{96,32},{128,64},{160,96},{192,128},{224,1... | collective-permute-start | bytes 522248 | tf_op jit(solution)/shard_map/ppermute | solution.py:447
  72.9 10.9 %collective-permute-start.14 = (bf16[680,128]{1,0:T(8,128)(2,1)S(1)}, bf16[680,128]{1,0:T(8,128)(2,1)S(1)}, u32[]{:S(2)}, u32[]{:S(2)}) collective-permute-start(bf16[680,128]{1,0:T(8,128)(2,1)S(1)} %get-tuple-element.43), channel_id=1, source_target_pairs={{0,224},{32,192},{64,32},{96,0},{128,96},{160,64},{192,160},{224,1... | collective-permute-start | bytes 522248 | tf_op jit(solution)/shard_map/ppermute | solution.py:447
  84.0 0.7 collective-permute-start.15
  86.0 48.8 %all-to-all-start.1 = ((bf16[8,672,128]{2,1,0:T(8,128)(2,1)}), bf16[8,672,128]{2,1,0:T(8,128)(2,1)S(1)}, u32[]{:S(2)}, u32[]{:S(2)}) async-start(bf16[8,672,128]{2,1,0:T(8,128)(2,1)} %gather.1), calls=%async_computation.1 | async-start | bytes 2752512 | tf_op jit(solution)/shard_map/all_to_all | solution.py:460
  102.5 4.3 %collective-permute-start.16 = (bf16[72,256]{1,0:T(8,128)(2,1)S(1)}, bf16[72,256]{1,0:T(8,128)(2,1)S(1)}, u32[]{:S(2)}, u32[]{:S(2)}) collective-permute-start(bf16[72,256]{1,0:T(8,128)(2,1)S(1)} %get-tuple-element.51), channel_id=1, source_target_pairs={{0,1},{1,0},{2,3},{3,2},{4,5},{5,4},{6,7},{7,6},{8,9},{9,8},{10,11... | collective-permute-start | bytes 110600 | tf_op jit(solution)/shard_map/ppermute | solution.py:501
  103.6 13.8 %collective-permute-start.17 = (bf16[72,256]{1,0:T(8,128)(2,1)S(1)}, bf16[72,256]{1,0:T(8,128)(2,1)S(1)}, u32[]{:S(2)}, u32[]{:S(2)}) collective-permute-start(bf16[72,256]{1,0:T(8,128)(2,1)S(1)} %get-tuple-element.52), channel_id=1, source_target_pairs={{0,2},{1,3},{2,0},{3,1},{4,6},{5,7},{6,4},{7,5},{8,10},{9,11},{10,... | collective-permute-start | bytes 110600 | tf_op jit(solution)/shard_map/ppermute | solution.py:501
  104.9 15.1 %collective-permute-start.18 = (bf16[72,256]{1,0:T(8,128)(2,1)S(1)}, bf16[72,256]{1,0:T(8,128)(2,1)S(1)}, u32[]{:S(2)}, u32[]{:S(2)}) collective-permute-start(bf16[72,256]{1,0:T(8,128)(2,1)S(1)} %get-tuple-element.53), channel_id=1, source_target_pairs={{0,3},{1,2},{2,1},{3,0},{4,7},{5,6},{6,5},{7,4},{8,11},{9,10},{10,... | collective-permute-start | bytes 110600 | tf_op jit(solution)/shard_map/ppermute | solution.py:501
  120.7 9.6 %collective-permute-start.25 = (bf16[136,256]{1,0:T(8,128)(2,1)S(1)}, bf16[136,256]{1,0:T(8,128)(2,1)S(1)}, u32[]{:S(2)}, u32[]{:S(2)}) collective-permute-start(bf16[136,256]{1,0:T(8,128)(2,1)S(1)} %share.1.refs_0_), channel_id=1, source_target_pairs={{0,28},{4,0},{8,4},{12,8},{16,12},{20,16},{24,20},{28,24},{1,29},{... | collective-permute-start | bytes 208904 | tf_op jit(solution)/shard_map/ppermute | solution.py:456
  123.7 9.8 %collective-permute-start.24 = (bf16[136,256]{1,0:T(8,128)(2,1)S(1)}, bf16[136,256]{1,0:T(8,128)(2,1)S(1)}, u32[]{:S(2)}, u32[]{:S(2)}) collective-permute-start(bf16[136,256]{1,0:T(8,128)(2,1)S(1)} %share.1.refs_0_), channel_id=1, source_target_pairs={{0,24},{4,28},{8,0},{12,4},{16,8},{20,12},{24,16},{28,20},{1,25},{... | collective-permute-start | bytes 208904 | tf_op jit(solution)/shard_map/ppermute | solution.py:456
  125.8 10.8 %collective-permute-start.23 = (bf16[136,256]{1,0:T(8,128)(2,1)S(1)}, bf16[136,256]{1,0:T(8,128)(2,1)S(1)}, u32[]{:S(2)}, u32[]{:S(2)}) collective-permute-start(bf16[136,256]{1,0:T(8,128)(2,1)S(1)} %share.1.refs_0_), channel_id=1, source_target_pairs={{0,20},{4,24},{8,28},{12,0},{16,4},{20,8},{24,12},{28,16},{1,21},{... | collective-permute-start | bytes 208904 | tf_op jit(solution)/shard_map/ppermute | solution.py:456
  127.0 9.6 %collective-permute-start.22 = (bf16[136,256]{1,0:T(8,128)(2,1)S(1)}, bf16[136,256]{1,0:T(8,128)(2,1)S(1)}, u32[]{:S(2)}, u32[]{:S(2)}) collective-permute-start(bf16[136,256]{1,0:T(8,128)(2,1)S(1)} %share.1.refs_0_), channel_id=1, source_target_pairs={{0,16},{4,20},{8,24},{12,28},{16,0},{20,4},{24,8},{28,12},{1,17},{... | collective-permute-start | bytes 208904 | tf_op jit(solution)/shard_map/ppermute | solution.py:456
  130.3 10.7 %collective-permute-start.21 = (bf16[136,256]{1,0:T(8,128)(2,1)S(1)}, bf16[136,256]{1,0:T(8,128)(2,1)S(1)}, u32[]{:S(2)}, u32[]{:S(2)}) collective-permute-start(bf16[136,256]{1,0:T(8,128)(2,1)S(1)} %share.1.refs_0_), channel_id=1, source_target_pairs={{0,12},{4,16},{8,20},{12,24},{16,28},{20,0},{24,4},{28,8},{1,13},{... | collective-permute-start | bytes 208904 | tf_op jit(solution)/shard_map/ppermute | solution.py:456
  130.3 13.4 %collective-permute-start.20 = (bf16[136,256]{1,0:T(8,128)(2,1)S(1)}, bf16[136,256]{1,0:T(8,128)(2,1)S(1)}, u32[]{:S(2)}, u32[]{:S(2)}) collective-permute-start(bf16[136,256]{1,0:T(8,128)(2,1)S(1)} %share.1.refs_0_), channel_id=1, source_target_pairs={{0,8},{4,12},{8,16},{12,20},{16,24},{20,28},{24,0},{28,4},{1,9},{5... | collective-permute-start | bytes 208904 | tf_op jit(solution)/shard_map/ppermute | solution.py:456
  133.6 10.1 %collective-permute-start.19 = (bf16[136,256]{1,0:T(8,128)(2,1)S(1)}, bf16[136,256]{1,0:T(8,128)(2,1)S(1)}, u32[]{:S(2)}, u32[]{:S(2)}) collective-permute-start(bf16[136,256]{1,0:T(8,128)(2,1)S(1)} %share.1.refs_0_), channel_id=1, source_target_pairs={{0,4},{4,8},{8,12},{12,16},{16,20},{20,24},{24,28},{28,0},{1,5},{5... | collective-permute-start | bytes 208904 | tf_op jit(solution)/shard_map/ppermute | solution.py:456
  (6 other events, 16.1 us)

commit v7 on v6

--- a/solution.py
+++ b/solution.py
@@ -89,19 +89,19 @@
     )(*blocks)
 
 
-def rows_kernel(s, x, out):
-    out[...] = x[...]
+def rows_kernel(s, x, out, sem):
+    rows = out.shape[0]
+    copy = pltpu.make_async_copy(x.at[pl.ds(pl.multiple_of(s[0] * rows, 16), rows)], out, sem)
+    copy.start()
+    copy.wait()
 
 
 def take_rows(x, at, rows):
     return pl.pallas_call(
         rows_kernel,
-        grid_spec=pltpu.PrefetchScalarGridSpec(
-            num_scalar_prefetch=1,
-            grid=(1,),
-            in_specs=[pl.BlockSpec((rows, 256), lambda i, s: (s[0], 0))],
-            out_specs=pl.BlockSpec((rows, 256), lambda i, s: (0, 0)),
-        ),
+        in_specs=[smem(), pl.BlockSpec(memory_space=pltpu.HBM)],
+        out_specs=vmem(1)[0],
+        scratch_shapes=[pltpu.SemaphoreType.DMA],
         out_shape=jax.ShapeDtypeStruct((rows, 256), BF16),
         compiler_params=params(),
         name="rows",
@@ -140,7 +140,7 @@
     rows = unit.shape[0]
     half = keep.shape[0]
     count = read_count(t2)
-    count_out[0, 0] = count
+    count_out[...] = jnp.full((1, 1), count, F32)
     u = [unit[:, 256 * q : 256 * q + 256] for q in range(4)]
 
     def dot(t, q):
@@ -210,7 +210,7 @@
                 pl.BlockSpec((classes // 2, rows), whole),
                 pl.BlockSpec((classes // 2, rows), whole),
                 pl.BlockSpec((8, 128), whole),
-                smem(),
+                pl.BlockSpec((1, 1), whole),
             ],
             scratch_shapes=[pltpu.VMEM((classes, rows), F32)],
         ),
@@ -353,18 +353,21 @@
     )(terms, loss)
 
 
-def gather_kernel(chunk, out):
-    rows = chunk[...]
-    for j in range(8):
-        out[j] = rows
+def gather_kernel(chunk, out, sems):
+    copies = [pltpu.make_async_copy(chunk, out.at[j], sems.at[j]) for j in range(8)]
+    for copy in copies:
+        copy.start()
+    for copy in copies:
+        copy.wait()
 
 
 def make_gather(chunk):
     return pl.pallas_call(
         gather_kernel,
         in_specs=vmem(1),
-        out_specs=vmem(1)[0],
+        out_specs=pl.BlockSpec(memory_space=pltpu.HBM),
         out_shape=in_hbm((8,) + chunk.shape, BF16),
+        scratch_shapes=[pltpu.SemaphoreType.DMA((8,))],
         compiler_params=params(),
         cost_estimate=cost(1e7),
         name="gather",
@@ -392,44 +395,40 @@
     )(scalars, *parts)
 
 
-def table_final_kernel(s, tables, out, token):
+def table_final_kernel(s, tables, out):
     for y in range(4):
         at = pl.multiple_of(672 * (s[E] ^ y), 32)
         for x in range(2):
             out[pl.ds(at, 672), 128 * x : 128 * x + 128] = tables[2 * y + x]
-    token[0, 0] = s[E]
 
 
 def make_table_final(scalars, tables):
     return pl.pallas_call(
         table_final_kernel,
         in_specs=[smem()] + vmem(1),
-        out_specs=vmem(1) + [smem()],
-        out_shape=[
-            jax.ShapeDtypeStruct((2688, 256), BF16),
-            jax.ShapeDtypeStruct((1, 1), jnp.int32),
-        ],
+        out_specs=vmem(1)[0],
+        out_shape=jax.ShapeDtypeStruct((2688, 256), BF16),
         compiler_params=params(),
         cost_estimate=cost(1e7),
         name="table_final",
     )(scalars, tables)
 
 
-def region_final_kernel(s, token, count, *refs):
+def region_final_kernel(s, count, *refs):
     regions, (out, loss_out) = refs[:8], refs[8:]
-    total = jnp.sum(sum(r[128:136, :].astype(F32) for r in regions))
+    total = jnp.sum(sum(r[128:136, :].astype(F32) for r in regions), keepdims=True)
     for d in range(8):
         source = (s[Z] + 8 - d) % 8
         for k in range(2):
             out[k, source] = regions[d][64 * k : 64 * k + 64, :]
-    loss_out[0, 0] = total / count[0, 0] / CLASSES
-
-
-def make_region_final(scalars, token, count, regions):
+    loss_out[...] = total / count[...] / CLASSES
+
+
+def make_region_final(scalars, count, regions):
     return pl.pallas_call(
         region_final_kernel,
-        in_specs=[smem()] * 3 + vmem(8),
-        out_specs=vmem(1) + [smem()],
+        in_specs=[smem()] + vmem(9),
+        out_specs=vmem(2),
         out_shape=[
             jax.ShapeDtypeStruct((2, 8, 64, 256), BF16),
             jax.ShapeDtypeStruct((1, 1), F32),
@@ -437,7 +436,7 @@
         compiler_params=params(),
         cost_estimate=cost(1e7),
         name="region_final",
-    )(scalars, token, count, *regions)
+    )(scalars, count, *regions)
 
 
 def over_img(x, dy, dx):
@@ -505,12 +504,12 @@
     shares = [share] * 8
     for d in ALONG_CLS:
         shares[d] = along_cls(share, d)
-    table_grad, token = make_table_final(scalars, table_all)
-    region_grad, total = make_region_final(scalars, token, count, shares)
+    table_grad = make_table_final(scalars, table_all)
+    region_grad, total = make_region_final(scalars, count, shares)
     return (total[0, 0], region_grad.reshape(rows, 256), table_grad)
 
 
-OVER_IMG = (5, 3, 7, 1, 4, 2, 6)
+OVER_IMG = (3, 6, 5, 2, 7, 4, 1)
 ALONG_CLS = (4, 3, 5, 2, 6, 1, 7)
 
 

time: 148 us -> 149 us (level)
  waiting for transfers between devices: 42.7 us -> 44.5 us
    ppermute x7, waiting for transfers between devices: 7.08 us -> 8.92 us  [along_cls(): return lax.ppermute(x, CLS, [(i, (i + d) % 8) for i in range(8)])]
  transfers between devices with their start and end apart: 29 -> 29, of which waited for: 11 -> 12; matrix products, arithmetic and copies ran while one was open for 2% -> 2% of each run, Pallas kernels for 6% -> 6%
where the time goes in v7:
time: 149 us; the launch traced here: 148 us
  starting transfers between devices  71.2 us (48%)
  waiting for transfers between devices  44.5 us (30%)
  Pallas kernels  23.9 us (16%)
  local copies, waits for them, and re-layouts  5.53 us (4%)
    all_to_all x3, starting transfers between devices, exchange(): return lax.all_to_all(x, axes, split_axis=0, concat_axis=0, tiled=True)  29 us
    ppermute x7, starting transfers between devices, along_cls(): return lax.ppermute(x, CLS, [(i, (i + d) % 8) for i in range(8)])  14 us
    ppermute x8, starting transfers between devices, swap(): return lax.ppermute(x, axis, [(0, 1), (1, 0)])  13.5 us
    ppermute x3, waiting for transfers between devices, shards(): parts[q] = lax.ppermute(parts[q], EMB, [(i, i ^ q) for i in range(4)])  13.1 us
    ppermute x7, waiting for transfers between devices, over_img(): return lax.ppermute(x, IMG, pairs)  10.4 us
    ppermute x7, starting transfers between devices, over_img(): return lax.ppermute(x, IMG, pairs)  9.81 us
    ppermute x7, waiting for transfers between devices, along_cls(): return lax.ppermute(x, CLS, [(i, (i + d) % 8) for i in range(8)])  8.92 us
    pallas_call x1, Pallas kernels, make_focal(): pl.pallas_call(focal_kernel, grid_spec=pltpu.PrefetchScalarGridSpec(num_s...  7.17 us
  transfers between devices with their start and end apart: 29, of which 12 were waited for; matrix products, arithmetic and copies ran while one was open for 2% of the time, Pallas kernels for 6%

profile of v7, /device:TPU:1, one launch (start us, length us, event | category | flops | bytes accessed | tf_op | source)
XLA Modules:
  0.0 147.5 jit_solution(3310027901558289577)
XLA Ops:
  1.6 3.6 %collective-permute-start.1 = (bf16[336,256]{1,0:T(8,128)(2,1)S(1)}, bf16[336,256]{1,0:T(8,128)(2,1)S(1)}, u32[]{:S(2)}, u32[]{:S(2)}) collective-permute-start(bf16[336,256]{1,0:T(8,128)(2,1)S(1)} %rows.1), channel_id=1, source_target_pairs={{0,2},{2,0},{1,3},{3,1},{4,6},{6,4},{5,7},{7,5},{8,10},{10,8},{9,1... | collective-permute-start | bytes 516104 | tf_op jit(solution)/shard_map/ppermute | solution.py:46
  6.9 2.2 %collective-permute-done.2.theirs = f32[8,128]{1,0:T(8,128)S(1)} collective-permute-done((f32[8,128]{1,0:T(8,128)S(1)}, f32[8,128]{1,0:T(8,128)S(1)}, u32[]{:S(2)}, u32[]{:S(2)}) %collective-permute-start.2) | collective-permute-done | bytes 4128 | tf_op jit(solution)/shard_map/ppermute | solution.py:46
  10.1 4.5 %all-to-all-start = ((bf16[4,344,256]{2,1,0:T(8,128)(2,1)}), bf16[4,344,256]{2,1,0:T(8,128)(2,1)S(1)}, u32[]{:S(2)}, u32[]{:S(2)}) async-start(bf16[4,344,256]{2,1,0:T(8,128)(2,1)} %message.1), calls=%async_computation | async-start | bytes 1409024 | tf_op jit(solution)/shard_map/all_to_all | solution.py:459
  14.5 2.6 %collective-permute-start.5 = (bf16[1024,256]{1,0:T(8,128)(2,1)}, bf16[1024,256]{1,0:T(8,128)(2,1)}, u32[]{:S(2)}, u32[]{:S(2)}) collective-permute-start(bf16[1024,256]{1,0:T(8,128)(2,1)} %a.1), channel_id=1, source_target_pairs={{0,2},{2,0},{1,3},{3,1},{4,6},{6,4},{5,7},{7,5},{8,10},{10,8},{9,1... | collective-permute-start | bytes 1572872 | tf_op jit(solution)/shard_map/ppermute | solution.py:46
  17.1 7.1 %all-to-all-done.t2 = bf16[4,344,256]{2,1,0:T(8,128)(2,1)S(1)} async-done(((bf16[4,344,256]{2,1,0:T(8,128)(2,1)}), bf16[4,344,256]{2,1,0:T(8,128)(2,1)S(1)}, u32[]{:S(2)}, u32[]{:S(2)}) %all-to-all-start) | async-done | bytes 704544 | tf_op jit(solution)/shard_map/all_to_all | solution.py:459
  24.2 2.7 %collective-permute-start.3 = (bf16[4,344,256]{2,1,0:T(8,128)(2,1)S(1)}, bf16[4,344,256]{2,1,0:T(8,128)(2,1)S(1)}, u32[]{:S(2)}, u32[]{:S(2)}) collective-permute-start(bf16[4,344,256]{2,1,0:T(8,128)(2,1)S(1)} %all-to-all-done.t2), channel_id=1, source_target_pairs={{0,1},{1,0},{2,3},{3,2},{4,5},{5,4},{6,7},{7,6},{8,9},{9,8},{10,11... | collective-permute-start | bytes 2113544 | tf_op jit(solution)/shard_map/ppermute | solution.py:46
  27.9 2.8 %collective-permute-start.6 = (bf16[1024,256]{1,0:T(8,128)(2,1)}, bf16[1024,256]{1,0:T(8,128)(2,1)}, u32[]{:S(2)}, u32[]{:S(2)}) collective-permute-start(bf16[1024,256]{1,0:T(8,128)(2,1)} %collective-permute-done.5.c), channel_id=1, source_target_pairs={{0,1},{1,0},{2,3},{3,2},{4,5},{5,4},{6,7},{7,6},{8,9},{9,8},{10,11... | collective-permute-start | bytes 1572872 | tf_op jit(solution)/shard_map/ppermute | solution.py:46
  32.6 2.3 %unit.1 = (bf16[1024,1024]{1,0:T(8,128)(2,1)S(1)}, bf16[1024,1024]{1,0:T(8,128)(2,1)S(1)}, f32[1024,128]{1,0:T(8,128)S(1)}) custom-call(bf16[1024,256]{1,0:T(8,128)(2,1)} %a.1, bf16[1024,256]{1,0:T(8,128)(2,1)} %collective-permute-done.4.b, bf16[1024,256]{1,0:T(8,128)(2,1)} %collective-permute-done.5.c, bf16[1024,256]{1,0:T(8,128)(2,1)} %collective-permute-done.6.d), custom_call_target="tpu_custom_call" | custom-call | flops 20000000 | bytes 1048576 | tf_op jit(solution)/shard_map/unit/pallas_call | solution.py:72
  34.9 7.2 %focal.1 = (bf16[672,512]{1,0:T(8,128)(2,1)S(1)}, bf16[672,512]{1,0:T(8,128)(2,1)S(1)}, f32[8,128]{1,0:T(8,128)S(1)}, f32[1,1]{1,0:T(1,128)}) custom-call(s32[6]{0:T(128)S(1)} %stack.27.s, bf16[1344,256]{1,0:T(8,128)(2,1)S(1)} %constant_dynamic-slice_fusion.t0, bf16[1344,256]{1,0:T(8,128)(2,1)S(1)} %collective-permute-done.t1, ...), custom_call_target="tpu_custom_call" | custom-call | flops 1400000000 | bytes 1048576 | tf_op jit(solution)/shard_map/focal/pallas_call | solution.py:196
  42.1 4.0 %region.1 = bf16[8,64,1024]{2,1,0:T(8,128)(2,1)} custom-call(s32[6]{0:T(128)S(1)} %stack.27.s, bf16[672,512]{1,0:T(8,128)(2,1)S(1)} %get-tuple-element.32.keep, bf16[672,512]{1,0:T(8,128)(2,1)S(1)} %get-tuple-element.33.send, bf16[1344,256]{1,0:T(8,128)(2,1)S(1)} %constant_dynamic-slice_fusion.t0, bf16[1344,256]{1,0:T(8,128)(2,1)S(1)} %collective-permute-done.t1, ...), custom_call_target="tpu_custom_call" | custom-call | flops 1400000000 | bytes 1048576 | tf_op jit(solution)/shard_map/region/pallas_call | solution.py:268
  47.8 8.2 %all-to-all-start.1 = ((bf16[8,64,1024]{2,1,0:T(8,128)(2,1)}), bf16[8,64,1024]{2,1,0:T(8,128)(2,1)S(1)}, u32[]{:S(2)}, u32[]{:S(2)}) async-start(bf16[8,64,1024]{2,1,0:T(8,128)(2,1)} %region.1), calls=%async_computation.1 | async-start | bytes 2097152 | tf_op jit(solution)/shard_map/all_to_all | solution.py:459
  56.7 2.0 %collective-permute-done.7.other = bf16[672,512]{1,0:T(8,128)(2,1)S(1)} collective-permute-done((bf16[672,512]{1,0:T(8,128)(2,1)}, bf16[672,512]{1,0:T(8,128)(2,1)S(1)}, u32[]{:S(2)}, u32[]{:S(2)}) %collective-permute-start.7) | collective-permute-done | bytes 688160 | tf_op jit(solution)/shard_map/ppermute | solution.py:46
  58.6 1.6 %copy-done.1 = bf16[1024,1024]{1,0:T(8,128)(2,1)S(1)} copy-done((bf16[1024,1024]{1,0:T(8,128)(2,1)S(1)}, bf16[1024,1024]{1,0:T(8,128)(2,1)}, u32[]{:S(2)}) %copy-start.1) | copy-done | bytes 2097176
  61.3 2.4 %table.1 = (bf16[680,128]{1,0:T(8,128)(2,1)S(1)}, bf16[680,128]{1,0:T(8,128)(2,1)S(1)}, bf16[680,128]{1,0:T(8,128)(2,1)S(1)}, bf16[680,128]{1,0:T(8,128)(2,1)S(1...) custom-call(s32[6]{0:T(128)S(1)} %stack.27.s, ...), custom_call_target="tpu_custom_call" | custom-call | flops 1400000000 | bytes 1048576 | tf_op jit(solution)/shard_map/table/pallas_call | solution.py:302
  65.0 1.5 collective-permute-start.9
  68.9 2.6 %collective-permute-start.12 = (bf16[680,128]{1,0:T(8,128)(2,1)S(1)}, bf16[680,128]{1,0:T(8,128)(2,1)S(1)}, u32[]{:S(2)}, u32[]{:S(2)}) collective-permute-start(bf16[680,128]{1,0:T(8,128)(2,1)S(1)} %get-tuple-element.42), channel_id=1, source_target_pairs={{0,160},{32,128},{64,224},{96,192},{128,32},{160,0},{192,96},{224,... | collective-permute-start | bytes 522248 | tf_op jit(solution)/shard_map/ppermute | solution.py:446
  71.5 1.5 %collective-permute-start.13 = (bf16[680,128]{1,0:T(8,128)(2,1)S(1)}, bf16[680,128]{1,0:T(8,128)(2,1)S(1)}, u32[]{:S(2)}, u32[]{:S(2)}) collective-permute-start(bf16[680,128]{1,0:T(8,128)(2,1)S(1)} %get-tuple-element.43), channel_id=1, source_target_pairs={{0,192},{32,224},{64,0},{96,32},{128,64},{160,96},{192,128},{224,1... | collective-permute-start | bytes 522248 | tf_op jit(solution)/shard_map/ppermute | solution.py:446
  73.6 2.1 %collective-permute-done.10.refs_3_ = bf16[680,128]{1,0:T(8,128)(2,1)S(1)} collective-permute-done((bf16[680,128]{1,0:T(8,128)(2,1)S(1)}, bf16[680,128]{1,0:T(8,128)(2,1)S(1)}, u32[]{:S(2)}, u32[]{:S(2)}) %collective-permute-start.10) | collective-permute-done | bytes 174112 | tf_op jit(solution)/shard_map/ppermute | solution.py:446
  75.6 8.2 %collective-permute-done.11.refs_4_ = bf16[680,128]{1,0:T(8,128)(2,1)S(1)} collective-permute-done((bf16[680,128]{1,0:T(8,128)(2,1)S(1)}, bf16[680,128]{1,0:T(8,128)(2,1)S(1)}, u32[]{:S(2)}, u32[]{:S(2)}) %collective-permute-start.11) | collective-permute-done | bytes 174112 | tf_op jit(solution)/shard_map/ppermute | solution.py:446
  85.9 16.3 %all-to-all-start.2 = ((bf16[8,672,128]{2,1,0:T(8,128)(2,1)}), bf16[8,672,128]{2,1,0:T(8,128)(2,1)S(1)}, u32[]{:S(2)}, u32[]{:S(2)}) async-start(bf16[8,672,128]{2,1,0:T(8,128)(2,1)} %gather.1), calls=%async_computation.2 | async-start | bytes 2752512 | tf_op jit(solution)/shard_map/all_to_all | solution.py:459
  104.8 2.0 %collective-permute-start.17 = (bf16[72,256]{1,0:T(8,128)(2,1)S(1)}, bf16[72,256]{1,0:T(8,128)(2,1)S(1)}, u32[]{:S(2)}, u32[]{:S(2)}) collective-permute-start(bf16[72,256]{1,0:T(8,128)(2,1)S(1)} %get-tuple-element.49), channel_id=1, source_target_pairs={{0,3},{1,2},{2,1},{3,0},{4,7},{5,6},{6,5},{7,4},{8,11},{9,10},{10,... | collective-permute-start | bytes 110600 | tf_op jit(solution)/shard_map/ppermute | solution.py:500
  106.8 10.6 %collective-permute-done.16.far = bf16[72,256]{1,0:T(8,128)(2,1)S(1)} collective-permute-done((bf16[72,256]{1,0:T(8,128)(2,1)S(1)}, bf16[72,256]{1,0:T(8,128)(2,1)S(1)}, u32[]{:S(2)}, u32[]{:S(2)}) %collective-permute-start.16) | collective-permute-done | bytes 36896 | tf_op jit(solution)/shard_map/ppermute | solution.py:500
  117.4 2.6 %collective-permute-done.17.both = bf16[72,256]{1,0:T(8,128)(2,1)S(1)} collective-permute-done((bf16[72,256]{1,0:T(8,128)(2,1)S(1)}, bf16[72,256]{1,0:T(8,128)(2,1)S(1)}, u32[]{:S(2)}, u32[]{:S(2)}) %collective-permute-start.17) | collective-permute-done | bytes 36896 | tf_op jit(solution)/shard_map/ppermute | solution.py:500
  120.6 3.0 %collective-permute-start.24 = (bf16[136,256]{1,0:T(8,128)(2,1)S(1)}, bf16[136,256]{1,0:T(8,128)(2,1)S(1)}, u32[]{:S(2)}, u32[]{:S(2)}) collective-permute-start(bf16[136,256]{1,0:T(8,128)(2,1)S(1)} %share.1.refs_0_), channel_id=1, source_target_pairs={{0,28},{4,0},{8,4},{12,8},{16,12},{20,16},{24,20},{28,24},{1,29},{... | collective-permute-start | bytes 208904 | tf_op jit(solution)/shard_map/ppermute | solution.py:455
  123.6 2.1 %collective-permute-start.23 = (bf16[136,256]{1,0:T(8,128)(2,1)S(1)}, bf16[136,256]{1,0:T(8,128)(2,1)S(1)}, u32[]{:S(2)}, u32[]{:S(2)}) collective-permute-start(bf16[136,256]{1,0:T(8,128)(2,1)S(1)} %share.1.refs_0_), channel_id=1, source_target_pairs={{0,24},{4,28},{8,0},{12,4},{16,8},{20,12},{24,16},{28,20},{1,25},{... | collective-permute-start | bytes 208904 | tf_op jit(solution)/shard_map/ppermute | solution.py:455
  126.9 3.3 %collective-permute-start.21 = (bf16[136,256]{1,0:T(8,128)(2,1)S(1)}, bf16[136,256]{1,0:T(8,128)(2,1)S(1)}, u32[]{:S(2)}, u32[]{:S(2)}) collective-permute-start(bf16[136,256]{1,0:T(8,128)(2,1)S(1)} %share.1.refs_0_), channel_id=1, source_target_pairs={{0,16},{4,20},{8,24},{12,28},{16,0},{20,4},{24,8},{28,12},{1,17},{... | collective-permute-start | bytes 208904 | tf_op jit(solution)/shard_map/ppermute | solution.py:455
  130.2 3.3 %collective-permute-start.19 = (bf16[136,256]{1,0:T(8,128)(2,1)S(1)}, bf16[136,256]{1,0:T(8,128)(2,1)S(1)}, u32[]{:S(2)}, u32[]{:S(2)}) collective-permute-start(bf16[136,256]{1,0:T(8,128)(2,1)S(1)} %share.1.refs_0_), channel_id=1, source_target_pairs={{0,8},{4,12},{8,16},{12,20},{16,24},{20,28},{24,0},{28,4},{1,9},{5... | collective-permute-start | bytes 208904 | tf_op jit(solution)/shard_map/ppermute | solution.py:455
  134.7 1.4 collective-permute-done.21.refs_4_
  136.0 4.8 %collective-permute-done.20.refs_3_ = bf16[136,256]{1,0:T(8,128)(2,1)S(1)} collective-permute-done((bf16[136,256]{1,0:T(8,128)(2,1)S(1)}, bf16[136,256]{1,0:T(8,128)(2,1)S(1)}, u32[]{:S(2)}, u32[]{:S(2)}) %collective-permute-start.20) | collective-permute-done | bytes 69664 | tf_op jit(solution)/shard_map/ppermute | solution.py:455
  140.9 2.7 %collective-permute-done.19.refs_2_ = bf16[136,256]{1,0:T(8,128)(2,1)S(1)} collective-permute-done((bf16[136,256]{1,0:T(8,128)(2,1)S(1)}, bf16[136,256]{1,0:T(8,128)(2,1)S(1)}, u32[]{:S(2)}, u32[]{:S(2)}) %collective-permute-start.19) | collective-permute-done | bytes 69664 | tf_op jit(solution)/shard_map/ppermute | solution.py:455
  143.6 2.1 %region_final.1 = (bf16[2,8,64,256]{3,2,1,0:T(8,128)(2,1)}, f32[1,1]{1,0:T(1,128)}) custom-call(s32[6]{0:T(128)S(1)} %stack.27.s, f32[1,1]{1,0:T(1,128)} %get-tuple-element.31.count, bf16[136,256]{1,0:T(8,128)(2,1)S(1)} %share.1.refs_0_, bf16[136,256]{1,0:T(8,128)(2,1)S(1)} %collective-permute-done.18.refs_1_, ...), custom_call_target="tpu_custom_call" | custom-call | flops 10000000 | bytes 1048576 | tf_op jit(solution)/shard_map/region_final/pallas_call | solution.py:428
  145.7 1.9 %table_final.1 = bf16[2688,256]{1,0:T(8,128)(2,1)} custom-call(s32[6]{0:T(128)S(1)} %stack.27.s, bf16[8,672,128]{2,1,0:T(8,128)(2,1)S(1)} %all-to-all-done.2.tables), custom_call_target="tpu_custom_call" | custom-call | flops 10000000 | bytes 1048576 | tf_op jit(solution)/shard_map/table_final/pallas_call | solution.py:406
  (65 shorter events, 21.7 us)
Async XLA Ops:
  1.6 25.3 %copy-start.6 = (bf16[2688,256]{1,0:T(8,128)(2,1)S(1)}, bf16[2688,256]{1,0:T(8,128)(2,1)}, u32[]{:S(2)}) copy-start(bf16[2688,256]{1,0:T(8,128)(2,1)} %x.1) | copy-start | bytes 4128772
  1.6 7.6 %collective-permute-start.1 = (bf16[336,256]{1,0:T(8,128)(2,1)S(1)}, bf16[336,256]{1,0:T(8,128)(2,1)S(1)}, u32[]{:S(2)}, u32[]{:S(2)}) collective-permute-start(bf16[336,256]{1,0:T(8,128)(2,1)S(1)} %rows.1), channel_id=1, source_target_pairs={{0,2},{2,0},{1,3},{3,1},{4,6},{6,4},{5,7},{7,5},{8,10},{10,8},{9,1... | collective-permute-start | bytes 516104 | tf_op jit(solution)/shard_map/ppermute | solution.py:46
  6.5 2.6 %collective-permute-start.2 = (f32[8,128]{1,0:T(8,128)S(1)}, f32[8,128]{1,0:T(8,128)S(1)}, u32[]{:S(2)}, u32[]{:S(2)}) collective-permute-start(f32[8,128]{1,0:T(8,128)S(1)} %broadcast_in_dim.15.mine), channel_id=1, source_target_pairs={{0,32},{32,0},{1,33},{33,1},{2,34},{34,2},{3,35},{35,3},{4,36},{36... | collective-permute-start | bytes 12296 | tf_op jit(solution)/shard_map/ppermute | solution.py:46
  10.1 14.1 %all-to-all-start = ((bf16[4,344,256]{2,1,0:T(8,128)(2,1)}), bf16[4,344,256]{2,1,0:T(8,128)(2,1)S(1)}, u32[]{:S(2)}, u32[]{:S(2)}) async-start(bf16[4,344,256]{2,1,0:T(8,128)(2,1)} %message.1), calls=%async_computation | async-start | bytes 1409024 | tf_op jit(solution)/shard_map/all_to_all | solution.py:459
  14.5 17.4 %copy-start.7 = (f32[1024]{0:T(1024)S(1)}, f32[1024]{0:T(1024)}, u32[]{:S(2)}) copy-start(f32[1024]{0:T(1024)} %param.9) | copy-start | bytes 12292
  14.5 17.4 %copy-start.8 = (f32[1024]{0:T(1024)S(1)}, f32[1024]{0:T(1024)}, u32[]{:S(2)}) copy-start(f32[1024]{0:T(1024)} %param.8) | copy-start | bytes 12292
  14.5 13.3 %collective-permute-start.5 = (bf16[1024,256]{1,0:T(8,128)(2,1)}, bf16[1024,256]{1,0:T(8,128)(2,1)}, u32[]{:S(2)}, u32[]{:S(2)}) collective-permute-start(bf16[1024,256]{1,0:T(8,128)(2,1)} %a.1), channel_id=1, source_target_pairs={{0,2},{2,0},{1,3},{3,1},{4,6},{6,4},{5,7},{7,5},{8,10},{10,8},{9,1... | collective-permute-start | bytes 1572872 | tf_op jit(solution)/shard_map/ppermute | solution.py:46
  24.2 10.7 %collective-permute-start.3 = (bf16[4,344,256]{2,1,0:T(8,128)(2,1)S(1)}, bf16[4,344,256]{2,1,0:T(8,128)(2,1)S(1)}, u32[]{:S(2)}, u32[]{:S(2)}) collective-permute-start(bf16[4,344,256]{2,1,0:T(8,128)(2,1)S(1)} %all-to-all-done.t2), channel_id=1, source_target_pairs={{0,1},{1,0},{2,3},{3,2},{4,5},{5,4},{6,7},{7,6},{8,9},{9,8},{10,11... | collective-permute-start | bytes 2113544 | tf_op jit(solution)/shard_map/ppermute | solution.py:46
  27.0 7.9 %collective-permute-start = (bf16[1344,256]{1,0:T(8,128)(2,1)S(1)}, bf16[1344,256]{1,0:T(8,128)(2,1)S(1)}, u32[]{:S(2)}, u32[]{:S(2)}) collective-permute-start(bf16[1344,256]{1,0:T(8,128)(2,1)S(1)} %constant_dynamic-slice_fusion.t0), channel_id=1, source_target_pairs={{0,1},{1,0},{2,3},{3,2},{4,5},{5,4},{6,7},{7,6},{8,9},{9,8},{10,11... | collective-permute-start | bytes 2064392 | tf_op jit(solution)/shard_map/ppermute | solution.py:46
  27.1 5.0 %collective-permute-start.4 = (bf16[1024,256]{1,0:T(8,128)(2,1)}, bf16[1024,256]{1,0:T(8,128)(2,1)}, u32[]{:S(2)}, u32[]{:S(2)}) collective-permute-start(bf16[1024,256]{1,0:T(8,128)(2,1)} %a.1), channel_id=1, source_target_pairs={{0,1},{1,0},{2,3},{3,2},{4,5},{5,4},{6,7},{7,6},{8,9},{9,8},{10,11... | collective-permute-start | bytes 1572872 | tf_op jit(solution)/shard_map/ppermute | solution.py:46
  27.9 4.7 %collective-permute-start.6 = (bf16[1024,256]{1,0:T(8,128)(2,1)}, bf16[1024,256]{1,0:T(8,128)(2,1)}, u32[]{:S(2)}, u32[]{:S(2)}) collective-permute-start(bf16[1024,256]{1,0:T(8,128)(2,1)} %collective-permute-done.5.c), channel_id=1, source_target_pairs={{0,1},{1,0},{2,3},{3,2},{4,5},{5,4},{6,7},{7,6},{8,9},{9,8},{10,11... | collective-permute-start | bytes 1572872 | tf_op jit(solution)/shard_map/ppermute | solution.py:46
  47.8 38.1 %all-to-all-start.1 = ((bf16[8,64,1024]{2,1,0:T(8,128)(2,1)}), bf16[8,64,1024]{2,1,0:T(8,128)(2,1)S(1)}, u32[]{:S(2)}, u32[]{:S(2)}) async-start(bf16[8,64,1024]{2,1,0:T(8,128)(2,1)} %region.1), calls=%async_computation.1 | async-start | bytes 2097152 | tf_op jit(solution)/shard_map/all_to_all | solution.py:459
  56.0 2.6 %collective-permute-start.7 = (bf16[672,512]{1,0:T(8,128)(2,1)}, bf16[672,512]{1,0:T(8,128)(2,1)S(1)}, u32[]{:S(2)}, u32[]{:S(2)}) collective-permute-start(bf16[672,512]{1,0:T(8,128)(2,1)} %copy-done.4), channel_id=1, source_target_pairs={{0,1},{1,0},{2,3},{3,2},{4,5},{5,4},{6,7},{7,6},{8,9},{9,8},{10,11... | collective-permute-start | bytes 2064392 | tf_op jit(solution)/shard_map/ppermute | solution.py:46
  63.7 7.8 %collective-permute-start.8 = (bf16[680,128]{1,0:T(8,128)(2,1)S(1)}, bf16[680,128]{1,0:T(8,128)(2,1)S(1)}, u32[]{:S(2)}, u32[]{:S(2)}) collective-permute-start(bf16[680,128]{1,0:T(8,128)(2,1)S(1)} %get-tuple-element.38), channel_id=1, source_target_pairs={{0,32},{32,0},{64,96},{96,64},{128,160},{160,128},{192,224},{224,1... | collective-permute-start | bytes 522248 | tf_op jit(solution)/shard_map/ppermute | solution.py:446
  65.0 8.0 %collective-permute-start.9 = (bf16[680,128]{1,0:T(8,128)(2,1)S(1)}, bf16[680,128]{1,0:T(8,128)(2,1)S(1)}, u32[]{:S(2)}, u32[]{:S(2)}) collective-permute-start(bf16[680,128]{1,0:T(8,128)(2,1)S(1)} %get-tuple-element.39), channel_id=1, source_target_pairs={{0,64},{32,96},{64,128},{96,160},{128,192},{160,224},{192,0},{224,... | collective-permute-start | bytes 522248 | tf_op jit(solution)/shard_map/ppermute | solution.py:446
  66.4 9.2 %collective-permute-start.10 = (bf16[680,128]{1,0:T(8,128)(2,1)S(1)}, bf16[680,128]{1,0:T(8,128)(2,1)S(1)}, u32[]{:S(2)}, u32[]{:S(2)}) collective-permute-start(bf16[680,128]{1,0:T(8,128)(2,1)S(1)} %get-tuple-element.40), channel_id=1, source_target_pairs={{0,96},{32,64},{64,160},{96,128},{128,224},{160,192},{192,32},{224... | collective-permute-start | bytes 522248 | tf_op jit(solution)/shard_map/ppermute | solution.py:446
  67.6 16.2 %collective-permute-start.11 = (bf16[680,128]{1,0:T(8,128)(2,1)S(1)}, bf16[680,128]{1,0:T(8,128)(2,1)S(1)}, u32[]{:S(2)}, u32[]{:S(2)}) collective-permute-start(bf16[680,128]{1,0:T(8,128)(2,1)S(1)} %get-tuple-element.41), channel_id=1, source_target_pairs={{0,128},{32,160},{64,192},{96,224},{128,0},{160,32},{192,64},{224,... | collective-permute-start | bytes 522248 | tf_op jit(solution)/shard_map/ppermute | solution.py:446
  68.9 15.0 %collective-permute-start.12 = (bf16[680,128]{1,0:T(8,128)(2,1)S(1)}, bf16[680,128]{1,0:T(8,128)(2,1)S(1)}, u32[]{:S(2)}, u32[]{:S(2)}) collective-permute-start(bf16[680,128]{1,0:T(8,128)(2,1)S(1)} %get-tuple-element.42), channel_id=1, source_target_pairs={{0,160},{32,128},{64,224},{96,192},{128,32},{160,0},{192,96},{224,... | collective-permute-start | bytes 522248 | tf_op jit(solution)/shard_map/ppermute | solution.py:446
  71.5 12.4 %collective-permute-start.13 = (bf16[680,128]{1,0:T(8,128)(2,1)S(1)}, bf16[680,128]{1,0:T(8,128)(2,1)S(1)}, u32[]{:S(2)}, u32[]{:S(2)}) collective-permute-start(bf16[680,128]{1,0:T(8,128)(2,1)S(1)} %get-tuple-element.43), channel_id=1, source_target_pairs={{0,192},{32,224},{64,0},{96,32},{128,64},{160,96},{192,128},{224,1... | collective-permute-start | bytes 522248 | tf_op jit(solution)/shard_map/ppermute | solution.py:446
  73.0 10.9 %collective-permute-start.14 = (bf16[680,128]{1,0:T(8,128)(2,1)S(1)}, bf16[680,128]{1,0:T(8,128)(2,1)S(1)}, u32[]{:S(2)}, u32[]{:S(2)}) collective-permute-start(bf16[680,128]{1,0:T(8,128)(2,1)S(1)} %get-tuple-element.44), channel_id=1, source_target_pairs={{0,224},{32,192},{64,32},{96,0},{128,96},{160,64},{192,160},{224,1... | collective-permute-start | bytes 522248 | tf_op jit(solution)/shard_map/ppermute | solution.py:446
  84.1 0.7 collective-permute-start.25
  85.9 59.7 %all-to-all-start.2 = ((bf16[8,672,128]{2,1,0:T(8,128)(2,1)}), bf16[8,672,128]{2,1,0:T(8,128)(2,1)S(1)}, u32[]{:S(2)}, u32[]{:S(2)}) async-start(bf16[8,672,128]{2,1,0:T(8,128)(2,1)} %gather.1), calls=%async_computation.2 | async-start | bytes 2752512 | tf_op jit(solution)/shard_map/all_to_all | solution.py:459
  102.5 4.3 %collective-permute-start.15 = (bf16[72,256]{1,0:T(8,128)(2,1)S(1)}, bf16[72,256]{1,0:T(8,128)(2,1)S(1)}, u32[]{:S(2)}, u32[]{:S(2)}) collective-permute-start(bf16[72,256]{1,0:T(8,128)(2,1)S(1)} %get-tuple-element.47), channel_id=1, source_target_pairs={{0,1},{1,0},{2,3},{3,2},{4,5},{5,4},{6,7},{7,6},{8,9},{9,8},{10,11... | collective-permute-start | bytes 110600 | tf_op jit(solution)/shard_map/ppermute | solution.py:500
  103.6 13.8 %collective-permute-start.16 = (bf16[72,256]{1,0:T(8,128)(2,1)S(1)}, bf16[72,256]{1,0:T(8,128)(2,1)S(1)}, u32[]{:S(2)}, u32[]{:S(2)}) collective-permute-start(bf16[72,256]{1,0:T(8,128)(2,1)S(1)} %get-tuple-element.48), channel_id=1, source_target_pairs={{0,2},{1,3},{2,0},{3,1},{4,6},{5,7},{6,4},{7,5},{8,10},{9,11},{10,... | collective-permute-start | bytes 110600 | tf_op jit(solution)/shard_map/ppermute | solution.py:500
  104.8 15.1 %collective-permute-start.17 = (bf16[72,256]{1,0:T(8,128)(2,1)S(1)}, bf16[72,256]{1,0:T(8,128)(2,1)S(1)}, u32[]{:S(2)}, u32[]{:S(2)}) collective-permute-start(bf16[72,256]{1,0:T(8,128)(2,1)S(1)} %get-tuple-element.49), channel_id=1, source_target_pairs={{0,3},{1,2},{2,1},{3,0},{4,7},{5,6},{6,5},{7,4},{8,11},{9,10},{10,... | collective-permute-start | bytes 110600 | tf_op jit(solution)/shard_map/ppermute | solution.py:500
  120.6 9.6 %collective-permute-start.24 = (bf16[136,256]{1,0:T(8,128)(2,1)S(1)}, bf16[136,256]{1,0:T(8,128)(2,1)S(1)}, u32[]{:S(2)}, u32[]{:S(2)}) collective-permute-start(bf16[136,256]{1,0:T(8,128)(2,1)S(1)} %share.1.refs_0_), channel_id=1, source_target_pairs={{0,28},{4,0},{8,4},{12,8},{16,12},{20,16},{24,20},{28,24},{1,29},{... | collective-permute-start | bytes 208904 | tf_op jit(solution)/shard_map/ppermute | solution.py:455
  123.6 9.8 %collective-permute-start.23 = (bf16[136,256]{1,0:T(8,128)(2,1)S(1)}, bf16[136,256]{1,0:T(8,128)(2,1)S(1)}, u32[]{:S(2)}, u32[]{:S(2)}) collective-permute-start(bf16[136,256]{1,0:T(8,128)(2,1)S(1)} %share.1.refs_0_), channel_id=1, source_target_pairs={{0,24},{4,28},{8,0},{12,4},{16,8},{20,12},{24,16},{28,20},{1,25},{... | collective-permute-start | bytes 208904 | tf_op jit(solution)/shard_map/ppermute | solution.py:455
  125.7 8.9 %collective-permute-start.22 = (bf16[136,256]{1,0:T(8,128)(2,1)S(1)}, bf16[136,256]{1,0:T(8,128)(2,1)S(1)}, u32[]{:S(2)}, u32[]{:S(2)}) collective-permute-start(bf16[136,256]{1,0:T(8,128)(2,1)S(1)} %share.1.refs_0_), channel_id=1, source_target_pairs={{0,20},{4,24},{8,28},{12,0},{16,4},{20,8},{24,12},{28,16},{1,21},{... | collective-permute-start | bytes 208904 | tf_op jit(solution)/shard_map/ppermute | solution.py:455
  126.9 9.1 %collective-permute-start.21 = (bf16[136,256]{1,0:T(8,128)(2,1)S(1)}, bf16[136,256]{1,0:T(8,128)(2,1)S(1)}, u32[]{:S(2)}, u32[]{:S(2)}) collective-permute-start(bf16[136,256]{1,0:T(8,128)(2,1)S(1)} %share.1.refs_0_), channel_id=1, source_target_pairs={{0,16},{4,20},{8,24},{12,28},{16,0},{20,4},{24,8},{28,12},{1,17},{... | collective-permute-start | bytes 208904 | tf_op jit(solution)/shard_map/ppermute | solution.py:455
  130.2 10.7 %collective-permute-start.20 = (bf16[136,256]{1,0:T(8,128)(2,1)S(1)}, bf16[136,256]{1,0:T(8,128)(2,1)S(1)}, u32[]{:S(2)}, u32[]{:S(2)}) collective-permute-start(bf16[136,256]{1,0:T(8,128)(2,1)S(1)} %share.1.refs_0_), channel_id=1, source_target_pairs={{0,12},{4,16},{8,20},{12,24},{16,28},{20,0},{24,4},{28,8},{1,13},{... | collective-permute-start | bytes 208904 | tf_op jit(solution)/shard_map/ppermute | solution.py:455
  130.2 13.4 %collective-permute-start.19 = (bf16[136,256]{1,0:T(8,128)(2,1)S(1)}, bf16[136,256]{1,0:T(8,128)(2,1)S(1)}, u32[]{:S(2)}, u32[]{:S(2)}) collective-permute-start(bf16[136,256]{1,0:T(8,128)(2,1)S(1)} %share.1.refs_0_), channel_id=1, source_target_pairs={{0,8},{4,12},{8,16},{12,20},{16,24},{20,28},{24,0},{28,4},{1,9},{5... | collective-permute-start | bytes 208904 | tf_op jit(solution)/shard_map/ppermute | solution.py:455
  133.5 10.1 %collective-permute-start.18 = (bf16[136,256]{1,0:T(8,128)(2,1)S(1)}, bf16[136,256]{1,0:T(8,128)(2,1)S(1)}, u32[]{:S(2)}, u32[]{:S(2)}) collective-permute-start(bf16[136,256]{1,0:T(8,128)(2,1)S(1)} %share.1.refs_0_), channel_id=1, source_target_pairs={{0,4},{4,8},{8,12},{12,16},{16,20},{20,24},{24,28},{28,0},{1,5},{5... | collective-permute-start | bytes 208904 | tf_op jit(solution)/shard_map/ppermute | solution.py:455
  (6 other events, 16.2 us)

commit v8 on v7

--- a/solution.py
+++ b/solution.py
@@ -226,8 +226,10 @@
     )(scalars, *tables, unit, lane_f, labels, mask)
 
 
-def region_kernel(s, keep, send, t0, t1, t2, t3, raw, inv_ref, out, acc):
+def region_kernel(s, keep, send, t0, t1, t2, t3, raw, inv_ref, out, kept, acc, sem):
     half = keep.shape[0]
+    copy = pltpu.make_async_copy(keep, kept, sem)
+    copy.start()
     k = s[K]
     tile = acc.shape[0]
     mine_at = pl.multiple_of(k * half, 32)
@@ -262,34 +264,43 @@
             for p in range(tile // 64):
                 z = tile // 64 * i + p
                 out[z, :, cols] = grad[64 * p : 64 * p + 64, :].astype(BF16)
+    copy.wait()
 
 
 def make_region(scalars, keep, send, tables, raw, inv):
     return pl.pallas_call(
         region_kernel,
         in_specs=[smem()] + vmem(8),
-        out_specs=vmem(1)[0],
-        out_shape=in_hbm((8, 64, 1024), BF16),
-        scratch_shapes=[pltpu.VMEM((256, 1024), F32)],
+        out_specs=vmem(1) + [pl.BlockSpec(memory_space=pltpu.HBM)],
+        out_shape=[in_hbm((8, 64, 1024), BF16), in_hbm(keep.shape, BF16)],
+        scratch_shapes=[pltpu.VMEM((256, 1024), F32), pltpu.SemaphoreType.DMA],
         compiler_params=params(24),
         cost_estimate=cost(1.4e9),
         name="region",
     )(scalars, keep, send, *tables, raw, inv)
 
 
-def table_kernel(s, keep, other, unit, loss, *refs):
-    outs, acc = refs[:8], refs[8]
+def table_kernel(s, kept, other, unit, loss, *refs):
+    outs, (acc, keep, theirs, sems) = refs[:8], refs[8:]
     half, rows = other.shape
-    mine = keep[...]
-    theirs = other[...]
+    other_copy = pltpu.make_async_copy(other, theirs, sems.at[0])
+    copy = pltpu.make_async_copy(kept, keep, sems.at[1])
+    other_copy.start()
+    copy.start()
+    other_copy.wait()
     mine_at = pl.multiple_of(s[K] * rows, rows)
     theirs_at = pl.multiple_of((1 - s[K]) * rows, rows)
     extra = split3(jnp.sum(loss[...]), 128).astype(BF16)
     for dy in range(4):
         cols = pl.ds(pl.multiple_of(256 * ((s[Y] + dy) % 4), 256), 256)
-        acc[...] = jnp.dot(
-            mine, unit[pl.ds(mine_at, rows), cols], preferred_element_type=F32
-        ) + jnp.dot(theirs, unit[pl.ds(theirs_at, rows), cols], preferred_element_type=F32)
+        part = jnp.dot(theirs[...], unit[pl.ds(theirs_at, rows), cols], preferred_element_type=F32)
+        if dy == 0:
+            acc[...] = part
+            copy.wait()
+            part = acc[...]
+        acc[...] = part + jnp.dot(
+            keep[...], unit[pl.ds(mine_at, rows), cols], preferred_element_type=F32
+        )
         for dx in range(2):
             at = pl.multiple_of(128 * (s[XL] ^ dx), 128)
             out = outs[2 * dy + dx]
@@ -297,18 +308,23 @@
             out[half : half + 8, :] = extra
 
 
-def make_table(scalars, keep, other, unit, loss):
+def make_table(scalars, kept, other, unit, loss):
     half = other.shape[0]
     return pl.pallas_call(
         table_kernel,
-        in_specs=[smem()] + vmem(4),
+        in_specs=[smem()] + [pl.BlockSpec(memory_space=pltpu.HBM)] * 2 + vmem(2),
         out_specs=vmem(8),
         out_shape=[jax.ShapeDtypeStruct((half + 8, 128), BF16)] * 8,
-        scratch_shapes=[pltpu.VMEM((half, 256), F32)],
+        scratch_shapes=[
+            pltpu.VMEM((half, 256), F32),
+            pltpu.VMEM(other.shape, BF16),
+            pltpu.VMEM(other.shape, BF16),
+            pltpu.SemaphoreType.DMA((2,)),
+        ],
         compiler_params=params(),
         cost_estimate=cost(1.4e9),
         name="table",
-    )(scalars, keep, other, unit, loss)
+    )(scalars, kept, other, unit, loss)
 
 
 def table_sum_kernel(*refs):
@@ -489,8 +505,9 @@
     keep, send, loss, count = make_focal(scalars, tables, unit, lane_f, labels[None], mask)
 
     theirs = swap(send, "emb_1")
-    terms = exchange(make_region(scalars, keep, send, tables, raw, inv), CLS)
-    chunks = list(make_table(scalars, keep, theirs, unit, loss))
+    terms, kept = make_region(scalars, keep, send, tables, raw, inv)
+    terms = exchange(terms, CLS)
+    chunks = list(make_table(scalars, kept, theirs, unit, loss))
     for o in OVER_IMG:
         chunks[o] = over_img(chunks[o], o // 2, o % 2)
     table_part, loss_part = make_table_sum(chunks)

time: 149 us -> 147 us (0.987)
  local copies, waits for them, and re-layouts: 5.53 us -> 2.75 us
    unnamed x18, local copies, waits for them, and re-layouts: 4.41 us -> 1.63 us
  transfers between devices with their start and end apart: 29 -> 29, of which waited for: 12 -> 12; matrix products, arithmetic and copies ran while one was open for 2% -> 2% of each run, Pallas kernels for 6% -> 7%
where the time goes in v8:
time: 147 us; the launch traced here: 145 us
  starting transfers between devices  71.5 us (49%)
  waiting for transfers between devices  44.3 us (30%)
  Pallas kernels  24.5 us (17%)
  local copies, waits for them, and re-layouts  2.75 us (2%)
    all_to_all x3, starting transfers between devices, exchange(): return lax.all_to_all(x, axes, split_axis=0, concat_axis=0, tiled=True)  29.1 us
    ppermute x7, starting transfers between devices, along_cls(): return lax.ppermute(x, CLS, [(i, (i + d) % 8) for i in range(8)])  14 us
    ppermute x8, starting transfers between devices, swap(): return lax.ppermute(x, axis, [(0, 1), (1, 0)])  13.5 us
    ppermute x3, waiting for transfers between devices, shards(): parts[q] = lax.ppermute(parts[q], EMB, [(i, i ^ q) for i in range(4)])  13 us
    ppermute x7, waiting for transfers between devices, over_img(): return lax.ppermute(x, IMG, pairs)  10.3 us
    ppermute x7, starting transfers between devices, over_img(): return lax.ppermute(x, IMG, pairs)  9.85 us
    ppermute x7, waiting for transfers between devices, along_cls(): return lax.ppermute(x, CLS, [(i, (i + d) % 8) for i in range(8)])  8.95 us
    pallas_call x1, Pallas kernels, make_focal(): pl.pallas_call(focal_kernel, grid_spec=pltpu.PrefetchScalarGridSpec(num_s...  7.08 us
  transfers between devices with their start and end apart: 29, of which 12 were waited for; matrix products, arithmetic and copies ran while one was open for 2% of the time, Pallas kernels for 7%

profile of v8, /device:TPU:1, one launch (start us, length us, event | category | flops | bytes accessed | tf_op | source)
XLA Modules:
  0.0 145.3 jit_solution(2667122770779368103)
XLA Ops:
  1.6 3.6 %collective-permute-start.1 = (bf16[336,256]{1,0:T(8,128)(2,1)S(1)}, bf16[336,256]{1,0:T(8,128)(2,1)S(1)}, u32[]{:S(2)}, u32[]{:S(2)}) collective-permute-start(bf16[336,256]{1,0:T(8,128)(2,1)S(1)} %rows.1), channel_id=1, source_target_pairs={{0,2},{2,0},{1,3},{3,1},{4,6},{6,4},{5,7},{7,5},{8,10},{10,8},{9,1... | collective-permute-start | bytes 516104 | tf_op jit(solution)/shard_map/ppermute | solution.py:46
  6.9 2.2 %collective-permute-done.2.theirs = f32[8,128]{1,0:T(8,128)S(1)} collective-permute-done((f32[8,128]{1,0:T(8,128)S(1)}, f32[8,128]{1,0:T(8,128)S(1)}, u32[]{:S(2)}, u32[]{:S(2)}) %collective-permute-start.2) | collective-permute-done | bytes 4128 | tf_op jit(solution)/shard_map/ppermute | solution.py:46
  10.1 4.5 %all-to-all-start = ((bf16[4,344,256]{2,1,0:T(8,128)(2,1)}), bf16[4,344,256]{2,1,0:T(8,128)(2,1)S(1)}, u32[]{:S(2)}, u32[]{:S(2)}) async-start(bf16[4,344,256]{2,1,0:T(8,128)(2,1)} %message.1), calls=%async_computation | async-start | bytes 1409024 | tf_op jit(solution)/shard_map/all_to_all | solution.py:475
  14.5 2.6 %collective-permute-start.5 = (bf16[1024,256]{1,0:T(8,128)(2,1)}, bf16[1024,256]{1,0:T(8,128)(2,1)}, u32[]{:S(2)}, u32[]{:S(2)}) collective-permute-start(bf16[1024,256]{1,0:T(8,128)(2,1)} %a.1), channel_id=1, source_target_pairs={{0,2},{2,0},{1,3},{3,1},{4,6},{6,4},{5,7},{7,5},{8,10},{10,8},{9,1... | collective-permute-start | bytes 1572872 | tf_op jit(solution)/shard_map/ppermute | solution.py:46
  17.1 7.1 %all-to-all-done.t2 = bf16[4,344,256]{2,1,0:T(8,128)(2,1)S(1)} async-done(((bf16[4,344,256]{2,1,0:T(8,128)(2,1)}), bf16[4,344,256]{2,1,0:T(8,128)(2,1)S(1)}, u32[]{:S(2)}, u32[]{:S(2)}) %all-to-all-start) | async-done | bytes 704544 | tf_op jit(solution)/shard_map/all_to_all | solution.py:475
  24.2 2.7 %collective-permute-start.3 = (bf16[4,344,256]{2,1,0:T(8,128)(2,1)S(1)}, bf16[4,344,256]{2,1,0:T(8,128)(2,1)S(1)}, u32[]{:S(2)}, u32[]{:S(2)}) collective-permute-start(bf16[4,344,256]{2,1,0:T(8,128)(2,1)S(1)} %all-to-all-done.t2), channel_id=1, source_target_pairs={{0,1},{1,0},{2,3},{3,2},{4,5},{5,4},{6,7},{7,6},{8,9},{9,8},{10,11... | collective-permute-start | bytes 2113544 | tf_op jit(solution)/shard_map/ppermute | solution.py:46
  27.9 2.8 %collective-permute-start.6 = (bf16[1024,256]{1,0:T(8,128)(2,1)}, bf16[1024,256]{1,0:T(8,128)(2,1)}, u32[]{:S(2)}, u32[]{:S(2)}) collective-permute-start(bf16[1024,256]{1,0:T(8,128)(2,1)} %collective-permute-done.5.c), channel_id=1, source_target_pairs={{0,1},{1,0},{2,3},{3,2},{4,5},{5,4},{6,7},{7,6},{8,9},{9,8},{10,11... | collective-permute-start | bytes 1572872 | tf_op jit(solution)/shard_map/ppermute | solution.py:46
  32.6 2.3 %unit.1 = (bf16[1024,1024]{1,0:T(8,128)(2,1)S(1)}, bf16[1024,1024]{1,0:T(8,128)(2,1)S(1)}, f32[1024,128]{1,0:T(8,128)S(1)}) custom-call(bf16[1024,256]{1,0:T(8,128)(2,1)} %a.1, bf16[1024,256]{1,0:T(8,128)(2,1)} %collective-permute-done.4.b, bf16[1024,256]{1,0:T(8,128)(2,1)} %collective-permute-done.5.c, bf16[1024,256]{1,0:T(8,128)(2,1)} %collective-permute-done.6.d), custom_call_target="tpu_custom_call" | custom-call | flops 20000000 | bytes 1048576 | tf_op jit(solution)/shard_map/unit/pallas_call | solution.py:72
  34.9 7.1 %focal.1 = (bf16[672,512]{1,0:T(8,128)(2,1)S(1)}, bf16[672,512]{1,0:T(8,128)(2,1)S(1)}, f32[8,128]{1,0:T(8,128)S(1)}, f32[1,1]{1,0:T(1,128)}) custom-call(s32[6]{0:T(128)S(1)} %stack.27.s, bf16[1344,256]{1,0:T(8,128)(2,1)S(1)} %constant_dynamic-slice_fusion.t0, bf16[1344,256]{1,0:T(8,128)(2,1)S(1)} %collective-permute-done.t1, ...), custom_call_target="tpu_custom_call" | custom-call | flops 1400000000 | bytes 1048576 | tf_op jit(solution)/shard_map/focal/pallas_call | solution.py:196
  42.0 4.1 %region.1 = (bf16[8,64,1024]{2,1,0:T(8,128)(2,1)}, bf16[672,512]{1,0:T(8,128)(2,1)}) custom-call(s32[6]{0:T(128)S(1)} %stack.27.s, bf16[672,512]{1,0:T(8,128)(2,1)S(1)} %get-tuple-element.34.keep, bf16[672,512]{1,0:T(8,128)(2,1)S(1)} %get-tuple-element.35.send, bf16[1344,256]{1,0:T(8,128)(2,1)S(1)} %constant_dynamic-slice_fusion.t0, ...), custom_call_target="tpu_custom_call" | custom-call | flops 1400000000 | bytes 1048576 | tf_op jit(solution)/shard_map/region/pallas_call | solution.py:271
  46.2 8.3 %all-to-all-start.1 = ((bf16[8,64,1024]{2,1,0:T(8,128)(2,1)}), bf16[8,64,1024]{2,1,0:T(8,128)(2,1)S(1)}, u32[]{:S(2)}, u32[]{:S(2)}) async-start(bf16[8,64,1024]{2,1,0:T(8,128)(2,1)} %get-tuple-element.38), calls=%async_computation.1 | async-start | bytes 2097152 | tf_op jit(solution)/shard_map/all_to_all | solution.py:475
  55.2 1.8 %collective-permute-done.7.other = bf16[672,512]{1,0:T(8,128)(2,1)S(1)} collective-permute-done((bf16[672,512]{1,0:T(8,128)(2,1)S(1)}, bf16[672,512]{1,0:T(8,128)(2,1)S(1)}, u32[]{:S(2)}, u32[]{:S(2)}) %collective-permute-start.7) | collective-permute-done | bytes 688160 | tf_op jit(solution)/shard_map/ppermute | solution.py:46
  57.0 1.6 %copy-done.1 = bf16[1024,1024]{1,0:T(8,128)(2,1)S(1)} copy-done((bf16[1024,1024]{1,0:T(8,128)(2,1)S(1)}, bf16[1024,1024]{1,0:T(8,128)(2,1)}, u32[]{:S(2)}) %copy-start.1) | copy-done | bytes 2097176
  58.6 3.1 %table.1 = (bf16[680,128]{1,0:T(8,128)(2,1)S(1)}, bf16[680,128]{1,0:T(8,128)(2,1)S(1)}, bf16[680,128]{1,0:T(8,128)(2,1)S(1)}, bf16[680,128]{1,0:T(8,128)(2,1)S(1...) custom-call(s32[6]{0:T(128)S(1)} %stack.27.s, ...), custom_call_target="tpu_custom_call" | custom-call | flops 1400000000 | bytes 1048576 | tf_op jit(solution)/shard_map/table/pallas_call | solution.py:313
  63.0 1.5 %collective-permute-start.9 = (bf16[680,128]{1,0:T(8,128)(2,1)S(1)}, bf16[680,128]{1,0:T(8,128)(2,1)S(1)}, u32[]{:S(2)}, u32[]{:S(2)}) collective-permute-start(bf16[680,128]{1,0:T(8,128)(2,1)S(1)} %get-tuple-element.43), channel_id=1, source_target_pairs={{0,64},{32,96},{64,128},{96,160},{128,192},{160,224},{192,0},{224,... | collective-permute-start | bytes 522248 | tf_op jit(solution)/shard_map/ppermute | solution.py:462
  67.0 2.6 %collective-permute-start.12 = (bf16[680,128]{1,0:T(8,128)(2,1)S(1)}, bf16[680,128]{1,0:T(8,128)(2,1)S(1)}, u32[]{:S(2)}, u32[]{:S(2)}) collective-permute-start(bf16[680,128]{1,0:T(8,128)(2,1)S(1)} %get-tuple-element.46), channel_id=1, source_target_pairs={{0,160},{32,128},{64,224},{96,192},{128,32},{160,0},{192,96},{224,... | collective-permute-start | bytes 522248 | tf_op jit(solution)/shard_map/ppermute | solution.py:462
  69.6 1.5 %collective-permute-start.13 = (bf16[680,128]{1,0:T(8,128)(2,1)S(1)}, bf16[680,128]{1,0:T(8,128)(2,1)S(1)}, u32[]{:S(2)}, u32[]{:S(2)}) collective-permute-start(bf16[680,128]{1,0:T(8,128)(2,1)S(1)} %get-tuple-element.47), channel_id=1, source_target_pairs={{0,192},{32,224},{64,0},{96,32},{128,64},{160,96},{192,128},{224,1... | collective-permute-start | bytes 522248 | tf_op jit(solution)/shard_map/ppermute | solution.py:462
  71.6 2.1 %collective-permute-done.10.refs_3_ = bf16[680,128]{1,0:T(8,128)(2,1)S(1)} collective-permute-done((bf16[680,128]{1,0:T(8,128)(2,1)S(1)}, bf16[680,128]{1,0:T(8,128)(2,1)S(1)}, u32[]{:S(2)}, u32[]{:S(2)}) %collective-permute-start.10) | collective-permute-done | bytes 174112 | tf_op jit(solution)/shard_map/ppermute | solution.py:462
  73.7 8.3 %collective-permute-done.11.refs_4_ = bf16[680,128]{1,0:T(8,128)(2,1)S(1)} collective-permute-done((bf16[680,128]{1,0:T(8,128)(2,1)S(1)}, bf16[680,128]{1,0:T(8,128)(2,1)S(1)}, u32[]{:S(2)}, u32[]{:S(2)}) %collective-permute-start.11) | collective-permute-done | bytes 174112 | tf_op jit(solution)/shard_map/ppermute | solution.py:462
  84.0 16.3 %all-to-all-start.2 = ((bf16[8,672,128]{2,1,0:T(8,128)(2,1)}), bf16[8,672,128]{2,1,0:T(8,128)(2,1)S(1)}, u32[]{:S(2)}, u32[]{:S(2)}) async-start(bf16[8,672,128]{2,1,0:T(8,128)(2,1)} %gather.1), calls=%async_computation.2 | async-start | bytes 2752512 | tf_op jit(solution)/shard_map/all_to_all | solution.py:475
  102.9 2.0 %collective-permute-start.17 = (bf16[72,256]{1,0:T(8,128)(2,1)S(1)}, bf16[72,256]{1,0:T(8,128)(2,1)S(1)}, u32[]{:S(2)}, u32[]{:S(2)}) collective-permute-start(bf16[72,256]{1,0:T(8,128)(2,1)S(1)} %get-tuple-element.53), channel_id=1, source_target_pairs={{0,3},{1,2},{2,1},{3,0},{4,7},{5,6},{6,5},{7,4},{8,11},{9,10},{10,... | collective-permute-start | bytes 110600 | tf_op jit(solution)/shard_map/ppermute | solution.py:517
  104.9 10.6 %collective-permute-done.16.far = bf16[72,256]{1,0:T(8,128)(2,1)S(1)} collective-permute-done((bf16[72,256]{1,0:T(8,128)(2,1)S(1)}, bf16[72,256]{1,0:T(8,128)(2,1)S(1)}, u32[]{:S(2)}, u32[]{:S(2)}) %collective-permute-start.16) | collective-permute-done | bytes 36896 | tf_op jit(solution)/shard_map/ppermute | solution.py:517
  115.5 2.4 %collective-permute-done.17.both = bf16[72,256]{1,0:T(8,128)(2,1)S(1)} collective-permute-done((bf16[72,256]{1,0:T(8,128)(2,1)S(1)}, bf16[72,256]{1,0:T(8,128)(2,1)S(1)}, u32[]{:S(2)}, u32[]{:S(2)}) %collective-permute-start.17) | collective-permute-done | bytes 36896 | tf_op jit(solution)/shard_map/ppermute | solution.py:517
  118.6 3.0 %collective-permute-start.24 = (bf16[136,256]{1,0:T(8,128)(2,1)S(1)}, bf16[136,256]{1,0:T(8,128)(2,1)S(1)}, u32[]{:S(2)}, u32[]{:S(2)}) collective-permute-start(bf16[136,256]{1,0:T(8,128)(2,1)S(1)} %share.1.refs_0_), channel_id=1, source_target_pairs={{0,28},{4,0},{8,4},{12,8},{16,12},{20,16},{24,20},{28,24},{1,29},{... | collective-permute-start | bytes 208904 | tf_op jit(solution)/shard_map/ppermute | solution.py:471
  121.6 2.1 %collective-permute-start.23 = (bf16[136,256]{1,0:T(8,128)(2,1)S(1)}, bf16[136,256]{1,0:T(8,128)(2,1)S(1)}, u32[]{:S(2)}, u32[]{:S(2)}) collective-permute-start(bf16[136,256]{1,0:T(8,128)(2,1)S(1)} %share.1.refs_0_), channel_id=1, source_target_pairs={{0,24},{4,28},{8,0},{12,4},{16,8},{20,12},{24,16},{28,20},{1,25},{... | collective-permute-start | bytes 208904 | tf_op jit(solution)/shard_map/ppermute | solution.py:471
  124.8 3.3 %collective-permute-start.21 = (bf16[136,256]{1,0:T(8,128)(2,1)S(1)}, bf16[136,256]{1,0:T(8,128)(2,1)S(1)}, u32[]{:S(2)}, u32[]{:S(2)}) collective-permute-start(bf16[136,256]{1,0:T(8,128)(2,1)S(1)} %share.1.refs_0_), channel_id=1, source_target_pairs={{0,16},{4,20},{8,24},{12,28},{16,0},{20,4},{24,8},{28,12},{1,17},{... | collective-permute-start | bytes 208904 | tf_op jit(solution)/shard_map/ppermute | solution.py:471
  128.1 3.3 %collective-permute-start.19 = (bf16[136,256]{1,0:T(8,128)(2,1)S(1)}, bf16[136,256]{1,0:T(8,128)(2,1)S(1)}, u32[]{:S(2)}, u32[]{:S(2)}) collective-permute-start(bf16[136,256]{1,0:T(8,128)(2,1)S(1)} %share.1.refs_0_), channel_id=1, source_target_pairs={{0,8},{4,12},{8,16},{12,20},{16,24},{20,28},{24,0},{28,4},{1,9},{5... | collective-permute-start | bytes 208904 | tf_op jit(solution)/shard_map/ppermute | solution.py:471
  132.6 1.4 collective-permute-done.21.refs_4_
  134.0 4.8 %collective-permute-done.20.refs_3_ = bf16[136,256]{1,0:T(8,128)(2,1)S(1)} collective-permute-done((bf16[136,256]{1,0:T(8,128)(2,1)S(1)}, bf16[136,256]{1,0:T(8,128)(2,1)S(1)}, u32[]{:S(2)}, u32[]{:S(2)}) %collective-permute-start.20) | collective-permute-done | bytes 69664 | tf_op jit(solution)/shard_map/ppermute | solution.py:471
  138.8 2.7 %collective-permute-done.19.refs_2_ = bf16[136,256]{1,0:T(8,128)(2,1)S(1)} collective-permute-done((bf16[136,256]{1,0:T(8,128)(2,1)S(1)}, bf16[136,256]{1,0:T(8,128)(2,1)S(1)}, u32[]{:S(2)}, u32[]{:S(2)}) %collective-permute-start.19) | collective-permute-done | bytes 69664 | tf_op jit(solution)/shard_map/ppermute | solution.py:471
  141.5 1.9 %region_final.1 = (bf16[2,8,64,256]{3,2,1,0:T(8,128)(2,1)}, f32[1,1]{1,0:T(1,128)}) custom-call(s32[6]{0:T(128)S(1)} %stack.27.s, f32[1,1]{1,0:T(1,128)} %get-tuple-element.33.count, bf16[136,256]{1,0:T(8,128)(2,1)S(1)} %share.1.refs_0_, bf16[136,256]{1,0:T(8,128)(2,1)S(1)} %collective-permute-done.18.refs_1_, ...), custom_call_target="tpu_custom_call" | custom-call | flops 10000000 | bytes 1048576 | tf_op jit(solution)/shard_map/region_final/pallas_call | solution.py:444
  143.5 1.9 %table_final.1 = bf16[2688,256]{1,0:T(8,128)(2,1)} custom-call(s32[6]{0:T(128)S(1)} %stack.27.s, bf16[8,672,128]{2,1,0:T(8,128)(2,1)S(1)} %all-to-all-done.2.tables), custom_call_target="tpu_custom_call" | custom-call | flops 10000000 | bytes 1048576 | tf_op jit(solution)/shard_map/table_final/pallas_call | solution.py:422
  (65 shorter events, 19.0 us)
Async XLA Ops:
  1.6 25.3 %copy-start.6 = (bf16[2688,256]{1,0:T(8,128)(2,1)S(1)}, bf16[2688,256]{1,0:T(8,128)(2,1)}, u32[]{:S(2)}) copy-start(bf16[2688,256]{1,0:T(8,128)(2,1)} %x.1) | copy-start | bytes 4128772
  1.6 7.6 %collective-permute-start.1 = (bf16[336,256]{1,0:T(8,128)(2,1)S(1)}, bf16[336,256]{1,0:T(8,128)(2,1)S(1)}, u32[]{:S(2)}, u32[]{:S(2)}) collective-permute-start(bf16[336,256]{1,0:T(8,128)(2,1)S(1)} %rows.1), channel_id=1, source_target_pairs={{0,2},{2,0},{1,3},{3,1},{4,6},{6,4},{5,7},{7,5},{8,10},{10,8},{9,1... | collective-permute-start | bytes 516104 | tf_op jit(solution)/shard_map/ppermute | solution.py:46
  6.5 2.6 %collective-permute-start.2 = (f32[8,128]{1,0:T(8,128)S(1)}, f32[8,128]{1,0:T(8,128)S(1)}, u32[]{:S(2)}, u32[]{:S(2)}) collective-permute-start(f32[8,128]{1,0:T(8,128)S(1)} %broadcast_in_dim.15.mine), channel_id=1, source_target_pairs={{0,32},{32,0},{1,33},{33,1},{2,34},{34,2},{3,35},{35,3},{4,36},{36... | collective-permute-start | bytes 12296 | tf_op jit(solution)/shard_map/ppermute | solution.py:46
  10.1 14.1 %all-to-all-start = ((bf16[4,344,256]{2,1,0:T(8,128)(2,1)}), bf16[4,344,256]{2,1,0:T(8,128)(2,1)S(1)}, u32[]{:S(2)}, u32[]{:S(2)}) async-start(bf16[4,344,256]{2,1,0:T(8,128)(2,1)} %message.1), calls=%async_computation | async-start | bytes 1409024 | tf_op jit(solution)/shard_map/all_to_all | solution.py:475
  14.5 17.4 %copy-start.7 = (f32[1024]{0:T(1024)S(1)}, f32[1024]{0:T(1024)}, u32[]{:S(2)}) copy-start(f32[1024]{0:T(1024)} %param.9) | copy-start | bytes 12292
  14.5 17.4 %copy-start.8 = (f32[1024]{0:T(1024)S(1)}, f32[1024]{0:T(1024)}, u32[]{:S(2)}) copy-start(f32[1024]{0:T(1024)} %param.8) | copy-start | bytes 12292
  14.5 13.3 %collective-permute-start.5 = (bf16[1024,256]{1,0:T(8,128)(2,1)}, bf16[1024,256]{1,0:T(8,128)(2,1)}, u32[]{:S(2)}, u32[]{:S(2)}) collective-permute-start(bf16[1024,256]{1,0:T(8,128)(2,1)} %a.1), channel_id=1, source_target_pairs={{0,2},{2,0},{1,3},{3,1},{4,6},{6,4},{5,7},{7,5},{8,10},{10,8},{9,1... | collective-permute-start | bytes 1572872 | tf_op jit(solution)/shard_map/ppermute | solution.py:46
  24.2 10.7 %collective-permute-start.3 = (bf16[4,344,256]{2,1,0:T(8,128)(2,1)S(1)}, bf16[4,344,256]{2,1,0:T(8,128)(2,1)S(1)}, u32[]{:S(2)}, u32[]{:S(2)}) collective-permute-start(bf16[4,344,256]{2,1,0:T(8,128)(2,1)S(1)} %all-to-all-done.t2), channel_id=1, source_target_pairs={{0,1},{1,0},{2,3},{3,2},{4,5},{5,4},{6,7},{7,6},{8,9},{9,8},{10,11... | collective-permute-start | bytes 2113544 | tf_op jit(solution)/shard_map/ppermute | solution.py:46
  27.0 7.9 %collective-permute-start = (bf16[1344,256]{1,0:T(8,128)(2,1)S(1)}, bf16[1344,256]{1,0:T(8,128)(2,1)S(1)}, u32[]{:S(2)}, u32[]{:S(2)}) collective-permute-start(bf16[1344,256]{1,0:T(8,128)(2,1)S(1)} %constant_dynamic-slice_fusion.t0), channel_id=1, source_target_pairs={{0,1},{1,0},{2,3},{3,2},{4,5},{5,4},{6,7},{7,6},{8,9},{9,8},{10,11... | collective-permute-start | bytes 2064392 | tf_op jit(solution)/shard_map/ppermute | solution.py:46
  27.1 5.0 %collective-permute-start.4 = (bf16[1024,256]{1,0:T(8,128)(2,1)}, bf16[1024,256]{1,0:T(8,128)(2,1)}, u32[]{:S(2)}, u32[]{:S(2)}) collective-permute-start(bf16[1024,256]{1,0:T(8,128)(2,1)} %a.1), channel_id=1, source_target_pairs={{0,1},{1,0},{2,3},{3,2},{4,5},{5,4},{6,7},{7,6},{8,9},{9,8},{10,11... | collective-permute-start | bytes 1572872 | tf_op jit(solution)/shard_map/ppermute | solution.py:46
  27.9 4.7 %collective-permute-start.6 = (bf16[1024,256]{1,0:T(8,128)(2,1)}, bf16[1024,256]{1,0:T(8,128)(2,1)}, u32[]{:S(2)}, u32[]{:S(2)}) collective-permute-start(bf16[1024,256]{1,0:T(8,128)(2,1)} %collective-permute-done.5.c), channel_id=1, source_target_pairs={{0,1},{1,0},{2,3},{3,2},{4,5},{5,4},{6,7},{7,6},{8,9},{9,8},{10,11... | collective-permute-start | bytes 1572872 | tf_op jit(solution)/shard_map/ppermute | solution.py:46
  46.2 37.8 %all-to-all-start.1 = ((bf16[8,64,1024]{2,1,0:T(8,128)(2,1)}), bf16[8,64,1024]{2,1,0:T(8,128)(2,1)S(1)}, u32[]{:S(2)}, u32[]{:S(2)}) async-start(bf16[8,64,1024]{2,1,0:T(8,128)(2,1)} %get-tuple-element.38), calls=%async_computation.1 | async-start | bytes 2097152 | tf_op jit(solution)/shard_map/all_to_all | solution.py:475
  54.5 2.5 %collective-permute-start.7 = (bf16[672,512]{1,0:T(8,128)(2,1)S(1)}, bf16[672,512]{1,0:T(8,128)(2,1)S(1)}, u32[]{:S(2)}, u32[]{:S(2)}) collective-permute-start(bf16[672,512]{1,0:T(8,128)(2,1)S(1)} %copy-done.3), channel_id=1, source_target_pairs={{0,1},{1,0},{2,3},{3,2},{4,5},{5,4},{6,7},{7,6},{8,9},{9,8},{10,11... | collective-permute-start | bytes 2064392 | tf_op jit(solution)/shard_map/ppermute | solution.py:46
  61.8 7.8 %collective-permute-start.8 = (bf16[680,128]{1,0:T(8,128)(2,1)S(1)}, bf16[680,128]{1,0:T(8,128)(2,1)S(1)}, u32[]{:S(2)}, u32[]{:S(2)}) collective-permute-start(bf16[680,128]{1,0:T(8,128)(2,1)S(1)} %get-tuple-element.42), channel_id=1, source_target_pairs={{0,32},{32,0},{64,96},{96,64},{128,160},{160,128},{192,224},{224,1... | collective-permute-start | bytes 522248 | tf_op jit(solution)/shard_map/ppermute | solution.py:462
  63.0 8.0 %collective-permute-start.9 = (bf16[680,128]{1,0:T(8,128)(2,1)S(1)}, bf16[680,128]{1,0:T(8,128)(2,1)S(1)}, u32[]{:S(2)}, u32[]{:S(2)}) collective-permute-start(bf16[680,128]{1,0:T(8,128)(2,1)S(1)} %get-tuple-element.43), channel_id=1, source_target_pairs={{0,64},{32,96},{64,128},{96,160},{128,192},{160,224},{192,0},{224,... | collective-permute-start | bytes 522248 | tf_op jit(solution)/shard_map/ppermute | solution.py:462
  64.5 9.2 %collective-permute-start.10 = (bf16[680,128]{1,0:T(8,128)(2,1)S(1)}, bf16[680,128]{1,0:T(8,128)(2,1)S(1)}, u32[]{:S(2)}, u32[]{:S(2)}) collective-permute-start(bf16[680,128]{1,0:T(8,128)(2,1)S(1)} %get-tuple-element.44), channel_id=1, source_target_pairs={{0,96},{32,64},{64,160},{96,128},{128,224},{160,192},{192,32},{224... | collective-permute-start | bytes 522248 | tf_op jit(solution)/shard_map/ppermute | solution.py:462
  65.7 16.3 %collective-permute-start.11 = (bf16[680,128]{1,0:T(8,128)(2,1)S(1)}, bf16[680,128]{1,0:T(8,128)(2,1)S(1)}, u32[]{:S(2)}, u32[]{:S(2)}) collective-permute-start(bf16[680,128]{1,0:T(8,128)(2,1)S(1)} %get-tuple-element.45), channel_id=1, source_target_pairs={{0,128},{32,160},{64,192},{96,224},{128,0},{160,32},{192,64},{224,... | collective-permute-start | bytes 522248 | tf_op jit(solution)/shard_map/ppermute | solution.py:462
  67.0 15.0 %collective-permute-start.12 = (bf16[680,128]{1,0:T(8,128)(2,1)S(1)}, bf16[680,128]{1,0:T(8,128)(2,1)S(1)}, u32[]{:S(2)}, u32[]{:S(2)}) collective-permute-start(bf16[680,128]{1,0:T(8,128)(2,1)S(1)} %get-tuple-element.46), channel_id=1, source_target_pairs={{0,160},{32,128},{64,224},{96,192},{128,32},{160,0},{192,96},{224,... | collective-permute-start | bytes 522248 | tf_op jit(solution)/shard_map/ppermute | solution.py:462
  69.6 12.4 %collective-permute-start.13 = (bf16[680,128]{1,0:T(8,128)(2,1)S(1)}, bf16[680,128]{1,0:T(8,128)(2,1)S(1)}, u32[]{:S(2)}, u32[]{:S(2)}) collective-permute-start(bf16[680,128]{1,0:T(8,128)(2,1)S(1)} %get-tuple-element.47), channel_id=1, source_target_pairs={{0,192},{32,224},{64,0},{96,32},{128,64},{160,96},{192,128},{224,1... | collective-permute-start | bytes 522248 | tf_op jit(solution)/shard_map/ppermute | solution.py:462
  71.1 10.9 %collective-permute-start.14 = (bf16[680,128]{1,0:T(8,128)(2,1)S(1)}, bf16[680,128]{1,0:T(8,128)(2,1)S(1)}, u32[]{:S(2)}, u32[]{:S(2)}) collective-permute-start(bf16[680,128]{1,0:T(8,128)(2,1)S(1)} %get-tuple-element.48), channel_id=1, source_target_pairs={{0,224},{32,192},{64,32},{96,0},{128,96},{160,64},{192,160},{224,1... | collective-permute-start | bytes 522248 | tf_op jit(solution)/shard_map/ppermute | solution.py:462
  82.2 0.7 collective-permute-start.25
  84.0 59.5 %all-to-all-start.2 = ((bf16[8,672,128]{2,1,0:T(8,128)(2,1)}), bf16[8,672,128]{2,1,0:T(8,128)(2,1)S(1)}, u32[]{:S(2)}, u32[]{:S(2)}) async-start(bf16[8,672,128]{2,1,0:T(8,128)(2,1)} %gather.1), calls=%async_computation.2 | async-start | bytes 2752512 | tf_op jit(solution)/shard_map/all_to_all | solution.py:475
  100.6 4.3 %collective-permute-start.15 = (bf16[72,256]{1,0:T(8,128)(2,1)S(1)}, bf16[72,256]{1,0:T(8,128)(2,1)S(1)}, u32[]{:S(2)}, u32[]{:S(2)}) collective-permute-start(bf16[72,256]{1,0:T(8,128)(2,1)S(1)} %get-tuple-element.51), channel_id=1, source_target_pairs={{0,1},{1,0},{2,3},{3,2},{4,5},{5,4},{6,7},{7,6},{8,9},{9,8},{10,11... | collective-permute-start | bytes 110600 | tf_op jit(solution)/shard_map/ppermute | solution.py:517
  101.7 13.8 %collective-permute-start.16 = (bf16[72,256]{1,0:T(8,128)(2,1)S(1)}, bf16[72,256]{1,0:T(8,128)(2,1)S(1)}, u32[]{:S(2)}, u32[]{:S(2)}) collective-permute-start(bf16[72,256]{1,0:T(8,128)(2,1)S(1)} %get-tuple-element.52), channel_id=1, source_target_pairs={{0,2},{1,3},{2,0},{3,1},{4,6},{5,7},{6,4},{7,5},{8,10},{9,11},{10,... | collective-permute-start | bytes 110600 | tf_op jit(solution)/shard_map/ppermute | solution.py:517
  102.9 15.1 %collective-permute-start.17 = (bf16[72,256]{1,0:T(8,128)(2,1)S(1)}, bf16[72,256]{1,0:T(8,128)(2,1)S(1)}, u32[]{:S(2)}, u32[]{:S(2)}) collective-permute-start(bf16[72,256]{1,0:T(8,128)(2,1)S(1)} %get-tuple-element.53), channel_id=1, source_target_pairs={{0,3},{1,2},{2,1},{3,0},{4,7},{5,6},{6,5},{7,4},{8,11},{9,10},{10,... | collective-permute-start | bytes 110600 | tf_op jit(solution)/shard_map/ppermute | solution.py:517
  118.6 9.5 %collective-permute-start.24 = (bf16[136,256]{1,0:T(8,128)(2,1)S(1)}, bf16[136,256]{1,0:T(8,128)(2,1)S(1)}, u32[]{:S(2)}, u32[]{:S(2)}) collective-permute-start(bf16[136,256]{1,0:T(8,128)(2,1)S(1)} %share.1.refs_0_), channel_id=1, source_target_pairs={{0,28},{4,0},{8,4},{12,8},{16,12},{20,16},{24,20},{28,24},{1,29},{... | collective-permute-start | bytes 208904 | tf_op jit(solution)/shard_map/ppermute | solution.py:471
  121.6 9.8 %collective-permute-start.23 = (bf16[136,256]{1,0:T(8,128)(2,1)S(1)}, bf16[136,256]{1,0:T(8,128)(2,1)S(1)}, u32[]{:S(2)}, u32[]{:S(2)}) collective-permute-start(bf16[136,256]{1,0:T(8,128)(2,1)S(1)} %share.1.refs_0_), channel_id=1, source_target_pairs={{0,24},{4,28},{8,0},{12,4},{16,8},{20,12},{24,16},{28,20},{1,25},{... | collective-permute-start | bytes 208904 | tf_op jit(solution)/shard_map/ppermute | solution.py:471
  123.7 9.0 %collective-permute-start.22 = (bf16[136,256]{1,0:T(8,128)(2,1)S(1)}, bf16[136,256]{1,0:T(8,128)(2,1)S(1)}, u32[]{:S(2)}, u32[]{:S(2)}) collective-permute-start(bf16[136,256]{1,0:T(8,128)(2,1)S(1)} %share.1.refs_0_), channel_id=1, source_target_pairs={{0,20},{4,24},{8,28},{12,0},{16,4},{20,8},{24,12},{28,16},{1,21},{... | collective-permute-start | bytes 208904 | tf_op jit(solution)/shard_map/ppermute | solution.py:471
  124.8 9.1 %collective-permute-start.21 = (bf16[136,256]{1,0:T(8,128)(2,1)S(1)}, bf16[136,256]{1,0:T(8,128)(2,1)S(1)}, u32[]{:S(2)}, u32[]{:S(2)}) collective-permute-start(bf16[136,256]{1,0:T(8,128)(2,1)S(1)} %share.1.refs_0_), channel_id=1, source_target_pairs={{0,16},{4,20},{8,24},{12,28},{16,0},{20,4},{24,8},{28,12},{1,17},{... | collective-permute-start | bytes 208904 | tf_op jit(solution)/shard_map/ppermute | solution.py:471
  128.1 10.7 %collective-permute-start.20 = (bf16[136,256]{1,0:T(8,128)(2,1)S(1)}, bf16[136,256]{1,0:T(8,128)(2,1)S(1)}, u32[]{:S(2)}, u32[]{:S(2)}) collective-permute-start(bf16[136,256]{1,0:T(8,128)(2,1)S(1)} %share.1.refs_0_), channel_id=1, source_target_pairs={{0,12},{4,16},{8,20},{12,24},{16,28},{20,0},{24,4},{28,8},{1,13},{... | collective-permute-start | bytes 208904 | tf_op jit(solution)/shard_map/ppermute | solution.py:471
  128.1 13.4 %collective-permute-start.19 = (bf16[136,256]{1,0:T(8,128)(2,1)S(1)}, bf16[136,256]{1,0:T(8,128)(2,1)S(1)}, u32[]{:S(2)}, u32[]{:S(2)}) collective-permute-start(bf16[136,256]{1,0:T(8,128)(2,1)S(1)} %share.1.refs_0_), channel_id=1, source_target_pairs={{0,8},{4,12},{8,16},{12,20},{16,24},{20,28},{24,0},{28,4},{1,9},{5... | collective-permute-start | bytes 208904 | tf_op jit(solution)/shard_map/ppermute | solution.py:471
  131.4 10.1 %collective-permute-start.18 = (bf16[136,256]{1,0:T(8,128)(2,1)S(1)}, bf16[136,256]{1,0:T(8,128)(2,1)S(1)}, u32[]{:S(2)}, u32[]{:S(2)}) collective-permute-start(bf16[136,256]{1,0:T(8,128)(2,1)S(1)} %share.1.refs_0_), channel_id=1, source_target_pairs={{0,4},{4,8},{8,12},{12,16},{16,20},{20,24},{24,28},{28,0},{1,5},{5... | collective-permute-start | bytes 208904 | tf_op jit(solution)/shard_map/ppermute | solution.py:471
  (6 other events, 36.7 us)
